TPU v7x, 256 devices: a whole 4x4x8 slice. The times are simulated.
256 devices in a mesh: img: 16 (over x, z_lo, core), patch: 16 (over y, z_hi).
Axes of the slice: x: 4, y: 4, z: 8 (z_hi: 4, z_lo: 2; z = z_hi * 2 + z_lo), core: 2. Of those that a mesh axis runs over, the one named last changes fastest.
Arguments:
- hidden: bfloat16 [32, 16, 128, 640], P('img', 'patch'), may hold values from -100 to 100
- stale_attn_in: bfloat16 [32, 16, 128, 640], P('img', 'patch'), may hold values from -100 to 100
- stale_conv_in: bfloat16 [32, 16, 128, 640], P('img', 'patch'), may hold values from -6 to 6
- ln_gain: float32 [640], replicated, may hold values from 0.25 to 1.75
- ln_bias: float32 [640], replicated, may hold values from -2 to 2
- w_qkv: bfloat16 [640, 1920], replicated, may hold values from -3 to 3
- w_out: bfloat16 [640, 640], replicated, may hold values from -0.25 to 0.25
- gn_gain: float32 [640], replicated, may hold values from 0.25 to 1.75
- gn_bias: float32 [640], replicated, may hold values from -1.5 to 1.5
- conv_weight: bfloat16 [3, 3, 640, 640], replicated, may hold values from -0.078125 to 0.078125
- conv_bias: float32 [640], replicated, may hold values from -1.5 to 1.5
- time_shift: float32 [32, 640], P('img'), may hold values from -6 to 6
Outputs:
- block_out: bfloat16 [32, 16, 128, 640], P('img', 'patch')
All inputs are finite; a program needn't handle non-finite values.
Results may differ from a plain program's by a relative error of at most 0.0075.
The roundings to bfloat16 on the way count: a program that leaves them out, or rounds other values in their place, can miss the bound.
Values may be sent and summed in bfloat16 or wider, within the bound.
No kernel may reach another device: no remote copies, remote signals or barrier semaphores. Data moves between devices by JAX's collectives and lax.ppermute only.
A program may use at most 128 MiB of HBM per device.

v0:
```python
import functools

import jax
import jax.numpy as jnp
from jax import lax
from jax.sharding import Mesh
from jax.sharding import PartitionSpec as P

GROUPS = 32
HEAD_DIM = 64
PATCH = ("patch_0", "patch_1")


EPSILON = 1e-05


def over_axes(shard, axes):
    return functools.reduce(lax.psum, axes, shard)


def extended(block, sides, width):
    for axis, dim in sides:
        count = lax.axis_size(axis)
        forward = [(i, i + 1) for i in range(count - 1)]
        backward = [(target, source) for source, target in forward]
        low = lax.ppermute(
            lax.slice_in_dim(block, block.shape[dim] - width, None, axis=dim), axis, forward
        )
        high = lax.ppermute(lax.slice_in_dim(block, 0, width, axis=dim), axis, backward)
        block = jnp.concatenate([low, block, high], axis=dim)
    return block


def layer_norm(values, gain, bias):
    values = values.astype(jnp.float32)
    centre = jnp.mean(values, -1, keepdims=True)
    centred = values - centre
    spread = jnp.mean(centred * centred, -1, keepdims=True)
    return (centred * lax.rsqrt(spread + EPSILON) * gain + bias).astype(jnp.bfloat16)


def absorb(softmax_state, queries, key_rows, value_rows, blocked):
    running_max, weight_sum, accum = softmax_state
    samples, key_count, channels = key_rows.shape
    head_count = channels // HEAD_DIM
    keys_split = key_rows.reshape(samples, key_count, head_count, HEAD_DIM)
    values_split = value_rows.reshape(samples, key_count, head_count, HEAD_DIM)
    scores = jnp.einsum(
        "sqhd,skhd->shqk", queries, keys_split, preferred_element_type=jnp.float32
    ) * HEAD_DIM ** (-0.5)
    scores = jnp.where(blocked[None, None, None, :], -jnp.inf, scores)
    new_max = jnp.maximum(running_max, jnp.max(scores, -1))
    rescale = jnp.exp(running_max - new_max)
    weights = jnp.exp(scores - new_max[..., None])
    weight_sum = weight_sum * rescale + jnp.sum(weights, -1)
    accum = accum * rescale[..., None] + jnp.einsum(
        "shqk,skhd->shqd",
        weights.astype(jnp.bfloat16),
        values_split,
        preferred_element_type=jnp.float32,
    )
    return (new_max, weight_sum, accum)


def shards(
    hidden,
    stale_attn_in,
    stale_conv_in,
    ln_gain,
    ln_bias,
    w_qkv,
    w_out,
    gn_gain,
    gn_bias,
    conv_weight,
    conv_bias,
    time_shift,
):
    samples, rows_dev, col_count, channels = hidden.shape
    head_count = channels // HEAD_DIM
    local_count = rows_dev * col_count
    own_start = lax.axis_index(PATCH) * local_count
    fresh_in = layer_norm(hidden, ln_gain, ln_bias).reshape(samples, local_count, channels)
    stale_in = layer_norm(stale_attn_in, ln_gain, ln_bias).reshape(samples, local_count, channels)
    fresh_qkv = jnp.einsum(
        "stc,cd->std", fresh_in, w_qkv, preferred_element_type=jnp.float32
    ).astype(jnp.bfloat16)
    queries = fresh_qkv[..., :channels].reshape(samples, local_count, head_count, HEAD_DIM)
    w_pair = w_qkv[:, channels:]
    initial = (
        jnp.full((samples, head_count, local_count), -jnp.inf, jnp.float32),
        jnp.zeros((samples, head_count, local_count), jnp.float32),
        jnp.zeros((samples, head_count, local_count, HEAD_DIM), jnp.float32),
    )
    no_block = jnp.zeros((local_count,), bool)
    softmax_state = absorb(
        initial,
        queries,
        fresh_qkv[..., channels : 2 * channels],
        fresh_qkv[..., 2 * channels :],
        no_block,
    )
    block_rows = lax.all_gather(stale_in, PATCH, axis=1, tiled=True)
    pair_rows = jnp.einsum(
        "snc,cd->snd", block_rows, w_pair, preferred_element_type=jnp.float32
    ).astype(jnp.bfloat16)
    positions = jnp.arange(block_rows.shape[1], dtype=jnp.int32)
    blocked = (positions >= own_start) & (positions < own_start + local_count)
    softmax_state = absorb(
        softmax_state, queries, pair_rows[..., :channels], pair_rows[..., channels:], blocked
    )
    running_max, weight_sum, accum = softmax_state
    attended = (
        (accum / weight_sum[..., None])
        .transpose(0, 2, 1, 3)
        .reshape(samples, local_count, channels)
        .astype(jnp.bfloat16)
    )
    attention_out = jnp.einsum("stc,cd->std", attended, w_out, preferred_element_type=jnp.float32)
    residual = (
        hidden.reshape(samples, local_count, channels).astype(jnp.float32) + attention_out
    ).astype(jnp.bfloat16)
    grouped = residual.astype(jnp.float32).reshape(samples, local_count, GROUPS, channels // GROUPS)
    cell_count = lax.axis_size(PATCH) * local_count * (channels // GROUPS)
    group_total, group_squares = (
        over_axes(jnp.sum(grouped, axis=(1, 3)), PATCH),
        over_axes(jnp.sum(grouped * grouped, axis=(1, 3)), PATCH),
    )
    group_mean = group_total / cell_count
    group_var = group_squares / cell_count - group_mean * group_mean
    centred = grouped - group_mean[:, None, :, None]
    normalized = (centred * lax.rsqrt(group_var + EPSILON)[:, None, :, None]).reshape(
        samples, local_count, channels
    )
    activated = (
        jax.nn.silu(normalized * gn_gain + gn_bias)
        .astype(jnp.bfloat16)
        .reshape(samples, rows_dev, col_count, channels)
    )
    stale_framed = extended(stale_conv_in, ((PATCH, 1),), 1)
    framed = jnp.concatenate([stale_framed[:, :1], activated, stale_framed[:, rows_dev + 1 :]], 1)
    framed = jnp.pad(framed, ((0, 0), (0, 0), (1, 1), (0, 0)))
    windows = [
        framed[:, tap_row : tap_row + rows_dev, tap_col : tap_col + col_count, :]
        for tap_row in range(3)
        for tap_col in range(3)
    ]
    unfolded = jnp.concatenate(windows, -1).reshape(samples * local_count, 9 * channels)
    convolved = jnp.dot(
        unfolded, conv_weight.reshape(9 * channels, channels), preferred_element_type=jnp.float32
    )
    summed_out = (
        convolved.reshape(samples, rows_dev, col_count, channels)
        + conv_bias
        + time_shift[:, None, None, :]
        + residual.astype(jnp.float32).reshape(samples, rows_dev, col_count, channels)
    )
    return summed_out.astype(jnp.bfloat16)


def solution(mesh):
    split = Mesh(mesh.devices.reshape(mesh.shape["img"], 4, 4), ("img", "patch_0", "patch_1"))
    return jax.shard_map(
        shards,
        mesh=split,
        in_specs=(
            P("img", PATCH, None, None),
            P("img", PATCH, None, None),
            P("img", PATCH, None, None),
            P(),
            P(),
            P(),
            P(),
            P(),
            P(),
            P(),
            P(),
            P("img", None),
        ),
        out_specs=P("img", PATCH, None, None),
        check_vma=False,
    )
```

profile of v0, /device:TPU:2, one launch (start us, length us, event | category | flops | bytes accessed | tf_op | source)
XLA Modules:
  0.0 191.6 jit_solution(10955897671697256372)
XLA Ops:
  6.5 0.0 copy-start
  6.5 0.0 all-gather.3.cloned.1.call-start
  6.5 1.2 convert_reduce_fusion.1
  7.7 1.2 fusion.54
  8.9 1.9 %fusion.57 = bf16[2,1,128,640]{3,2,0,1:T(8,128)(2,1)} fusion(bf16[2,1,128,640]{3,2,1,0:T(8,128)(2,1)} %param.13, f32[2,128]{1,0:T(2,128)S(1)} %add_rsqrt_fusion.1, f32[2,128]{1,0:T(2,128)S(1)} %broadcast_multiply_fusion.1, f32[640]{0:T(1024)} %param.16, f32[640]{0:T(1024)} %param.15), kind=kLoop, calls=%fused_computation.59 | loop fusion | flops 983040 | bytes 662528 | tf_op jit(solution)/shard_map/convert_element_type | solution.py:39
  10.9 0.0 all-gather.3.cloned.1.call-update
  10.9 1.3 collective-permute-start.1
  12.2 5.8 %collective-permute-start = (bf16[2,1,128,640]{3,2,0,1:T(8,128)(2,1)}, bf16[2,1,128,640]{3,2,0,1:T(8,128)(2,1)S(1)}, u32[]{:S(2)}, u32[]{:S(2)}) collective-permute-start(bf16[2,1,128,640]{3,2,0,1:T(8,128)(2,1)} %bitcast.118), channel_id=1, source_target_pairs={{0,1},{1,2},{2,3},{3,4},{4,5},{5,6},{6,7},{7,8},{8,9},{9,10},{10,1... | collective-permute-start | bytes 983048 | tf_op jit(solution)/shard_map/ppermute | solution.py:26
  18.0 1.1 convert_reduce_fusion
  19.1 1.2 fusion.50
  20.3 2.9 %convolution_convert_fusion.1 = bf16[2,128,1920]{2,1,0:T(8,128)(2,1)S(1)} fusion(bf16[640,1920]{1,0:T(8,128)(2,1)} %param.17, bf16[2,1,128,640]{3,2,1,0:T(8,128)(2,1)} %param.12, f32[640]{0:T(1024)} %param.16, f32[640]{0:T(1024)} %param.15, f32[2,128]{1,0:T(2,128)S(1)} %add_rsqrt_fusion.2, f32[2,128]{1,0:T(2,128)S(1)} %broadcast_multiply_fusion.2), kind=kOutput, calls=%fused_computation.13 | convolution fusion | flops 630620160 | bytes 3775488 | tf_op jit(solution)/shard_map/stc,cd->std/dot_general | solution.py:85
  23.3 0.1 fusion.78
  23.4 0.2 copy.27
  23.6 0.2 copy.28
  23.8 0.9 copy.29
  24.7 0.4 fusion.79
  25.1 0.2 fusion.41
  25.3 75.6 %all-gather.3.cloned.1.call-done = bf16[2,1,2048,640]{3,2,0,1:T(8,128)(2,1)} async-done(((bf16[2,1,128,640]{3,2,0,1:T(8,128)(2,1)}), bf16[2,1,2048,640]{3,2,0,1:T(8,128)(2,1)}) %all-gather.3.cloned.1.call-update) | async-done | bytes 5242896 | tf_op jit(solution)/shard_map/all_gather | solution.py:103
  101.0 13.2 %convolution_convert_fusion = bf16[2,2048,1280]{1,2,0:T(8,128)(2,1)} fusion(bf16[2,1,2048,640]{3,2,0,1:T(8,128)(2,1)} %all-gather.3.cloned.1.call-done, bf16[640,1920]{1,0:T(8,128)(2,1)} %param.17), kind=kOutput, calls=%fused_computation.5 | convolution fusion | flops 6716129280 | bytes 17367040 | tf_op jit(solution)/shard_map/snc,cd->snd/dot_general | solution.py:104
  114.2 10.2 %fusion.77 = (bf16[2,2048,640]{1,2,0:T(8,128)(2,1)}, bf16[2,2048,640]{1,2,0:T(8,128)(2,1)}) fusion(bf16[2,2048,1280]{1,2,0:T(8,128)(2,1)} %convolution_convert_fusion), kind=kLoop, calls=%fused_computation.99 | loop fusion | bytes 20971520 | tf_op jit(solution)/shard_map/slice | solution.py:110
  124.4 5.1 %fusion = (f32[2,10,128]{2,1,0:T(8,128)S(1)}, f32[2,10,128,2048]{3,2,1,0:T(8,128)S(1)}) fusion(pred[2048]{0:T(1024)(128)(4,1)S(1)} %fusion.72, bf16[2,128,10,64]{1,3,2,0:T(8,128)(2,1)S(1)} %bitcast.112, bf16[2,2048,10,64]{1,3,2,0:T(8,128)(2,1)} %bitcast.109), kind=kOutput, calls=%fused_computation.2 | convolution fusion | flops 686814720 | bytes 26554368 | tf_op jit(solution)/shard_map/sqhd,skhd->shqk/dot_general | solution.py:48
  129.5 0.0 copy-start.1
  129.5 4.7 %fusion.1 = f32[2,10,128]{2,1,0:T(8,128)S(1)} fusion(f32[2,10,128,2048]{3,2,1,0:T(8,128)S(1)} %get-tuple-element.24, f32[2,10,128]{2,1,0:T(8,128)S(1)} %max.18, pred[2048]{0:T(1024)(128)(4,1)S(1)} %fusion.72), kind=kLoop, calls=%fused_computation.3 | loop fusion | flops 20968960 | bytes 20994048 | tf_op jit(solution)/shard_map/reduce_sum | solution.py:55
  134.2 2.3 %copy-done.1 = f32[2,10,128,2048]{3,2,1,0:T(8,128)} copy-done((f32[2,10,128,2048]{3,2,1,0:T(8,128)}, f32[2,10,128,2048]{3,2,1,0:T(8,128)S(1)}, u32[]{:S(2)}) %copy-start.1) | copy-done | bytes 20971544
  136.5 0.0 copy-start.3
  136.5 10.8 %fusion.17 = f32[2,128,10,64]{1,3,2,0:T(8,128)S(1)} fusion(bf16[2,2048,10,64]{1,3,2,0:T(8,128)(2,1)} %bitcast.110, f32[2,10,128,2048]{3,2,1,0:T(8,128)} %copy-done.1, f32[2,10,128]{2,1,0:T(8,128)S(1)} %max.18, pred[2048]{0:T(1024)(128)(4,1)S(1)} %fusion.72), kind=kOutput, calls=%fused_computation.26 | convolution fusion | flops 692060160 | bytes 26882048 | tf_op jit(solution)/shard_map/shqk,skhd->shqd/dot_general | solution.py:56
  147.3 0.0 copy-start.2
  147.4 0.0 copy-done.3
  147.4 0.0 copy-start.4
  147.4 0.0 copy-start.5
  147.4 0.3 fusion.31
  147.8 0.0 copy-done
  147.8 0.5 copy-done.2
  148.3 0.5 fusion.75
  148.8 0.1 reduce_sum.102
  148.9 0.1 reduce_sum.99
  149.1 0.1 reduce_sum.103
  149.1 0.1 reduce_sum.100
  149.2 10.2 %all-reduce.2 = (f32[2,32]{1,0:T(2,128)S(1)}, f32[2,32]{1,0:T(2,128)S(1)}) all-reduce(f32[2,32]{1,0:T(2,128)S(1)} %reduce_sum.103, f32[2,32]{1,0:T(2,128)S(1)} %reduce_sum.100), channel_id=1, replica_groups=mesh['img'=16,'patch_0'=4,'patch_1'=4] {'patch_0'}, use_global_device_ids=true, to_apply=%region_14.15 | all-reduce | flops 128 | bytes 1024 | tf_op jit(solution)/shard_map/psum | solution.py:18
  159.4 17.1 %all-reduce.1 = (f32[2,32]{1,0:T(2,128)S(1)}, f32[2,32]{1,0:T(2,128)S(1)}) all-reduce(f32[2,32]{1,0:T(2,128)S(1)} %get-tuple-element.9, f32[2,32]{1,0:T(2,128)S(1)} %get-tuple-element.10), channel_id=1, replica_groups=mesh['img'=16,'patch_0'=4,'patch_1'=4] {'patch_1'}, use_global_device_ids=true, to_apply=%region_15.16 | all-reduce | flops 128 | bytes 1024 | tf_op jit(solution)/shard_map/psum | solution.py:18
  176.6 0.1 mul.129
  176.7 0.1 mul.130
  176.8 0.1 sub.82
  176.9 0.1 sub.83
  177.0 0.0 copy-done.4
  177.0 0.0 copy-done.5
  177.0 0.2 fusion.67
  177.2 0.0 collective-permute-done.1
  177.2 0.0 collective-permute-done
  177.2 0.3 fusion.44
  177.6 0.0 copy-start.6
  177.6 0.0 copy-start.7
  177.6 0.1 slice_dynamic-update-slice_fusion.4
  177.8 0.3 constant_dynamic-update-slice_fusion.1
  178.0 0.1 slice_dynamic-update-slice_fusion.2
  178.2 0.1 slice_dynamic-update-slice_fusion
  178.4 0.0 copy-done.6
  178.4 0.0 copy-done.7
  178.4 6.4 %fusion.38 = bf16[2,1,128,640]{3,2,1,0:T(8,128)(2,1)} fusion(f32[2,128,640]{2,1,0:T(8,128)S(1)} %get-tuple-element.25, bf16[5760,640,1]{1,0,2:T(8,128)(2,1)} %bitcast.116, bf16[2,1,128,5760]{3,2,0,1:T(8,128)(2,1)S(1)} %slice_dynamic-update-slice_fusion, f32[2,640]{1,0:T(2,128)S(1)} %copy-done.6, f32[640]{0:T(1024)S(1)} %copy-done.7), kind=kOutput, calls=%fused_computation.37 | convolution fusion | flops 1888092160 | bytes 11312640 | tf_op jit(solution)/shard_map/dot_general | solution.py:149
  (13 shorter events, 0.3 us)
Async XLA Ops:
  6.5 141.2 %copy-start = (bf16[640,640]{1,0:T(8,128)(2,1)S(1)}, bf16[640,640]{1,0:T(8,128)(2,1)}, u32[]{:S(2)}) copy-start(bf16[640,640]{1,0:T(8,128)(2,1)} %param.18) | copy-start | bytes 2457604
  6.5 94.4 %all-gather.3.cloned.1.call-start = ((), (), s32[]{:S(2)}) async-start(), calls=%async_computation | async-start | bytes 5570560 | tf_op jit(solution)/shard_map/all_gather | solution.py:103
  10.9 166.3 %collective-permute-start.1 = (bf16[2,1,128,640]{3,2,0,1:T(8,128)(2,1)}, bf16[2,1,128,640]{3,2,0,1:T(8,128)(2,1)S(1)}, u32[]{:S(2)}, u32[]{:S(2)}) collective-permute-start(bf16[2,1,128,640]{3,2,0,1:T(8,128)(2,1)} %bitcast.117), channel_id=1, source_target_pairs={{1,0},{2,1},{3,2},{4,3},{5,4},{6,5},{7,6},{8,7},{9,8},{10,9},{11,1... | collective-permute-start | bytes 983048 | tf_op jit(solution)/shard_map/ppermute | solution.py:29
  12.2 165.0 %collective-permute-start = (bf16[2,1,128,640]{3,2,0,1:T(8,128)(2,1)}, bf16[2,1,128,640]{3,2,0,1:T(8,128)(2,1)S(1)}, u32[]{:S(2)}, u32[]{:S(2)}) collective-permute-start(bf16[2,1,128,640]{3,2,0,1:T(8,128)(2,1)} %bitcast.118), channel_id=1, source_target_pairs={{0,1},{1,2},{2,3},{3,4},{4,5},{5,6},{6,7},{7,8},{8,9},{9,10},{10,1... | collective-permute-start | bytes 983048 | tf_op jit(solution)/shard_map/ppermute | solution.py:26
  129.5 7.0 %copy-start.1 = (f32[2,10,128,2048]{3,2,1,0:T(8,128)}, f32[2,10,128,2048]{3,2,1,0:T(8,128)S(1)}, u32[]{:S(2)}) copy-start(f32[2,10,128,2048]{3,2,1,0:T(8,128)S(1)} %get-tuple-element.24) | copy-start | bytes 62914564
  136.5 10.9 %copy-start.3 = (bf16[2,128,640]{1,2,0:T(8,128)(2,1)S(1)}, bf16[2,128,640]{1,2,0:T(8,128)(2,1)}, u32[]{:S(2)}) copy-start(bf16[2,128,640]{1,2,0:T(8,128)(2,1)} %copy.29) | copy-start | bytes 983044
  147.3 1.0 copy-start.2
  147.4 29.6 %copy-start.4 = (f32[640]{0:T(1024)S(1)}, f32[640]{0:T(1024)}, u32[]{:S(2)}) copy-start(f32[640]{0:T(1024)} %param.20) | copy-start | bytes 7684
  147.4 29.6 %copy-start.5 = (f32[640]{0:T(1024)S(1)}, f32[640]{0:T(1024)}, u32[]{:S(2)}) copy-start(f32[640]{0:T(1024)} %param.19) | copy-start | bytes 7684
  177.6 0.8 copy-start.6
  177.6 0.8 copy-start.7
Sparse Core Ops, SparseCore 0:
  11.0 89.9 all-gather.2
where the time goes:
time: 192 us
  waiting for transfers between devices  75.7 us (39%)
  matrix products  39.7 us (21%)
  blocking collectives  27.3 us (14%)
  local copies, waits for them, and re-layouts  15.5 us (8%)
  between operations  13.7 us (7%)
  other arithmetic  12.5 us (7%)
  starting transfers between devices  7.12 us (4%)
    all_gather x1, waiting for transfers between devices, shards(): block_rows = lax.all_gather(stale_in, PATCH, axis=1, tiled=True)  75.6 us
    psum x2, blocking collectives, over_axes(): return functools.reduce(lax.psum, axes, shard)  27.3 us
    dot_general x1, matrix products, shards(): jnp.einsum('snc,cd->snd', block_rows, w_pair, preferred_element_type=jnp....  13.2 us
    dot_general x2, matrix products, absorb(): jnp.einsum('shqk,skhd->shqd', weights.astype(jnp.bfloat16), values_split,...  11.2 us
    slice x1, local copies, waits for them, and re-layouts, shards(): pair_rows[..., :channels]  10.2 us
    dot_general x1, matrix products, shards(): jnp.dot(unfolded, conv_weight.reshape(9 * channels, channels), preferred_...  6.36 us
    ppermute x1, starting transfers between devices, extended(): lax.ppermute(lax.slice_in_dim(block, block.shape[dim] - width, None, axis...  5.83 us
    dot_general x2, matrix products, absorb(): jnp.einsum('sqhd,skhd->shqk', queries, keys_split, preferred_element_type...  5.51 us
  transfers between devices with their start and end apart: 3, of which 1 were waited for; matrix products, arithmetic and copies ran while one was open for 28% of the time, Pallas kernels for 0%

commit v1 on v0

v1 whole, which is shorter than its diff:
```python
import functools

import jax
import jax.numpy as jnp
import numpy as np
from jax import lax
from jax.experimental import pallas as pl
from jax.experimental.pallas import tpu as pltpu
from jax.sharding import Mesh
from jax.sharding import PartitionSpec as P

GROUPS = 32
HEAD_DIM = 64
EPSILON = 1e-05
LANES = 128
PIECES = 8


F32 = jnp.float32
BF16 = jnp.bfloat16


def normalize(values, gain, bias):
    values = values.astype(F32)
    centre = jnp.mean(values, -1, keepdims=True)
    centred = values - centre
    spread = jnp.mean(centred * centred, -1, keepdims=True)
    return (centred * lax.rsqrt(spread + EPSILON) * gain + bias).astype(BF16)


def as_row(ref):
    return ref[...].reshape(1, -1)


def stale_norm_kernel(x_ref, gain_ref, bias_ref, *out_refs):
    rows = out_refs[0].shape[0]
    gain, bias = as_row(gain_ref), as_row(bias_ref)
    for index, out_ref in enumerate(out_refs):
        out_ref[...] = normalize(x_ref[index * rows : (index + 1) * rows, :], gain, bias)


def query_kernel(x_ref, gain_ref, bias_ref, w_ref, *out_refs):
    normed = normalize(x_ref[...], as_row(gain_ref), as_row(bias_ref))
    projected = jnp.dot(normed, w_ref[...], preferred_element_type=F32).astype(BF16)
    scaled = (projected.astype(F32) * HEAD_DIM ** (-0.5)).astype(BF16)
    rows = out_refs[0].shape[0]
    half = len(out_refs) // 2
    for index in range(half):
        part = slice(index * rows, (index + 1) * rows)
        out_refs[index][...] = scaled[part]
        out_refs[half + index][...] = normed[part]


def scores_of(queries, keys):
    return lax.dot_general(
        queries, keys, (((1,), (1,)), ((), ())), preferred_element_type=F32
    )


def attend_kernel(
    q0_ref, q1_ref, q2_ref, q3_ref,
    z1_ref, z2_ref, z3_ref, fresh_ref, own_ref,
    wk_ref, wv_ref,
    o0_ref, o1_ref, o2_ref, o3_ref,
    x_scr, tile_scr,
):
    pair = pl.program_id(0)
    rows = fresh_ref.shape[0]
    channels = fresh_ref.shape[1]
    out_refs = (o0_ref, o1_ref, o2_ref, o3_ref)

    @pl.when(pair == 0)
    def _():
        for index, ref in enumerate((z1_ref, z2_ref, z3_ref, fresh_ref, own_ref)):
            x_scr[index * rows : (index + 1) * rows, :] = ref[...]
        tile_scr[...] = jnp.zeros_like(tile_scr)

    weights = jnp.concatenate([wk_ref[...], wv_ref[...]], axis=1)
    pairs = jnp.dot(x_scr[...], weights, preferred_element_type=F32).astype(BF16)
    keys, values = pairs[:, :LANES], pairs[:, LANES:]
    low_all = lax.broadcasted_iota(jnp.int32, keys.shape, 1) < HEAD_DIM
    zero = jnp.zeros((), BF16)
    one = jnp.ones((), BF16)
    low_values = jnp.concatenate(
        [jnp.where(low_all, values, zero), jnp.where(low_all, one, zero)], axis=1
    )
    high_values = jnp.concatenate(
        [jnp.where(low_all, zero, values), jnp.where(low_all, zero, one)], axis=1
    )
    common, fresh, own = slice(0, 3 * rows), slice(3 * rows, 4 * rows), slice(4 * rows, 5 * rows)
    queries = jnp.concatenate([q0_ref[...], q1_ref[...], q2_ref[...], q3_ref[...]], 0)
    lane = lax.broadcasted_iota(jnp.int32, queries.shape, 1)
    low = lane < HEAD_DIM
    shared_weights, single_weights, tops = [], [], []
    for part in (jnp.where(low, queries, zero), jnp.where(low, zero, queries)):
        shared = scores_of(part, keys[common])
        single = jnp.concatenate(
            [scores_of(part[:rows], keys[fresh]), scores_of(part[rows:], keys[own])], 0
        )
        top = single
        for index in range(3):
            top = jnp.maximum(top, shared[:, index * LANES : (index + 1) * LANES])
        top = jnp.max(top, -1, keepdims=True)
        tops.append(top)
        shared_weights.append(jnp.exp(shared - top).astype(BF16))
        single_weights.append(jnp.exp(single - top).astype(BF16))
    summed = jnp.dot(
        jnp.concatenate(shared_weights, 1),
        jnp.concatenate([low_values[common], high_values[common]], 0),
        preferred_element_type=F32,
    )
    single = jnp.concatenate(single_weights, 1)
    summed = summed + jnp.concatenate(
        [
            jnp.dot(
                single[:rows],
                jnp.concatenate([low_values[fresh], high_values[fresh]], 0),
                preferred_element_type=F32,
            ),
            jnp.dot(
                single[rows:],
                jnp.concatenate([low_values[own], high_values[own]], 0),
                preferred_element_type=F32,
            ),
        ],
        0,
    )
    total = summed[:, LANES:]
    mixed = (summed[:, :LANES] / total).astype(BF16)
    lanes = pl.ds(pl.multiple_of(pair * LANES, LANES), LANES)
    for index, o_ref in enumerate(out_refs):
        o_ref[:, lanes] = mixed[index * rows : (index + 1) * rows]
    rest = jnp.where(low, tops[0], tops[1]) + jnp.log(total)
    slot = lane & (HEAD_DIM - 1)
    tile = tile_scr[...]
    for piece in range(3):
        rounded = rest.astype(BF16).astype(F32)
        tile = jnp.where(slot == pair + piece * PIECES, rounded, tile)
        rest = rest - rounded
    tile_scr[...] = tile

    @pl.when(pair == pl.num_programs(0) - 1)
    def _():
        for index, o_ref in enumerate(out_refs):
            o_ref[:, channels:] = tile_scr[index * rows : (index + 1) * rows, :].astype(BF16)


def spread_matrix(channels):
    out = np.zeros((LANES, channels), np.float32)
    for channel in range(channels):
        head = channel // HEAD_DIM
        base = (head % 2) * HEAD_DIM + head // 2
        for piece in range(3):
            out[base + piece * PIECES, channel] = 1
    return out


def exact_dot(x, ones):
    total = None
    for _ in range(3):
        rounded = x.astype(BF16)
        part = jnp.dot(rounded, ones, preferred_element_type=F32)
        total = part if total is None else total + part
        x = x - rounded.astype(F32)
    return total


def merge_kernel(
    o0_ref, o1_ref, o2_ref, o3_ref, hidden_ref, w_ref, spread_ref, gather_ref, *rest_refs, sample
):
    channels = hidden_ref.shape[1]
    rows = hidden_ref.shape[0]
    refs = (o0_ref, o1_ref, o2_ref, o3_ref)
    tiles = jnp.concatenate([ref[:, channels:] for ref in refs], 0)
    logs = jnp.dot(tiles, spread_ref[...], preferred_element_type=F32)
    logs = [logs[index * rows : (index + 1) * rows] for index in range(4)]
    top = jnp.maximum(jnp.maximum(logs[0], logs[1]), jnp.maximum(logs[2], logs[3]))
    numer = denom = None
    for ref, one in zip(refs, logs):
        factor = jnp.exp(one - top)
        upper = factor * ref[:, :channels].astype(F32)
        numer, denom = (upper, factor) if numer is None else (numer + upper, denom + factor)
    attended = (numer / denom).astype(BF16)
    residual = (
        hidden_ref[...].astype(F32) + jnp.dot(attended, w_ref[...], preferred_element_type=F32)
    ).astype(BF16)
    res_ref, stat_ref = rest_refs[-2:]
    res_ref[...] = residual
    wide = residual.astype(F32)
    sums = jnp.concatenate(
        [jnp.sum(wide, 0, keepdims=True), jnp.sum(wide * wide, 0, keepdims=True)]
        + [jnp.zeros((6, channels), F32)],
        0,
    )
    sums = exact_dot(sums, gather_ref[...])
    if sample:
        sums = pltpu.roll(sums, 2 * sample, 0) + rest_refs[0][...]
        stat_ref[...] = jnp.broadcast_to(sums[None], stat_ref.shape)
    else:
        stat_ref[...] = sums


def shifted(x, by, cols):
    rolled = pltpu.roll(x, by % x.shape[0], 0)
    col = lax.broadcasted_iota(jnp.int32, x.shape, 0) & (cols - 1)
    edge = 0 if by == 1 else cols - 1
    return jnp.where(col == edge, 0.0, rolled).astype(BF16)


def taps(x, w_ref, cols):
    wide = x.astype(F32)
    total = jnp.dot(shifted(wide, 1, cols), w_ref[0], preferred_element_type=F32)
    total += jnp.dot(x, w_ref[1], preferred_element_type=F32)
    total += jnp.dot(shifted(wide, -1, cols), w_ref[2], preferred_element_type=F32)
    return total


def rim_kernel(above_ref, below_ref, w_ref, bias_ref, shift_ref, out_ref, *, cols):
    step = pl.program_id(0)

    @pl.when(step == 0)
    def _():
        first = taps(above_ref[...], w_ref, cols) + as_row(bias_ref)
        samples = first.shape[0] // cols
        for sample in range(samples):
            part = slice(sample * cols, (sample + 1) * cols)
            out_ref[part, :] = first[part] + shift_ref[sample : sample + 1, :]

    @pl.when(step == 1)
    def _():
        out_ref[...] += taps(below_ref[...], w_ref, cols)


def final_kernel(
    res0_ref, res1_ref, stat_ref, gain_ref, bias_ref, scatter_ref, w_ref, rim_ref, out_ref,
    *, cols, cells
):
    activated = []
    wide = []
    sums = exact_dot(jnp.sum(stat_ref[...], 0), scatter_ref[...])
    gain, bias = as_row(gain_ref), as_row(bias_ref)
    for sample, res_ref in enumerate((res0_ref, res1_ref)):
        mean = sums[2 * sample : 2 * sample + 1] / cells
        var = sums[2 * sample + 1 : 2 * sample + 2] / cells - mean * mean
        residual = res_ref[...].astype(F32)
        wide.append(residual)
        normalized = (residual - mean) * lax.rsqrt(var + EPSILON)
        value = normalized * gain + bias
        activated.append((value / (1.0 + jnp.exp(-value))).astype(BF16))
    x = jnp.concatenate(activated, 0)
    out_ref[...] = (
        taps(x, w_ref, cols) + rim_ref[...] + jnp.concatenate(wide, 0)
    ).astype(BF16)


def ring(by, count):
    return [(i, (i + by) % count) for i in range(count)]


def call(kernel, out_shape, *args, flops=1000000, **kwargs):
    return pl.pallas_call(
        kernel,
        out_shape=out_shape,
        cost_estimate=pl.CostEstimate(flops=flops, bytes_accessed=1000000, transcendentals=0),
        **kwargs,
    )(*args)


def shards(
    hidden, stale_attn_in, stale_conv_in, ln_gain, ln_bias, w_qkv, w_out,
    gn_gain, gn_bias, conv_weight, conv_bias, time_shift,
):
    samples, rows_dev, cols, channels = hidden.shape
    tokens = rows_dev * cols
    every = samples * tokens
    pair_count = channels // LANES
    y_count, z_count = lax.axis_size("y"), lax.axis_size("z")
    count = y_count * z_count
    hid = hidden.reshape(every, channels)
    block = jax.ShapeDtypeStruct((tokens, channels), BF16)
    full = pl.BlockSpec((every, channels), lambda i: (0, 0))
    vector = pl.BlockSpec((channels,), lambda i: (0,))
    whole = pl.BlockSpec((tokens, channels), lambda i: (0, 0))
    shifts = (1, 3, 2)

    stale = call(
        stale_norm_kernel, [block] * samples,
        stale_attn_in.reshape(every, channels), ln_gain, ln_bias,
    )
    along = [[lax.ppermute(one, "z", ring(by, z_count)) for by in shifts] for one in stale]
    outs = call(
        query_kernel, [block] * (2 * samples), hid, ln_gain, ln_bias, w_qkv,
        grid=(1,),
        in_specs=[full, vector, vector, pl.BlockSpec((channels, channels), lambda i: (0, 0))],
        out_specs=[whole] * (2 * samples),
        flops=2 * every * channels * channels,
    )
    queries, fresh = outs[:samples], outs[samples:]
    all_queries = [
        [one] + [lax.ppermute(one, "y", ring(by, y_count)) for by in shifts]
        for one in queries
    ]
    conv_rows = stale_conv_in.reshape(every, channels)
    above = lax.ppermute(conv_rows, ("y", "z"), [(i, i + 1) for i in range(count - 1)])
    below = lax.ppermute(conv_rows, ("y", "z"), [(i + 1, i) for i in range(count - 1)])

    wide = channels + LANES
    spread = jnp.asarray(spread_matrix(channels), BF16)
    group = np.arange(channels) // (channels // GROUPS)
    gather = group[:, None] == np.arange(LANES)[None, :]
    ext = jax.ShapeDtypeStruct((tokens, wide), BF16)
    back = []
    for s in range(samples):
        outs = call(
            attend_kernel, [ext] * 4,
            *all_queries[s], along[s][0], along[s][2], along[s][1], fresh[s], stale[s],
            w_qkv, w_qkv,
            grid=(pair_count,),
            in_specs=[pl.BlockSpec((tokens, LANES), lambda p: (0, p))] * 4
            + [whole] * 5
            + [
                pl.BlockSpec((channels, LANES), lambda p: (0, pair_count + p)),
                pl.BlockSpec((channels, LANES), lambda p: (0, 2 * pair_count + p)),
            ],
            out_specs=[pl.BlockSpec((tokens, wide), lambda p: (0, 0))] * 4,
            scratch_shapes=[
                pltpu.VMEM((5 * tokens, channels), BF16),
                pltpu.VMEM((4 * tokens, LANES), F32),
            ],
            flops=6 * 10 ** 9,
        )
        back.append(
            [outs[0]]
            + [lax.ppermute(one, "y", ring(-by, y_count)) for one, by in zip(outs[1:], shifts)]
        )
    rim = call(
        functools.partial(rim_kernel, cols=cols),
        jax.ShapeDtypeStruct((every, channels), F32),
        above, below, conv_weight, conv_bias, time_shift,
        grid=(2,),
        in_specs=[
            full, full,
            pl.BlockSpec((None, 3, channels, channels), lambda i: (2 * i, 0, 0, 0)),
            vector,
            pl.BlockSpec((samples, channels), lambda i: (0, 0)),
        ],
        out_specs=full,
        flops=12 * every * channels * channels,
    )
    residuals, stats = [], []
    for s in range(samples):
        small = jax.ShapeDtypeStruct((8, LANES), F32)
        if s:
            small = jax.ShapeDtypeStruct((count, 8, LANES), F32)
        res, stat = call(
            functools.partial(merge_kernel, sample=s), [block, small],
            *back[s], hid, w_out, spread, jnp.asarray(gather, BF16), *stats,
            grid=(1,),
            in_specs=[pl.BlockSpec((tokens, wide), lambda i: (0, 0))] * 4
            + [
                pl.BlockSpec((tokens, channels), lambda i, s=s: (s, 0)),
                pl.BlockSpec((channels, channels), lambda i: (0, 0)),
                pl.BlockSpec((LANES, channels), lambda i: (0, 0)),
                pl.BlockSpec((channels, LANES), lambda i: (0, 0)),
            ]
            + [pl.BlockSpec((8, LANES), lambda i: (0, 0))] * len(stats),
            out_specs=[whole, pl.BlockSpec(small.shape, lambda i, n=small.ndim: (0,) * n)],
            flops=10 ** 9,
        )
        residuals.append(res)
        stats = [stat]
    shared = lax.all_to_all(stats[0], ("y", "z"), 0, 0)
    out = call(
        functools.partial(
            final_kernel, cols=cols, cells=float(count * tokens * (channels // GROUPS))
        ),
        jax.ShapeDtypeStruct((every, channels), BF16),
        *residuals, shared, gn_gain, gn_bias, jnp.asarray(gather.T, BF16), conv_weight, rim,
        grid=(1,),
        in_specs=[
            whole, whole,
            pl.BlockSpec((count, 8, LANES), lambda i: (0, 0, 0)),
            vector, vector,
            pl.BlockSpec((LANES, channels), lambda i: (0, 0)),
            pl.BlockSpec((None, 3, channels, channels), lambda i: (1, 0, 0, 0)),
            full,
        ],
        out_specs=full,
        flops=6 * every * channels * channels,
    )
    return out.reshape(hidden.shape)


def solution(mesh):
    split = Mesh(mesh.devices.reshape(mesh.shape["img"], 4, 4), ("img", "y", "z"))
    rows = P("img", ("y", "z"), None, None)

    return jax.shard_map(
        shards,
        mesh=split,
        in_specs=(rows, rows, rows, P(), P(), P(), P(), P(), P(), P(), P(), P("img", None)),
        out_specs=rows,
        check_vma=False,
    )
```

time: 192 us -> 110 us (0.57)
  waiting for transfers between devices: 75.7 us -> 12.5 us
  starting transfers between devices: 7.12 us -> 50.8 us
  Pallas kernels: 0 us -> 43 us
  matrix products: 39.7 us -> 0 us
  blocking collectives: 27.3 us -> 0 us
  between operations: 13.7 us -> 0.25 us
  local copies, waits for them, and re-layouts: 15.5 us -> 2.85 us
  other arithmetic: 12.5 us -> 0 us
    all_gather x1 -> x0, waiting for transfers between devices: 75.6 us -> none  [shards(): block_rows = lax.all_gather(stale_in, PATCH, axis=1, tiled=True)]
    pallas_call x0 -> x8, Pallas kernels: none -> 43 us  [call(): pl.pallas_call(kernel, out_shape=out_shape, cost_estimate=pl.CostEstimate...]
    dot_general x8 -> x0, matrix products: 39.7 us -> none  [the longest x1 13.2 us: shards(): jnp.einsum('snc,cd->snd', block_rows, w_pair, preferred_element_type=jnp....]
    ppermute x2 -> x20, starting transfers between devices: 7.12 us -> 45.6 us  [the longest x6 20.2 us: shards(): lax.ppermute(one, 'z', ring(by, z_count))]
    psum x2 -> x0, blocking collectives: 27.3 us -> none  [over_axes(): return functools.reduce(lax.psum, axes, shard)]
    slice x5 -> x0, local copies, waits for them, and re-layouts: 11.6 us -> none  [the longest x1 10.2 us: shards(): pair_rows[..., :channels]]
    reduce_sum x8 -> x0, other arithmetic: 9.7 us -> none  [the longest x2 4.87 us: absorb(): weight_sum = weight_sum * rescale + jnp.sum(weights, -1)]
    ppermute x2 -> x20, waiting for transfers between devices: 0.01 us -> 8.59 us  [the longest x6 5 us: shards(): lax.ppermute(one, 'z', ring(by, z_count))]
  transfers between devices with their start and end apart: 3 -> 21, of which waited for: 1 -> 3; matrix products, arithmetic and copies ran while one was open for 28% -> 0% of each run, Pallas kernels for 0% -> 33%
where the time goes in v1:
time: 110 us; the launch traced here: 109 us
  starting transfers between devices  50.8 us (46%)
  Pallas kernels  43 us (39%)
  waiting for transfers between devices  12.5 us (11%)
  local copies, waits for them, and re-layouts  2.85 us (3%)
    pallas_call x8, Pallas kernels, call(): pl.pallas_call(kernel, out_shape=out_shape, cost_estimate=pl.CostEstimate...  43 us
    ppermute x6, starting transfers between devices, shards(): lax.ppermute(one, 'z', ring(by, z_count))  20.2 us
    ppermute x6, starting transfers between devices, shards(): lax.ppermute(one, 'y', ring(-by, y_count))  11 us
    ppermute x6, starting transfers between devices, shards(): lax.ppermute(one, 'y', ring(by, y_count))  8.2 us
    all_to_all x1, starting transfers between devices, shards(): shared = lax.all_to_all(stats[0], ('y', 'z'), 0, 0)  5.28 us
    ppermute x6, waiting for transfers between devices, shards(): lax.ppermute(one, 'z', ring(by, z_count))  5 us
    ppermute x1, starting transfers between devices, shards(): lax.ppermute(conv_rows, ('y', 'z'), [(i, i + 1) for i in range(count - 1)])  4.82 us
    all_to_all x1, waiting for transfers between devices, shards(): shared = lax.all_to_all(stats[0], ('y', 'z'), 0, 0)  3.95 us
  transfers between devices with their start and end apart: 21, of which 3 were waited for; matrix products, arithmetic and copies ran while one was open for 0% of the time, Pallas kernels for 33%

profile of v1, /device:TPU:2, one launch (start us, length us, event | category | flops | bytes accessed | tf_op | source)
XLA Modules:
  0.0 109.5 jit_solution(13245333576886340776)
XLA Ops:
  0.0 2.7 %shard_map.154 = (bf16[128,640]{1,0:T(8,128)(2,1)}, bf16[128,640]{1,0:T(8,128)(2,1)}, bf16[128,640]{1,0:T(8,128)(2,1)}, bf16[128,640]{1,0:T(8,128)(2,1)}) custom-call(bf16[256,640]{1,0:T(8,128)(2,1)} %bitcast.7, f32[640]{0:T(1024)} %gain_ref.4, f32[640]{0:T(1024)} %bias_ref.5, bf16[640,1920]{1,0:T(8,128)(2,1)} %wv_ref.3), custom_call_target="tpu_custom_call" | custom-call | flops 209715200 | bytes 1000000 | tf_op jit(solution)/shard_map/pallas_call | solution.py:261
  2.7 1.6 %collective-permute-start = (bf16[128,640]{1,0:T(8,128)(2,1)}, bf16[128,640]{1,0:T(8,128)(2,1)S(1)}, u32[]{:S(2)}, u32[]{:S(2)}) collective-permute-start(bf16[128,640]{1,0:T(8,128)(2,1)} %get-tuple-element.23.q0_ref), channel_id=1, source_target_pairs={{0,4},{4,8},{8,12},{12,0},{1,5},{5,9},{9,13},{13,1},{2,6},{6,10},{... | collective-permute-start | bytes 491528 | tf_op jit(solution)/shard_map/ppermute | solution.py:300
  4.3 1.7 %collective-permute-start.1 = (bf16[128,640]{1,0:T(8,128)(2,1)}, bf16[128,640]{1,0:T(8,128)(2,1)S(1)}, u32[]{:S(2)}, u32[]{:S(2)}) collective-permute-start(bf16[128,640]{1,0:T(8,128)(2,1)} %get-tuple-element.23.q0_ref), channel_id=1, source_target_pairs={{0,12},{4,0},{8,4},{12,8},{1,13},{5,1},{9,5},{13,9},{2,14},{6,2},{... | collective-permute-start | bytes 491528 | tf_op jit(solution)/shard_map/ppermute | solution.py:300
  6.0 2.0 %collective-permute-start.2 = (bf16[128,640]{1,0:T(8,128)(2,1)}, bf16[128,640]{1,0:T(8,128)(2,1)S(1)}, u32[]{:S(2)}, u32[]{:S(2)}) collective-permute-start(bf16[128,640]{1,0:T(8,128)(2,1)} %get-tuple-element.23.q0_ref), channel_id=1, source_target_pairs={{0,8},{4,12},{8,0},{12,4},{1,9},{5,13},{9,1},{13,5},{2,10},{6,14},... | collective-permute-start | bytes 491528 | tf_op jit(solution)/shard_map/ppermute | solution.py:300
  7.9 2.0 %shard_map.155 = (bf16[128,640]{1,0:T(8,128)(2,1)}, bf16[128,640]{1,0:T(8,128)(2,1)}) custom-call(bf16[256,640]{1,0:T(8,128)(2,1)} %bitcast.6, f32[640]{0:T(1024)} %gain_ref.4, f32[640]{0:T(1024)} %bias_ref.5), custom_call_target="tpu_custom_call" | custom-call | flops 1000000 | bytes 1000000 | tf_op jit(solution)/shard_map/pallas_call | solution.py:261
  9.9 3.3 %collective-permute-start.3 = (bf16[128,640]{1,0:T(8,128)(2,1)}, bf16[128,640]{1,0:T(8,128)(2,1)S(1)}, u32[]{:S(2)}, u32[]{:S(2)}) collective-permute-start(bf16[128,640]{1,0:T(8,128)(2,1)} %get-tuple-element.24.own_ref), channel_id=1, source_target_pairs={{0,1},{1,2},{2,3},{3,0},{4,5},{5,6},{6,7},{7,4},{8,9},{9,10},{10,1... | collective-permute-start | bytes 491528 | tf_op jit(solution)/shard_map/ppermute | solution.py:290
  13.2 5.4 %collective-permute-start.4 = (bf16[128,640]{1,0:T(8,128)(2,1)}, bf16[128,640]{1,0:T(8,128)(2,1)S(1)}, u32[]{:S(2)}, u32[]{:S(2)}) collective-permute-start(bf16[128,640]{1,0:T(8,128)(2,1)} %get-tuple-element.24.own_ref), channel_id=1, source_target_pairs={{0,2},{1,3},{2,0},{3,1},{4,6},{5,7},{6,4},{7,5},{8,10},{9,11},{10,... | collective-permute-start | bytes 491528 | tf_op jit(solution)/shard_map/ppermute | solution.py:290
  18.6 0.0 collective-permute-done.q1_ref
  18.6 2.7 %collective-permute-start.5 = (bf16[128,640]{1,0:T(8,128)(2,1)}, bf16[128,640]{1,0:T(8,128)(2,1)S(1)}, u32[]{:S(2)}, u32[]{:S(2)}) collective-permute-start(bf16[128,640]{1,0:T(8,128)(2,1)} %get-tuple-element.24.own_ref), channel_id=1, source_target_pairs={{0,3},{1,0},{2,1},{3,2},{4,7},{5,4},{6,5},{7,6},{8,11},{9,8},{10,9... | collective-permute-start | bytes 491528 | tf_op jit(solution)/shard_map/ppermute | solution.py:290
  21.2 0.0 collective-permute-done.1.q2_ref
  21.2 1.1 collective-permute-start.10
  22.3 0.0 collective-permute-done.2.q3_ref
  22.3 1.7 %collective-permute-start.11 = (bf16[128,640]{1,0:T(8,128)(2,1)}, bf16[128,640]{1,0:T(8,128)(2,1)S(1)}, u32[]{:S(2)}, u32[]{:S(2)}) collective-permute-start(bf16[128,640]{1,0:T(8,128)(2,1)} %get-tuple-element.31.q0_ref), channel_id=1, source_target_pairs={{0,8},{4,12},{8,0},{12,4},{1,9},{5,13},{9,1},{13,5},{2,10},{6,14},... | collective-permute-start | bytes 491528 | tf_op jit(solution)/shard_map/ppermute | solution.py:300
  24.0 0.0 collective-permute-done.3.z1_ref
  24.0 0.2 collective-permute-start.9
  24.2 5.0 %collective-permute-done.4.z2_ref = bf16[128,640]{1,0:T(8,128)(2,1)S(1)} collective-permute-done((bf16[128,640]{1,0:T(8,128)(2,1)}, bf16[128,640]{1,0:T(8,128)(2,1)S(1)}, u32[]{:S(2)}, u32[]{:S(2)}) %collective-permute-start.4) | collective-permute-done | bytes 163872 | tf_op jit(solution)/shard_map/ppermute | solution.py:290
  29.2 3.6 %collective-permute-start.12 = (bf16[128,640]{1,0:T(8,128)(2,1)}, bf16[128,640]{1,0:T(8,128)(2,1)S(1)}, u32[]{:S(2)}, u32[]{:S(2)}) collective-permute-start(bf16[128,640]{1,0:T(8,128)(2,1)} %get-tuple-element.32.own_ref), channel_id=1, source_target_pairs={{0,1},{1,2},{2,3},{3,0},{4,5},{5,6},{6,7},{7,4},{8,9},{9,10},{10,1... | collective-permute-start | bytes 491528 | tf_op jit(solution)/shard_map/ppermute | solution.py:290
  32.9 0.0 collective-permute-done.5.z3_ref
  32.9 5.3 %collective-permute-start.13 = (bf16[128,640]{1,0:T(8,128)(2,1)}, bf16[128,640]{1,0:T(8,128)(2,1)S(1)}, u32[]{:S(2)}, u32[]{:S(2)}) collective-permute-start(bf16[128,640]{1,0:T(8,128)(2,1)} %get-tuple-element.32.own_ref), channel_id=1, source_target_pairs={{0,2},{1,3},{2,0},{3,1},{4,6},{5,7},{6,4},{7,5},{8,10},{9,11},{10,... | collective-permute-start | bytes 491528 | tf_op jit(solution)/shard_map/ppermute | solution.py:290
  38.1 0.0 collective-permute-done.10.q2_ref
  38.1 0.0 collective-permute-start.14
  38.2 0.0 copy-done.13
  38.2 0.0 copy-done.15
  38.2 0.0 copy-done.16
  38.2 0.0 copy-done.18
  38.2 0.0 copy-done.20
  38.2 0.0 copy-done.21
  38.2 0.0 copy-start.3
  38.2 11.5 %shard_map.156 = (bf16[128,768]{1,0:T(8,128)(2,1)}, bf16[128,768]{1,0:T(8,128)(2,1)}, bf16[128,768]{1,0:T(8,128)(2,1)}, bf16[128,768]{1,0:T(8,128)(2,1)}) custom-call(bf16[128,640]{1,0:T(8,128)(2,1)} %get-tuple-element.23.q0_ref, bf16[128,640]{1,0:T(8,128)(2,1)} %copy-done.13, bf16[128,640]{1,0:T(8,128)(2,1)} %copy-done.15, bf16[128,640]{1,0:T(8,128)(2,1)} %copy-done.16, ...), custom_call_target="tpu_custom_call" | custom-call | flops 6000000000 | bytes 1000000 | tf_op jit(solution)/shard_map/pallas_call | solution.py:261
  49.7 0.0 collective-permute-done.11.q3_ref
  49.7 0.0 copy-start.11
  49.7 4.8 %collective-permute-start.18 = (bf16[256,640]{1,0:T(8,128)(2,1)S(1)}, bf16[256,640]{1,0:T(8,128)(2,1)S(1)}, u32[]{:S(2)}, u32[]{:S(2)}) collective-permute-start(bf16[256,640]{1,0:T(8,128)(2,1)S(1)} %bitcast.10), channel_id=1, source_target_pairs={{0,1},{1,2},{2,3},{3,4},{4,5},{5,6},{6,7},{7,8},{8,9},{9,10},{10,1... | collective-permute-start | bytes 983048 | tf_op jit(solution)/shard_map/ppermute | solution.py:304
  54.5 0.0 collective-permute-done.9.q1_ref
  54.6 1.3 %collective-permute-start.19 = (bf16[256,640]{1,0:T(8,128)(2,1)S(1)}, bf16[256,640]{1,0:T(8,128)(2,1)S(1)}, u32[]{:S(2)}, u32[]{:S(2)}) collective-permute-start(bf16[256,640]{1,0:T(8,128)(2,1)S(1)} %bitcast.11), channel_id=1, source_target_pairs={{1,0},{2,1},{3,2},{4,3},{5,4},{6,5},{7,6},{8,7},{9,8},{10,9},{11,1... | collective-permute-start | bytes 983048 | tf_op jit(solution)/shard_map/ppermute | solution.py:305
  55.9 0.0 collective-permute-done.12.z1_ref
  55.9 4.7 %collective-permute-start.6 = (bf16[128,768]{1,0:T(8,128)(2,1)}, bf16[128,768]{1,0:T(8,128)(2,1)S(1)}, u32[]{:S(2)}, u32[]{:S(2)}) collective-permute-start(bf16[128,768]{1,0:T(8,128)(2,1)} %get-tuple-element.27), channel_id=1, source_target_pairs={{0,12},{4,0},{8,4},{12,8},{1,13},{5,1},{9,5},{13,9},{2,14},{6,2},{... | collective-permute-start | bytes 589832 | tf_op jit(solution)/shard_map/ppermute | solution.py:334
  60.6 0.0 collective-permute-done.13.z2_ref
  60.6 0.0 collective-permute-start.7
  60.6 0.0 collective-permute-done.14.z3_ref
  60.6 1.8 %collective-permute-start.8 = (bf16[128,768]{1,0:T(8,128)(2,1)}, bf16[128,768]{1,0:T(8,128)(2,1)S(1)}, u32[]{:S(2)}, u32[]{:S(2)}) collective-permute-start(bf16[128,768]{1,0:T(8,128)(2,1)} %get-tuple-element.29), channel_id=1, source_target_pairs={{0,8},{4,12},{8,0},{12,4},{1,9},{5,13},{9,1},{13,5},{2,10},{6,14},... | collective-permute-start | bytes 589832 | tf_op jit(solution)/shard_map/ppermute | solution.py:334
  62.5 11.5 %shard_map.158 = (bf16[128,768]{1,0:T(8,128)(2,1)}, bf16[128,768]{1,0:T(8,128)(2,1)}, bf16[128,768]{1,0:T(8,128)(2,1)}, bf16[128,768]{1,0:T(8,128)(2,1)}) custom-call(bf16[128,640]{1,0:T(8,128)(2,1)} %get-tuple-element.31.q0_ref, bf16[128,640]{1,0:T(8,128)(2,1)} %copy-done.12, bf16[128,640]{1,0:T(8,128)(2,1)} %copy-done.10, bf16[128,640]{1,0:T(8,128)(2,1)} %copy-done.11, ...), custom_call_target="tpu_custom_call" | custom-call | flops 6000000000 | bytes 1000000 | tf_op jit(solution)/shard_map/pallas_call | solution.py:261
  74.0 0.0 collective-permute-done.6.o1_ref
  74.0 2.0 %collective-permute-start.15 = (bf16[128,768]{1,0:T(8,128)(2,1)}, bf16[128,768]{1,0:T(8,128)(2,1)S(1)}, u32[]{:S(2)}, u32[]{:S(2)}) collective-permute-start(bf16[128,768]{1,0:T(8,128)(2,1)} %get-tuple-element.35), channel_id=1, source_target_pairs={{0,12},{4,0},{8,4},{12,8},{1,13},{5,1},{9,5},{13,9},{2,14},{6,2},{... | collective-permute-start | bytes 589832 | tf_op jit(solution)/shard_map/ppermute | solution.py:334
  76.0 0.0 collective-permute-done.7.o2_ref
  76.0 0.4 collective-permute-start.16
  76.4 0.0 collective-permute-done.8.o3_ref
  76.4 2.1 %collective-permute-start.17 = (bf16[128,768]{1,0:T(8,128)(2,1)}, bf16[128,768]{1,0:T(8,128)(2,1)S(1)}, u32[]{:S(2)}, u32[]{:S(2)}) collective-permute-start(bf16[128,768]{1,0:T(8,128)(2,1)} %get-tuple-element.37), channel_id=1, source_target_pairs={{0,8},{4,12},{8,0},{12,4},{1,9},{5,13},{9,1},{13,5},{2,10},{6,14},... | collective-permute-start | bytes 589832 | tf_op jit(solution)/shard_map/ppermute | solution.py:334
  78.5 3.2 %shard_map.157 = (bf16[128,640]{1,0:T(8,128)(2,1)}, f32[8,128]{1,0:T(8,128)}) custom-call(bf16[128,768]{1,0:T(8,128)(2,1)} %get-tuple-element.26.o0_ref, bf16[128,768]{1,0:T(8,128)(2,1)} %copy-done.4, bf16[128,768]{1,0:T(8,128)(2,1)} %copy-done.5, bf16[128,768]{1,0:T(8,128)(2,1)} %copy-done.6, bf16[256,640]{1,0:T(8,128)(2,1)} %bitcast.8, ...), custom_call_target="tpu_custom_call" | custom-call | flops 1000000000 | bytes 1000000 | tf_op jit(solution)/shard_map/pallas_call | solution.py:261
  81.7 0.0 collective-permute-done.15.o1_ref
  81.7 3.6 %collective-permute-done.16.o2_ref = bf16[128,768]{1,0:T(8,128)(2,1)S(1)} collective-permute-done((bf16[128,768]{1,0:T(8,128)(2,1)}, bf16[128,768]{1,0:T(8,128)(2,1)S(1)}, u32[]{:S(2)}, u32[]{:S(2)}) %collective-permute-start.16) | collective-permute-done | bytes 196640 | tf_op jit(solution)/shard_map/ppermute | solution.py:334
  85.2 0.0 collective-permute-done.17.o3_ref
  85.2 0.7 copy-done.8
  85.9 0.1 copy-done.9
  86.0 3.2 %shard_map.159 = (bf16[128,640]{1,0:T(8,128)(2,1)}, f32[16,8,128]{2,1,0:T(8,128)}) custom-call(bf16[128,768]{1,0:T(8,128)(2,1)} %get-tuple-element.34.o0_ref, bf16[128,768]{1,0:T(8,128)(2,1)} %copy-done.7, bf16[128,768]{1,0:T(8,128)(2,1)} %copy-done.8, bf16[128,768]{1,0:T(8,128)(2,1)} %copy-done.9, bf16[256,640]{1,0:T(8,128)(2,1)} %bitcast.9, ...), custom_call_target="tpu_custom_call" | custom-call | flops 1000000000 | bytes 1000000 | tf_op jit(solution)/shard_map/pallas_call | solution.py:261
  89.2 5.3 %all-to-all-start = ((f32[16,8,128]{2,1,0:T(8,128)}), f32[16,8,128]{2,1,0:T(8,128)S(1)}, u32[]{:S(2)}, u32[]{:S(2)}) async-start(f32[16,8,128]{2,1,0:T(8,128)} %get-tuple-element.40), calls=%async_computation | async-start | bytes 131072 | tf_op jit(solution)/shard_map/all_to_all | solution.py:372
  94.5 0.0 collective-permute-done.18.above_ref
  94.5 0.0 copy-start
  94.5 0.0 collective-permute-done.19.below_ref
  94.5 0.7 copy-done
  95.2 0.7 copy-done.1
  95.9 4.8 %shard_map.160.rim_ref = f32[256,640]{1,0:T(8,128)} custom-call(bf16[256,640]{1,0:T(8,128)(2,1)} %copy-done, bf16[256,640]{1,0:T(8,128)(2,1)} %copy-done.1, bf16[3,3,640,640]{3,2,1,0:T(8,128)(2,1)} %w_ref.9, f32[640]{0:T(1024)} %bias_ref.6, f32[2,640]{1,0:T(2,128)} %shift_ref.1), custom_call_target="tpu_custom_call" | custom-call | flops 1258291200 | bytes 1000000 | tf_op jit(solution)/shard_map/pallas_call | solution.py:261
  100.7 4.0 %all-to-all-done.stat_ref = f32[16,8,128]{2,1,0:T(8,128)S(1)} async-done(((f32[16,8,128]{2,1,0:T(8,128)}), f32[16,8,128]{2,1,0:T(8,128)S(1)}, u32[]{:S(2)}, u32[]{:S(2)}) %all-to-all-start) | async-done | bytes 65568 | tf_op jit(solution)/shard_map/all_to_all | solution.py:372
  104.7 0.6 copy-done.2
  105.3 4.2 %shard_map.161 = bf16[256,640]{1,0:T(8,128)(2,1)} custom-call(bf16[128,640]{1,0:T(8,128)(2,1)} %get-tuple-element.30.res0_ref, bf16[128,640]{1,0:T(8,128)(2,1)} %get-tuple-element.39.res1_ref, f32[16,8,128]{2,1,0:T(8,128)} %copy-done.2, f32[640]{0:T(1024)} %gain_ref.5, f32[640]{0:T(1024)} %bias_ref.7, bf16[128,640]{1,0:T(8,128)(2,1)} %constant.8.clone.scatter_ref, ...), custom_call_target="tpu_custom_call" | custom-call | flops 629145600 | bytes 1000000 | tf_op jit(solution)/shard_map/pallas_call | solution.py:261
  (30 shorter events, 0.1 us)
Async XLA Ops:
  2.7 15.9 %collective-permute-start = (bf16[128,640]{1,0:T(8,128)(2,1)}, bf16[128,640]{1,0:T(8,128)(2,1)S(1)}, u32[]{:S(2)}, u32[]{:S(2)}) collective-permute-start(bf16[128,640]{1,0:T(8,128)(2,1)} %get-tuple-element.23.q0_ref), channel_id=1, source_target_pairs={{0,4},{4,8},{8,12},{12,0},{1,5},{5,9},{9,13},{13,1},{2,6},{6,10},{... | collective-permute-start | bytes 491528 | tf_op jit(solution)/shard_map/ppermute | solution.py:300
  4.3 16.9 %collective-permute-start.1 = (bf16[128,640]{1,0:T(8,128)(2,1)}, bf16[128,640]{1,0:T(8,128)(2,1)S(1)}, u32[]{:S(2)}, u32[]{:S(2)}) collective-permute-start(bf16[128,640]{1,0:T(8,128)(2,1)} %get-tuple-element.23.q0_ref), channel_id=1, source_target_pairs={{0,12},{4,0},{8,4},{12,8},{1,13},{5,1},{9,5},{13,9},{2,14},{6,2},{... | collective-permute-start | bytes 491528 | tf_op jit(solution)/shard_map/ppermute | solution.py:300
  6.0 16.3 %collective-permute-start.2 = (bf16[128,640]{1,0:T(8,128)(2,1)}, bf16[128,640]{1,0:T(8,128)(2,1)S(1)}, u32[]{:S(2)}, u32[]{:S(2)}) collective-permute-start(bf16[128,640]{1,0:T(8,128)(2,1)} %get-tuple-element.23.q0_ref), channel_id=1, source_target_pairs={{0,8},{4,12},{8,0},{12,4},{1,9},{5,13},{9,1},{13,5},{2,10},{6,14},... | collective-permute-start | bytes 491528 | tf_op jit(solution)/shard_map/ppermute | solution.py:300
  9.9 14.1 %collective-permute-start.3 = (bf16[128,640]{1,0:T(8,128)(2,1)}, bf16[128,640]{1,0:T(8,128)(2,1)S(1)}, u32[]{:S(2)}, u32[]{:S(2)}) collective-permute-start(bf16[128,640]{1,0:T(8,128)(2,1)} %get-tuple-element.24.own_ref), channel_id=1, source_target_pairs={{0,1},{1,2},{2,3},{3,0},{4,5},{5,6},{6,7},{7,4},{8,9},{9,10},{10,1... | collective-permute-start | bytes 491528 | tf_op jit(solution)/shard_map/ppermute | solution.py:290
  13.2 16.0 %collective-permute-start.4 = (bf16[128,640]{1,0:T(8,128)(2,1)}, bf16[128,640]{1,0:T(8,128)(2,1)S(1)}, u32[]{:S(2)}, u32[]{:S(2)}) collective-permute-start(bf16[128,640]{1,0:T(8,128)(2,1)} %get-tuple-element.24.own_ref), channel_id=1, source_target_pairs={{0,2},{1,3},{2,0},{3,1},{4,6},{5,7},{6,4},{7,5},{8,10},{9,11},{10,... | collective-permute-start | bytes 491528 | tf_op jit(solution)/shard_map/ppermute | solution.py:290
  18.6 19.6 %copy-start.13 = (bf16[128,640]{1,0:T(8,128)(2,1)}, bf16[128,640]{1,0:T(8,128)(2,1)S(1)}, u32[]{:S(2)}) copy-start(bf16[128,640]{1,0:T(8,128)(2,1)S(1)} %collective-permute-done.q1_ref) | copy-start | bytes 491524
  18.6 14.3 %collective-permute-start.5 = (bf16[128,640]{1,0:T(8,128)(2,1)}, bf16[128,640]{1,0:T(8,128)(2,1)S(1)}, u32[]{:S(2)}, u32[]{:S(2)}) collective-permute-start(bf16[128,640]{1,0:T(8,128)(2,1)} %get-tuple-element.24.own_ref), channel_id=1, source_target_pairs={{0,3},{1,0},{2,1},{3,2},{4,7},{5,4},{6,5},{7,6},{8,11},{9,8},{10,9... | collective-permute-start | bytes 491528 | tf_op jit(solution)/shard_map/ppermute | solution.py:290
  21.2 16.9 %copy-start.15 = (bf16[128,640]{1,0:T(8,128)(2,1)}, bf16[128,640]{1,0:T(8,128)(2,1)S(1)}, u32[]{:S(2)}) copy-start(bf16[128,640]{1,0:T(8,128)(2,1)S(1)} %collective-permute-done.1.q2_ref) | copy-start | bytes 491524
  21.2 16.9 %collective-permute-start.10 = (bf16[128,640]{1,0:T(8,128)(2,1)}, bf16[128,640]{1,0:T(8,128)(2,1)S(1)}, u32[]{:S(2)}, u32[]{:S(2)}) collective-permute-start(bf16[128,640]{1,0:T(8,128)(2,1)} %get-tuple-element.31.q0_ref), channel_id=1, source_target_pairs={{0,12},{4,0},{8,4},{12,8},{1,13},{5,1},{9,5},{13,9},{2,14},{6,2},{... | collective-permute-start | bytes 491528 | tf_op jit(solution)/shard_map/ppermute | solution.py:300
  22.3 15.9 %copy-start.16 = (bf16[128,640]{1,0:T(8,128)(2,1)}, bf16[128,640]{1,0:T(8,128)(2,1)S(1)}, u32[]{:S(2)}) copy-start(bf16[128,640]{1,0:T(8,128)(2,1)S(1)} %collective-permute-done.2.q3_ref) | copy-start | bytes 491524
  22.3 27.4 %collective-permute-start.11 = (bf16[128,640]{1,0:T(8,128)(2,1)}, bf16[128,640]{1,0:T(8,128)(2,1)S(1)}, u32[]{:S(2)}, u32[]{:S(2)}) collective-permute-start(bf16[128,640]{1,0:T(8,128)(2,1)} %get-tuple-element.31.q0_ref), channel_id=1, source_target_pairs={{0,8},{4,12},{8,0},{12,4},{1,9},{5,13},{9,1},{13,5},{2,10},{6,14},... | collective-permute-start | bytes 491528 | tf_op jit(solution)/shard_map/ppermute | solution.py:300
  24.0 14.2 %copy-start.18 = (bf16[128,640]{1,0:T(8,128)(2,1)}, bf16[128,640]{1,0:T(8,128)(2,1)S(1)}, u32[]{:S(2)}) copy-start(bf16[128,640]{1,0:T(8,128)(2,1)S(1)} %collective-permute-done.3.z1_ref) | copy-start | bytes 491524
  24.0 30.6 %collective-permute-start.9 = (bf16[128,640]{1,0:T(8,128)(2,1)}, bf16[128,640]{1,0:T(8,128)(2,1)S(1)}, u32[]{:S(2)}, u32[]{:S(2)}) collective-permute-start(bf16[128,640]{1,0:T(8,128)(2,1)} %get-tuple-element.31.q0_ref), channel_id=1, source_target_pairs={{0,4},{4,8},{8,12},{12,0},{1,5},{5,9},{9,13},{13,1},{2,6},{6,10},{... | collective-permute-start | bytes 491528 | tf_op jit(solution)/shard_map/ppermute | solution.py:300
  29.2 9.0 %copy-start.20 = (bf16[128,640]{1,0:T(8,128)(2,1)}, bf16[128,640]{1,0:T(8,128)(2,1)S(1)}, u32[]{:S(2)}) copy-start(bf16[128,640]{1,0:T(8,128)(2,1)S(1)} %collective-permute-done.4.z2_ref) | copy-start | bytes 491524
  29.2 26.6 %collective-permute-start.12 = (bf16[128,640]{1,0:T(8,128)(2,1)}, bf16[128,640]{1,0:T(8,128)(2,1)S(1)}, u32[]{:S(2)}, u32[]{:S(2)}) collective-permute-start(bf16[128,640]{1,0:T(8,128)(2,1)} %get-tuple-element.32.own_ref), channel_id=1, source_target_pairs={{0,1},{1,2},{2,3},{3,0},{4,5},{5,6},{6,7},{7,4},{8,9},{9,10},{10,1... | collective-permute-start | bytes 491528 | tf_op jit(solution)/shard_map/ppermute | solution.py:290
  32.9 5.3 %copy-start.21 = (bf16[128,640]{1,0:T(8,128)(2,1)}, bf16[128,640]{1,0:T(8,128)(2,1)S(1)}, u32[]{:S(2)}) copy-start(bf16[128,640]{1,0:T(8,128)(2,1)S(1)} %collective-permute-done.5.z3_ref) | copy-start | bytes 491524
  32.9 27.7 %collective-permute-start.13 = (bf16[128,640]{1,0:T(8,128)(2,1)}, bf16[128,640]{1,0:T(8,128)(2,1)S(1)}, u32[]{:S(2)}, u32[]{:S(2)}) collective-permute-start(bf16[128,640]{1,0:T(8,128)(2,1)} %get-tuple-element.32.own_ref), channel_id=1, source_target_pairs={{0,2},{1,3},{2,0},{3,1},{4,6},{5,7},{6,4},{7,5},{8,10},{9,11},{10,... | collective-permute-start | bytes 491528 | tf_op jit(solution)/shard_map/ppermute | solution.py:290
  38.1 11.5 %copy-start.10 = (bf16[128,640]{1,0:T(8,128)(2,1)}, bf16[128,640]{1,0:T(8,128)(2,1)S(1)}, u32[]{:S(2)}) copy-start(bf16[128,640]{1,0:T(8,128)(2,1)S(1)} %collective-permute-done.10.q2_ref) | copy-start | bytes 491524
  38.1 22.4 %collective-permute-start.14 = (bf16[128,640]{1,0:T(8,128)(2,1)}, bf16[128,640]{1,0:T(8,128)(2,1)S(1)}, u32[]{:S(2)}, u32[]{:S(2)}) collective-permute-start(bf16[128,640]{1,0:T(8,128)(2,1)} %get-tuple-element.32.own_ref), channel_id=1, source_target_pairs={{0,3},{1,0},{2,1},{3,2},{4,7},{5,4},{6,5},{7,6},{8,11},{9,8},{10,9... | collective-permute-start | bytes 491528 | tf_op jit(solution)/shard_map/ppermute | solution.py:290
  38.2 11.5 %copy-start.3 = (bf16[2,1,128,640]{3,2,1,0:T(8,128)(2,1)S(1)}, bf16[2,1,128,640]{3,2,1,0:T(8,128)(2,1)}, u32[]{:S(2)}) copy-start(bf16[2,1,128,640]{3,2,1,0:T(8,128)(2,1)} %param.18) | copy-start | bytes 983044
  49.7 12.8 %copy-start.11 = (bf16[128,640]{1,0:T(8,128)(2,1)}, bf16[128,640]{1,0:T(8,128)(2,1)S(1)}, u32[]{:S(2)}) copy-start(bf16[128,640]{1,0:T(8,128)(2,1)S(1)} %collective-permute-done.11.q3_ref) | copy-start | bytes 491524
  49.7 44.7 %collective-permute-start.18 = (bf16[256,640]{1,0:T(8,128)(2,1)S(1)}, bf16[256,640]{1,0:T(8,128)(2,1)S(1)}, u32[]{:S(2)}, u32[]{:S(2)}) collective-permute-start(bf16[256,640]{1,0:T(8,128)(2,1)S(1)} %bitcast.10), channel_id=1, source_target_pairs={{0,1},{1,2},{2,3},{3,4},{4,5},{5,6},{6,7},{7,8},{8,9},{9,10},{10,1... | collective-permute-start | bytes 983048 | tf_op jit(solution)/shard_map/ppermute | solution.py:304
  54.6 7.9 %copy-start.12 = (bf16[128,640]{1,0:T(8,128)(2,1)}, bf16[128,640]{1,0:T(8,128)(2,1)S(1)}, u32[]{:S(2)}) copy-start(bf16[128,640]{1,0:T(8,128)(2,1)S(1)} %collective-permute-done.9.q1_ref) | copy-start | bytes 491524
  54.6 39.9 %collective-permute-start.19 = (bf16[256,640]{1,0:T(8,128)(2,1)S(1)}, bf16[256,640]{1,0:T(8,128)(2,1)S(1)}, u32[]{:S(2)}, u32[]{:S(2)}) collective-permute-start(bf16[256,640]{1,0:T(8,128)(2,1)S(1)} %bitcast.11), channel_id=1, source_target_pairs={{1,0},{2,1},{3,2},{4,3},{5,4},{6,5},{7,6},{8,7},{9,8},{10,9},{11,1... | collective-permute-start | bytes 983048 | tf_op jit(solution)/shard_map/ppermute | solution.py:305
  55.9 6.6 %copy-start.14 = (bf16[128,640]{1,0:T(8,128)(2,1)}, bf16[128,640]{1,0:T(8,128)(2,1)S(1)}, u32[]{:S(2)}) copy-start(bf16[128,640]{1,0:T(8,128)(2,1)S(1)} %collective-permute-done.12.z1_ref) | copy-start | bytes 491524
  55.9 18.1 %collective-permute-start.6 = (bf16[128,768]{1,0:T(8,128)(2,1)}, bf16[128,768]{1,0:T(8,128)(2,1)S(1)}, u32[]{:S(2)}, u32[]{:S(2)}) collective-permute-start(bf16[128,768]{1,0:T(8,128)(2,1)} %get-tuple-element.27), channel_id=1, source_target_pairs={{0,12},{4,0},{8,4},{12,8},{1,13},{5,1},{9,5},{13,9},{2,14},{6,2},{... | collective-permute-start | bytes 589832 | tf_op jit(solution)/shard_map/ppermute | solution.py:334
  60.6 1.9 %copy-start.17 = (bf16[128,640]{1,0:T(8,128)(2,1)}, bf16[128,640]{1,0:T(8,128)(2,1)S(1)}, u32[]{:S(2)}) copy-start(bf16[128,640]{1,0:T(8,128)(2,1)S(1)} %collective-permute-done.13.z2_ref) | copy-start | bytes 491524
  60.6 15.4 %collective-permute-start.7 = (bf16[128,768]{1,0:T(8,128)(2,1)}, bf16[128,768]{1,0:T(8,128)(2,1)S(1)}, u32[]{:S(2)}, u32[]{:S(2)}) collective-permute-start(bf16[128,768]{1,0:T(8,128)(2,1)} %get-tuple-element.28), channel_id=1, source_target_pairs={{0,4},{4,8},{8,12},{12,0},{1,5},{5,9},{9,13},{13,1},{2,6},{6,10},{... | collective-permute-start | bytes 589832 | tf_op jit(solution)/shard_map/ppermute | solution.py:334
  60.6 1.9 %copy-start.19 = (bf16[128,640]{1,0:T(8,128)(2,1)}, bf16[128,640]{1,0:T(8,128)(2,1)S(1)}, u32[]{:S(2)}) copy-start(bf16[128,640]{1,0:T(8,128)(2,1)S(1)} %collective-permute-done.14.z3_ref) | copy-start | bytes 491524
  60.6 15.8 %collective-permute-start.8 = (bf16[128,768]{1,0:T(8,128)(2,1)}, bf16[128,768]{1,0:T(8,128)(2,1)S(1)}, u32[]{:S(2)}, u32[]{:S(2)}) collective-permute-start(bf16[128,768]{1,0:T(8,128)(2,1)} %get-tuple-element.29), channel_id=1, source_target_pairs={{0,8},{4,12},{8,0},{12,4},{1,9},{5,13},{9,1},{13,5},{2,10},{6,14},... | collective-permute-start | bytes 589832 | tf_op jit(solution)/shard_map/ppermute | solution.py:334
  74.0 4.5 %copy-start.4 = (bf16[128,768]{1,0:T(8,128)(2,1)}, bf16[128,768]{1,0:T(8,128)(2,1)S(1)}, u32[]{:S(2)}) copy-start(bf16[128,768]{1,0:T(8,128)(2,1)S(1)} %collective-permute-done.6.o1_ref) | copy-start | bytes 589828
  74.0 7.7 %collective-permute-start.15 = (bf16[128,768]{1,0:T(8,128)(2,1)}, bf16[128,768]{1,0:T(8,128)(2,1)S(1)}, u32[]{:S(2)}, u32[]{:S(2)}) collective-permute-start(bf16[128,768]{1,0:T(8,128)(2,1)} %get-tuple-element.35), channel_id=1, source_target_pairs={{0,12},{4,0},{8,4},{12,8},{1,13},{5,1},{9,5},{13,9},{2,14},{6,2},{... | collective-permute-start | bytes 589832 | tf_op jit(solution)/shard_map/ppermute | solution.py:334
  76.0 2.4 %copy-start.5 = (bf16[128,768]{1,0:T(8,128)(2,1)}, bf16[128,768]{1,0:T(8,128)(2,1)S(1)}, u32[]{:S(2)}) copy-start(bf16[128,768]{1,0:T(8,128)(2,1)S(1)} %collective-permute-done.7.o2_ref) | copy-start | bytes 589828
  76.0 9.2 %collective-permute-start.16 = (bf16[128,768]{1,0:T(8,128)(2,1)}, bf16[128,768]{1,0:T(8,128)(2,1)S(1)}, u32[]{:S(2)}, u32[]{:S(2)}) collective-permute-start(bf16[128,768]{1,0:T(8,128)(2,1)} %get-tuple-element.36), channel_id=1, source_target_pairs={{0,4},{4,8},{8,12},{12,0},{1,5},{5,9},{9,13},{13,1},{2,6},{6,10},{... | collective-permute-start | bytes 589832 | tf_op jit(solution)/shard_map/ppermute | solution.py:334
  76.4 2.1 %copy-start.6 = (bf16[128,768]{1,0:T(8,128)(2,1)}, bf16[128,768]{1,0:T(8,128)(2,1)S(1)}, u32[]{:S(2)}) copy-start(bf16[128,768]{1,0:T(8,128)(2,1)S(1)} %collective-permute-done.8.o3_ref) | copy-start | bytes 589828
  76.4 8.8 %collective-permute-start.17 = (bf16[128,768]{1,0:T(8,128)(2,1)}, bf16[128,768]{1,0:T(8,128)(2,1)S(1)}, u32[]{:S(2)}, u32[]{:S(2)}) collective-permute-start(bf16[128,768]{1,0:T(8,128)(2,1)} %get-tuple-element.37), channel_id=1, source_target_pairs={{0,8},{4,12},{8,0},{12,4},{1,9},{5,13},{9,1},{13,5},{2,10},{6,14},... | collective-permute-start | bytes 589832 | tf_op jit(solution)/shard_map/ppermute | solution.py:334
  81.7 3.6 %copy-start.7 = (bf16[128,768]{1,0:T(8,128)(2,1)}, bf16[128,768]{1,0:T(8,128)(2,1)S(1)}, u32[]{:S(2)}) copy-start(bf16[128,768]{1,0:T(8,128)(2,1)S(1)} %collective-permute-done.15.o1_ref) | copy-start | bytes 589828
  85.2 0.7 copy-start.8
  85.2 0.7 copy-start.9
  89.2 15.5 %all-to-all-start = ((f32[16,8,128]{2,1,0:T(8,128)}), f32[16,8,128]{2,1,0:T(8,128)S(1)}, u32[]{:S(2)}, u32[]{:S(2)}) async-start(f32[16,8,128]{2,1,0:T(8,128)} %get-tuple-element.40), calls=%async_computation | async-start | bytes 131072 | tf_op jit(solution)/shard_map/all_to_all | solution.py:372
  94.5 0.7 copy-start
  95.2 0.7 copy-start.1
  104.7 0.6 copy-start.2

commit v2 on v1

--- a/solution.py
+++ b/solution.py
@@ -18,6 +18,7 @@
 
 F32 = jnp.float32
 BF16 = jnp.bfloat16
+VMEM = pl.BlockSpec(memory_space=pltpu.VMEM)
 
 
 def normalize(values, gain, bias):
@@ -57,12 +58,17 @@
     )
 
 
+def project(x, wk_ref, wv_ref, kv_scr, slot):
+    weights = jnp.concatenate([wk_ref[...], wv_ref[...]], axis=1)
+    kv_scr[slot] = jnp.dot(x, weights, preferred_element_type=F32).astype(BF16)
+
+
 def attend_kernel(
     q0_ref, q1_ref, q2_ref, q3_ref,
     z1_ref, z2_ref, z3_ref, fresh_ref, own_ref,
-    wk_ref, wv_ref,
+    wk0_ref, wv0_ref, wk_ref, wv_ref,
     o0_ref, o1_ref, o2_ref, o3_ref,
-    x_scr, tile_scr,
+    x_scr, kv_scr, tile_scr,
 ):
     pair = pl.program_id(0)
     rows = fresh_ref.shape[0]
@@ -74,10 +80,10 @@
         for index, ref in enumerate((z1_ref, z2_ref, z3_ref, fresh_ref, own_ref)):
             x_scr[index * rows : (index + 1) * rows, :] = ref[...]
         tile_scr[...] = jnp.zeros_like(tile_scr)
-
-    weights = jnp.concatenate([wk_ref[...], wv_ref[...]], axis=1)
-    pairs = jnp.dot(x_scr[...], weights, preferred_element_type=F32).astype(BF16)
-    keys, values = pairs[:, :LANES], pairs[:, LANES:]
+        project(x_scr[...], wk0_ref, wv0_ref, kv_scr, 0)
+
+    current = pair & 1
+    keys, values = kv_scr[current, :, :LANES], kv_scr[current, :, LANES:]
     low_all = lax.broadcasted_iota(jnp.int32, keys.shape, 1) < HEAD_DIM
     zero = jnp.zeros((), BF16)
     one = jnp.ones((), BF16)
@@ -88,28 +94,36 @@
         [jnp.where(low_all, zero, values), jnp.where(low_all, zero, one)], axis=1
     )
     common, fresh, own = slice(0, 3 * rows), slice(3 * rows, 4 * rows), slice(4 * rows, 5 * rows)
-    queries = jnp.concatenate([q0_ref[...], q1_ref[...], q2_ref[...], q3_ref[...]], 0)
-    lane = lax.broadcasted_iota(jnp.int32, queries.shape, 1)
-    low = lane < HEAD_DIM
-    shared_weights, single_weights, tops = [], [], []
-    for part in (jnp.where(low, queries, zero), jnp.where(low, zero, queries)):
-        shared = scores_of(part, keys[common])
-        single = jnp.concatenate(
-            [scores_of(part[:rows], keys[fresh]), scores_of(part[rows:], keys[own])], 0
+    lanes = pl.ds(pl.multiple_of(pair * LANES, LANES), LANES)
+    mine = q0_ref[:, lanes]
+    others = jnp.concatenate([q1_ref[:, lanes], q2_ref[:, lanes], q3_ref[:, lanes]], 0)
+
+    def halves(x):
+        low_part = lax.broadcasted_iota(jnp.int32, x.shape, 1) < HEAD_DIM
+        return jnp.concatenate([jnp.where(low_part, x, zero), jnp.where(low_part, zero, x)], 0)
+
+    mine, others = halves(mine), halves(others)
+    shared = scores_of(jnp.concatenate([mine, others], 0), keys[common])
+    single = jnp.concatenate([scores_of(mine, keys[fresh]), scores_of(others, keys[own])], 0)
+    top = single
+    for index in range(3):
+        top = jnp.maximum(top, shared[:, index * LANES : (index + 1) * LANES])
+    top = jnp.max(top, -1, keepdims=True)
+    shared = jnp.exp(shared - top).astype(BF16)
+    single = jnp.exp(single - top).astype(BF16)
+
+    def paired(x):
+        return (
+            jnp.concatenate([x[:rows], x[2 * rows : 5 * rows]], 0),
+            jnp.concatenate([x[rows : 2 * rows], x[5 * rows :]], 0),
         )
-        top = single
-        for index in range(3):
-            top = jnp.maximum(top, shared[:, index * LANES : (index + 1) * LANES])
-        top = jnp.max(top, -1, keepdims=True)
-        tops.append(top)
-        shared_weights.append(jnp.exp(shared - top).astype(BF16))
-        single_weights.append(jnp.exp(single - top).astype(BF16))
+
     summed = jnp.dot(
-        jnp.concatenate(shared_weights, 1),
+        jnp.concatenate(paired(shared), 1),
         jnp.concatenate([low_values[common], high_values[common]], 0),
         preferred_element_type=F32,
     )
-    single = jnp.concatenate(single_weights, 1)
+    single = jnp.concatenate(paired(single), 1)
     summed = summed + jnp.concatenate(
         [
             jnp.dot(
@@ -127,10 +141,11 @@
     )
     total = summed[:, LANES:]
     mixed = (summed[:, :LANES] / total).astype(BF16)
-    lanes = pl.ds(pl.multiple_of(pair * LANES, LANES), LANES)
     for index, o_ref in enumerate(out_refs):
         o_ref[:, lanes] = mixed[index * rows : (index + 1) * rows]
-    rest = jnp.where(low, tops[0], tops[1]) + jnp.log(total)
+    lane = lax.broadcasted_iota(jnp.int32, total.shape, 1)
+    low_top, high_top = paired(top)
+    rest = jnp.where(lane < HEAD_DIM, low_top, high_top) + jnp.log(total)
     slot = lane & (HEAD_DIM - 1)
     tile = tile_scr[...]
     for piece in range(3):
@@ -138,6 +153,7 @@
         tile = jnp.where(slot == pair + piece * PIECES, rounded, tile)
         rest = rest - rounded
     tile_scr[...] = tile
+    project(x_scr[...], wk_ref, wv_ref, kv_scr, 1 - current)
 
     @pl.when(pair == pl.num_programs(0) - 1)
     def _():
@@ -207,28 +223,19 @@
     return jnp.where(col == edge, 0.0, rolled).astype(BF16)
 
 
-def taps(x, w_ref, cols):
+def taps(x, weights, cols):
     wide = x.astype(F32)
-    total = jnp.dot(shifted(wide, 1, cols), w_ref[0], preferred_element_type=F32)
-    total += jnp.dot(x, w_ref[1], preferred_element_type=F32)
-    total += jnp.dot(shifted(wide, -1, cols), w_ref[2], preferred_element_type=F32)
-    return total
+    unfolded = jnp.concatenate([shifted(wide, 1, cols), x, shifted(wide, -1, cols)], 1)
+    weights = weights.reshape(-1, weights.shape[-1])
+    return jnp.dot(unfolded, weights, preferred_element_type=F32)
 
 
 def rim_kernel(above_ref, below_ref, w_ref, bias_ref, shift_ref, out_ref, *, cols):
-    step = pl.program_id(0)
-
-    @pl.when(step == 0)
-    def _():
-        first = taps(above_ref[...], w_ref, cols) + as_row(bias_ref)
-        samples = first.shape[0] // cols
-        for sample in range(samples):
-            part = slice(sample * cols, (sample + 1) * cols)
-            out_ref[part, :] = first[part] + shift_ref[sample : sample + 1, :]
-
-    @pl.when(step == 1)
-    def _():
-        out_ref[...] += taps(below_ref[...], w_ref, cols)
+    total = taps(above_ref[...], w_ref[0], cols) + taps(below_ref[...], w_ref[2], cols)
+    total += as_row(bias_ref)
+    for sample in range(total.shape[0] // cols):
+        part = slice(sample * cols, (sample + 1) * cols)
+        out_ref[part, :] = total[part] + shift_ref[sample : sample + 1, :]
 
 
 def final_kernel(
@@ -249,7 +256,7 @@
         activated.append((value / (1.0 + jnp.exp(-value))).astype(BF16))
     x = jnp.concatenate(activated, 0)
     out_ref[...] = (
-        taps(x, w_ref, cols) + rim_ref[...] + jnp.concatenate(wide, 0)
+        taps(x, w_ref[1], cols) + rim_ref[...] + jnp.concatenate(wide, 0)
     ).astype(BF16)
 
 
@@ -257,10 +264,16 @@
     return [(i, (i + by) % count) for i in range(count)]
 
 
-def call(kernel, out_shape, *args, flops=1000000, **kwargs):
+def on_chip(x):
+    return pltpu.with_memory_space_constraint(x, pltpu.VMEM)
+
+
+def call(kernel, out_shape, *args, flops=1000000, chip=(), **kwargs):
+    args = [on_chip(x) if index in chip else x for index, x in enumerate(args)]
     return pl.pallas_call(
         kernel,
         out_shape=out_shape,
+        compiler_params=pltpu.CompilerParams(vmem_limit_bytes=24 * 2 ** 20),
         cost_estimate=pl.CostEstimate(flops=flops, bytes_accessed=1000000, transcendentals=0),
         **kwargs,
     )(*args)
@@ -277,22 +290,21 @@
     y_count, z_count = lax.axis_size("y"), lax.axis_size("z")
     count = y_count * z_count
     hid = hidden.reshape(every, channels)
-    block = jax.ShapeDtypeStruct((tokens, channels), BF16)
+    block = pltpu.VMEM((tokens, channels), BF16)
     full = pl.BlockSpec((every, channels), lambda i: (0, 0))
-    vector = pl.BlockSpec((channels,), lambda i: (0,))
-    whole = pl.BlockSpec((tokens, channels), lambda i: (0, 0))
     shifts = (1, 3, 2)
 
     stale = call(
         stale_norm_kernel, [block] * samples,
         stale_attn_in.reshape(every, channels), ln_gain, ln_bias,
+        in_specs=[VMEM] * 3, out_specs=[VMEM] * samples,
     )
     along = [[lax.ppermute(one, "z", ring(by, z_count)) for by in shifts] for one in stale]
     outs = call(
         query_kernel, [block] * (2 * samples), hid, ln_gain, ln_bias, w_qkv,
         grid=(1,),
-        in_specs=[full, vector, vector, pl.BlockSpec((channels, channels), lambda i: (0, 0))],
-        out_specs=[whole] * (2 * samples),
+        in_specs=[VMEM, VMEM, VMEM, pl.BlockSpec((channels, channels), lambda i: (0, 0))],
+        out_specs=[VMEM] * (2 * samples),
         flops=2 * every * channels * channels,
     )
     queries, fresh = outs[:samples], outs[samples:]
@@ -308,26 +320,29 @@
     spread = jnp.asarray(spread_matrix(channels), BF16)
     group = np.arange(channels) // (channels // GROUPS)
     gather = group[:, None] == np.arange(LANES)[None, :]
-    ext = jax.ShapeDtypeStruct((tokens, wide), BF16)
+    ext = pltpu.VMEM((tokens, wide), BF16)
     back = []
     for s in range(samples):
         outs = call(
             attend_kernel, [ext] * 4,
             *all_queries[s], along[s][0], along[s][2], along[s][1], fresh[s], stale[s],
-            w_qkv, w_qkv,
+            w_qkv, w_qkv, w_qkv, w_qkv,
             grid=(pair_count,),
-            in_specs=[pl.BlockSpec((tokens, LANES), lambda p: (0, p))] * 4
-            + [whole] * 5
+            in_specs=[VMEM] * 9
             + [
-                pl.BlockSpec((channels, LANES), lambda p: (0, pair_count + p)),
-                pl.BlockSpec((channels, LANES), lambda p: (0, 2 * pair_count + p)),
+                pl.BlockSpec((channels, LANES), lambda p: (0, pair_count)),
+                pl.BlockSpec((channels, LANES), lambda p: (0, 2 * pair_count)),
+                pl.BlockSpec((channels, LANES), lambda p: (0, jnp.minimum(pair_count + p + 1, 2 * pair_count - 1))),
+                pl.BlockSpec((channels, LANES), lambda p: (0, jnp.minimum(2 * pair_count + p + 1, 3 * pair_count - 1))),
             ],
-            out_specs=[pl.BlockSpec((tokens, wide), lambda p: (0, 0))] * 4,
+            out_specs=[VMEM] * 4,
             scratch_shapes=[
                 pltpu.VMEM((5 * tokens, channels), BF16),
+                pltpu.VMEM((2, 5 * tokens, 2 * LANES), BF16),
                 pltpu.VMEM((4 * tokens, LANES), F32),
             ],
             flops=6 * 10 ** 9,
+            chip=range(9),
         )
         back.append(
             [outs[0]]
@@ -335,37 +350,28 @@
         )
     rim = call(
         functools.partial(rim_kernel, cols=cols),
-        jax.ShapeDtypeStruct((every, channels), F32),
+        pltpu.VMEM((every, channels), F32),
         above, below, conv_weight, conv_bias, time_shift,
-        grid=(2,),
-        in_specs=[
-            full, full,
-            pl.BlockSpec((None, 3, channels, channels), lambda i: (2 * i, 0, 0, 0)),
-            vector,
-            pl.BlockSpec((samples, channels), lambda i: (0, 0)),
-        ],
-        out_specs=full,
+        in_specs=[VMEM] * 5,
+        out_specs=VMEM,
         flops=12 * every * channels * channels,
+        chip=(0, 1, 2),
     )
     residuals, stats = [], []
     for s in range(samples):
-        small = jax.ShapeDtypeStruct((8, LANES), F32)
+        small = pltpu.VMEM((8, LANES), F32)
         if s:
-            small = jax.ShapeDtypeStruct((count, 8, LANES), F32)
+            small = pltpu.VMEM((count, 8, LANES), F32)
         res, stat = call(
             functools.partial(merge_kernel, sample=s), [block, small],
             *back[s], hid, w_out, spread, jnp.asarray(gather, BF16), *stats,
             grid=(1,),
-            in_specs=[pl.BlockSpec((tokens, wide), lambda i: (0, 0))] * 4
-            + [
-                pl.BlockSpec((tokens, channels), lambda i, s=s: (s, 0)),
-                pl.BlockSpec((channels, channels), lambda i: (0, 0)),
-                pl.BlockSpec((LANES, channels), lambda i: (0, 0)),
-                pl.BlockSpec((channels, LANES), lambda i: (0, 0)),
-            ]
-            + [pl.BlockSpec((8, LANES), lambda i: (0, 0))] * len(stats),
-            out_specs=[whole, pl.BlockSpec(small.shape, lambda i, n=small.ndim: (0,) * n)],
+            in_specs=[VMEM] * 4
+            + [pl.BlockSpec((tokens, channels), lambda i, s=s: (s, 0))]
+            + [VMEM] * (3 + len(stats)),
+            out_specs=[VMEM, VMEM],
             flops=10 ** 9,
+            chip=(0, 1, 2, 3, 5) + (8,) * s,
         )
         residuals.append(res)
         stats = [stat]
@@ -376,16 +382,9 @@
         ),
         jax.ShapeDtypeStruct((every, channels), BF16),
         *residuals, shared, gn_gain, gn_bias, jnp.asarray(gather.T, BF16), conv_weight, rim,
-        grid=(1,),
-        in_specs=[
-            whole, whole,
-            pl.BlockSpec((count, 8, LANES), lambda i: (0, 0, 0)),
-            vector, vector,
-            pl.BlockSpec((LANES, channels), lambda i: (0, 0)),
-            pl.BlockSpec((None, 3, channels, channels), lambda i: (1, 0, 0, 0)),
-            full,
-        ],
-        out_specs=full,
+        in_specs=[VMEM] * 8,
+        out_specs=VMEM,
+        chip=(0, 1, 2, 6, 7),
         flops=6 * every * channels * channels,
     )
     return out.reshape(hidden.shape)

time: 110 us -> 106 us (0.964)
  Pallas kernels: 43 us -> 22 us
  local copies, waits for them, and re-layouts: 2.85 us -> 14.3 us
  waiting for transfers between devices: 12.5 us -> 19.4 us
  starting transfers between devices: 50.8 us -> 49.6 us
    pallas_call x8, Pallas kernels: 43 us -> 22 us  [call(): pl.pallas_call(kernel, out_shape=out_shape, compiler_params=pltpu.Compile...]
    unnamed x44 -> x40, local copies, waits for them, and re-layouts: 2.85 us -> 14.3 us
    ppermute x6, waiting for transfers between devices: 3.56 us -> 9.12 us  [shards(): lax.ppermute(one, 'y', ring(-by, y_count))]
    all_to_all x1, waiting for transfers between devices: 3.95 us -> 5.25 us  [shards(): shared = lax.all_to_all(stats[0], ('y', 'z'), 0, 0)]
    ppermute x6, starting transfers between devices: 11 us -> 9.9 us  [shards(): lax.ppermute(one, 'y', ring(-by, y_count))]
  transfers between devices with their start and end apart: 21 -> 21, of which waited for: 3 -> 6; matrix products, arithmetic and copies ran while one was open for 0% -> 0% of each run, Pallas kernels for 33% -> 18%
where the time goes in v2:
time: 106 us; the launch traced here: 105 us
  starting transfers between devices  49.6 us (47%)
  Pallas kernels  22 us (21%)
  waiting for transfers between devices  19.4 us (18%)
  local copies, waits for them, and re-layouts  14.3 us (13%)
    pallas_call x8, Pallas kernels, call(): pl.pallas_call(kernel, out_shape=out_shape, compiler_params=pltpu.Compile...  22 us
    ppermute x6, starting transfers between devices, shards(): lax.ppermute(one, 'z', ring(by, z_count))  21.1 us
    unnamed x40, local copies, waits for them, and re-layouts  14.3 us
    ppermute x6, starting transfers between devices, shards(): lax.ppermute(one, 'y', ring(-by, y_count))  9.9 us
    ppermute x6, waiting for transfers between devices, shards(): lax.ppermute(one, 'y', ring(-by, y_count))  9.12 us
    ppermute x6, starting transfers between devices, shards(): lax.ppermute(one, 'y', ring(by, y_count))  8.27 us
    all_to_all x1, waiting for transfers between devices, shards(): shared = lax.all_to_all(stats[0], ('y', 'z'), 0, 0)  5.25 us
    ppermute x6, waiting for transfers between devices, shards(): lax.ppermute(one, 'z', ring(by, z_count))  4.97 us
  transfers between devices with their start and end apart: 21, of which 6 were waited for; matrix products, arithmetic and copies ran while one was open for 0% of the time, Pallas kernels for 18%

profile of v2, /device:TPU:2, one launch (start us, length us, event | category | flops | bytes accessed | tf_op | source)
XLA Modules:
  0.0 105.4 jit_solution(6422030165624698708)
XLA Ops:
  0.0 1.7 %copy-done.2 = bf16[640,1920]{1,0:T(8,128)(2,1)S(1)} copy-done((bf16[640,1920]{1,0:T(8,128)(2,1)S(1)}, bf16[640,1920]{1,0:T(8,128)(2,1)}, u32[]{:S(2)}) %copy-start.2) | copy-done | bytes 2457624
  1.7 1.0 copy-done.5
  2.7 0.7 copy-done.8
  3.4 0.7 copy-done.10
  4.0 0.7 shard_map.154
  4.7 1.7 %collective-permute-start = (bf16[128,640]{1,0:T(8,128)(2,1)S(1)}, bf16[128,640]{1,0:T(8,128)(2,1)S(1)}, u32[]{:S(2)}, u32[]{:S(2)}) collective-permute-start(bf16[128,640]{1,0:T(8,128)(2,1)S(1)} %get-tuple-element.23.q0_ref), channel_id=1, source_target_pairs={{0,4},{4,8},{8,12},{12,0},{1,5},{5,9},{9,13},{13,1},{2,6},{6,10},{... | collective-permute-start | bytes 491528 | tf_op jit(solution)/shard_map/ppermute | solution.py:312
  6.4 1.7 %collective-permute-start.1 = (bf16[128,640]{1,0:T(8,128)(2,1)S(1)}, bf16[128,640]{1,0:T(8,128)(2,1)S(1)}, u32[]{:S(2)}, u32[]{:S(2)}) collective-permute-start(bf16[128,640]{1,0:T(8,128)(2,1)S(1)} %get-tuple-element.23.q0_ref), channel_id=1, source_target_pairs={{0,12},{4,0},{8,4},{12,8},{1,13},{5,1},{9,5},{13,9},{2,14},{6,2},{... | collective-permute-start | bytes 491528 | tf_op jit(solution)/shard_map/ppermute | solution.py:312
  8.1 2.0 %collective-permute-start.2 = (bf16[128,640]{1,0:T(8,128)(2,1)S(1)}, bf16[128,640]{1,0:T(8,128)(2,1)S(1)}, u32[]{:S(2)}, u32[]{:S(2)}) collective-permute-start(bf16[128,640]{1,0:T(8,128)(2,1)S(1)} %get-tuple-element.23.q0_ref), channel_id=1, source_target_pairs={{0,8},{4,12},{8,0},{12,4},{1,9},{5,13},{9,1},{13,5},{2,10},{6,14},... | collective-permute-start | bytes 491528 | tf_op jit(solution)/shard_map/ppermute | solution.py:312
  10.1 1.0 copy-done.4
  11.0 0.7 copy-done.9
  11.7 0.7 copy-done.11
  12.4 0.3 shard_map.155
  12.7 3.4 %collective-permute-start.3 = (bf16[128,640]{1,0:T(8,128)(2,1)S(1)}, bf16[128,640]{1,0:T(8,128)(2,1)S(1)}, u32[]{:S(2)}, u32[]{:S(2)}) collective-permute-start(bf16[128,640]{1,0:T(8,128)(2,1)S(1)} %get-tuple-element.24.own_ref), channel_id=1, source_target_pairs={{0,1},{1,2},{2,3},{3,0},{4,5},{5,6},{6,7},{7,4},{8,9},{9,10},{10,1... | collective-permute-start | bytes 491528 | tf_op jit(solution)/shard_map/ppermute | solution.py:302
  16.0 5.4 %collective-permute-start.4 = (bf16[128,640]{1,0:T(8,128)(2,1)S(1)}, bf16[128,640]{1,0:T(8,128)(2,1)S(1)}, u32[]{:S(2)}, u32[]{:S(2)}) collective-permute-start(bf16[128,640]{1,0:T(8,128)(2,1)S(1)} %get-tuple-element.24.own_ref), channel_id=1, source_target_pairs={{0,2},{1,3},{2,0},{3,1},{4,6},{5,7},{6,4},{7,5},{8,10},{9,11},{10,... | collective-permute-start | bytes 491528 | tf_op jit(solution)/shard_map/ppermute | solution.py:302
  21.4 0.0 collective-permute-done.q1_ref
  21.4 2.7 %collective-permute-start.5 = (bf16[128,640]{1,0:T(8,128)(2,1)S(1)}, bf16[128,640]{1,0:T(8,128)(2,1)S(1)}, u32[]{:S(2)}, u32[]{:S(2)}) collective-permute-start(bf16[128,640]{1,0:T(8,128)(2,1)S(1)} %get-tuple-element.24.own_ref), channel_id=1, source_target_pairs={{0,3},{1,0},{2,1},{3,2},{4,7},{5,4},{6,5},{7,6},{8,11},{9,8},{10,9... | collective-permute-start | bytes 491528 | tf_op jit(solution)/shard_map/ppermute | solution.py:302
  24.1 0.0 collective-permute-done.1.q2_ref
  24.1 1.1 %collective-permute-start.10 = (bf16[128,640]{1,0:T(8,128)(2,1)S(1)}, bf16[128,640]{1,0:T(8,128)(2,1)S(1)}, u32[]{:S(2)}, u32[]{:S(2)}) collective-permute-start(bf16[128,640]{1,0:T(8,128)(2,1)S(1)} %get-tuple-element.31.q0_ref), channel_id=1, source_target_pairs={{0,12},{4,0},{8,4},{12,8},{1,13},{5,1},{9,5},{13,9},{2,14},{6,2},{... | collective-permute-start | bytes 491528 | tf_op jit(solution)/shard_map/ppermute | solution.py:312
  25.2 0.0 collective-permute-done.2.q3_ref
  25.2 1.7 %collective-permute-start.11 = (bf16[128,640]{1,0:T(8,128)(2,1)S(1)}, bf16[128,640]{1,0:T(8,128)(2,1)S(1)}, u32[]{:S(2)}, u32[]{:S(2)}) collective-permute-start(bf16[128,640]{1,0:T(8,128)(2,1)S(1)} %get-tuple-element.31.q0_ref), channel_id=1, source_target_pairs={{0,8},{4,12},{8,0},{12,4},{1,9},{5,13},{9,1},{13,5},{2,10},{6,14},... | collective-permute-start | bytes 491528 | tf_op jit(solution)/shard_map/ppermute | solution.py:312
  26.8 0.0 collective-permute-done.3.z1_ref
  26.8 0.2 collective-permute-start.9
  27.1 4.8 %collective-permute-done.4.z2_ref = bf16[128,640]{1,0:T(8,128)(2,1)S(1)} collective-permute-done((bf16[128,640]{1,0:T(8,128)(2,1)S(1)}, bf16[128,640]{1,0:T(8,128)(2,1)S(1)}, u32[]{:S(2)}, u32[]{:S(2)}) %collective-permute-start.4) | collective-permute-done | bytes 163872 | tf_op jit(solution)/shard_map/ppermute | solution.py:302
  31.9 3.5 %collective-permute-start.12 = (bf16[128,640]{1,0:T(8,128)(2,1)S(1)}, bf16[128,640]{1,0:T(8,128)(2,1)S(1)}, u32[]{:S(2)}, u32[]{:S(2)}) collective-permute-start(bf16[128,640]{1,0:T(8,128)(2,1)S(1)} %get-tuple-element.32.own_ref), channel_id=1, source_target_pairs={{0,1},{1,2},{2,3},{3,0},{4,5},{5,6},{6,7},{7,4},{8,9},{9,10},{10,1... | collective-permute-start | bytes 491528 | tf_op jit(solution)/shard_map/ppermute | solution.py:302
  35.4 0.2 collective-permute-done.5.z3_ref
  35.6 6.1 %collective-permute-start.13 = (bf16[128,640]{1,0:T(8,128)(2,1)S(1)}, bf16[128,640]{1,0:T(8,128)(2,1)S(1)}, u32[]{:S(2)}, u32[]{:S(2)}) collective-permute-start(bf16[128,640]{1,0:T(8,128)(2,1)S(1)} %get-tuple-element.32.own_ref), channel_id=1, source_target_pairs={{0,2},{1,3},{2,0},{3,1},{4,6},{5,7},{6,4},{7,5},{8,10},{9,11},{10,... | collective-permute-start | bytes 491528 | tf_op jit(solution)/shard_map/ppermute | solution.py:302
  41.7 0.0 collective-permute-done.10.q2_ref
  41.7 0.0 collective-permute-start.14
  41.7 1.7 %copy-done.3 = bf16[640,1920]{1,0:T(8,128)(2,1)S(1)} copy-done((bf16[640,1920]{1,0:T(8,128)(2,1)S(1)}, bf16[640,1920]{1,0:T(8,128)(2,1)}, u32[]{:S(2)}) %copy-start.3) | copy-done | bytes 2457624
  43.4 7.2 %shard_map.156 = (bf16[128,768]{1,0:T(8,128)(2,1)S(1)}, bf16[128,768]{1,0:T(8,128)(2,1)S(1)}, bf16[128,768]{1,0:T(8,128)(2,1)S(1)}, bf16[128,768]{1,0:T(8,128)(2,1)S(1)}) custom-call(bf16[128,640]{1,0:T(8,128)(2,1)S(1)} %get-tuple-element.23.q0_ref, bf16[128,640]{1,0:T(8,128)(2,1)S(1)} %collective-permute-done.q1_ref, ...), custom_call_target="tpu_custom_call" | custom-call | flops 6000000000 | bytes 1000000 | tf_op jit(solution)/shard_map/pallas_call | solution.py:273
  50.6 0.0 collective-permute-done.11.q3_ref
  50.7 4.8 %collective-permute-start.18 = (bf16[256,640]{1,0:T(8,128)(2,1)S(1)}, bf16[256,640]{1,0:T(8,128)(2,1)S(1)}, u32[]{:S(2)}, u32[]{:S(2)}) collective-permute-start(bf16[256,640]{1,0:T(8,128)(2,1)S(1)} %bitcast.10), channel_id=1, source_target_pairs={{0,1},{1,2},{2,3},{3,4},{4,5},{5,6},{6,7},{7,8},{8,9},{9,10},{10,1... | collective-permute-start | bytes 983048 | tf_op jit(solution)/shard_map/ppermute | solution.py:316
  55.5 0.0 collective-permute-done.9.q1_ref
  55.5 1.3 %collective-permute-start.19 = (bf16[256,640]{1,0:T(8,128)(2,1)S(1)}, bf16[256,640]{1,0:T(8,128)(2,1)S(1)}, u32[]{:S(2)}, u32[]{:S(2)}) collective-permute-start(bf16[256,640]{1,0:T(8,128)(2,1)S(1)} %bitcast.11), channel_id=1, source_target_pairs={{1,0},{2,1},{3,2},{4,3},{5,4},{6,5},{7,6},{8,7},{9,8},{10,9},{11,1... | collective-permute-start | bytes 983048 | tf_op jit(solution)/shard_map/ppermute | solution.py:317
  56.8 3.8 %collective-permute-start.6 = (bf16[128,768]{1,0:T(8,128)(2,1)S(1)}, bf16[128,768]{1,0:T(8,128)(2,1)S(1)}, u32[]{:S(2)}, u32[]{:S(2)}) collective-permute-start(bf16[128,768]{1,0:T(8,128)(2,1)S(1)} %get-tuple-element.27), channel_id=1, source_target_pairs={{0,12},{4,0},{8,4},{12,8},{1,13},{5,1},{9,5},{13,9},{2,14},{6,2},{... | collective-permute-start | bytes 589832 | tf_op jit(solution)/shard_map/ppermute | solution.py:349
  60.6 0.0 collective-permute-done.13.z2_ref
  60.6 0.0 collective-permute-start.7
  60.6 0.0 collective-permute-done.14.z3_ref
  60.6 2.9 %collective-permute-start.8 = (bf16[128,768]{1,0:T(8,128)(2,1)S(1)}, bf16[128,768]{1,0:T(8,128)(2,1)S(1)}, u32[]{:S(2)}, u32[]{:S(2)}) collective-permute-start(bf16[128,768]{1,0:T(8,128)(2,1)S(1)} %get-tuple-element.29), channel_id=1, source_target_pairs={{0,8},{4,12},{8,0},{12,4},{1,9},{5,13},{9,1},{13,5},{2,10},{6,14},... | collective-permute-start | bytes 589832 | tf_op jit(solution)/shard_map/ppermute | solution.py:349
  63.5 7.3 %shard_map.158 = (bf16[128,768]{1,0:T(8,128)(2,1)S(1)}, bf16[128,768]{1,0:T(8,128)(2,1)S(1)}, bf16[128,768]{1,0:T(8,128)(2,1)S(1)}, bf16[128,768]{1,0:T(8,128)(2,1)S(1)}) custom-call(bf16[128,640]{1,0:T(8,128)(2,1)S(1)} %get-tuple-element.31.q0_ref, bf16[128,640]{1,0:T(8,128)(2,1)S(1)} %collective-permute-done.9.q1_ref, ...), custom_call_target="tpu_custom_call" | custom-call | flops 6000000000 | bytes 1000000 | tf_op jit(solution)/shard_map/pallas_call | solution.py:273
  70.8 0.0 copy-start.12
  70.8 0.0 copy-start.15
  70.8 0.0 collective-permute-done.6.o1_ref
  70.8 1.0 collective-permute-start.15
  71.8 0.0 collective-permute-done.7.o2_ref
  71.8 1.1 %collective-permute-start.16 = (bf16[128,768]{1,0:T(8,128)(2,1)S(1)}, bf16[128,768]{1,0:T(8,128)(2,1)S(1)}, u32[]{:S(2)}, u32[]{:S(2)}) collective-permute-start(bf16[128,768]{1,0:T(8,128)(2,1)S(1)} %get-tuple-element.36), channel_id=1, source_target_pairs={{0,4},{4,8},{8,12},{12,0},{1,5},{5,9},{9,13},{13,1},{2,6},{6,10},{... | collective-permute-start | bytes 589832 | tf_op jit(solution)/shard_map/ppermute | solution.py:349
  72.9 4.1 %collective-permute-done.8.o3_ref = bf16[128,768]{1,0:T(8,128)(2,1)S(1)} collective-permute-done((bf16[128,768]{1,0:T(8,128)(2,1)S(1)}, bf16[128,768]{1,0:T(8,128)(2,1)S(1)}, u32[]{:S(2)}, u32[]{:S(2)}) %collective-permute-start.8) | collective-permute-done | bytes 196640 | tf_op jit(solution)/shard_map/ppermute | solution.py:349
  77.0 1.2 %collective-permute-start.17 = (bf16[128,768]{1,0:T(8,128)(2,1)S(1)}, bf16[128,768]{1,0:T(8,128)(2,1)S(1)}, u32[]{:S(2)}, u32[]{:S(2)}) collective-permute-start(bf16[128,768]{1,0:T(8,128)(2,1)S(1)} %get-tuple-element.37), channel_id=1, source_target_pairs={{0,8},{4,12},{8,0},{12,4},{1,9},{5,13},{9,1},{13,5},{2,10},{6,14},... | collective-permute-start | bytes 589832 | tf_op jit(solution)/shard_map/ppermute | solution.py:349
  78.1 0.0 copy-start.7
  78.1 0.0 copy-start.13
  78.2 0.0 copy-start.14
  78.2 1.0 shard_map.157
  79.2 1.2 %collective-permute-done.16.o2_ref = bf16[128,768]{1,0:T(8,128)(2,1)S(1)} collective-permute-done((bf16[128,768]{1,0:T(8,128)(2,1)S(1)}, bf16[128,768]{1,0:T(8,128)(2,1)S(1)}, u32[]{:S(2)}, u32[]{:S(2)}) %collective-permute-start.16) | collective-permute-done | bytes 196640 | tf_op jit(solution)/shard_map/ppermute | solution.py:349
  80.4 3.9 %collective-permute-done.17.o3_ref = bf16[128,768]{1,0:T(8,128)(2,1)S(1)} collective-permute-done((bf16[128,768]{1,0:T(8,128)(2,1)S(1)}, bf16[128,768]{1,0:T(8,128)(2,1)S(1)}, u32[]{:S(2)}, u32[]{:S(2)}) %collective-permute-start.17) | collective-permute-done | bytes 196640 | tf_op jit(solution)/shard_map/ppermute | solution.py:349
  84.2 1.7 %shard_map.159 = (bf16[128,640]{1,0:T(8,128)(2,1)S(1)}, f32[16,8,128]{2,1,0:T(8,128)}) custom-call(bf16[128,768]{1,0:T(8,128)(2,1)S(1)} %get-tuple-element.34.o0_ref, bf16[128,768]{1,0:T(8,128)(2,1)S(1)} %collective-permute-done.15.o1_ref, bf16[128,768]{1,0:T(8,128)(2,1)S(1)} %collective-permute-done.16.o2_ref, ...), custom_call_target="tpu_custom_call" | custom-call | flops 1000000000 | bytes 1000000 | tf_op jit(solution)/shard_map/pallas_call | solution.py:273
  85.9 4.2 %all-to-all-start = ((f32[16,8,128]{2,1,0:T(8,128)}), f32[16,8,128]{2,1,0:T(8,128)S(1)}, u32[]{:S(2)}, u32[]{:S(2)}) async-start(f32[16,8,128]{2,1,0:T(8,128)} %get-tuple-element.40), calls=%async_computation | async-start | bytes 131072 | tf_op jit(solution)/shard_map/all_to_all | solution.py:378
  90.1 0.0 collective-permute-done.18.above_ref
  90.1 0.0 copy-start
  90.2 3.1 %copy-done = bf16[3,3,640,640]{3,2,1,0:T(8,128)(2,1)S(1)} copy-done((bf16[3,3,640,640]{3,2,1,0:T(8,128)(2,1)S(1)}, bf16[3,3,640,640]{3,2,1,0:T(8,128)(2,1)}, u32[]{:S(2)}) %copy-start) | copy-done | bytes 7372824
  93.2 1.8 %shard_map.160.rim_ref = f32[256,640]{1,0:T(8,128)S(1)} custom-call(bf16[256,640]{1,0:T(8,128)(2,1)S(1)} %collective-permute-done.18.above_ref, bf16[256,640]{1,0:T(8,128)(2,1)S(1)} %collective-permute-done.19.below_ref, bf16[3,3,640,640]{3,2,1,0:T(8,128)(2,1)S(1)} %copy-done, f32[640]{0:T(1024)S(1)} %copy-done.15, f32[2,640]{1,0:T(2,128)S(1)} %copy-done.12), custom_call_target="tpu_custom_call" | custom-call | flops 1258291200 | bytes 1000000 | tf_op jit(solution)/shard_map/pallas_call | solution.py:273
  95.0 5.2 %all-to-all-done.stat_ref = f32[16,8,128]{2,1,0:T(8,128)S(1)} async-done(((f32[16,8,128]{2,1,0:T(8,128)}), f32[16,8,128]{2,1,0:T(8,128)S(1)}, u32[]{:S(2)}, u32[]{:S(2)}) %all-to-all-start) | async-done | bytes 65568 | tf_op jit(solution)/shard_map/all_to_all | solution.py:378
  100.3 0.0 copy-start.1
  100.3 3.1 %copy-done.1 = bf16[3,3,640,640]{3,2,1,0:T(8,128)(2,1)S(1)} copy-done((bf16[3,3,640,640]{3,2,1,0:T(8,128)(2,1)S(1)}, bf16[3,3,640,640]{3,2,1,0:T(8,128)(2,1)}, u32[]{:S(2)}) %copy-start.1) | copy-done | bytes 7372824
  103.4 2.0 %shard_map.161 = bf16[256,640]{1,0:T(8,128)(2,1)} custom-call(bf16[128,640]{1,0:T(8,128)(2,1)S(1)} %get-tuple-element.30.res0_ref, bf16[128,640]{1,0:T(8,128)(2,1)S(1)} %get-tuple-element.39.res1_ref, f32[16,8,128]{2,1,0:T(8,128)S(1)} %all-to-all-done.stat_ref, f32[640]{0:T(1024)S(1)} %copy-done.13, f32[640]{0:T(1024)S(1)} %copy-done.14, ...), custom_call_target="tpu_custom_call" | custom-call | flops 629145600 | bytes 1000000 | tf_op jit(solution)/shard_map/pallas_call | solution.py:273
  (26 shorter events, 0.0 us)
Async XLA Ops:
  0.0 1.7 %copy-start.2 = (bf16[640,1920]{1,0:T(8,128)(2,1)S(1)}, bf16[640,1920]{1,0:T(8,128)(2,1)}, u32[]{:S(2)}) copy-start(bf16[640,1920]{1,0:T(8,128)(2,1)} %wv_ref.3) | copy-start | bytes 7372804
  1.7 1.0 copy-start.5
  2.7 0.7 copy-start.8
  3.4 0.7 copy-start.10
  4.7 16.7 %collective-permute-start = (bf16[128,640]{1,0:T(8,128)(2,1)S(1)}, bf16[128,640]{1,0:T(8,128)(2,1)S(1)}, u32[]{:S(2)}, u32[]{:S(2)}) collective-permute-start(bf16[128,640]{1,0:T(8,128)(2,1)S(1)} %get-tuple-element.23.q0_ref), channel_id=1, source_target_pairs={{0,4},{4,8},{8,12},{12,0},{1,5},{5,9},{9,13},{13,1},{2,6},{6,10},{... | collective-permute-start | bytes 491528 | tf_op jit(solution)/shard_map/ppermute | solution.py:312
  6.4 17.7 %collective-permute-start.1 = (bf16[128,640]{1,0:T(8,128)(2,1)S(1)}, bf16[128,640]{1,0:T(8,128)(2,1)S(1)}, u32[]{:S(2)}, u32[]{:S(2)}) collective-permute-start(bf16[128,640]{1,0:T(8,128)(2,1)S(1)} %get-tuple-element.23.q0_ref), channel_id=1, source_target_pairs={{0,12},{4,0},{8,4},{12,8},{1,13},{5,1},{9,5},{13,9},{2,14},{6,2},{... | collective-permute-start | bytes 491528 | tf_op jit(solution)/shard_map/ppermute | solution.py:312
  8.1 17.1 %collective-permute-start.2 = (bf16[128,640]{1,0:T(8,128)(2,1)S(1)}, bf16[128,640]{1,0:T(8,128)(2,1)S(1)}, u32[]{:S(2)}, u32[]{:S(2)}) collective-permute-start(bf16[128,640]{1,0:T(8,128)(2,1)S(1)} %get-tuple-element.23.q0_ref), channel_id=1, source_target_pairs={{0,8},{4,12},{8,0},{12,4},{1,9},{5,13},{9,1},{13,5},{2,10},{6,14},... | collective-permute-start | bytes 491528 | tf_op jit(solution)/shard_map/ppermute | solution.py:312
  10.1 1.0 copy-start.4
  11.0 0.7 copy-start.9
  11.7 0.7 copy-start.11
  12.7 14.2 %collective-permute-start.3 = (bf16[128,640]{1,0:T(8,128)(2,1)S(1)}, bf16[128,640]{1,0:T(8,128)(2,1)S(1)}, u32[]{:S(2)}, u32[]{:S(2)}) collective-permute-start(bf16[128,640]{1,0:T(8,128)(2,1)S(1)} %get-tuple-element.24.own_ref), channel_id=1, source_target_pairs={{0,1},{1,2},{2,3},{3,0},{4,5},{5,6},{6,7},{7,4},{8,9},{9,10},{10,1... | collective-permute-start | bytes 491528 | tf_op jit(solution)/shard_map/ppermute | solution.py:302
  16.0 15.8 %collective-permute-start.4 = (bf16[128,640]{1,0:T(8,128)(2,1)S(1)}, bf16[128,640]{1,0:T(8,128)(2,1)S(1)}, u32[]{:S(2)}, u32[]{:S(2)}) collective-permute-start(bf16[128,640]{1,0:T(8,128)(2,1)S(1)} %get-tuple-element.24.own_ref), channel_id=1, source_target_pairs={{0,2},{1,3},{2,0},{3,1},{4,6},{5,7},{6,4},{7,5},{8,10},{9,11},{10,... | collective-permute-start | bytes 491528 | tf_op jit(solution)/shard_map/ppermute | solution.py:302
  21.4 14.2 %collective-permute-start.5 = (bf16[128,640]{1,0:T(8,128)(2,1)S(1)}, bf16[128,640]{1,0:T(8,128)(2,1)S(1)}, u32[]{:S(2)}, u32[]{:S(2)}) collective-permute-start(bf16[128,640]{1,0:T(8,128)(2,1)S(1)} %get-tuple-element.24.own_ref), channel_id=1, source_target_pairs={{0,3},{1,0},{2,1},{3,2},{4,7},{5,4},{6,5},{7,6},{8,11},{9,8},{10,9... | collective-permute-start | bytes 491528 | tf_op jit(solution)/shard_map/ppermute | solution.py:302
  24.1 17.6 %collective-permute-start.10 = (bf16[128,640]{1,0:T(8,128)(2,1)S(1)}, bf16[128,640]{1,0:T(8,128)(2,1)S(1)}, u32[]{:S(2)}, u32[]{:S(2)}) collective-permute-start(bf16[128,640]{1,0:T(8,128)(2,1)S(1)} %get-tuple-element.31.q0_ref), channel_id=1, source_target_pairs={{0,12},{4,0},{8,4},{12,8},{1,13},{5,1},{9,5},{13,9},{2,14},{6,2},{... | collective-permute-start | bytes 491528 | tf_op jit(solution)/shard_map/ppermute | solution.py:312
  25.2 25.5 %collective-permute-start.11 = (bf16[128,640]{1,0:T(8,128)(2,1)S(1)}, bf16[128,640]{1,0:T(8,128)(2,1)S(1)}, u32[]{:S(2)}, u32[]{:S(2)}) collective-permute-start(bf16[128,640]{1,0:T(8,128)(2,1)S(1)} %get-tuple-element.31.q0_ref), channel_id=1, source_target_pairs={{0,8},{4,12},{8,0},{12,4},{1,9},{5,13},{9,1},{13,5},{2,10},{6,14},... | collective-permute-start | bytes 491528 | tf_op jit(solution)/shard_map/ppermute | solution.py:312
  26.8 28.7 %collective-permute-start.9 = (bf16[128,640]{1,0:T(8,128)(2,1)S(1)}, bf16[128,640]{1,0:T(8,128)(2,1)S(1)}, u32[]{:S(2)}, u32[]{:S(2)}) collective-permute-start(bf16[128,640]{1,0:T(8,128)(2,1)S(1)} %get-tuple-element.31.q0_ref), channel_id=1, source_target_pairs={{0,4},{4,8},{8,12},{12,0},{1,5},{5,9},{9,13},{13,1},{2,6},{6,10},{... | collective-permute-start | bytes 491528 | tf_op jit(solution)/shard_map/ppermute | solution.py:312
  31.9 25.0 %collective-permute-start.12 = (bf16[128,640]{1,0:T(8,128)(2,1)S(1)}, bf16[128,640]{1,0:T(8,128)(2,1)S(1)}, u32[]{:S(2)}, u32[]{:S(2)}) collective-permute-start(bf16[128,640]{1,0:T(8,128)(2,1)S(1)} %get-tuple-element.32.own_ref), channel_id=1, source_target_pairs={{0,1},{1,2},{2,3},{3,0},{4,5},{5,6},{6,7},{7,4},{8,9},{9,10},{10,1... | collective-permute-start | bytes 491528 | tf_op jit(solution)/shard_map/ppermute | solution.py:302
  35.6 25.0 %collective-permute-start.13 = (bf16[128,640]{1,0:T(8,128)(2,1)S(1)}, bf16[128,640]{1,0:T(8,128)(2,1)S(1)}, u32[]{:S(2)}, u32[]{:S(2)}) collective-permute-start(bf16[128,640]{1,0:T(8,128)(2,1)S(1)} %get-tuple-element.32.own_ref), channel_id=1, source_target_pairs={{0,2},{1,3},{2,0},{3,1},{4,6},{5,7},{6,4},{7,5},{8,10},{9,11},{10,... | collective-permute-start | bytes 491528 | tf_op jit(solution)/shard_map/ppermute | solution.py:302
  41.7 18.9 %collective-permute-start.14 = (bf16[128,640]{1,0:T(8,128)(2,1)S(1)}, bf16[128,640]{1,0:T(8,128)(2,1)S(1)}, u32[]{:S(2)}, u32[]{:S(2)}) collective-permute-start(bf16[128,640]{1,0:T(8,128)(2,1)S(1)} %get-tuple-element.32.own_ref), channel_id=1, source_target_pairs={{0,3},{1,0},{2,1},{3,2},{4,7},{5,4},{6,5},{7,6},{8,11},{9,8},{10,9... | collective-permute-start | bytes 491528 | tf_op jit(solution)/shard_map/ppermute | solution.py:302
  41.7 1.7 %copy-start.3 = (bf16[640,1920]{1,0:T(8,128)(2,1)S(1)}, bf16[640,1920]{1,0:T(8,128)(2,1)}, u32[]{:S(2)}) copy-start(bf16[640,1920]{1,0:T(8,128)(2,1)} %wv_ref.3) | copy-start | bytes 7372804
  43.4 7.3 %copy-start.19 = (bf16[2,1,128,640]{3,2,1,0:T(8,128)(2,1)S(1)}, bf16[2,1,128,640]{3,2,1,0:T(8,128)(2,1)}, u32[]{:S(2)}) copy-start(bf16[2,1,128,640]{3,2,1,0:T(8,128)(2,1)} %param.18) | copy-start | bytes 983044
  50.7 39.4 %collective-permute-start.18 = (bf16[256,640]{1,0:T(8,128)(2,1)S(1)}, bf16[256,640]{1,0:T(8,128)(2,1)S(1)}, u32[]{:S(2)}, u32[]{:S(2)}) collective-permute-start(bf16[256,640]{1,0:T(8,128)(2,1)S(1)} %bitcast.10), channel_id=1, source_target_pairs={{0,1},{1,2},{2,3},{3,4},{4,5},{5,6},{6,7},{7,8},{8,9},{9,10},{10,1... | collective-permute-start | bytes 983048 | tf_op jit(solution)/shard_map/ppermute | solution.py:316
  55.5 34.6 %collective-permute-start.19 = (bf16[256,640]{1,0:T(8,128)(2,1)S(1)}, bf16[256,640]{1,0:T(8,128)(2,1)S(1)}, u32[]{:S(2)}, u32[]{:S(2)}) collective-permute-start(bf16[256,640]{1,0:T(8,128)(2,1)S(1)} %bitcast.11), channel_id=1, source_target_pairs={{1,0},{2,1},{3,2},{4,3},{5,4},{6,5},{7,6},{8,7},{9,8},{10,9},{11,1... | collective-permute-start | bytes 983048 | tf_op jit(solution)/shard_map/ppermute | solution.py:317
  56.8 14.0 %collective-permute-start.6 = (bf16[128,768]{1,0:T(8,128)(2,1)S(1)}, bf16[128,768]{1,0:T(8,128)(2,1)S(1)}, u32[]{:S(2)}, u32[]{:S(2)}) collective-permute-start(bf16[128,768]{1,0:T(8,128)(2,1)S(1)} %get-tuple-element.27), channel_id=1, source_target_pairs={{0,12},{4,0},{8,4},{12,8},{1,13},{5,1},{9,5},{13,9},{2,14},{6,2},{... | collective-permute-start | bytes 589832 | tf_op jit(solution)/shard_map/ppermute | solution.py:349
  60.6 11.2 %collective-permute-start.7 = (bf16[128,768]{1,0:T(8,128)(2,1)S(1)}, bf16[128,768]{1,0:T(8,128)(2,1)S(1)}, u32[]{:S(2)}, u32[]{:S(2)}) collective-permute-start(bf16[128,768]{1,0:T(8,128)(2,1)S(1)} %get-tuple-element.28), channel_id=1, source_target_pairs={{0,4},{4,8},{8,12},{12,0},{1,5},{5,9},{9,13},{13,1},{2,6},{6,10},{... | collective-permute-start | bytes 589832 | tf_op jit(solution)/shard_map/ppermute | solution.py:349
  60.6 16.4 %collective-permute-start.8 = (bf16[128,768]{1,0:T(8,128)(2,1)S(1)}, bf16[128,768]{1,0:T(8,128)(2,1)S(1)}, u32[]{:S(2)}, u32[]{:S(2)}) collective-permute-start(bf16[128,768]{1,0:T(8,128)(2,1)S(1)} %get-tuple-element.29), channel_id=1, source_target_pairs={{0,8},{4,12},{8,0},{12,4},{1,9},{5,13},{9,1},{13,5},{2,10},{6,14},... | collective-permute-start | bytes 589832 | tf_op jit(solution)/shard_map/ppermute | solution.py:349
  63.5 14.6 %copy-start.6 = (bf16[2,1,128,640]{3,2,1,0:T(8,128)(2,1)S(1)}, bf16[2,1,128,640]{3,2,1,0:T(8,128)(2,1)}, u32[]{:S(2)}) copy-start(bf16[2,1,128,640]{3,2,1,0:T(8,128)(2,1)} %param.16) | copy-start | bytes 983044
  63.5 14.6 %copy-start.16 = (bf16[640,640]{1,0:T(8,128)(2,1)S(1)}, bf16[640,640]{1,0:T(8,128)(2,1)}, u32[]{:S(2)}) copy-start(bf16[640,640]{1,0:T(8,128)(2,1)} %w_ref.7) | copy-start | bytes 2457604
  63.5 14.6 %copy-start.17 = (bf16[128,640]{1,0:T(8,128)(2,1)S(1)}, bf16[128,640]{1,0:T(8,128)(2,1)}, u32[]{:S(2)}) copy-start(bf16[128,640]{1,0:T(8,128)(2,1)} %constant.6.clone.spread_ref) | copy-start | bytes 491524
  63.5 14.6 %copy-start.18 = (bf16[640,128]{1,0:T(8,128)(2,1)S(1)}, bf16[640,128]{1,0:T(8,128)(2,1)}, u32[]{:S(2)}) copy-start(bf16[640,128]{1,0:T(8,128)(2,1)} %constant.7.clone.gather_ref) | copy-start | bytes 491524
  70.8 19.4 %copy-start.12 = (f32[2,640]{1,0:T(2,128)S(1)}, f32[2,640]{1,0:T(2,128)}, u32[]{:S(2)}) copy-start(f32[2,640]{1,0:T(2,128)} %shift_ref.1) | copy-start | bytes 15364
  70.8 19.4 %copy-start.15 = (f32[640]{0:T(1024)S(1)}, f32[640]{0:T(1024)}, u32[]{:S(2)}) copy-start(f32[640]{0:T(1024)} %bias_ref.6) | copy-start | bytes 7684
  70.8 8.4 %collective-permute-start.15 = (bf16[128,768]{1,0:T(8,128)(2,1)S(1)}, bf16[128,768]{1,0:T(8,128)(2,1)S(1)}, u32[]{:S(2)}, u32[]{:S(2)}) collective-permute-start(bf16[128,768]{1,0:T(8,128)(2,1)S(1)} %get-tuple-element.35), channel_id=1, source_target_pairs={{0,12},{4,0},{8,4},{12,8},{1,13},{5,1},{9,5},{13,9},{2,14},{6,2},{... | collective-permute-start | bytes 589832 | tf_op jit(solution)/shard_map/ppermute | solution.py:349
  71.8 8.6 %collective-permute-start.16 = (bf16[128,768]{1,0:T(8,128)(2,1)S(1)}, bf16[128,768]{1,0:T(8,128)(2,1)S(1)}, u32[]{:S(2)}, u32[]{:S(2)}) collective-permute-start(bf16[128,768]{1,0:T(8,128)(2,1)S(1)} %get-tuple-element.36), channel_id=1, source_target_pairs={{0,4},{4,8},{8,12},{12,0},{1,5},{5,9},{9,13},{13,1},{2,6},{6,10},{... | collective-permute-start | bytes 589832 | tf_op jit(solution)/shard_map/ppermute | solution.py:349
  77.0 7.2 %collective-permute-start.17 = (bf16[128,768]{1,0:T(8,128)(2,1)S(1)}, bf16[128,768]{1,0:T(8,128)(2,1)S(1)}, u32[]{:S(2)}, u32[]{:S(2)}) collective-permute-start(bf16[128,768]{1,0:T(8,128)(2,1)S(1)} %get-tuple-element.37), channel_id=1, source_target_pairs={{0,8},{4,12},{8,0},{12,4},{1,9},{5,13},{9,1},{13,5},{2,10},{6,14},... | collective-permute-start | bytes 589832 | tf_op jit(solution)/shard_map/ppermute | solution.py:349
  78.1 22.1 %copy-start.7 = (bf16[128,640]{1,0:T(8,128)(2,1)S(1)}, bf16[128,640]{1,0:T(8,128)(2,1)}, u32[]{:S(2)}) copy-start(bf16[128,640]{1,0:T(8,128)(2,1)} %constant.8.clone.scatter_ref) | copy-start | bytes 491524
  78.1 22.1 %copy-start.13 = (f32[640]{0:T(1024)S(1)}, f32[640]{0:T(1024)}, u32[]{:S(2)}) copy-start(f32[640]{0:T(1024)} %gain_ref.5) | copy-start | bytes 7684
  78.2 22.1 %copy-start.14 = (f32[640]{0:T(1024)S(1)}, f32[640]{0:T(1024)}, u32[]{:S(2)}) copy-start(f32[640]{0:T(1024)} %bias_ref.7) | copy-start | bytes 7684
  85.9 14.4 %all-to-all-start = ((f32[16,8,128]{2,1,0:T(8,128)}), f32[16,8,128]{2,1,0:T(8,128)S(1)}, u32[]{:S(2)}, u32[]{:S(2)}) async-start(f32[16,8,128]{2,1,0:T(8,128)} %get-tuple-element.40), calls=%async_computation | async-start | bytes 131072 | tf_op jit(solution)/shard_map/all_to_all | solution.py:378
  90.1 3.1 %copy-start = (bf16[3,3,640,640]{3,2,1,0:T(8,128)(2,1)S(1)}, bf16[3,3,640,640]{3,2,1,0:T(8,128)(2,1)}, u32[]{:S(2)}) copy-start(bf16[3,3,640,640]{3,2,1,0:T(8,128)(2,1)} %w_ref.9) | copy-start | bytes 22118404
  100.3 3.1 %copy-start.1 = (bf16[3,3,640,640]{3,2,1,0:T(8,128)(2,1)S(1)}, bf16[3,3,640,640]{3,2,1,0:T(8,128)(2,1)}, u32[]{:S(2)}) copy-start(bf16[3,3,640,640]{3,2,1,0:T(8,128)(2,1)} %w_ref.9) | copy-start | bytes 22118404

commit v3 on v2

--- a/solution.py
+++ b/solution.py
@@ -33,23 +33,19 @@
     return ref[...].reshape(1, -1)
 
 
-def stale_norm_kernel(x_ref, gain_ref, bias_ref, *out_refs):
+def stale_norm_kernel(x_ref, gain_ref, bias_ref, all_ref, *out_refs):
+    normed = normalize(x_ref[...], as_row(gain_ref), as_row(bias_ref))
+    all_ref[...] = normed
     rows = out_refs[0].shape[0]
-    gain, bias = as_row(gain_ref), as_row(bias_ref)
     for index, out_ref in enumerate(out_refs):
-        out_ref[...] = normalize(x_ref[index * rows : (index + 1) * rows, :], gain, bias)
-
-
-def query_kernel(x_ref, gain_ref, bias_ref, w_ref, *out_refs):
+        out_ref[...] = normed[index * rows : (index + 1) * rows]
+
+
+def query_kernel(x_ref, gain_ref, bias_ref, w_ref, q_ref, normed_ref):
     normed = normalize(x_ref[...], as_row(gain_ref), as_row(bias_ref))
+    normed_ref[...] = normed
     projected = jnp.dot(normed, w_ref[...], preferred_element_type=F32).astype(BF16)
-    scaled = (projected.astype(F32) * HEAD_DIM ** (-0.5)).astype(BF16)
-    rows = out_refs[0].shape[0]
-    half = len(out_refs) // 2
-    for index in range(half):
-        part = slice(index * rows, (index + 1) * rows)
-        out_refs[index][...] = scaled[part]
-        out_refs[half + index][...] = normed[part]
+    q_ref[...] = (projected.astype(F32) * HEAD_DIM ** (-0.5)).astype(BF16)
 
 
 def scores_of(queries, keys):
@@ -69,16 +65,18 @@
     wk0_ref, wv0_ref, wk_ref, wv_ref,
     o0_ref, o1_ref, o2_ref, o3_ref,
     x_scr, kv_scr, tile_scr,
+    *, sample,
 ):
     pair = pl.program_id(0)
-    rows = fresh_ref.shape[0]
+    rows = z2_ref.shape[0]
     channels = fresh_ref.shape[1]
+    part = slice(sample * rows, (sample + 1) * rows)
     out_refs = (o0_ref, o1_ref, o2_ref, o3_ref)
 
     @pl.when(pair == 0)
     def _():
         for index, ref in enumerate((z1_ref, z2_ref, z3_ref, fresh_ref, own_ref)):
-            x_scr[index * rows : (index + 1) * rows, :] = ref[...]
+            x_scr[index * rows : (index + 1) * rows, :] = ref[...] if index == 1 else ref[part, :]
         tile_scr[...] = jnp.zeros_like(tile_scr)
         project(x_scr[...], wk0_ref, wv0_ref, kv_scr, 0)
 
@@ -95,8 +93,8 @@
     )
     common, fresh, own = slice(0, 3 * rows), slice(3 * rows, 4 * rows), slice(4 * rows, 5 * rows)
     lanes = pl.ds(pl.multiple_of(pair * LANES, LANES), LANES)
-    mine = q0_ref[:, lanes]
-    others = jnp.concatenate([q1_ref[:, lanes], q2_ref[:, lanes], q3_ref[:, lanes]], 0)
+    mine = q0_ref[part, lanes]
+    others = jnp.concatenate([ref[part, lanes] for ref in (q1_ref, q2_ref, q3_ref)], 0)
 
     def halves(x):
         low_part = lax.broadcasted_iota(jnp.int32, x.shape, 1) < HEAD_DIM
@@ -264,12 +262,12 @@
     return [(i, (i + by) % count) for i in range(count)]
 
 
-def on_chip(x):
-    return pltpu.with_memory_space_constraint(x, pltpu.VMEM)
-
-
-def call(kernel, out_shape, *args, flops=1000000, chip=(), **kwargs):
-    args = [on_chip(x) if index in chip else x for index, x in enumerate(args)]
+def call(kernel, out_shape, *args, flops=1000000, chip=(), slow=(), **kwargs):
+    spaces = {**dict.fromkeys(chip, pltpu.VMEM), **dict.fromkeys(slow, pltpu.HBM)}
+    args = [
+        pltpu.with_memory_space_constraint(x, spaces[index]) if index in spaces else x
+        for index, x in enumerate(args)
+    ]
     return pl.pallas_call(
         kernel,
         out_shape=out_shape,
@@ -292,26 +290,29 @@
     hid = hidden.reshape(every, channels)
     block = pltpu.VMEM((tokens, channels), BF16)
     full = pl.BlockSpec((every, channels), lambda i: (0, 0))
+    vector = pl.BlockSpec((channels,), lambda i: (0,))
     shifts = (1, 3, 2)
 
-    stale = call(
-        stale_norm_kernel, [block] * samples,
+    both = pltpu.VMEM((every, channels), BF16)
+    stale, *parts = call(
+        stale_norm_kernel, [both] + [block] * samples,
         stale_attn_in.reshape(every, channels), ln_gain, ln_bias,
-        in_specs=[VMEM] * 3, out_specs=[VMEM] * samples,
-    )
-    along = [[lax.ppermute(one, "z", ring(by, z_count)) for by in shifts] for one in stale]
-    outs = call(
-        query_kernel, [block] * (2 * samples), hid, ln_gain, ln_bias, w_qkv,
+        grid=(1,),
+        in_specs=[full, vector, vector],
+        out_specs=[VMEM] * (1 + samples),
+        slow=(0, 1, 2),
+        flops=6 * 10 ** 9,
+    )
+    beside = [lax.ppermute(stale, "z", ring(by, z_count)) for by in (1, 3)]
+    across = [lax.ppermute(one, "z", ring(2, z_count)) for one in parts]
+    queries, fresh = call(
+        query_kernel, [both] * 2, hid, ln_gain, ln_bias, w_qkv,
         grid=(1,),
         in_specs=[VMEM, VMEM, VMEM, pl.BlockSpec((channels, channels), lambda i: (0, 0))],
-        out_specs=[VMEM] * (2 * samples),
-        flops=2 * every * channels * channels,
-    )
-    queries, fresh = outs[:samples], outs[samples:]
-    all_queries = [
-        [one] + [lax.ppermute(one, "y", ring(by, y_count)) for by in shifts]
-        for one in queries
-    ]
+        out_specs=[VMEM] * 2,
+        flops=6 * 10 ** 9,
+    )
+    all_queries = [queries] + [lax.ppermute(queries, "y", ring(by, y_count)) for by in shifts]
     conv_rows = stale_conv_in.reshape(every, channels)
     above = lax.ppermute(conv_rows, ("y", "z"), [(i, i + 1) for i in range(count - 1)])
     below = lax.ppermute(conv_rows, ("y", "z"), [(i + 1, i) for i in range(count - 1)])
@@ -324,8 +325,8 @@
     back = []
     for s in range(samples):
         outs = call(
-            attend_kernel, [ext] * 4,
-            *all_queries[s], along[s][0], along[s][2], along[s][1], fresh[s], stale[s],
+            functools.partial(attend_kernel, sample=s), [ext] * 4,
+            *all_queries, beside[0], across[s], beside[1], fresh, stale,
             w_qkv, w_qkv, w_qkv, w_qkv,
             grid=(pair_count,),
             in_specs=[VMEM] * 9

time: 106 us -> 101 us (0.953)
  local copies, waits for them, and re-layouts: 14.3 us -> 6.24 us
  waiting for transfers between devices: 19.4 us -> 22.4 us
  Pallas kernels: 22 us -> 23.1 us
    unnamed x40 -> x30, local copies, waits for them, and re-layouts: 14.3 us -> 6.24 us
    ppermute x6, starting transfers between devices: 9.9 us -> 14.8 us  [shards(): lax.ppermute(one, 'y', ring(-by, y_count))]
    ppermute x12 -> x7, waiting for transfers between devices: 4.99 us -> 8.95 us  [the longest x2 5.71 us: shards(): beside = [lax.ppermute(stale, 'z', ring(by, z_count)) for by in (1, 3)]]
    ppermute x12 -> x7, starting transfers between devices: 29.3 us -> 25.4 us  [the longest x2 12.5 us: shards(): across = [lax.ppermute(one, 'z', ring(2, z_count)) for one in parts]]
    ppermute x1, starting transfers between devices: 4.84 us -> 1.3 us  [shards(): lax.ppermute(conv_rows, ('y', 'z'), [(i, i + 1) for i in range(count - 1)])]
    all_to_all x1, starting transfers between devices: 4.22 us -> 5.98 us  [shards(): shared = lax.all_to_all(stats[0], ('y', 'z'), 0, 0)]
    pallas_call x8, Pallas kernels: 22 us -> 23.1 us  [call(): pl.pallas_call(kernel, out_shape=out_shape, compiler_params=pltpu.Compile...]
  transfers between devices with their start and end apart: 21 -> 16, of which waited for: 6 -> 7; matrix products, arithmetic and copies ran while one was open for 0% -> 0% of each run, Pallas kernels for 18% -> 19%
where the time goes in v3:
time: 101 us
  starting transfers between devices  48.8 us (48%)
  Pallas kernels  23.1 us (23%)
  waiting for transfers between devices  22.4 us (22%)
  local copies, waits for them, and re-layouts  6.24 us (6%)
    pallas_call x8, Pallas kernels, call(): pl.pallas_call(kernel, out_shape=out_shape, compiler_params=pltpu.Compile...  23.1 us
    ppermute x6, starting transfers between devices, shards(): lax.ppermute(one, 'y', ring(-by, y_count))  14.8 us
    ppermute x2, starting transfers between devices, shards(): across = [lax.ppermute(one, 'z', ring(2, z_count)) for one in parts]  12.5 us
    ppermute x6, waiting for transfers between devices, shards(): lax.ppermute(one, 'y', ring(-by, y_count))  8.23 us
    ppermute x2, starting transfers between devices, shards(): beside = [lax.ppermute(stale, 'z', ring(by, z_count)) for by in (1, 3)]  7.57 us
    unnamed x30, local copies, waits for them, and re-layouts  6.24 us
    all_to_all x1, starting transfers between devices, shards(): shared = lax.all_to_all(stats[0], ('y', 'z'), 0, 0)  5.98 us
    ppermute x2, waiting for transfers between devices, shards(): beside = [lax.ppermute(stale, 'z', ring(by, z_count)) for by in (1, 3)]  5.71 us
  transfers between devices with their start and end apart: 16, of which 7 were waited for; matrix products, arithmetic and copies ran while one was open for 0% of the time, Pallas kernels for 19%

profile of v3, /device:TPU:2, one launch (start us, length us, event | category | flops | bytes accessed | tf_op | source)
XLA Modules:
  0.0 100.8 jit_solution(18228702143118928562)
XLA Ops:
  0.0 0.0 copy-start.11
  0.0 1.4 %shard_map.155 = (bf16[256,640]{1,0:T(8,128)(2,1)S(1)}, bf16[128,640]{1,0:T(8,128)(2,1)S(1)}, bf16[128,640]{1,0:T(8,128)(2,1)S(1)}) custom-call(bf16[256,640]{1,0:T(8,128)(2,1)} %bitcast.9, f32[640]{0:T(1024)} %gain_ref.4, f32[640]{0:T(1024)} %bias_ref.5), custom_call_target="tpu_custom_call" | custom-call | flops 6000000000 | bytes 1000000 | tf_op jit(solution)/shard_map/pallas_call | solution.py:271
  1.5 7.3 %collective-permute-start.4 = (bf16[128,640]{1,0:T(8,128)(2,1)S(1)}, bf16[128,640]{1,0:T(8,128)(2,1)S(1)}, u32[]{:S(2)}, u32[]{:S(2)}) collective-permute-start(bf16[128,640]{1,0:T(8,128)(2,1)S(1)} %get-tuple-element.24), channel_id=1, source_target_pairs={{0,2},{1,3},{2,0},{3,1},{4,6},{5,7},{6,4},{7,5},{8,10},{9,11},{10,... | collective-permute-start | bytes 491528 | tf_op jit(solution)/shard_map/ppermute | solution.py:307
  8.7 0.0 copy-done.7
  8.7 0.0 copy-done.9
  8.7 0.0 copy-done.10
  8.7 0.0 copy-done.11
  8.7 0.0 copy-start.14
  8.8 0.7 shard_map.154
  9.4 1.7 %collective-permute-start = (bf16[256,640]{1,0:T(8,128)(2,1)S(1)}, bf16[256,640]{1,0:T(8,128)(2,1)S(1)}, u32[]{:S(2)}, u32[]{:S(2)}) collective-permute-start(bf16[256,640]{1,0:T(8,128)(2,1)S(1)} %get-tuple-element.22.q0_ref), channel_id=1, source_target_pairs={{0,4},{4,8},{8,12},{12,0},{1,5},{5,9},{9,13},{13,1},{2,6},{6,10},{... | collective-permute-start | bytes 983048 | tf_op jit(solution)/shard_map/ppermute | solution.py:315
  11.1 1.7 %collective-permute-start.1 = (bf16[256,640]{1,0:T(8,128)(2,1)S(1)}, bf16[256,640]{1,0:T(8,128)(2,1)S(1)}, u32[]{:S(2)}, u32[]{:S(2)}) collective-permute-start(bf16[256,640]{1,0:T(8,128)(2,1)S(1)} %get-tuple-element.22.q0_ref), channel_id=1, source_target_pairs={{0,12},{4,0},{8,4},{12,8},{1,13},{5,1},{9,5},{13,9},{2,14},{6,2},{... | collective-permute-start | bytes 983048 | tf_op jit(solution)/shard_map/ppermute | solution.py:315
  12.8 2.0 %collective-permute-start.2 = (bf16[256,640]{1,0:T(8,128)(2,1)S(1)}, bf16[256,640]{1,0:T(8,128)(2,1)S(1)}, u32[]{:S(2)}, u32[]{:S(2)}) collective-permute-start(bf16[256,640]{1,0:T(8,128)(2,1)S(1)} %get-tuple-element.22.q0_ref), channel_id=1, source_target_pairs={{0,8},{4,12},{8,0},{12,4},{1,9},{5,13},{9,1},{13,5},{2,10},{6,14},... | collective-permute-start | bytes 983048 | tf_op jit(solution)/shard_map/ppermute | solution.py:315
  14.7 1.5 %collective-permute-start.3 = (bf16[256,640]{1,0:T(8,128)(2,1)S(1)}, bf16[256,640]{1,0:T(8,128)(2,1)S(1)}, u32[]{:S(2)}, u32[]{:S(2)}) collective-permute-start(bf16[256,640]{1,0:T(8,128)(2,1)S(1)} %get-tuple-element.23.own_ref), channel_id=1, source_target_pairs={{0,1},{1,2},{2,3},{3,0},{4,5},{5,6},{6,7},{7,4},{8,9},{9,10},{10,1... | collective-permute-start | bytes 983048 | tf_op jit(solution)/shard_map/ppermute | solution.py:306
  16.2 0.0 collective-permute-done.4.z2_ref
  16.2 6.1 %collective-permute-start.5 = (bf16[256,640]{1,0:T(8,128)(2,1)S(1)}, bf16[256,640]{1,0:T(8,128)(2,1)S(1)}, u32[]{:S(2)}, u32[]{:S(2)}) collective-permute-start(bf16[256,640]{1,0:T(8,128)(2,1)S(1)} %get-tuple-element.23.own_ref), channel_id=1, source_target_pairs={{0,3},{1,0},{2,1},{3,2},{4,7},{5,4},{6,5},{7,6},{8,11},{9,8},{10,9... | collective-permute-start | bytes 983048 | tf_op jit(solution)/shard_map/ppermute | solution.py:306
  22.3 0.0 collective-permute-done.q1_ref
  22.3 0.0 copy-done.14
  22.3 1.3 %collective-permute-start.13 = (bf16[256,640]{1,0:T(8,128)(2,1)S(1)}, bf16[256,640]{1,0:T(8,128)(2,1)S(1)}, u32[]{:S(2)}, u32[]{:S(2)}) collective-permute-start(bf16[256,640]{1,0:T(8,128)(2,1)S(1)} %bitcast.10), channel_id=1, source_target_pairs={{0,1},{1,2},{2,3},{3,4},{4,5},{5,6},{6,7},{7,8},{8,9},{9,10},{10,1... | collective-permute-start | bytes 983048 | tf_op jit(solution)/shard_map/ppermute | solution.py:317
  23.6 2.7 %collective-permute-done.1.q2_ref = bf16[256,640]{1,0:T(8,128)(2,1)S(1)} collective-permute-done((bf16[256,640]{1,0:T(8,128)(2,1)S(1)}, bf16[256,640]{1,0:T(8,128)(2,1)S(1)}, u32[]{:S(2)}, u32[]{:S(2)}) %collective-permute-start.1) | collective-permute-done | bytes 327712 | tf_op jit(solution)/shard_map/ppermute | solution.py:315
  26.4 1.3 %collective-permute-start.14 = (bf16[256,640]{1,0:T(8,128)(2,1)S(1)}, bf16[256,640]{1,0:T(8,128)(2,1)S(1)}, u32[]{:S(2)}, u32[]{:S(2)}) collective-permute-start(bf16[256,640]{1,0:T(8,128)(2,1)S(1)} %bitcast.11), channel_id=1, source_target_pairs={{1,0},{2,1},{3,2},{4,3},{5,4},{6,5},{7,6},{8,7},{9,8},{10,9},{11,1... | collective-permute-start | bytes 983048 | tf_op jit(solution)/shard_map/ppermute | solution.py:318
  27.7 0.5 collective-permute-done.2.q3_ref
  28.2 5.3 %collective-permute-start.9 = (bf16[128,640]{1,0:T(8,128)(2,1)S(1)}, bf16[128,640]{1,0:T(8,128)(2,1)S(1)}, u32[]{:S(2)}, u32[]{:S(2)}) collective-permute-start(bf16[128,640]{1,0:T(8,128)(2,1)S(1)} %get-tuple-element.31), channel_id=1, source_target_pairs={{0,2},{1,3},{2,0},{3,1},{4,6},{5,7},{6,4},{7,5},{8,10},{9,11},{10,... | collective-permute-start | bytes 491528 | tf_op jit(solution)/shard_map/ppermute | solution.py:307
  33.4 0.0 collective-permute-done.3.z1_ref
  33.4 5.7 %collective-permute-done.5.z3_ref = bf16[256,640]{1,0:T(8,128)(2,1)S(1)} collective-permute-done((bf16[256,640]{1,0:T(8,128)(2,1)S(1)}, bf16[256,640]{1,0:T(8,128)(2,1)S(1)}, u32[]{:S(2)}, u32[]{:S(2)}) %collective-permute-start.5) | collective-permute-done | bytes 327712 | tf_op jit(solution)/shard_map/ppermute | solution.py:306
  39.1 7.2 %shard_map.156 = (bf16[128,768]{1,0:T(8,128)(2,1)S(1)}, bf16[128,768]{1,0:T(8,128)(2,1)S(1)}, bf16[128,768]{1,0:T(8,128)(2,1)S(1)}, bf16[128,768]{1,0:T(8,128)(2,1)S(1)}) custom-call(bf16[256,640]{1,0:T(8,128)(2,1)S(1)} %get-tuple-element.22.q0_ref, bf16[256,640]{1,0:T(8,128)(2,1)S(1)} %collective-permute-done.q1_ref, ...), custom_call_target="tpu_custom_call" | custom-call | flops 6000000000 | bytes 1000000 | tf_op jit(solution)/shard_map/pallas_call | solution.py:271
  46.4 10.1 %collective-permute-start.6 = (bf16[128,768]{1,0:T(8,128)(2,1)S(1)}, bf16[128,768]{1,0:T(8,128)(2,1)S(1)}, u32[]{:S(2)}, u32[]{:S(2)}) collective-permute-start(bf16[128,768]{1,0:T(8,128)(2,1)S(1)} %get-tuple-element.27), channel_id=1, source_target_pairs={{0,12},{4,0},{8,4},{12,8},{1,13},{5,1},{9,5},{13,9},{2,14},{6,2},{... | collective-permute-start | bytes 589832 | tf_op jit(solution)/shard_map/ppermute | solution.py:350
  56.5 0.0 collective-permute-start.7
  56.5 0.0 collective-permute-done.9.z2_ref
  56.5 0.0 copy-start.12
  56.5 0.0 copy-start.13
  56.5 1.6 %collective-permute-start.8 = (bf16[128,768]{1,0:T(8,128)(2,1)S(1)}, bf16[128,768]{1,0:T(8,128)(2,1)S(1)}, u32[]{:S(2)}, u32[]{:S(2)}) collective-permute-start(bf16[128,768]{1,0:T(8,128)(2,1)S(1)} %get-tuple-element.29), channel_id=1, source_target_pairs={{0,8},{4,12},{8,0},{12,4},{1,9},{5,13},{9,1},{13,5},{2,10},{6,14},... | collective-permute-start | bytes 589832 | tf_op jit(solution)/shard_map/ppermute | solution.py:350
  58.1 7.2 %shard_map.158 = (bf16[128,768]{1,0:T(8,128)(2,1)S(1)}, bf16[128,768]{1,0:T(8,128)(2,1)S(1)}, bf16[128,768]{1,0:T(8,128)(2,1)S(1)}, bf16[128,768]{1,0:T(8,128)(2,1)S(1)}) custom-call(bf16[256,640]{1,0:T(8,128)(2,1)S(1)} %get-tuple-element.22.q0_ref, bf16[256,640]{1,0:T(8,128)(2,1)S(1)} %collective-permute-done.q1_ref, ...), custom_call_target="tpu_custom_call" | custom-call | flops 6000000000 | bytes 1000000 | tf_op jit(solution)/shard_map/pallas_call | solution.py:271
  65.4 0.0 copy-start.3
  65.4 0.0 copy-start.6
  65.4 0.0 collective-permute-done.6.o1_ref
  65.4 1.8 %collective-permute-start.10 = (bf16[128,768]{1,0:T(8,128)(2,1)S(1)}, bf16[128,768]{1,0:T(8,128)(2,1)S(1)}, u32[]{:S(2)}, u32[]{:S(2)}) collective-permute-start(bf16[128,768]{1,0:T(8,128)(2,1)S(1)} %get-tuple-element.33), channel_id=1, source_target_pairs={{0,12},{4,0},{8,4},{12,8},{1,13},{5,1},{9,5},{13,9},{2,14},{6,2},{... | collective-permute-start | bytes 589832 | tf_op jit(solution)/shard_map/ppermute | solution.py:350
  67.2 1.6 %collective-permute-done.7.o2_ref = bf16[128,768]{1,0:T(8,128)(2,1)S(1)} collective-permute-done((bf16[128,768]{1,0:T(8,128)(2,1)S(1)}, bf16[128,768]{1,0:T(8,128)(2,1)S(1)}, u32[]{:S(2)}, u32[]{:S(2)}) %collective-permute-start.7) | collective-permute-done | bytes 196640 | tf_op jit(solution)/shard_map/ppermute | solution.py:350
  68.8 0.0 collective-permute-start.11
  68.8 0.0 collective-permute-done.8.o3_ref
  68.8 1.3 %collective-permute-start.12 = (bf16[128,768]{1,0:T(8,128)(2,1)S(1)}, bf16[128,768]{1,0:T(8,128)(2,1)S(1)}, u32[]{:S(2)}, u32[]{:S(2)}) collective-permute-start(bf16[128,768]{1,0:T(8,128)(2,1)S(1)} %get-tuple-element.35), channel_id=1, source_target_pairs={{0,8},{4,12},{8,0},{12,4},{1,9},{5,13},{9,1},{13,5},{2,10},{6,14},... | collective-permute-start | bytes 589832 | tf_op jit(solution)/shard_map/ppermute | solution.py:350
  70.2 0.0 copy-done.8
  70.2 0.0 copy-done.12
  70.2 0.0 copy-done.13
  70.2 0.0 copy-start.4
  70.2 0.0 copy-start.5
  70.2 1.0 %shard_map.157 = (bf16[128,640]{1,0:T(8,128)(2,1)S(1)}, f32[8,128]{1,0:T(8,128)S(1)}) custom-call(bf16[128,768]{1,0:T(8,128)(2,1)S(1)} %get-tuple-element.26.o0_ref, bf16[128,768]{1,0:T(8,128)(2,1)S(1)} %collective-permute-done.6.o1_ref, bf16[128,768]{1,0:T(8,128)(2,1)S(1)} %collective-permute-done.7.o2_ref, ...), custom_call_target="tpu_custom_call" | custom-call | flops 1000000000 | bytes 1000000 | tf_op jit(solution)/shard_map/pallas_call | solution.py:271
  71.2 0.4 collective-permute-done.10.o1_ref
  71.7 6.2 %collective-permute-done.11.o2_ref = bf16[128,768]{1,0:T(8,128)(2,1)S(1)} collective-permute-done((bf16[128,768]{1,0:T(8,128)(2,1)S(1)}, bf16[128,768]{1,0:T(8,128)(2,1)S(1)}, u32[]{:S(2)}, u32[]{:S(2)}) %collective-permute-start.11) | collective-permute-done | bytes 196640 | tf_op jit(solution)/shard_map/ppermute | solution.py:350
  77.8 0.0 collective-permute-done.12.o3_ref
  77.8 1.7 %shard_map.159 = (bf16[128,640]{1,0:T(8,128)(2,1)S(1)}, f32[16,8,128]{2,1,0:T(8,128)}) custom-call(bf16[128,768]{1,0:T(8,128)(2,1)S(1)} %get-tuple-element.32.o0_ref, bf16[128,768]{1,0:T(8,128)(2,1)S(1)} %collective-permute-done.10.o1_ref, bf16[128,768]{1,0:T(8,128)(2,1)S(1)} %collective-permute-done.11.o2_ref, ...), custom_call_target="tpu_custom_call" | custom-call | flops 1000000000 | bytes 1000000 | tf_op jit(solution)/shard_map/pallas_call | solution.py:271
  79.5 6.0 %all-to-all-start = ((f32[16,8,128]{2,1,0:T(8,128)}), f32[16,8,128]{2,1,0:T(8,128)S(1)}, u32[]{:S(2)}, u32[]{:S(2)}) async-start(f32[16,8,128]{2,1,0:T(8,128)} %get-tuple-element.38), calls=%async_computation | async-start | bytes 131072 | tf_op jit(solution)/shard_map/all_to_all | solution.py:379
  85.5 0.0 collective-permute-done.13.above_ref
  85.5 0.0 collective-permute-done.14.below_ref
  85.5 0.0 copy-done.3
  85.5 0.0 copy-done.6
  85.5 0.0 copy-start
  85.5 3.1 %copy-done = bf16[3,3,640,640]{3,2,1,0:T(8,128)(2,1)S(1)} copy-done((bf16[3,3,640,640]{3,2,1,0:T(8,128)(2,1)S(1)}, bf16[3,3,640,640]{3,2,1,0:T(8,128)(2,1)}, u32[]{:S(2)}) %copy-start) | copy-done | bytes 7372824
  88.6 1.8 %shard_map.160.rim_ref = f32[256,640]{1,0:T(8,128)S(1)} custom-call(bf16[256,640]{1,0:T(8,128)(2,1)S(1)} %collective-permute-done.13.above_ref, bf16[256,640]{1,0:T(8,128)(2,1)S(1)} %collective-permute-done.14.below_ref, bf16[3,3,640,640]{3,2,1,0:T(8,128)(2,1)S(1)} %copy-done, f32[640]{0:T(1024)S(1)} %copy-done.6, f32[2,640]{1,0:T(2,128)S(1)} %copy-done.3), custom_call_target="tpu_custom_call" | custom-call | flops 1258291200 | bytes 1000000 | tf_op jit(solution)/shard_map/pallas_call | solution.py:271
  90.4 5.3 %all-to-all-done.stat_ref = f32[16,8,128]{2,1,0:T(8,128)S(1)} async-done(((f32[16,8,128]{2,1,0:T(8,128)}), f32[16,8,128]{2,1,0:T(8,128)S(1)}, u32[]{:S(2)}, u32[]{:S(2)}) %all-to-all-start) | async-done | bytes 65568 | tf_op jit(solution)/shard_map/all_to_all | solution.py:379
  95.7 0.0 copy-done.2
  95.7 0.0 copy-done.5
  95.7 0.0 copy-start.1
  95.7 3.1 %copy-done.1 = bf16[3,3,640,640]{3,2,1,0:T(8,128)(2,1)S(1)} copy-done((bf16[3,3,640,640]{3,2,1,0:T(8,128)(2,1)S(1)}, bf16[3,3,640,640]{3,2,1,0:T(8,128)(2,1)}, u32[]{:S(2)}) %copy-start.1) | copy-done | bytes 7372824
  98.8 2.0 %shard_map.161 = bf16[256,640]{1,0:T(8,128)(2,1)} custom-call(bf16[128,640]{1,0:T(8,128)(2,1)S(1)} %get-tuple-element.30.res0_ref, bf16[128,640]{1,0:T(8,128)(2,1)S(1)} %get-tuple-element.37.res1_ref, f32[16,8,128]{2,1,0:T(8,128)S(1)} %all-to-all-done.stat_ref, f32[640]{0:T(1024)S(1)} %copy-done.4, f32[640]{0:T(1024)S(1)} %copy-done.5, ...), custom_call_target="tpu_custom_call" | custom-call | flops 629145600 | bytes 1000000 | tf_op jit(solution)/shard_map/pallas_call | solution.py:271
  (6 shorter events, 0.0 us)
Async XLA Ops:
  0.0 8.7 %copy-start.7 = (bf16[640,1920]{1,0:T(8,128)(2,1)S(1)}, bf16[640,1920]{1,0:T(8,128)(2,1)}, u32[]{:S(2)}) copy-start(bf16[640,1920]{1,0:T(8,128)(2,1)} %wv_ref.3) | copy-start | bytes 7372804
  0.0 8.7 %copy-start.9 = (bf16[2,1,128,640]{3,2,1,0:T(8,128)(2,1)S(1)}, bf16[2,1,128,640]{3,2,1,0:T(8,128)(2,1)}, u32[]{:S(2)}) copy-start(bf16[2,1,128,640]{3,2,1,0:T(8,128)(2,1)} %param.16) | copy-start | bytes 983044
  0.0 8.7 %copy-start.10 = (f32[640]{0:T(1024)S(1)}, f32[640]{0:T(1024)}, u32[]{:S(2)}) copy-start(f32[640]{0:T(1024)} %gain_ref.4) | copy-start | bytes 7684
  0.0 8.7 %copy-start.11 = (f32[640]{0:T(1024)S(1)}, f32[640]{0:T(1024)}, u32[]{:S(2)}) copy-start(f32[640]{0:T(1024)} %bias_ref.5) | copy-start | bytes 7684
  1.5 14.8 %collective-permute-start.4 = (bf16[128,640]{1,0:T(8,128)(2,1)S(1)}, bf16[128,640]{1,0:T(8,128)(2,1)S(1)}, u32[]{:S(2)}, u32[]{:S(2)}) collective-permute-start(bf16[128,640]{1,0:T(8,128)(2,1)S(1)} %get-tuple-element.24), channel_id=1, source_target_pairs={{0,2},{1,3},{2,0},{3,1},{4,6},{5,7},{6,4},{7,5},{8,10},{9,11},{10,... | collective-permute-start | bytes 491528 | tf_op jit(solution)/shard_map/ppermute | solution.py:307
  8.7 13.6 %copy-start.14 = (bf16[2,1,128,640]{3,2,1,0:T(8,128)(2,1)S(1)}, bf16[2,1,128,640]{3,2,1,0:T(8,128)(2,1)}, u32[]{:S(2)}) copy-start(bf16[2,1,128,640]{3,2,1,0:T(8,128)(2,1)} %param.18) | copy-start | bytes 983044
  9.4 12.9 %collective-permute-start = (bf16[256,640]{1,0:T(8,128)(2,1)S(1)}, bf16[256,640]{1,0:T(8,128)(2,1)S(1)}, u32[]{:S(2)}, u32[]{:S(2)}) collective-permute-start(bf16[256,640]{1,0:T(8,128)(2,1)S(1)} %get-tuple-element.22.q0_ref), channel_id=1, source_target_pairs={{0,4},{4,8},{8,12},{12,0},{1,5},{5,9},{9,13},{13,1},{2,6},{6,10},{... | collective-permute-start | bytes 983048 | tf_op jit(solution)/shard_map/ppermute | solution.py:315
  11.1 15.3 %collective-permute-start.1 = (bf16[256,640]{1,0:T(8,128)(2,1)S(1)}, bf16[256,640]{1,0:T(8,128)(2,1)S(1)}, u32[]{:S(2)}, u32[]{:S(2)}) collective-permute-start(bf16[256,640]{1,0:T(8,128)(2,1)S(1)} %get-tuple-element.22.q0_ref), channel_id=1, source_target_pairs={{0,12},{4,0},{8,4},{12,8},{1,13},{5,1},{9,5},{13,9},{2,14},{6,2},{... | collective-permute-start | bytes 983048 | tf_op jit(solution)/shard_map/ppermute | solution.py:315
  12.8 15.4 %collective-permute-start.2 = (bf16[256,640]{1,0:T(8,128)(2,1)S(1)}, bf16[256,640]{1,0:T(8,128)(2,1)S(1)}, u32[]{:S(2)}, u32[]{:S(2)}) collective-permute-start(bf16[256,640]{1,0:T(8,128)(2,1)S(1)} %get-tuple-element.22.q0_ref), channel_id=1, source_target_pairs={{0,8},{4,12},{8,0},{12,4},{1,9},{5,13},{9,1},{13,5},{2,10},{6,14},... | collective-permute-start | bytes 983048 | tf_op jit(solution)/shard_map/ppermute | solution.py:315
  14.7 18.7 %collective-permute-start.3 = (bf16[256,640]{1,0:T(8,128)(2,1)S(1)}, bf16[256,640]{1,0:T(8,128)(2,1)S(1)}, u32[]{:S(2)}, u32[]{:S(2)}) collective-permute-start(bf16[256,640]{1,0:T(8,128)(2,1)S(1)} %get-tuple-element.23.own_ref), channel_id=1, source_target_pairs={{0,1},{1,2},{2,3},{3,0},{4,5},{5,6},{6,7},{7,4},{8,9},{9,10},{10,1... | collective-permute-start | bytes 983048 | tf_op jit(solution)/shard_map/ppermute | solution.py:306
  16.2 22.9 %collective-permute-start.5 = (bf16[256,640]{1,0:T(8,128)(2,1)S(1)}, bf16[256,640]{1,0:T(8,128)(2,1)S(1)}, u32[]{:S(2)}, u32[]{:S(2)}) collective-permute-start(bf16[256,640]{1,0:T(8,128)(2,1)S(1)} %get-tuple-element.23.own_ref), channel_id=1, source_target_pairs={{0,3},{1,0},{2,1},{3,2},{4,7},{5,4},{6,5},{7,6},{8,11},{9,8},{10,9... | collective-permute-start | bytes 983048 | tf_op jit(solution)/shard_map/ppermute | solution.py:306
  22.3 63.2 %collective-permute-start.13 = (bf16[256,640]{1,0:T(8,128)(2,1)S(1)}, bf16[256,640]{1,0:T(8,128)(2,1)S(1)}, u32[]{:S(2)}, u32[]{:S(2)}) collective-permute-start(bf16[256,640]{1,0:T(8,128)(2,1)S(1)} %bitcast.10), channel_id=1, source_target_pairs={{0,1},{1,2},{2,3},{3,4},{4,5},{5,6},{6,7},{7,8},{8,9},{9,10},{10,1... | collective-permute-start | bytes 983048 | tf_op jit(solution)/shard_map/ppermute | solution.py:317
  26.4 59.1 %collective-permute-start.14 = (bf16[256,640]{1,0:T(8,128)(2,1)S(1)}, bf16[256,640]{1,0:T(8,128)(2,1)S(1)}, u32[]{:S(2)}, u32[]{:S(2)}) collective-permute-start(bf16[256,640]{1,0:T(8,128)(2,1)S(1)} %bitcast.11), channel_id=1, source_target_pairs={{1,0},{2,1},{3,2},{4,3},{5,4},{6,5},{7,6},{8,7},{9,8},{10,9},{11,1... | collective-permute-start | bytes 983048 | tf_op jit(solution)/shard_map/ppermute | solution.py:318
  28.2 28.3 %collective-permute-start.9 = (bf16[128,640]{1,0:T(8,128)(2,1)S(1)}, bf16[128,640]{1,0:T(8,128)(2,1)S(1)}, u32[]{:S(2)}, u32[]{:S(2)}) collective-permute-start(bf16[128,640]{1,0:T(8,128)(2,1)S(1)} %get-tuple-element.31), channel_id=1, source_target_pairs={{0,2},{1,3},{2,0},{3,1},{4,6},{5,7},{6,4},{7,5},{8,10},{9,11},{10,... | collective-permute-start | bytes 491528 | tf_op jit(solution)/shard_map/ppermute | solution.py:307
  46.4 19.0 %collective-permute-start.6 = (bf16[128,768]{1,0:T(8,128)(2,1)S(1)}, bf16[128,768]{1,0:T(8,128)(2,1)S(1)}, u32[]{:S(2)}, u32[]{:S(2)}) collective-permute-start(bf16[128,768]{1,0:T(8,128)(2,1)S(1)} %get-tuple-element.27), channel_id=1, source_target_pairs={{0,12},{4,0},{8,4},{12,8},{1,13},{5,1},{9,5},{13,9},{2,14},{6,2},{... | collective-permute-start | bytes 589832 | tf_op jit(solution)/shard_map/ppermute | solution.py:350
  56.5 12.4 %collective-permute-start.7 = (bf16[128,768]{1,0:T(8,128)(2,1)S(1)}, bf16[128,768]{1,0:T(8,128)(2,1)S(1)}, u32[]{:S(2)}, u32[]{:S(2)}) collective-permute-start(bf16[128,768]{1,0:T(8,128)(2,1)S(1)} %get-tuple-element.28), channel_id=1, source_target_pairs={{0,4},{4,8},{8,12},{12,0},{1,5},{5,9},{9,13},{13,1},{2,6},{6,10},{... | collective-permute-start | bytes 589832 | tf_op jit(solution)/shard_map/ppermute | solution.py:350
  56.5 13.7 %copy-start.8 = (bf16[640,640]{1,0:T(8,128)(2,1)S(1)}, bf16[640,640]{1,0:T(8,128)(2,1)}, u32[]{:S(2)}) copy-start(bf16[640,640]{1,0:T(8,128)(2,1)} %w_ref.7) | copy-start | bytes 2457604
  56.5 13.7 %copy-start.12 = (bf16[128,640]{1,0:T(8,128)(2,1)S(1)}, bf16[128,640]{1,0:T(8,128)(2,1)}, u32[]{:S(2)}) copy-start(bf16[128,640]{1,0:T(8,128)(2,1)} %constant.6.clone.spread_ref) | copy-start | bytes 491524
  56.5 13.7 %copy-start.13 = (bf16[640,128]{1,0:T(8,128)(2,1)S(1)}, bf16[640,128]{1,0:T(8,128)(2,1)}, u32[]{:S(2)}) copy-start(bf16[640,128]{1,0:T(8,128)(2,1)} %constant.7.clone.gather_ref) | copy-start | bytes 491524
  56.5 12.3 %collective-permute-start.8 = (bf16[128,768]{1,0:T(8,128)(2,1)S(1)}, bf16[128,768]{1,0:T(8,128)(2,1)S(1)}, u32[]{:S(2)}, u32[]{:S(2)}) collective-permute-start(bf16[128,768]{1,0:T(8,128)(2,1)S(1)} %get-tuple-element.29), channel_id=1, source_target_pairs={{0,8},{4,12},{8,0},{12,4},{1,9},{5,13},{9,1},{13,5},{2,10},{6,14},... | collective-permute-start | bytes 589832 | tf_op jit(solution)/shard_map/ppermute | solution.py:350
  65.4 20.1 %copy-start.3 = (f32[2,640]{1,0:T(2,128)S(1)}, f32[2,640]{1,0:T(2,128)}, u32[]{:S(2)}) copy-start(f32[2,640]{1,0:T(2,128)} %shift_ref.1) | copy-start | bytes 15364
  65.4 20.1 %copy-start.6 = (f32[640]{0:T(1024)S(1)}, f32[640]{0:T(1024)}, u32[]{:S(2)}) copy-start(f32[640]{0:T(1024)} %bias_ref.6) | copy-start | bytes 7684
  65.4 6.3 %collective-permute-start.10 = (bf16[128,768]{1,0:T(8,128)(2,1)S(1)}, bf16[128,768]{1,0:T(8,128)(2,1)S(1)}, u32[]{:S(2)}, u32[]{:S(2)}) collective-permute-start(bf16[128,768]{1,0:T(8,128)(2,1)S(1)} %get-tuple-element.33), channel_id=1, source_target_pairs={{0,12},{4,0},{8,4},{12,8},{1,13},{5,1},{9,5},{13,9},{2,14},{6,2},{... | collective-permute-start | bytes 589832 | tf_op jit(solution)/shard_map/ppermute | solution.py:350
  68.8 9.0 %collective-permute-start.11 = (bf16[128,768]{1,0:T(8,128)(2,1)S(1)}, bf16[128,768]{1,0:T(8,128)(2,1)S(1)}, u32[]{:S(2)}, u32[]{:S(2)}) collective-permute-start(bf16[128,768]{1,0:T(8,128)(2,1)S(1)} %get-tuple-element.34), channel_id=1, source_target_pairs={{0,4},{4,8},{8,12},{12,0},{1,5},{5,9},{9,13},{13,1},{2,6},{6,10},{... | collective-permute-start | bytes 589832 | tf_op jit(solution)/shard_map/ppermute | solution.py:350
  68.8 9.0 %collective-permute-start.12 = (bf16[128,768]{1,0:T(8,128)(2,1)S(1)}, bf16[128,768]{1,0:T(8,128)(2,1)S(1)}, u32[]{:S(2)}, u32[]{:S(2)}) collective-permute-start(bf16[128,768]{1,0:T(8,128)(2,1)S(1)} %get-tuple-element.35), channel_id=1, source_target_pairs={{0,8},{4,12},{8,0},{12,4},{1,9},{5,13},{9,1},{13,5},{2,10},{6,14},... | collective-permute-start | bytes 589832 | tf_op jit(solution)/shard_map/ppermute | solution.py:350
  70.2 25.5 %copy-start.2 = (bf16[128,640]{1,0:T(8,128)(2,1)S(1)}, bf16[128,640]{1,0:T(8,128)(2,1)}, u32[]{:S(2)}) copy-start(bf16[128,640]{1,0:T(8,128)(2,1)} %constant.8.clone.scatter_ref) | copy-start | bytes 491524
  70.2 25.5 %copy-start.4 = (f32[640]{0:T(1024)S(1)}, f32[640]{0:T(1024)}, u32[]{:S(2)}) copy-start(f32[640]{0:T(1024)} %gain_ref.5) | copy-start | bytes 7684
  70.2 25.5 %copy-start.5 = (f32[640]{0:T(1024)S(1)}, f32[640]{0:T(1024)}, u32[]{:S(2)}) copy-start(f32[640]{0:T(1024)} %bias_ref.7) | copy-start | bytes 7684
  79.5 16.2 %all-to-all-start = ((f32[16,8,128]{2,1,0:T(8,128)}), f32[16,8,128]{2,1,0:T(8,128)S(1)}, u32[]{:S(2)}, u32[]{:S(2)}) async-start(f32[16,8,128]{2,1,0:T(8,128)} %get-tuple-element.38), calls=%async_computation | async-start | bytes 131072 | tf_op jit(solution)/shard_map/all_to_all | solution.py:379
  85.5 3.1 %copy-start = (bf16[3,3,640,640]{3,2,1,0:T(8,128)(2,1)S(1)}, bf16[3,3,640,640]{3,2,1,0:T(8,128)(2,1)}, u32[]{:S(2)}) copy-start(bf16[3,3,640,640]{3,2,1,0:T(8,128)(2,1)} %w_ref.9) | copy-start | bytes 22118404
  95.7 3.1 %copy-start.1 = (bf16[3,3,640,640]{3,2,1,0:T(8,128)(2,1)S(1)}, bf16[3,3,640,640]{3,2,1,0:T(8,128)(2,1)}, u32[]{:S(2)}) copy-start(bf16[3,3,640,640]{3,2,1,0:T(8,128)(2,1)} %w_ref.9) | copy-start | bytes 22118404

commit v4 on v3

--- a/solution.py
+++ b/solution.py
@@ -33,9 +33,8 @@
     return ref[...].reshape(1, -1)
 
 
-def stale_norm_kernel(x_ref, gain_ref, bias_ref, all_ref, *out_refs):
+def stale_norm_kernel(x_ref, gain_ref, bias_ref, *out_refs):
     normed = normalize(x_ref[...], as_row(gain_ref), as_row(bias_ref))
-    all_ref[...] = normed
     rows = out_refs[0].shape[0]
     for index, out_ref in enumerate(out_refs):
         out_ref[...] = normed[index * rows : (index + 1) * rows]
@@ -62,12 +61,13 @@
 def attend_kernel(
     q0_ref, q1_ref, q2_ref, q3_ref,
     z1_ref, z2_ref, z3_ref, fresh_ref, own_ref,
-    wk0_ref, wv0_ref, wk_ref, wv_ref,
+    wk0_ref, wv0_ref, wk_ref, wv_ref, conv_ref,
     o0_ref, o1_ref, o2_ref, o3_ref,
-    x_scr, kv_scr, tile_scr,
-    *, sample,
+    *refs, sample,
 ):
+    x_scr, kv_scr, tile_scr = refs[-4:-1]
     pair = pl.program_id(0)
+    fetch = pltpu.make_async_copy(conv_ref, refs[0], refs[-1]) if len(refs) > 4 else None
     rows = z2_ref.shape[0]
     channels = fresh_ref.shape[1]
     part = slice(sample * rows, (sample + 1) * rows)
@@ -75,8 +75,10 @@
 
     @pl.when(pair == 0)
     def _():
+        if fetch:
+            fetch.start()
         for index, ref in enumerate((z1_ref, z2_ref, z3_ref, fresh_ref, own_ref)):
-            x_scr[index * rows : (index + 1) * rows, :] = ref[...] if index == 1 else ref[part, :]
+            x_scr[index * rows : (index + 1) * rows, :] = ref[part, :] if index == 3 else ref[...]
         tile_scr[...] = jnp.zeros_like(tile_scr)
         project(x_scr[...], wk0_ref, wv0_ref, kv_scr, 0)
 
@@ -155,6 +157,8 @@
 
     @pl.when(pair == pl.num_programs(0) - 1)
     def _():
+        if fetch:
+            fetch.wait()
         for index, o_ref in enumerate(out_refs):
             o_ref[:, channels:] = tile_scr[index * rows : (index + 1) * rows, :].astype(BF16)
 
@@ -209,9 +213,7 @@
     sums = exact_dot(sums, gather_ref[...])
     if sample:
         sums = pltpu.roll(sums, 2 * sample, 0) + rest_refs[0][...]
-        stat_ref[...] = jnp.broadcast_to(sums[None], stat_ref.shape)
-    else:
-        stat_ref[...] = sums
+    stat_ref[...] = sums
 
 
 def shifted(x, by, cols):
@@ -236,13 +238,18 @@
         out_ref[part, :] = total[part] + shift_ref[sample : sample + 1, :]
 
 
+def add_kernel(*refs):
+    refs[-1][...] = (refs[0][...] + refs[1][...]) + (refs[2][...] + refs[3][...])
+
+
 def final_kernel(
-    res0_ref, res1_ref, stat_ref, gain_ref, bias_ref, scatter_ref, w_ref, rim_ref, out_ref,
+    res0_ref, res1_ref, s0_ref, s1_ref, s2_ref, s3_ref, gain_ref, bias_ref, scatter_ref, w_ref, rim_ref, out_ref,
     *, cols, cells
 ):
     activated = []
     wide = []
-    sums = exact_dot(jnp.sum(stat_ref[...], 0), scatter_ref[...])
+    sums = (s0_ref[...] + s1_ref[...]) + (s2_ref[...] + s3_ref[...])
+    sums = exact_dot(sums, scatter_ref[...])
     gain, bias = as_row(gain_ref), as_row(bias_ref)
     for sample, res_ref in enumerate((res0_ref, res1_ref)):
         mean = sums[2 * sample : 2 * sample + 1] / cells
@@ -294,17 +301,16 @@
     shifts = (1, 3, 2)
 
     both = pltpu.VMEM((every, channels), BF16)
-    stale, *parts = call(
-        stale_norm_kernel, [both] + [block] * samples,
+    stale = call(
+        stale_norm_kernel, [block] * samples,
         stale_attn_in.reshape(every, channels), ln_gain, ln_bias,
         grid=(1,),
         in_specs=[full, vector, vector],
-        out_specs=[VMEM] * (1 + samples),
+        out_specs=[VMEM] * samples,
         slow=(0, 1, 2),
         flops=6 * 10 ** 9,
     )
-    beside = [lax.ppermute(stale, "z", ring(by, z_count)) for by in (1, 3)]
-    across = [lax.ppermute(one, "z", ring(2, z_count)) for one in parts]
+    along = [[lax.ppermute(one, "z", ring(by, z_count)) for by in (1, 2, 3)] for one in stale]
     queries, fresh = call(
         query_kernel, [both] * 2, hid, ln_gain, ln_bias, w_qkv,
         grid=(1,),
@@ -324,10 +330,11 @@
     ext = pltpu.VMEM((tokens, wide), BF16)
     back = []
     for s in range(samples):
+        extra = [pltpu.VMEM(conv_weight.shape, BF16)] * (s == samples - 1)
         outs = call(
-            functools.partial(attend_kernel, sample=s), [ext] * 4,
-            *all_queries, beside[0], across[s], beside[1], fresh, stale,
-            w_qkv, w_qkv, w_qkv, w_qkv,
+            functools.partial(attend_kernel, sample=s), [ext] * 4 + extra,
+            *all_queries, *along[s], fresh, stale[s],
+            w_qkv, w_qkv, w_qkv, w_qkv, conv_weight,
             grid=(pair_count,),
             in_specs=[VMEM] * 9
             + [
@@ -335,24 +342,28 @@
                 pl.BlockSpec((channels, LANES), lambda p: (0, 2 * pair_count)),
                 pl.BlockSpec((channels, LANES), lambda p: (0, jnp.minimum(pair_count + p + 1, 2 * pair_count - 1))),
                 pl.BlockSpec((channels, LANES), lambda p: (0, jnp.minimum(2 * pair_count + p + 1, 3 * pair_count - 1))),
+                pl.BlockSpec(memory_space=pl.ANY),
             ],
-            out_specs=[VMEM] * 4,
+            out_specs=[VMEM] * (4 + len(extra)),
             scratch_shapes=[
                 pltpu.VMEM((5 * tokens, channels), BF16),
                 pltpu.VMEM((2, 5 * tokens, 2 * LANES), BF16),
                 pltpu.VMEM((4 * tokens, LANES), F32),
+                pltpu.SemaphoreType.DMA,
             ],
             flops=6 * 10 ** 9,
             chip=range(9),
+            slow=(13,),
         )
         back.append(
             [outs[0]]
-            + [lax.ppermute(one, "y", ring(-by, y_count)) for one, by in zip(outs[1:], shifts)]
+            + [lax.ppermute(one, "y", ring(-by, y_count)) for one, by in zip(outs[1:4], shifts)]
         )
+    conv_on_chip = outs[4]
     rim = call(
         functools.partial(rim_kernel, cols=cols),
         pltpu.VMEM((every, channels), F32),
-        above, below, conv_weight, conv_bias, time_shift,
+        above, below, conv_on_chip, conv_bias, time_shift,
         in_specs=[VMEM] * 5,
         out_specs=VMEM,
         flops=12 * every * channels * channels,
@@ -361,8 +372,6 @@
     residuals, stats = [], []
     for s in range(samples):
         small = pltpu.VMEM((8, LANES), F32)
-        if s:
-            small = pltpu.VMEM((count, 8, LANES), F32)
         res, stat = call(
             functools.partial(merge_kernel, sample=s), [block, small],
             *back[s], hid, w_out, spread, jnp.asarray(gather, BF16), *stats,
@@ -371,21 +380,24 @@
             + [pl.BlockSpec((tokens, channels), lambda i, s=s: (s, 0))]
             + [VMEM] * (3 + len(stats)),
             out_specs=[VMEM, VMEM],
-            flops=10 ** 9,
+            flops=6 * 10 ** 9,
             chip=(0, 1, 2, 3, 5) + (8,) * s,
         )
         residuals.append(res)
         stats = [stat]
-    shared = lax.all_to_all(stats[0], ("y", "z"), 0, 0)
+    stat = stats[0]
+    along_y = [stat] + [lax.ppermute(stat, "y", ring(by, y_count)) for by in shifts]
+    stat = call(add_kernel, small, *along_y, in_specs=[VMEM] * 4, out_specs=VMEM, chip=range(4))
+    along_z = [stat] + [lax.ppermute(stat, "z", ring(by, z_count)) for by in shifts]
     out = call(
         functools.partial(
             final_kernel, cols=cols, cells=float(count * tokens * (channels // GROUPS))
         ),
         jax.ShapeDtypeStruct((every, channels), BF16),
-        *residuals, shared, gn_gain, gn_bias, jnp.asarray(gather.T, BF16), conv_weight, rim,
-        in_specs=[VMEM] * 8,
+        *residuals, *along_z, gn_gain, gn_bias, jnp.asarray(gather.T, BF16), conv_on_chip, rim,
+        in_specs=[VMEM] * 11,
         out_specs=VMEM,
-        chip=(0, 1, 2, 6, 7),
+        chip=(0, 1, 2, 3, 4, 5, 9, 10),
         flops=6 * every * channels * channels,
     )
     return out.reshape(hidden.shape)

time: 101 us -> 113 us (1.12)
  waiting for transfers between devices: 22.4 us -> 35.9 us
  local copies, waits for them, and re-layouts: 6.24 us -> 0.05 us
  starting transfers between devices: 48.8 us -> 54.2 us
    ppermute x4 -> x12, waiting for transfers between devices: 5.71 us -> 29.5 us  [the longest x6 21.9 us: shards(): lax.ppermute(one, 'z', ring(by, z_count))]
    ppermute x4 -> x12, starting transfers between devices: 20.1 us -> 29.2 us  [the longest x6 18.6 us: shards(): lax.ppermute(one, 'z', ring(by, z_count))]
    unnamed x30 -> x26, local copies, waits for them, and re-layouts: 6.24 us -> 0.05 us
    all_to_all x1 -> x0, starting transfers between devices: 5.98 us -> none  [shards(): shared = lax.all_to_all(stats[0], ('y', 'z'), 0, 0)]
    all_to_all x1 -> x0, waiting for transfers between devices: 5.25 us -> none  [shards(): shared = lax.all_to_all(stats[0], ('y', 'z'), 0, 0)]
    ppermute x3, waiting for transfers between devices: 3.24 us -> 0.01 us  [shards(): lax.ppermute(queries, 'y', ring(by, y_count))]
    ppermute x1, starting transfers between devices: 1.3 us -> 4.31 us  [shards(): lax.ppermute(conv_rows, ('y', 'z'), [(i, i + 1) for i in range(count - 1)])]
    ppermute x6, waiting for transfers between devices: 8.23 us -> 6.48 us  [shards(): lax.ppermute(one, 'y', ring(-by, y_count))]
  transfers between devices with their start and end apart: 16 -> 23, of which waited for: 7 -> 7; matrix products, arithmetic and copies ran while one was open for 0% -> 0% of each run, Pallas kernels for 19% -> 17%
where the time goes in v4:
time: 113 us
  starting transfers between devices  54.2 us (48%)
  waiting for transfers between devices  35.9 us (32%)
  Pallas kernels  22.6 us (20%)
    pallas_call x9, Pallas kernels, call(): pl.pallas_call(kernel, out_shape=out_shape, compiler_params=pltpu.Compile...  22.6 us
    ppermute x6, waiting for transfers between devices, shards(): lax.ppermute(one, 'z', ring(by, z_count))  21.9 us
    ppermute x6, starting transfers between devices, shards(): lax.ppermute(one, 'z', ring(by, z_count))  18.6 us
    ppermute x6, starting transfers between devices, shards(): lax.ppermute(one, 'y', ring(-by, y_count))  14.1 us
    ppermute x3, starting transfers between devices, shards(): lax.ppermute(stat, 'z', ring(by, z_count))  7.33 us
    ppermute x6, waiting for transfers between devices, shards(): lax.ppermute(one, 'y', ring(-by, y_count))  6.48 us
    ppermute x3, starting transfers between devices, shards(): lax.ppermute(queries, 'y', ring(by, y_count))  5.31 us
    ppermute x3, waiting for transfers between devices, shards(): lax.ppermute(stat, 'y', ring(by, y_count))  5.11 us
  transfers between devices with their start and end apart: 23, of which 7 were waited for; matrix products, arithmetic and copies ran while one was open for 0% of the time, Pallas kernels for 17%

profile of v4, /device:TPU:2, one launch (start us, length us, event | category | flops | bytes accessed | tf_op | source)
XLA Modules:
  0.0 113.0 jit_solution(15929357524170128090)
XLA Ops:
  0.0 0.0 copy-start.9
  0.0 1.4 %shard_map.155 = (bf16[128,640]{1,0:T(8,128)(2,1)S(1)}, bf16[128,640]{1,0:T(8,128)(2,1)S(1)}) custom-call(bf16[256,640]{1,0:T(8,128)(2,1)} %bitcast.9, f32[640]{0:T(1024)} %gain_ref.4, f32[640]{0:T(1024)} %bias_ref.5), custom_call_target="tpu_custom_call" | custom-call | flops 6000000000 | bytes 1000000 | tf_op jit(solution)/shard_map/pallas_call | solution.py:278
  1.4 3.3 %collective-permute-start.3 = (bf16[128,640]{1,0:T(8,128)(2,1)S(1)}, bf16[128,640]{1,0:T(8,128)(2,1)S(1)}, u32[]{:S(2)}, u32[]{:S(2)}) collective-permute-start(bf16[128,640]{1,0:T(8,128)(2,1)S(1)} %get-tuple-element.23.own_ref), channel_id=1, source_target_pairs={{0,1},{1,2},{2,3},{3,0},{4,5},{5,6},{6,7},{7,4},{8,9},{9,10},{10,1... | collective-permute-start | bytes 491528 | tf_op jit(solution)/shard_map/ppermute | solution.py:313
  4.8 0.0 copy-done.5
  4.8 0.0 copy-done.7
  4.8 0.0 copy-done.8
  4.8 0.0 copy-done.9
  4.8 0.0 copy-start.12
  4.8 0.7 shard_map.154
  5.5 1.7 %collective-permute-start = (bf16[256,640]{1,0:T(8,128)(2,1)S(1)}, bf16[256,640]{1,0:T(8,128)(2,1)S(1)}, u32[]{:S(2)}, u32[]{:S(2)}) collective-permute-start(bf16[256,640]{1,0:T(8,128)(2,1)S(1)} %get-tuple-element.22.q0_ref), channel_id=1, source_target_pairs={{0,4},{4,8},{8,12},{12,0},{1,5},{5,9},{9,13},{13,1},{2,6},{6,10},{... | collective-permute-start | bytes 983048 | tf_op jit(solution)/shard_map/ppermute | solution.py:321
  7.2 1.7 %collective-permute-start.1 = (bf16[256,640]{1,0:T(8,128)(2,1)S(1)}, bf16[256,640]{1,0:T(8,128)(2,1)S(1)}, u32[]{:S(2)}, u32[]{:S(2)}) collective-permute-start(bf16[256,640]{1,0:T(8,128)(2,1)S(1)} %get-tuple-element.22.q0_ref), channel_id=1, source_target_pairs={{0,12},{4,0},{8,4},{12,8},{1,13},{5,1},{9,5},{13,9},{2,14},{6,2},{... | collective-permute-start | bytes 983048 | tf_op jit(solution)/shard_map/ppermute | solution.py:321
  8.8 2.0 %collective-permute-start.2 = (bf16[256,640]{1,0:T(8,128)(2,1)S(1)}, bf16[256,640]{1,0:T(8,128)(2,1)S(1)}, u32[]{:S(2)}, u32[]{:S(2)}) collective-permute-start(bf16[256,640]{1,0:T(8,128)(2,1)S(1)} %get-tuple-element.22.q0_ref), channel_id=1, source_target_pairs={{0,8},{4,12},{8,0},{12,4},{1,9},{5,13},{9,1},{13,5},{2,10},{6,14},... | collective-permute-start | bytes 983048 | tf_op jit(solution)/shard_map/ppermute | solution.py:321
  10.8 5.4 %collective-permute-start.4 = (bf16[128,640]{1,0:T(8,128)(2,1)S(1)}, bf16[128,640]{1,0:T(8,128)(2,1)S(1)}, u32[]{:S(2)}, u32[]{:S(2)}) collective-permute-start(bf16[128,640]{1,0:T(8,128)(2,1)S(1)} %get-tuple-element.23.own_ref), channel_id=1, source_target_pairs={{0,2},{1,3},{2,0},{3,1},{4,6},{5,7},{6,4},{7,5},{8,10},{9,11},{10,... | collective-permute-start | bytes 491528 | tf_op jit(solution)/shard_map/ppermute | solution.py:313
  16.2 0.0 collective-permute-done.3.z1_ref
  16.2 2.7 %collective-permute-start.5 = (bf16[128,640]{1,0:T(8,128)(2,1)S(1)}, bf16[128,640]{1,0:T(8,128)(2,1)S(1)}, u32[]{:S(2)}, u32[]{:S(2)}) collective-permute-start(bf16[128,640]{1,0:T(8,128)(2,1)S(1)} %get-tuple-element.23.own_ref), channel_id=1, source_target_pairs={{0,3},{1,0},{2,1},{3,2},{4,7},{5,4},{6,5},{7,6},{8,11},{9,8},{10,9... | collective-permute-start | bytes 491528 | tf_op jit(solution)/shard_map/ppermute | solution.py:313
  18.9 3.7 %collective-permute-done.4.z2_ref = bf16[128,640]{1,0:T(8,128)(2,1)S(1)} collective-permute-done((bf16[128,640]{1,0:T(8,128)(2,1)S(1)}, bf16[128,640]{1,0:T(8,128)(2,1)S(1)}, u32[]{:S(2)}, u32[]{:S(2)}) %collective-permute-start.4) | collective-permute-done | bytes 163872 | tf_op jit(solution)/shard_map/ppermute | solution.py:313
  22.6 4.3 %collective-permute-start.10 = (bf16[128,640]{1,0:T(8,128)(2,1)S(1)}, bf16[128,640]{1,0:T(8,128)(2,1)S(1)}, u32[]{:S(2)}, u32[]{:S(2)}) collective-permute-start(bf16[128,640]{1,0:T(8,128)(2,1)S(1)} %get-tuple-element.30.own_ref), channel_id=1, source_target_pairs={{0,2},{1,3},{2,0},{3,1},{4,6},{5,7},{6,4},{7,5},{8,10},{9,11},{10,... | collective-permute-start | bytes 491528 | tf_op jit(solution)/shard_map/ppermute | solution.py:313
  26.9 18.2 %collective-permute-done.5.z3_ref = bf16[128,640]{1,0:T(8,128)(2,1)S(1)} collective-permute-done((bf16[128,640]{1,0:T(8,128)(2,1)S(1)}, bf16[128,640]{1,0:T(8,128)(2,1)S(1)}, u32[]{:S(2)}, u32[]{:S(2)}) %collective-permute-start.5) | collective-permute-done | bytes 163872 | tf_op jit(solution)/shard_map/ppermute | solution.py:313
  45.0 0.0 collective-permute-start.11
  45.0 0.0 collective-permute-done.q1_ref
  45.0 2.9 %collective-permute-start.9 = (bf16[128,640]{1,0:T(8,128)(2,1)S(1)}, bf16[128,640]{1,0:T(8,128)(2,1)S(1)}, u32[]{:S(2)}, u32[]{:S(2)}) collective-permute-start(bf16[128,640]{1,0:T(8,128)(2,1)S(1)} %get-tuple-element.30.own_ref), channel_id=1, source_target_pairs={{0,1},{1,2},{2,3},{3,0},{4,5},{5,6},{6,7},{7,4},{8,9},{9,10},{10,1... | collective-permute-start | bytes 491528 | tf_op jit(solution)/shard_map/ppermute | solution.py:313
  48.0 0.0 collective-permute-done.1.q2_ref
  48.0 0.0 copy-done.12
  48.0 4.3 %collective-permute-start.21 = (bf16[256,640]{1,0:T(8,128)(2,1)S(1)}, bf16[256,640]{1,0:T(8,128)(2,1)S(1)}, u32[]{:S(2)}, u32[]{:S(2)}) collective-permute-start(bf16[256,640]{1,0:T(8,128)(2,1)S(1)} %bitcast.10), channel_id=1, source_target_pairs={{0,1},{1,2},{2,3},{3,4},{4,5},{5,6},{6,7},{7,8},{8,9},{9,10},{10,1... | collective-permute-start | bytes 983048 | tf_op jit(solution)/shard_map/ppermute | solution.py:323
  52.3 0.0 collective-permute-done.2.q3_ref
  52.3 1.3 %collective-permute-start.22 = (bf16[256,640]{1,0:T(8,128)(2,1)S(1)}, bf16[256,640]{1,0:T(8,128)(2,1)S(1)}, u32[]{:S(2)}, u32[]{:S(2)}) collective-permute-start(bf16[256,640]{1,0:T(8,128)(2,1)S(1)} %bitcast.11), channel_id=1, source_target_pairs={{1,0},{2,1},{3,2},{4,3},{5,4},{6,5},{7,6},{8,7},{9,8},{10,9},{11,1... | collective-permute-start | bytes 983048 | tf_op jit(solution)/shard_map/ppermute | solution.py:324
  53.6 7.3 %shard_map.156 = (bf16[128,768]{1,0:T(8,128)(2,1)S(1)}, bf16[128,768]{1,0:T(8,128)(2,1)S(1)}, bf16[128,768]{1,0:T(8,128)(2,1)S(1)}, bf16[128,768]{1,0:T(8,128)(2,1)S(1)}) custom-call(bf16[256,640]{1,0:T(8,128)(2,1)S(1)} %get-tuple-element.22.q0_ref, bf16[256,640]{1,0:T(8,128)(2,1)S(1)} %collective-permute-done.q1_ref, ...), custom_call_target="tpu_custom_call" | custom-call | flops 6000000000 | bytes 1000000 | tf_op jit(solution)/shard_map/pallas_call | solution.py:278
  60.9 0.0 collective-permute-done.10.z2_ref
  60.9 5.4 %collective-permute-start.6 = (bf16[128,768]{1,0:T(8,128)(2,1)S(1)}, bf16[128,768]{1,0:T(8,128)(2,1)S(1)}, u32[]{:S(2)}, u32[]{:S(2)}) collective-permute-start(bf16[128,768]{1,0:T(8,128)(2,1)S(1)} %get-tuple-element.26), channel_id=1, source_target_pairs={{0,12},{4,0},{8,4},{12,8},{1,13},{5,1},{9,5},{13,9},{2,14},{6,2},{... | collective-permute-start | bytes 589832 | tf_op jit(solution)/shard_map/ppermute | solution.py:360
  66.3 0.0 collective-permute-done.11.z3_ref
  66.3 2.2 %collective-permute-start.7 = (bf16[128,768]{1,0:T(8,128)(2,1)S(1)}, bf16[128,768]{1,0:T(8,128)(2,1)S(1)}, u32[]{:S(2)}, u32[]{:S(2)}) collective-permute-start(bf16[128,768]{1,0:T(8,128)(2,1)S(1)} %get-tuple-element.27), channel_id=1, source_target_pairs={{0,4},{4,8},{8,12},{12,0},{1,5},{5,9},{9,13},{13,1},{2,6},{6,10},{... | collective-permute-start | bytes 589832 | tf_op jit(solution)/shard_map/ppermute | solution.py:360
  68.5 0.0 collective-permute-done.9.z1_ref
  68.5 2.8 %collective-permute-start.8 = (bf16[128,768]{1,0:T(8,128)(2,1)S(1)}, bf16[128,768]{1,0:T(8,128)(2,1)S(1)}, u32[]{:S(2)}, u32[]{:S(2)}) collective-permute-start(bf16[128,768]{1,0:T(8,128)(2,1)S(1)} %get-tuple-element.28), channel_id=1, source_target_pairs={{0,8},{4,12},{8,0},{12,4},{1,9},{5,13},{9,1},{13,5},{2,10},{6,14},... | collective-permute-start | bytes 589832 | tf_op jit(solution)/shard_map/ppermute | solution.py:360
  71.3 7.3 %shard_map.158 = (bf16[128,768]{1,0:T(8,128)(2,1)S(1)}, bf16[128,768]{1,0:T(8,128)(2,1)S(1)}, bf16[128,768]{1,0:T(8,128)(2,1)S(1)}, bf16[128,768]{1,0:T(8,128)(2,1)S(1)}, bf16[3,3,640,640]{3,2,1,0:T(8,128)(2,1)S(1)}) custom-call(bf16[256,640]{1,0:T(8,128)(2,1)S(1)} %get-tuple-element.22.q0_ref, bf16[256,640]{1,0:T(8,128)(2,1)S(1)} %collective-permute-done.q1_ref, ...), custom_call_target="tpu_custom_call" | custom-call | flops 6000000000 | bytes 1000000 | tf_op jit(solution)/shard_map/pallas_call | solution.py:278
  78.6 0.0 collective-permute-done.6.o1_ref
  78.6 2.1 %collective-permute-start.12 = (bf16[128,768]{1,0:T(8,128)(2,1)S(1)}, bf16[128,768]{1,0:T(8,128)(2,1)S(1)}, u32[]{:S(2)}, u32[]{:S(2)}) collective-permute-start(bf16[128,768]{1,0:T(8,128)(2,1)S(1)} %get-tuple-element.32), channel_id=1, source_target_pairs={{0,12},{4,0},{8,4},{12,8},{1,13},{5,1},{9,5},{13,9},{2,14},{6,2},{... | collective-permute-start | bytes 589832 | tf_op jit(solution)/shard_map/ppermute | solution.py:360
  80.7 0.0 collective-permute-done.7.o2_ref
  80.7 0.0 collective-permute-start.13
  80.7 0.0 collective-permute-done.8.o3_ref
  80.7 1.6 %collective-permute-start.14 = (bf16[128,768]{1,0:T(8,128)(2,1)S(1)}, bf16[128,768]{1,0:T(8,128)(2,1)S(1)}, u32[]{:S(2)}, u32[]{:S(2)}) collective-permute-start(bf16[128,768]{1,0:T(8,128)(2,1)S(1)} %get-tuple-element.34), channel_id=1, source_target_pairs={{0,8},{4,12},{8,0},{12,4},{1,9},{5,13},{9,1},{13,5},{2,10},{6,14},... | collective-permute-start | bytes 589832 | tf_op jit(solution)/shard_map/ppermute | solution.py:360
  82.3 0.0 copy-done.6
  82.3 0.0 copy-done.10
  82.3 1.0 shard_map.157
  83.3 1.0 collective-permute-done.12.o1_ref
  84.3 5.5 %collective-permute-done.13.o2_ref = bf16[128,768]{1,0:T(8,128)(2,1)S(1)} collective-permute-done((bf16[128,768]{1,0:T(8,128)(2,1)S(1)}, bf16[128,768]{1,0:T(8,128)(2,1)S(1)}, u32[]{:S(2)}, u32[]{:S(2)}) %collective-permute-start.13) | collective-permute-done | bytes 196640 | tf_op jit(solution)/shard_map/ppermute | solution.py:360
  89.8 0.0 collective-permute-done.14.o3_ref
  89.8 1.0 shard_map.159
  90.8 0.1 collective-permute-start.15
  90.9 3.2 %collective-permute-start.16 = (f32[8,128]{1,0:T(8,128)S(1)}, f32[8,128]{1,0:T(8,128)S(1)}, u32[]{:S(2)}, u32[]{:S(2)}) collective-permute-start(f32[8,128]{1,0:T(8,128)S(1)} %get-tuple-element.37.refs_0_), channel_id=1, source_target_pairs={{0,12},{4,0},{8,4},{12,8},{1,13},{5,1},{9,5},{13,9},{2,14},{6,2},{... | collective-permute-start | bytes 12296 | tf_op jit(solution)/shard_map/ppermute | solution.py:389
  94.2 0.0 collective-permute-start.17
  94.2 1.6 %collective-permute-done.15.refs_1_ = f32[8,128]{1,0:T(8,128)S(1)} collective-permute-done((f32[8,128]{1,0:T(8,128)S(1)}, f32[8,128]{1,0:T(8,128)S(1)}, u32[]{:S(2)}, u32[]{:S(2)}) %collective-permute-start.15) | collective-permute-done | bytes 4128 | tf_op jit(solution)/shard_map/ppermute | solution.py:389
  95.7 0.0 collective-permute-done.16.refs_2_
  95.7 3.5 %collective-permute-done.17.refs_3_ = f32[8,128]{1,0:T(8,128)S(1)} collective-permute-done((f32[8,128]{1,0:T(8,128)S(1)}, f32[8,128]{1,0:T(8,128)S(1)}, u32[]{:S(2)}, u32[]{:S(2)}) %collective-permute-start.17) | collective-permute-done | bytes 4128 | tf_op jit(solution)/shard_map/ppermute | solution.py:389
  99.3 0.0 collective-permute-start.18
  99.3 4.1 %collective-permute-start.19 = (f32[8,128]{1,0:T(8,128)S(1)}, f32[8,128]{1,0:T(8,128)S(1)}, u32[]{:S(2)}, u32[]{:S(2)}) collective-permute-start(f32[8,128]{1,0:T(8,128)S(1)} %shard_map.160.s0_ref), channel_id=1, source_target_pairs={{0,3},{1,0},{2,1},{3,2},{4,7},{5,4},{6,5},{7,6},{8,11},{9,8},{10,9... | collective-permute-start | bytes 12296 | tf_op jit(solution)/shard_map/ppermute | solution.py:391
  103.4 3.2 %collective-permute-start.20 = (f32[8,128]{1,0:T(8,128)S(1)}, f32[8,128]{1,0:T(8,128)S(1)}, u32[]{:S(2)}, u32[]{:S(2)}) collective-permute-start(f32[8,128]{1,0:T(8,128)S(1)} %shard_map.160.s0_ref), channel_id=1, source_target_pairs={{0,2},{1,3},{2,0},{3,1},{4,6},{5,7},{6,4},{7,5},{8,10},{9,11},{10,... | collective-permute-start | bytes 12296 | tf_op jit(solution)/shard_map/ppermute | solution.py:391
  106.6 0.0 collective-permute-done.21.above_ref
  106.6 0.0 collective-permute-done.22.below_ref
  106.6 1.8 %shard_map.161.rim_ref = f32[256,640]{1,0:T(8,128)S(1)} custom-call(bf16[256,640]{1,0:T(8,128)(2,1)S(1)} %collective-permute-done.21.above_ref, bf16[256,640]{1,0:T(8,128)(2,1)S(1)} %collective-permute-done.22.below_ref, bf16[3,3,640,640]{3,2,1,0:T(8,128)(2,1)S(1)} %get-tuple-element.38.w_ref, f32[640]{0:T(1024)S(1)} %copy-done.4, f32[2,640]{1,0:T(2,128)S(1)} %copy-done.1), custom_call_target="tpu_custom_call" | custom-call | flops 1258291200 | bytes 1000000 | tf_op jit(solution)/shard_map/pallas_call | solution.py:278
  108.5 0.0 collective-permute-done.18.s1_ref
  108.5 0.0 collective-permute-done.19.s2_ref
  108.5 2.4 %collective-permute-done.20.s3_ref = f32[8,128]{1,0:T(8,128)S(1)} collective-permute-done((f32[8,128]{1,0:T(8,128)S(1)}, f32[8,128]{1,0:T(8,128)S(1)}, u32[]{:S(2)}, u32[]{:S(2)}) %collective-permute-start.20) | collective-permute-done | bytes 4128 | tf_op jit(solution)/shard_map/ppermute | solution.py:391
  110.9 0.0 copy-done
  110.9 2.1 %shard_map.162 = bf16[256,640]{1,0:T(8,128)(2,1)} custom-call(bf16[128,640]{1,0:T(8,128)(2,1)S(1)} %get-tuple-element.29.res0_ref, bf16[128,640]{1,0:T(8,128)(2,1)S(1)} %get-tuple-element.36.res1_ref, f32[8,128]{1,0:T(8,128)S(1)} %shard_map.160.s0_ref, f32[8,128]{1,0:T(8,128)S(1)} %collective-permute-done.18.s1_ref, ...), custom_call_target="tpu_custom_call" | custom-call | flops 629145600 | bytes 1000000 | tf_op jit(solution)/shard_map/pallas_call | solution.py:278
  (17 shorter events, 0.0 us)
Async XLA Ops:
  0.0 4.8 %copy-start.5 = (bf16[640,1920]{1,0:T(8,128)(2,1)S(1)}, bf16[640,1920]{1,0:T(8,128)(2,1)}, u32[]{:S(2)}) copy-start(bf16[640,1920]{1,0:T(8,128)(2,1)} %wv_ref.3) | copy-start | bytes 7372804
  0.0 4.8 %copy-start.7 = (bf16[2,1,128,640]{3,2,1,0:T(8,128)(2,1)S(1)}, bf16[2,1,128,640]{3,2,1,0:T(8,128)(2,1)}, u32[]{:S(2)}) copy-start(bf16[2,1,128,640]{3,2,1,0:T(8,128)(2,1)} %param.16) | copy-start | bytes 983044
  0.0 4.8 %copy-start.8 = (f32[640]{0:T(1024)S(1)}, f32[640]{0:T(1024)}, u32[]{:S(2)}) copy-start(f32[640]{0:T(1024)} %gain_ref.4) | copy-start | bytes 7684
  0.0 4.8 %copy-start.9 = (f32[640]{0:T(1024)S(1)}, f32[640]{0:T(1024)}, u32[]{:S(2)}) copy-start(f32[640]{0:T(1024)} %bias_ref.5) | copy-start | bytes 7684
  1.4 14.8 %collective-permute-start.3 = (bf16[128,640]{1,0:T(8,128)(2,1)S(1)}, bf16[128,640]{1,0:T(8,128)(2,1)S(1)}, u32[]{:S(2)}, u32[]{:S(2)}) collective-permute-start(bf16[128,640]{1,0:T(8,128)(2,1)S(1)} %get-tuple-element.23.own_ref), channel_id=1, source_target_pairs={{0,1},{1,2},{2,3},{3,0},{4,5},{5,6},{6,7},{7,4},{8,9},{9,10},{10,1... | collective-permute-start | bytes 491528 | tf_op jit(solution)/shard_map/ppermute | solution.py:313
  4.8 43.2 %copy-start.12 = (bf16[2,1,128,640]{3,2,1,0:T(8,128)(2,1)S(1)}, bf16[2,1,128,640]{3,2,1,0:T(8,128)(2,1)}, u32[]{:S(2)}) copy-start(bf16[2,1,128,640]{3,2,1,0:T(8,128)(2,1)} %param.18) | copy-start | bytes 983044
  5.5 39.5 %collective-permute-start = (bf16[256,640]{1,0:T(8,128)(2,1)S(1)}, bf16[256,640]{1,0:T(8,128)(2,1)S(1)}, u32[]{:S(2)}, u32[]{:S(2)}) collective-permute-start(bf16[256,640]{1,0:T(8,128)(2,1)S(1)} %get-tuple-element.22.q0_ref), channel_id=1, source_target_pairs={{0,4},{4,8},{8,12},{12,0},{1,5},{5,9},{9,13},{13,1},{2,6},{6,10},{... | collective-permute-start | bytes 983048 | tf_op jit(solution)/shard_map/ppermute | solution.py:321
  7.2 40.8 %collective-permute-start.1 = (bf16[256,640]{1,0:T(8,128)(2,1)S(1)}, bf16[256,640]{1,0:T(8,128)(2,1)S(1)}, u32[]{:S(2)}, u32[]{:S(2)}) collective-permute-start(bf16[256,640]{1,0:T(8,128)(2,1)S(1)} %get-tuple-element.22.q0_ref), channel_id=1, source_target_pairs={{0,12},{4,0},{8,4},{12,8},{1,13},{5,1},{9,5},{13,9},{2,14},{6,2},{... | collective-permute-start | bytes 983048 | tf_op jit(solution)/shard_map/ppermute | solution.py:321
  8.8 43.5 %collective-permute-start.2 = (bf16[256,640]{1,0:T(8,128)(2,1)S(1)}, bf16[256,640]{1,0:T(8,128)(2,1)S(1)}, u32[]{:S(2)}, u32[]{:S(2)}) collective-permute-start(bf16[256,640]{1,0:T(8,128)(2,1)S(1)} %get-tuple-element.22.q0_ref), channel_id=1, source_target_pairs={{0,8},{4,12},{8,0},{12,4},{1,9},{5,13},{9,1},{13,5},{2,10},{6,14},... | collective-permute-start | bytes 983048 | tf_op jit(solution)/shard_map/ppermute | solution.py:321
  10.8 11.8 %collective-permute-start.4 = (bf16[128,640]{1,0:T(8,128)(2,1)S(1)}, bf16[128,640]{1,0:T(8,128)(2,1)S(1)}, u32[]{:S(2)}, u32[]{:S(2)}) collective-permute-start(bf16[128,640]{1,0:T(8,128)(2,1)S(1)} %get-tuple-element.23.own_ref), channel_id=1, source_target_pairs={{0,2},{1,3},{2,0},{3,1},{4,6},{5,7},{6,4},{7,5},{8,10},{9,11},{10,... | collective-permute-start | bytes 491528 | tf_op jit(solution)/shard_map/ppermute | solution.py:313
  16.2 28.8 %collective-permute-start.5 = (bf16[128,640]{1,0:T(8,128)(2,1)S(1)}, bf16[128,640]{1,0:T(8,128)(2,1)S(1)}, u32[]{:S(2)}, u32[]{:S(2)}) collective-permute-start(bf16[128,640]{1,0:T(8,128)(2,1)S(1)} %get-tuple-element.23.own_ref), channel_id=1, source_target_pairs={{0,3},{1,0},{2,1},{3,2},{4,7},{5,4},{6,5},{7,6},{8,11},{9,8},{10,9... | collective-permute-start | bytes 491528 | tf_op jit(solution)/shard_map/ppermute | solution.py:313
  22.6 38.3 %collective-permute-start.10 = (bf16[128,640]{1,0:T(8,128)(2,1)S(1)}, bf16[128,640]{1,0:T(8,128)(2,1)S(1)}, u32[]{:S(2)}, u32[]{:S(2)}) collective-permute-start(bf16[128,640]{1,0:T(8,128)(2,1)S(1)} %get-tuple-element.30.own_ref), channel_id=1, source_target_pairs={{0,2},{1,3},{2,0},{3,1},{4,6},{5,7},{6,4},{7,5},{8,10},{9,11},{10,... | collective-permute-start | bytes 491528 | tf_op jit(solution)/shard_map/ppermute | solution.py:313
  45.0 21.2 %collective-permute-start.11 = (bf16[128,640]{1,0:T(8,128)(2,1)S(1)}, bf16[128,640]{1,0:T(8,128)(2,1)S(1)}, u32[]{:S(2)}, u32[]{:S(2)}) collective-permute-start(bf16[128,640]{1,0:T(8,128)(2,1)S(1)} %get-tuple-element.30.own_ref), channel_id=1, source_target_pairs={{0,3},{1,0},{2,1},{3,2},{4,7},{5,4},{6,5},{7,6},{8,11},{9,8},{10,9... | collective-permute-start | bytes 491528 | tf_op jit(solution)/shard_map/ppermute | solution.py:313
  45.0 23.5 %collective-permute-start.9 = (bf16[128,640]{1,0:T(8,128)(2,1)S(1)}, bf16[128,640]{1,0:T(8,128)(2,1)S(1)}, u32[]{:S(2)}, u32[]{:S(2)}) collective-permute-start(bf16[128,640]{1,0:T(8,128)(2,1)S(1)} %get-tuple-element.30.own_ref), channel_id=1, source_target_pairs={{0,1},{1,2},{2,3},{3,0},{4,5},{5,6},{6,7},{7,4},{8,9},{9,10},{10,1... | collective-permute-start | bytes 491528 | tf_op jit(solution)/shard_map/ppermute | solution.py:313
  48.0 58.6 %collective-permute-start.21 = (bf16[256,640]{1,0:T(8,128)(2,1)S(1)}, bf16[256,640]{1,0:T(8,128)(2,1)S(1)}, u32[]{:S(2)}, u32[]{:S(2)}) collective-permute-start(bf16[256,640]{1,0:T(8,128)(2,1)S(1)} %bitcast.10), channel_id=1, source_target_pairs={{0,1},{1,2},{2,3},{3,4},{4,5},{5,6},{6,7},{7,8},{8,9},{9,10},{10,1... | collective-permute-start | bytes 983048 | tf_op jit(solution)/shard_map/ppermute | solution.py:323
  52.3 54.3 %collective-permute-start.22 = (bf16[256,640]{1,0:T(8,128)(2,1)S(1)}, bf16[256,640]{1,0:T(8,128)(2,1)S(1)}, u32[]{:S(2)}, u32[]{:S(2)}) collective-permute-start(bf16[256,640]{1,0:T(8,128)(2,1)S(1)} %bitcast.11), channel_id=1, source_target_pairs={{1,0},{2,1},{3,2},{4,3},{5,4},{6,5},{7,6},{8,7},{9,8},{10,9},{11,1... | collective-permute-start | bytes 983048 | tf_op jit(solution)/shard_map/ppermute | solution.py:324
  60.9 17.7 %collective-permute-start.6 = (bf16[128,768]{1,0:T(8,128)(2,1)S(1)}, bf16[128,768]{1,0:T(8,128)(2,1)S(1)}, u32[]{:S(2)}, u32[]{:S(2)}) collective-permute-start(bf16[128,768]{1,0:T(8,128)(2,1)S(1)} %get-tuple-element.26), channel_id=1, source_target_pairs={{0,12},{4,0},{8,4},{12,8},{1,13},{5,1},{9,5},{13,9},{2,14},{6,2},{... | collective-permute-start | bytes 589832 | tf_op jit(solution)/shard_map/ppermute | solution.py:360
  66.3 14.4 %collective-permute-start.7 = (bf16[128,768]{1,0:T(8,128)(2,1)S(1)}, bf16[128,768]{1,0:T(8,128)(2,1)S(1)}, u32[]{:S(2)}, u32[]{:S(2)}) collective-permute-start(bf16[128,768]{1,0:T(8,128)(2,1)S(1)} %get-tuple-element.27), channel_id=1, source_target_pairs={{0,4},{4,8},{8,12},{12,0},{1,5},{5,9},{9,13},{13,1},{2,6},{6,10},{... | collective-permute-start | bytes 589832 | tf_op jit(solution)/shard_map/ppermute | solution.py:360
  68.5 13.8 %copy-start.6 = (bf16[640,640]{1,0:T(8,128)(2,1)S(1)}, bf16[640,640]{1,0:T(8,128)(2,1)}, u32[]{:S(2)}) copy-start(bf16[640,640]{1,0:T(8,128)(2,1)} %w_ref.5) | copy-start | bytes 2457604
  68.5 13.8 %copy-start.10 = (bf16[128,640]{1,0:T(8,128)(2,1)S(1)}, bf16[128,640]{1,0:T(8,128)(2,1)}, u32[]{:S(2)}) copy-start(bf16[128,640]{1,0:T(8,128)(2,1)} %constant.6.clone.spread_ref) | copy-start | bytes 491524
  68.5 13.8 %copy-start.11 = (bf16[640,128]{1,0:T(8,128)(2,1)S(1)}, bf16[640,128]{1,0:T(8,128)(2,1)}, u32[]{:S(2)}) copy-start(bf16[640,128]{1,0:T(8,128)(2,1)} %constant.7.clone.gather_ref) | copy-start | bytes 491524
  68.5 12.2 %collective-permute-start.8 = (bf16[128,768]{1,0:T(8,128)(2,1)S(1)}, bf16[128,768]{1,0:T(8,128)(2,1)S(1)}, u32[]{:S(2)}, u32[]{:S(2)}) collective-permute-start(bf16[128,768]{1,0:T(8,128)(2,1)S(1)} %get-tuple-element.28), channel_id=1, source_target_pairs={{0,8},{4,12},{8,0},{12,4},{1,9},{5,13},{9,1},{13,5},{2,10},{6,14},... | collective-permute-start | bytes 589832 | tf_op jit(solution)/shard_map/ppermute | solution.py:360
  78.6 5.7 %collective-permute-start.12 = (bf16[128,768]{1,0:T(8,128)(2,1)S(1)}, bf16[128,768]{1,0:T(8,128)(2,1)S(1)}, u32[]{:S(2)}, u32[]{:S(2)}) collective-permute-start(bf16[128,768]{1,0:T(8,128)(2,1)S(1)} %get-tuple-element.32), channel_id=1, source_target_pairs={{0,12},{4,0},{8,4},{12,8},{1,13},{5,1},{9,5},{13,9},{2,14},{6,2},{... | collective-permute-start | bytes 589832 | tf_op jit(solution)/shard_map/ppermute | solution.py:360
  80.7 9.1 %collective-permute-start.13 = (bf16[128,768]{1,0:T(8,128)(2,1)S(1)}, bf16[128,768]{1,0:T(8,128)(2,1)S(1)}, u32[]{:S(2)}, u32[]{:S(2)}) collective-permute-start(bf16[128,768]{1,0:T(8,128)(2,1)S(1)} %get-tuple-element.33), channel_id=1, source_target_pairs={{0,4},{4,8},{8,12},{12,0},{1,5},{5,9},{9,13},{13,1},{2,6},{6,10},{... | collective-permute-start | bytes 589832 | tf_op jit(solution)/shard_map/ppermute | solution.py:360
  80.7 9.1 %collective-permute-start.14 = (bf16[128,768]{1,0:T(8,128)(2,1)S(1)}, bf16[128,768]{1,0:T(8,128)(2,1)S(1)}, u32[]{:S(2)}, u32[]{:S(2)}) collective-permute-start(bf16[128,768]{1,0:T(8,128)(2,1)S(1)} %get-tuple-element.34), channel_id=1, source_target_pairs={{0,8},{4,12},{8,0},{12,4},{1,9},{5,13},{9,1},{13,5},{2,10},{6,14},... | collective-permute-start | bytes 589832 | tf_op jit(solution)/shard_map/ppermute | solution.py:360
  89.8 16.8 %copy-start.1 = (f32[2,640]{1,0:T(2,128)S(1)}, f32[2,640]{1,0:T(2,128)}, u32[]{:S(2)}) copy-start(f32[2,640]{1,0:T(2,128)} %shift_ref.1) | copy-start | bytes 15364
  89.8 16.8 %copy-start.4 = (f32[640]{0:T(1024)S(1)}, f32[640]{0:T(1024)}, u32[]{:S(2)}) copy-start(f32[640]{0:T(1024)} %bias_ref.6) | copy-start | bytes 7684
  90.8 20.1 %copy-start = (bf16[128,640]{1,0:T(8,128)(2,1)S(1)}, bf16[128,640]{1,0:T(8,128)(2,1)}, u32[]{:S(2)}) copy-start(bf16[128,640]{1,0:T(8,128)(2,1)} %constant.8.clone.scatter_ref) | copy-start | bytes 491524
  90.8 20.1 %copy-start.2 = (f32[640]{0:T(1024)S(1)}, f32[640]{0:T(1024)}, u32[]{:S(2)}) copy-start(f32[640]{0:T(1024)} %gain_ref.5) | copy-start | bytes 7684
  90.8 20.1 %copy-start.3 = (f32[640]{0:T(1024)S(1)}, f32[640]{0:T(1024)}, u32[]{:S(2)}) copy-start(f32[640]{0:T(1024)} %bias_ref.7) | copy-start | bytes 7684
  90.8 4.9 %collective-permute-start.15 = (f32[8,128]{1,0:T(8,128)S(1)}, f32[8,128]{1,0:T(8,128)S(1)}, u32[]{:S(2)}, u32[]{:S(2)}) collective-permute-start(f32[8,128]{1,0:T(8,128)S(1)} %get-tuple-element.37.refs_0_), channel_id=1, source_target_pairs={{0,4},{4,8},{8,12},{12,0},{1,5},{5,9},{9,13},{13,1},{2,6},{6,10},{... | collective-permute-start | bytes 12296 | tf_op jit(solution)/shard_map/ppermute | solution.py:389
  90.9 4.8 %collective-permute-start.16 = (f32[8,128]{1,0:T(8,128)S(1)}, f32[8,128]{1,0:T(8,128)S(1)}, u32[]{:S(2)}, u32[]{:S(2)}) collective-permute-start(f32[8,128]{1,0:T(8,128)S(1)} %get-tuple-element.37.refs_0_), channel_id=1, source_target_pairs={{0,12},{4,0},{8,4},{12,8},{1,13},{5,1},{9,5},{13,9},{2,14},{6,2},{... | collective-permute-start | bytes 12296 | tf_op jit(solution)/shard_map/ppermute | solution.py:389
  94.2 5.1 %collective-permute-start.17 = (f32[8,128]{1,0:T(8,128)S(1)}, f32[8,128]{1,0:T(8,128)S(1)}, u32[]{:S(2)}, u32[]{:S(2)}) collective-permute-start(f32[8,128]{1,0:T(8,128)S(1)} %get-tuple-element.37.refs_0_), channel_id=1, source_target_pairs={{0,8},{4,12},{8,0},{12,4},{1,9},{5,13},{9,1},{13,5},{2,10},{6,14},... | collective-permute-start | bytes 12296 | tf_op jit(solution)/shard_map/ppermute | solution.py:389
  99.3 9.2 %collective-permute-start.18 = (f32[8,128]{1,0:T(8,128)S(1)}, f32[8,128]{1,0:T(8,128)S(1)}, u32[]{:S(2)}, u32[]{:S(2)}) collective-permute-start(f32[8,128]{1,0:T(8,128)S(1)} %shard_map.160.s0_ref), channel_id=1, source_target_pairs={{0,1},{1,2},{2,3},{3,0},{4,5},{5,6},{6,7},{7,4},{8,9},{9,10},{10,1... | collective-permute-start | bytes 12296 | tf_op jit(solution)/shard_map/ppermute | solution.py:391
  99.3 9.2 %collective-permute-start.19 = (f32[8,128]{1,0:T(8,128)S(1)}, f32[8,128]{1,0:T(8,128)S(1)}, u32[]{:S(2)}, u32[]{:S(2)}) collective-permute-start(f32[8,128]{1,0:T(8,128)S(1)} %shard_map.160.s0_ref), channel_id=1, source_target_pairs={{0,3},{1,0},{2,1},{3,2},{4,7},{5,4},{6,5},{7,6},{8,11},{9,8},{10,9... | collective-permute-start | bytes 12296 | tf_op jit(solution)/shard_map/ppermute | solution.py:391
  103.4 7.5 %collective-permute-start.20 = (f32[8,128]{1,0:T(8,128)S(1)}, f32[8,128]{1,0:T(8,128)S(1)}, u32[]{:S(2)}, u32[]{:S(2)}) collective-permute-start(f32[8,128]{1,0:T(8,128)S(1)} %shard_map.160.s0_ref), channel_id=1, source_target_pairs={{0,2},{1,3},{2,0},{3,1},{4,6},{5,7},{6,4},{7,5},{8,10},{9,11},{10,... | collective-permute-start | bytes 12296 | tf_op jit(solution)/shard_map/ppermute | solution.py:391

commit v5 on v4

--- a/solution.py
+++ b/solution.py
@@ -310,7 +310,13 @@
         slow=(0, 1, 2),
         flops=6 * 10 ** 9,
     )
-    along = [[lax.ppermute(one, "z", ring(by, z_count)) for by in (1, 2, 3)] for one in stale]
+    along = []
+    for s, one in enumerate(stale):
+        up, down = (lax.ppermute(one, "z", ring(by, z_count)) for by in (1, 3))
+        far = lax.ppermute(up, "z", ring(1, z_count)) if s % 2 == 0 else lax.ppermute(
+            down, "z", ring(3, z_count)
+        )
+        along.append((up, far, down))
     queries, fresh = call(
         query_kernel, [both] * 2, hid, ln_gain, ln_bias, w_qkv,
         grid=(1,),

time: 113 us -> 104 us (0.920)
  the two profiles are of different devices: /device:TPU:2 before, /device:TPU:6 now
where the time goes in v5:
time: 104 us
  starting transfers between devices  53.2 us (51%)
  waiting for transfers between devices  28.2 us (27%)
  Pallas kernels  22.6 us (22%)
    pallas_call x9, Pallas kernels, call(): pl.pallas_call(kernel, out_shape=out_shape, compiler_params=pltpu.Compile...  22.6 us
    ppermute x4, starting transfers between devices, shards(): up, down = (lax.ppermute(one, 'z', ring(by, z_count)) for by in (1, 3))  12.8 us
    ppermute x6, starting transfers between devices, shards(): lax.ppermute(one, 'y', ring(-by, y_count))  9.27 us
    ppermute x3, starting transfers between devices, shards(): lax.ppermute(stat, 'z', ring(by, z_count))  9.14 us
    ppermute x4, waiting for transfers between devices, shards(): up, down = (lax.ppermute(one, 'z', ring(by, z_count)) for by in (1, 3))  7.75 us
    ppermute x6, waiting for transfers between devices, shards(): lax.ppermute(one, 'y', ring(-by, y_count))  6.81 us
    ppermute x3, starting transfers between devices, shards(): lax.ppermute(queries, 'y', ring(by, y_count))  5.29 us
    ppermute x1, starting transfers between devices, shards(): lax.ppermute(down, 'z', ring(3, z_count))  5.18 us
  transfers between devices with their start and end apart: 23, of which 8 were waited for; matrix products, arithmetic and copies ran while one was open for 0% of the time, Pallas kernels for 18%

profile of v5, /device:TPU:6, one launch (start us, length us, event | category | flops | bytes accessed | tf_op | source)
XLA Modules:
  0.0 104.2 jit_solution(15029061314236233513)
XLA Ops:
  0.0 0.0 copy-start.9
  0.0 1.4 %shard_map.155 = (bf16[128,640]{1,0:T(8,128)(2,1)S(1)}, bf16[128,640]{1,0:T(8,128)(2,1)S(1)}) custom-call(bf16[256,640]{1,0:T(8,128)(2,1)} %bitcast.9, f32[640]{0:T(1024)} %gain_ref.4, f32[640]{0:T(1024)} %bias_ref.5), custom_call_target="tpu_custom_call" | custom-call | flops 6000000000 | bytes 1000000 | tf_op jit(solution)/shard_map/pallas_call | solution.py:278
  1.4 3.3 %collective-permute-start.3 = (bf16[128,640]{1,0:T(8,128)(2,1)S(1)}, bf16[128,640]{1,0:T(8,128)(2,1)S(1)}, u32[]{:S(2)}, u32[]{:S(2)}) collective-permute-start(bf16[128,640]{1,0:T(8,128)(2,1)S(1)} %get-tuple-element.23.own_ref), channel_id=1, source_target_pairs={{0,1},{1,2},{2,3},{3,0},{4,5},{5,6},{6,7},{7,4},{8,9},{9,10},{10,1... | collective-permute-start | bytes 491528 | tf_op jit(solution)/shard_map/ppermute | solution.py:315
  4.8 0.0 copy-done.5
  4.8 0.0 copy-done.7
  4.8 0.0 copy-done.8
  4.8 0.0 copy-done.9
  4.8 0.0 copy-start.12
  4.8 0.7 shard_map.154
  5.5 1.7 %collective-permute-start = (bf16[256,640]{1,0:T(8,128)(2,1)S(1)}, bf16[256,640]{1,0:T(8,128)(2,1)S(1)}, u32[]{:S(2)}, u32[]{:S(2)}) collective-permute-start(bf16[256,640]{1,0:T(8,128)(2,1)S(1)} %get-tuple-element.22.q0_ref), channel_id=1, source_target_pairs={{0,4},{4,8},{8,12},{12,0},{1,5},{5,9},{9,13},{13,1},{2,6},{6,10},{... | collective-permute-start | bytes 983048 | tf_op jit(solution)/shard_map/ppermute | solution.py:327
  7.2 1.7 %collective-permute-start.1 = (bf16[256,640]{1,0:T(8,128)(2,1)S(1)}, bf16[256,640]{1,0:T(8,128)(2,1)S(1)}, u32[]{:S(2)}, u32[]{:S(2)}) collective-permute-start(bf16[256,640]{1,0:T(8,128)(2,1)S(1)} %get-tuple-element.22.q0_ref), channel_id=1, source_target_pairs={{0,12},{4,0},{8,4},{12,8},{1,13},{5,1},{9,5},{13,9},{2,14},{6,2},{... | collective-permute-start | bytes 983048 | tf_op jit(solution)/shard_map/ppermute | solution.py:327
  8.8 2.0 %collective-permute-start.2 = (bf16[256,640]{1,0:T(8,128)(2,1)S(1)}, bf16[256,640]{1,0:T(8,128)(2,1)S(1)}, u32[]{:S(2)}, u32[]{:S(2)}) collective-permute-start(bf16[256,640]{1,0:T(8,128)(2,1)S(1)} %get-tuple-element.22.q0_ref), channel_id=1, source_target_pairs={{0,8},{4,12},{8,0},{12,4},{1,9},{5,13},{9,1},{13,5},{2,10},{6,14},... | collective-permute-start | bytes 983048 | tf_op jit(solution)/shard_map/ppermute | solution.py:327
  10.8 3.3 %collective-permute-start.5 = (bf16[128,640]{1,0:T(8,128)(2,1)S(1)}, bf16[128,640]{1,0:T(8,128)(2,1)S(1)}, u32[]{:S(2)}, u32[]{:S(2)}) collective-permute-start(bf16[128,640]{1,0:T(8,128)(2,1)S(1)} %get-tuple-element.23.own_ref), channel_id=1, source_target_pairs={{0,3},{1,0},{2,1},{3,2},{4,7},{5,4},{6,5},{7,6},{8,11},{9,8},{10,9... | collective-permute-start | bytes 491528 | tf_op jit(solution)/shard_map/ppermute | solution.py:315
  14.1 0.0 collective-permute-done.3.z1_ref
  14.2 4.1 %collective-permute-start.10 = (bf16[128,640]{1,0:T(8,128)(2,1)S(1)}, bf16[128,640]{1,0:T(8,128)(2,1)S(1)}, u32[]{:S(2)}, u32[]{:S(2)}) collective-permute-start(bf16[128,640]{1,0:T(8,128)(2,1)S(1)} %get-tuple-element.30.own_ref), channel_id=1, source_target_pairs={{0,3},{1,0},{2,1},{3,2},{4,7},{5,4},{6,5},{7,6},{8,11},{9,8},{10,9... | collective-permute-start | bytes 491528 | tf_op jit(solution)/shard_map/ppermute | solution.py:315
  18.2 7.7 %collective-permute-done.5.z3_ref = bf16[128,640]{1,0:T(8,128)(2,1)S(1)} collective-permute-done((bf16[128,640]{1,0:T(8,128)(2,1)S(1)}, bf16[128,640]{1,0:T(8,128)(2,1)S(1)}, u32[]{:S(2)}, u32[]{:S(2)}) %collective-permute-start.5) | collective-permute-done | bytes 163872 | tf_op jit(solution)/shard_map/ppermute | solution.py:315
  26.0 4.5 %collective-permute-start.4 = (bf16[128,640]{1,0:T(8,128)(2,1)S(1)}, bf16[128,640]{1,0:T(8,128)(2,1)S(1)}, u32[]{:S(2)}, u32[]{:S(2)}) collective-permute-start(bf16[128,640]{1,0:T(8,128)(2,1)S(1)} %collective-permute-done.3.z1_ref), channel_id=1, source_target_pairs={{0,1},{1,2},{2,3},{3,0},{4,5},{5,6},{6,7},{7,4},{8,9},{9,10},{10,1... | collective-permute-start | bytes 491528 | tf_op jit(solution)/shard_map/ppermute | solution.py:316
  30.5 0.0 collective-permute-done.10.z3_ref
  30.5 2.1 %collective-permute-start.9 = (bf16[128,640]{1,0:T(8,128)(2,1)S(1)}, bf16[128,640]{1,0:T(8,128)(2,1)S(1)}, u32[]{:S(2)}, u32[]{:S(2)}) collective-permute-start(bf16[128,640]{1,0:T(8,128)(2,1)S(1)} %get-tuple-element.30.own_ref), channel_id=1, source_target_pairs={{0,1},{1,2},{2,3},{3,0},{4,5},{5,6},{6,7},{7,4},{8,9},{9,10},{10,1... | collective-permute-start | bytes 491528 | tf_op jit(solution)/shard_map/ppermute | solution.py:315
  32.6 0.0 collective-permute-done.q1_ref
  32.6 0.0 copy-done.12
  32.6 2.4 %collective-permute-start.21 = (bf16[256,640]{1,0:T(8,128)(2,1)S(1)}, bf16[256,640]{1,0:T(8,128)(2,1)S(1)}, u32[]{:S(2)}, u32[]{:S(2)}) collective-permute-start(bf16[256,640]{1,0:T(8,128)(2,1)S(1)} %bitcast.10), channel_id=1, source_target_pairs={{0,1},{1,2},{2,3},{3,4},{4,5},{5,6},{6,7},{7,8},{8,9},{9,10},{10,1... | collective-permute-start | bytes 983048 | tf_op jit(solution)/shard_map/ppermute | solution.py:329
  35.0 0.0 collective-permute-done.1.q2_ref
  35.0 1.3 %collective-permute-start.22 = (bf16[256,640]{1,0:T(8,128)(2,1)S(1)}, bf16[256,640]{1,0:T(8,128)(2,1)S(1)}, u32[]{:S(2)}, u32[]{:S(2)}) collective-permute-start(bf16[256,640]{1,0:T(8,128)(2,1)S(1)} %bitcast.11), channel_id=1, source_target_pairs={{1,0},{2,1},{3,2},{4,3},{5,4},{6,5},{7,6},{8,7},{9,8},{10,9},{11,1... | collective-permute-start | bytes 983048 | tf_op jit(solution)/shard_map/ppermute | solution.py:330
  36.3 0.0 collective-permute-done.2.q3_ref
  36.3 5.2 %collective-permute-start.11 = (bf16[128,640]{1,0:T(8,128)(2,1)S(1)}, bf16[128,640]{1,0:T(8,128)(2,1)S(1)}, u32[]{:S(2)}, u32[]{:S(2)}) collective-permute-start(bf16[128,640]{1,0:T(8,128)(2,1)S(1)} %collective-permute-done.10.z3_ref), channel_id=1, source_target_pairs={{0,3},{1,0},{2,1},{3,2},{4,7},{5,4},{6,5},{7,6},{8,11},{9,8},{10,9... | collective-permute-start | bytes 491528 | tf_op jit(solution)/shard_map/ppermute | solution.py:316
  41.5 2.6 %collective-permute-done.4.z2_ref = bf16[128,640]{1,0:T(8,128)(2,1)S(1)} collective-permute-done((bf16[128,640]{1,0:T(8,128)(2,1)S(1)}, bf16[128,640]{1,0:T(8,128)(2,1)S(1)}, u32[]{:S(2)}, u32[]{:S(2)}) %collective-permute-start.4) | collective-permute-done | bytes 163872 | tf_op jit(solution)/shard_map/ppermute | solution.py:316
  44.0 7.2 %shard_map.156 = (bf16[128,768]{1,0:T(8,128)(2,1)S(1)}, bf16[128,768]{1,0:T(8,128)(2,1)S(1)}, bf16[128,768]{1,0:T(8,128)(2,1)S(1)}, bf16[128,768]{1,0:T(8,128)(2,1)S(1)}) custom-call(bf16[256,640]{1,0:T(8,128)(2,1)S(1)} %get-tuple-element.22.q0_ref, bf16[256,640]{1,0:T(8,128)(2,1)S(1)} %collective-permute-done.q1_ref, ...), custom_call_target="tpu_custom_call" | custom-call | flops 6000000000 | bytes 1000000 | tf_op jit(solution)/shard_map/pallas_call | solution.py:278
  51.3 0.1 collective-permute-start.6
  51.4 0.0 collective-permute-done.9.z1_ref
  51.4 2.0 %collective-permute-start.7 = (bf16[128,768]{1,0:T(8,128)(2,1)S(1)}, bf16[128,768]{1,0:T(8,128)(2,1)S(1)}, u32[]{:S(2)}, u32[]{:S(2)}) collective-permute-start(bf16[128,768]{1,0:T(8,128)(2,1)S(1)} %get-tuple-element.27), channel_id=1, source_target_pairs={{0,4},{4,8},{8,12},{12,0},{1,5},{5,9},{9,13},{13,1},{2,6},{6,10},{... | collective-permute-start | bytes 589832 | tf_op jit(solution)/shard_map/ppermute | solution.py:366
  53.4 2.6 %collective-permute-done.11.z2_ref = bf16[128,640]{1,0:T(8,128)(2,1)S(1)} collective-permute-done((bf16[128,640]{1,0:T(8,128)(2,1)S(1)}, bf16[128,640]{1,0:T(8,128)(2,1)S(1)}, u32[]{:S(2)}, u32[]{:S(2)}) %collective-permute-start.11) | collective-permute-done | bytes 163872 | tf_op jit(solution)/shard_map/ppermute | solution.py:316
  56.0 3.9 %collective-permute-start.8 = (bf16[128,768]{1,0:T(8,128)(2,1)S(1)}, bf16[128,768]{1,0:T(8,128)(2,1)S(1)}, u32[]{:S(2)}, u32[]{:S(2)}) collective-permute-start(bf16[128,768]{1,0:T(8,128)(2,1)S(1)} %get-tuple-element.28), channel_id=1, source_target_pairs={{0,8},{4,12},{8,0},{12,4},{1,9},{5,13},{9,1},{13,5},{2,10},{6,14},... | collective-permute-start | bytes 589832 | tf_op jit(solution)/shard_map/ppermute | solution.py:366
  59.9 7.2 %shard_map.158 = (bf16[128,768]{1,0:T(8,128)(2,1)S(1)}, bf16[128,768]{1,0:T(8,128)(2,1)S(1)}, bf16[128,768]{1,0:T(8,128)(2,1)S(1)}, bf16[128,768]{1,0:T(8,128)(2,1)S(1)}, bf16[3,3,640,640]{3,2,1,0:T(8,128)(2,1)S(1)}) custom-call(bf16[256,640]{1,0:T(8,128)(2,1)S(1)} %get-tuple-element.22.q0_ref, bf16[256,640]{1,0:T(8,128)(2,1)S(1)} %collective-permute-done.q1_ref, ...), custom_call_target="tpu_custom_call" | custom-call | flops 6000000000 | bytes 1000000 | tf_op jit(solution)/shard_map/pallas_call | solution.py:278
  67.2 0.0 collective-permute-done.6.o1_ref
  67.2 1.7 %collective-permute-start.12 = (bf16[128,768]{1,0:T(8,128)(2,1)S(1)}, bf16[128,768]{1,0:T(8,128)(2,1)S(1)}, u32[]{:S(2)}, u32[]{:S(2)}) collective-permute-start(bf16[128,768]{1,0:T(8,128)(2,1)S(1)} %get-tuple-element.32), channel_id=1, source_target_pairs={{0,12},{4,0},{8,4},{12,8},{1,13},{5,1},{9,5},{13,9},{2,14},{6,2},{... | collective-permute-start | bytes 589832 | tf_op jit(solution)/shard_map/ppermute | solution.py:366
  68.9 0.0 collective-permute-done.7.o2_ref
  68.9 0.4 collective-permute-start.13
  69.3 0.0 collective-permute-done.8.o3_ref
  69.3 1.2 %collective-permute-start.14 = (bf16[128,768]{1,0:T(8,128)(2,1)S(1)}, bf16[128,768]{1,0:T(8,128)(2,1)S(1)}, u32[]{:S(2)}, u32[]{:S(2)}) collective-permute-start(bf16[128,768]{1,0:T(8,128)(2,1)S(1)} %get-tuple-element.34), channel_id=1, source_target_pairs={{0,8},{4,12},{8,0},{12,4},{1,9},{5,13},{9,1},{13,5},{2,10},{6,14},... | collective-permute-start | bytes 589832 | tf_op jit(solution)/shard_map/ppermute | solution.py:366
  70.4 0.0 copy-done.10
  70.4 1.0 shard_map.157
  71.5 3.2 %collective-permute-done.12.o1_ref = bf16[128,768]{1,0:T(8,128)(2,1)S(1)} collective-permute-done((bf16[128,768]{1,0:T(8,128)(2,1)S(1)}, bf16[128,768]{1,0:T(8,128)(2,1)S(1)}, u32[]{:S(2)}, u32[]{:S(2)}) %collective-permute-start.12) | collective-permute-done | bytes 196640 | tf_op jit(solution)/shard_map/ppermute | solution.py:366
  74.6 3.6 %collective-permute-done.13.o2_ref = bf16[128,768]{1,0:T(8,128)(2,1)S(1)} collective-permute-done((bf16[128,768]{1,0:T(8,128)(2,1)S(1)}, bf16[128,768]{1,0:T(8,128)(2,1)S(1)}, u32[]{:S(2)}, u32[]{:S(2)}) %collective-permute-start.13) | collective-permute-done | bytes 196640 | tf_op jit(solution)/shard_map/ppermute | solution.py:366
  78.3 0.0 collective-permute-done.14.o3_ref
  78.3 1.0 shard_map.159
  79.3 0.1 collective-permute-start.15
  79.4 3.2 %collective-permute-start.16 = (f32[8,128]{1,0:T(8,128)S(1)}, f32[8,128]{1,0:T(8,128)S(1)}, u32[]{:S(2)}, u32[]{:S(2)}) collective-permute-start(f32[8,128]{1,0:T(8,128)S(1)} %get-tuple-element.37.refs_0_), channel_id=1, source_target_pairs={{0,12},{4,0},{8,4},{12,8},{1,13},{5,1},{9,5},{13,9},{2,14},{6,2},{... | collective-permute-start | bytes 12296 | tf_op jit(solution)/shard_map/ppermute | solution.py:395
  82.6 0.0 collective-permute-start.17
  82.7 1.6 %collective-permute-done.15.refs_1_ = f32[8,128]{1,0:T(8,128)S(1)} collective-permute-done((f32[8,128]{1,0:T(8,128)S(1)}, f32[8,128]{1,0:T(8,128)S(1)}, u32[]{:S(2)}, u32[]{:S(2)}) %collective-permute-start.15) | collective-permute-done | bytes 4128 | tf_op jit(solution)/shard_map/ppermute | solution.py:395
  84.2 0.0 collective-permute-done.16.refs_2_
  84.2 3.5 %collective-permute-done.17.refs_3_ = f32[8,128]{1,0:T(8,128)S(1)} collective-permute-done((f32[8,128]{1,0:T(8,128)S(1)}, f32[8,128]{1,0:T(8,128)S(1)}, u32[]{:S(2)}, u32[]{:S(2)}) %collective-permute-start.17) | collective-permute-done | bytes 4128 | tf_op jit(solution)/shard_map/ppermute | solution.py:395
  87.8 3.8 %collective-permute-start.18 = (f32[8,128]{1,0:T(8,128)S(1)}, f32[8,128]{1,0:T(8,128)S(1)}, u32[]{:S(2)}, u32[]{:S(2)}) collective-permute-start(f32[8,128]{1,0:T(8,128)S(1)} %shard_map.160.s0_ref), channel_id=1, source_target_pairs={{0,1},{1,2},{2,3},{3,0},{4,5},{5,6},{6,7},{7,4},{8,9},{9,10},{10,1... | collective-permute-start | bytes 12296 | tf_op jit(solution)/shard_map/ppermute | solution.py:397
  91.6 3.0 %collective-permute-start.19 = (f32[8,128]{1,0:T(8,128)S(1)}, f32[8,128]{1,0:T(8,128)S(1)}, u32[]{:S(2)}, u32[]{:S(2)}) collective-permute-start(f32[8,128]{1,0:T(8,128)S(1)} %shard_map.160.s0_ref), channel_id=1, source_target_pairs={{0,3},{1,0},{2,1},{3,2},{4,7},{5,4},{6,5},{7,6},{8,11},{9,8},{10,9... | collective-permute-start | bytes 12296 | tf_op jit(solution)/shard_map/ppermute | solution.py:397
  94.6 2.3 %collective-permute-start.20 = (f32[8,128]{1,0:T(8,128)S(1)}, f32[8,128]{1,0:T(8,128)S(1)}, u32[]{:S(2)}, u32[]{:S(2)}) collective-permute-start(f32[8,128]{1,0:T(8,128)S(1)} %shard_map.160.s0_ref), channel_id=1, source_target_pairs={{0,2},{1,3},{2,0},{3,1},{4,6},{5,7},{6,4},{7,5},{8,10},{9,11},{10,... | collective-permute-start | bytes 12296 | tf_op jit(solution)/shard_map/ppermute | solution.py:397
  96.9 0.0 collective-permute-done.21.above_ref
  96.9 0.0 collective-permute-done.22.below_ref
  96.9 0.0 copy-done.4
  96.9 1.8 %shard_map.161.rim_ref = f32[256,640]{1,0:T(8,128)S(1)} custom-call(bf16[256,640]{1,0:T(8,128)(2,1)S(1)} %collective-permute-done.21.above_ref, bf16[256,640]{1,0:T(8,128)(2,1)S(1)} %collective-permute-done.22.below_ref, bf16[3,3,640,640]{3,2,1,0:T(8,128)(2,1)S(1)} %get-tuple-element.38.w_ref, f32[640]{0:T(1024)S(1)} %copy-done.4, f32[2,640]{1,0:T(2,128)S(1)} %copy-done.1), custom_call_target="tpu_custom_call" | custom-call | flops 1258291200 | bytes 1000000 | tf_op jit(solution)/shard_map/pallas_call | solution.py:278
  98.8 0.0 collective-permute-done.18.s1_ref
  98.8 0.0 collective-permute-done.19.s2_ref
  98.8 3.3 %collective-permute-done.20.s3_ref = f32[8,128]{1,0:T(8,128)S(1)} collective-permute-done((f32[8,128]{1,0:T(8,128)S(1)}, f32[8,128]{1,0:T(8,128)S(1)}, u32[]{:S(2)}, u32[]{:S(2)}) %collective-permute-start.20) | collective-permute-done | bytes 4128 | tf_op jit(solution)/shard_map/ppermute | solution.py:397
  102.1 0.0 copy-done
  102.2 2.1 %shard_map.162 = bf16[256,640]{1,0:T(8,128)(2,1)} custom-call(bf16[128,640]{1,0:T(8,128)(2,1)S(1)} %get-tuple-element.29.res0_ref, bf16[128,640]{1,0:T(8,128)(2,1)S(1)} %get-tuple-element.36.res1_ref, f32[8,128]{1,0:T(8,128)S(1)} %shard_map.160.s0_ref, f32[8,128]{1,0:T(8,128)S(1)} %collective-permute-done.18.s1_ref, ...), custom_call_target="tpu_custom_call" | custom-call | flops 629145600 | bytes 1000000 | tf_op jit(solution)/shard_map/pallas_call | solution.py:278
  (17 shorter events, 0.0 us)
Async XLA Ops:
  0.0 4.8 %copy-start.5 = (bf16[640,1920]{1,0:T(8,128)(2,1)S(1)}, bf16[640,1920]{1,0:T(8,128)(2,1)}, u32[]{:S(2)}) copy-start(bf16[640,1920]{1,0:T(8,128)(2,1)} %wv_ref.3) | copy-start | bytes 7372804
  0.0 4.8 %copy-start.7 = (bf16[2,1,128,640]{3,2,1,0:T(8,128)(2,1)S(1)}, bf16[2,1,128,640]{3,2,1,0:T(8,128)(2,1)}, u32[]{:S(2)}) copy-start(bf16[2,1,128,640]{3,2,1,0:T(8,128)(2,1)} %param.16) | copy-start | bytes 983044
  0.0 4.8 %copy-start.8 = (f32[640]{0:T(1024)S(1)}, f32[640]{0:T(1024)}, u32[]{:S(2)}) copy-start(f32[640]{0:T(1024)} %gain_ref.4) | copy-start | bytes 7684
  0.0 4.8 %copy-start.9 = (f32[640]{0:T(1024)S(1)}, f32[640]{0:T(1024)}, u32[]{:S(2)}) copy-start(f32[640]{0:T(1024)} %bias_ref.5) | copy-start | bytes 7684
  1.4 12.7 %collective-permute-start.3 = (bf16[128,640]{1,0:T(8,128)(2,1)S(1)}, bf16[128,640]{1,0:T(8,128)(2,1)S(1)}, u32[]{:S(2)}, u32[]{:S(2)}) collective-permute-start(bf16[128,640]{1,0:T(8,128)(2,1)S(1)} %get-tuple-element.23.own_ref), channel_id=1, source_target_pairs={{0,1},{1,2},{2,3},{3,0},{4,5},{5,6},{6,7},{7,4},{8,9},{9,10},{10,1... | collective-permute-start | bytes 491528 | tf_op jit(solution)/shard_map/ppermute | solution.py:315
  4.8 27.8 %copy-start.12 = (bf16[2,1,128,640]{3,2,1,0:T(8,128)(2,1)S(1)}, bf16[2,1,128,640]{3,2,1,0:T(8,128)(2,1)}, u32[]{:S(2)}) copy-start(bf16[2,1,128,640]{3,2,1,0:T(8,128)(2,1)} %param.18) | copy-start | bytes 983044
  5.5 27.0 %collective-permute-start = (bf16[256,640]{1,0:T(8,128)(2,1)S(1)}, bf16[256,640]{1,0:T(8,128)(2,1)S(1)}, u32[]{:S(2)}, u32[]{:S(2)}) collective-permute-start(bf16[256,640]{1,0:T(8,128)(2,1)S(1)} %get-tuple-element.22.q0_ref), channel_id=1, source_target_pairs={{0,4},{4,8},{8,12},{12,0},{1,5},{5,9},{9,13},{13,1},{2,6},{6,10},{... | collective-permute-start | bytes 983048 | tf_op jit(solution)/shard_map/ppermute | solution.py:327
  7.2 27.8 %collective-permute-start.1 = (bf16[256,640]{1,0:T(8,128)(2,1)S(1)}, bf16[256,640]{1,0:T(8,128)(2,1)S(1)}, u32[]{:S(2)}, u32[]{:S(2)}) collective-permute-start(bf16[256,640]{1,0:T(8,128)(2,1)S(1)} %get-tuple-element.22.q0_ref), channel_id=1, source_target_pairs={{0,12},{4,0},{8,4},{12,8},{1,13},{5,1},{9,5},{13,9},{2,14},{6,2},{... | collective-permute-start | bytes 983048 | tf_op jit(solution)/shard_map/ppermute | solution.py:327
  8.8 27.4 %collective-permute-start.2 = (bf16[256,640]{1,0:T(8,128)(2,1)S(1)}, bf16[256,640]{1,0:T(8,128)(2,1)S(1)}, u32[]{:S(2)}, u32[]{:S(2)}) collective-permute-start(bf16[256,640]{1,0:T(8,128)(2,1)S(1)} %get-tuple-element.22.q0_ref), channel_id=1, source_target_pairs={{0,8},{4,12},{8,0},{12,4},{1,9},{5,13},{9,1},{13,5},{2,10},{6,14},... | collective-permute-start | bytes 983048 | tf_op jit(solution)/shard_map/ppermute | solution.py:327
  10.8 15.1 %collective-permute-start.5 = (bf16[128,640]{1,0:T(8,128)(2,1)S(1)}, bf16[128,640]{1,0:T(8,128)(2,1)S(1)}, u32[]{:S(2)}, u32[]{:S(2)}) collective-permute-start(bf16[128,640]{1,0:T(8,128)(2,1)S(1)} %get-tuple-element.23.own_ref), channel_id=1, source_target_pairs={{0,3},{1,0},{2,1},{3,2},{4,7},{5,4},{6,5},{7,6},{8,11},{9,8},{10,9... | collective-permute-start | bytes 491528 | tf_op jit(solution)/shard_map/ppermute | solution.py:315
  14.2 16.3 %collective-permute-start.10 = (bf16[128,640]{1,0:T(8,128)(2,1)S(1)}, bf16[128,640]{1,0:T(8,128)(2,1)S(1)}, u32[]{:S(2)}, u32[]{:S(2)}) collective-permute-start(bf16[128,640]{1,0:T(8,128)(2,1)S(1)} %get-tuple-element.30.own_ref), channel_id=1, source_target_pairs={{0,3},{1,0},{2,1},{3,2},{4,7},{5,4},{6,5},{7,6},{8,11},{9,8},{10,9... | collective-permute-start | bytes 491528 | tf_op jit(solution)/shard_map/ppermute | solution.py:315
  26.0 18.1 %collective-permute-start.4 = (bf16[128,640]{1,0:T(8,128)(2,1)S(1)}, bf16[128,640]{1,0:T(8,128)(2,1)S(1)}, u32[]{:S(2)}, u32[]{:S(2)}) collective-permute-start(bf16[128,640]{1,0:T(8,128)(2,1)S(1)} %collective-permute-done.3.z1_ref), channel_id=1, source_target_pairs={{0,1},{1,2},{2,3},{3,0},{4,5},{5,6},{6,7},{7,4},{8,9},{9,10},{10,1... | collective-permute-start | bytes 491528 | tf_op jit(solution)/shard_map/ppermute | solution.py:316
  30.5 20.9 %collective-permute-start.9 = (bf16[128,640]{1,0:T(8,128)(2,1)S(1)}, bf16[128,640]{1,0:T(8,128)(2,1)S(1)}, u32[]{:S(2)}, u32[]{:S(2)}) collective-permute-start(bf16[128,640]{1,0:T(8,128)(2,1)S(1)} %get-tuple-element.30.own_ref), channel_id=1, source_target_pairs={{0,1},{1,2},{2,3},{3,0},{4,5},{5,6},{6,7},{7,4},{8,9},{9,10},{10,1... | collective-permute-start | bytes 491528 | tf_op jit(solution)/shard_map/ppermute | solution.py:315
  32.6 64.3 %collective-permute-start.21 = (bf16[256,640]{1,0:T(8,128)(2,1)S(1)}, bf16[256,640]{1,0:T(8,128)(2,1)S(1)}, u32[]{:S(2)}, u32[]{:S(2)}) collective-permute-start(bf16[256,640]{1,0:T(8,128)(2,1)S(1)} %bitcast.10), channel_id=1, source_target_pairs={{0,1},{1,2},{2,3},{3,4},{4,5},{5,6},{6,7},{7,8},{8,9},{9,10},{10,1... | collective-permute-start | bytes 983048 | tf_op jit(solution)/shard_map/ppermute | solution.py:329
  35.0 61.9 %collective-permute-start.22 = (bf16[256,640]{1,0:T(8,128)(2,1)S(1)}, bf16[256,640]{1,0:T(8,128)(2,1)S(1)}, u32[]{:S(2)}, u32[]{:S(2)}) collective-permute-start(bf16[256,640]{1,0:T(8,128)(2,1)S(1)} %bitcast.11), channel_id=1, source_target_pairs={{1,0},{2,1},{3,2},{4,3},{5,4},{6,5},{7,6},{8,7},{9,8},{10,9},{11,1... | collective-permute-start | bytes 983048 | tf_op jit(solution)/shard_map/ppermute | solution.py:330
  36.3 19.7 %collective-permute-start.11 = (bf16[128,640]{1,0:T(8,128)(2,1)S(1)}, bf16[128,640]{1,0:T(8,128)(2,1)S(1)}, u32[]{:S(2)}, u32[]{:S(2)}) collective-permute-start(bf16[128,640]{1,0:T(8,128)(2,1)S(1)} %collective-permute-done.10.z3_ref), channel_id=1, source_target_pairs={{0,3},{1,0},{2,1},{3,2},{4,7},{5,4},{6,5},{7,6},{8,11},{9,8},{10,9... | collective-permute-start | bytes 491528 | tf_op jit(solution)/shard_map/ppermute | solution.py:316
  51.3 15.9 %collective-permute-start.6 = (bf16[128,768]{1,0:T(8,128)(2,1)S(1)}, bf16[128,768]{1,0:T(8,128)(2,1)S(1)}, u32[]{:S(2)}, u32[]{:S(2)}) collective-permute-start(bf16[128,768]{1,0:T(8,128)(2,1)S(1)} %get-tuple-element.26), channel_id=1, source_target_pairs={{0,12},{4,0},{8,4},{12,8},{1,13},{5,1},{9,5},{13,9},{2,14},{6,2},{... | collective-permute-start | bytes 589832 | tf_op jit(solution)/shard_map/ppermute | solution.py:366
  51.4 17.5 %collective-permute-start.7 = (bf16[128,768]{1,0:T(8,128)(2,1)S(1)}, bf16[128,768]{1,0:T(8,128)(2,1)S(1)}, u32[]{:S(2)}, u32[]{:S(2)}) collective-permute-start(bf16[128,768]{1,0:T(8,128)(2,1)S(1)} %get-tuple-element.27), channel_id=1, source_target_pairs={{0,4},{4,8},{8,12},{12,0},{1,5},{5,9},{9,13},{13,1},{2,6},{6,10},{... | collective-permute-start | bytes 589832 | tf_op jit(solution)/shard_map/ppermute | solution.py:366
  56.0 14.5 %copy-start.6 = (bf16[640,640]{1,0:T(8,128)(2,1)S(1)}, bf16[640,640]{1,0:T(8,128)(2,1)}, u32[]{:S(2)}) copy-start(bf16[640,640]{1,0:T(8,128)(2,1)} %w_ref.5) | copy-start | bytes 2457604
  56.0 14.5 %copy-start.10 = (bf16[128,640]{1,0:T(8,128)(2,1)S(1)}, bf16[128,640]{1,0:T(8,128)(2,1)}, u32[]{:S(2)}) copy-start(bf16[128,640]{1,0:T(8,128)(2,1)} %constant.6.clone.spread_ref) | copy-start | bytes 491524
  56.0 14.5 %copy-start.11 = (bf16[640,128]{1,0:T(8,128)(2,1)S(1)}, bf16[640,128]{1,0:T(8,128)(2,1)}, u32[]{:S(2)}) copy-start(bf16[640,128]{1,0:T(8,128)(2,1)} %constant.7.clone.gather_ref) | copy-start | bytes 491524
  56.0 13.3 %collective-permute-start.8 = (bf16[128,768]{1,0:T(8,128)(2,1)S(1)}, bf16[128,768]{1,0:T(8,128)(2,1)S(1)}, u32[]{:S(2)}, u32[]{:S(2)}) collective-permute-start(bf16[128,768]{1,0:T(8,128)(2,1)S(1)} %get-tuple-element.28), channel_id=1, source_target_pairs={{0,8},{4,12},{8,0},{12,4},{1,9},{5,13},{9,1},{13,5},{2,10},{6,14},... | collective-permute-start | bytes 589832 | tf_op jit(solution)/shard_map/ppermute | solution.py:366
  67.2 7.5 %collective-permute-start.12 = (bf16[128,768]{1,0:T(8,128)(2,1)S(1)}, bf16[128,768]{1,0:T(8,128)(2,1)S(1)}, u32[]{:S(2)}, u32[]{:S(2)}) collective-permute-start(bf16[128,768]{1,0:T(8,128)(2,1)S(1)} %get-tuple-element.32), channel_id=1, source_target_pairs={{0,12},{4,0},{8,4},{12,8},{1,13},{5,1},{9,5},{13,9},{2,14},{6,2},{... | collective-permute-start | bytes 589832 | tf_op jit(solution)/shard_map/ppermute | solution.py:366
  68.9 9.4 %collective-permute-start.13 = (bf16[128,768]{1,0:T(8,128)(2,1)S(1)}, bf16[128,768]{1,0:T(8,128)(2,1)S(1)}, u32[]{:S(2)}, u32[]{:S(2)}) collective-permute-start(bf16[128,768]{1,0:T(8,128)(2,1)S(1)} %get-tuple-element.33), channel_id=1, source_target_pairs={{0,4},{4,8},{8,12},{12,0},{1,5},{5,9},{9,13},{13,1},{2,6},{6,10},{... | collective-permute-start | bytes 589832 | tf_op jit(solution)/shard_map/ppermute | solution.py:366
  69.3 9.0 %collective-permute-start.14 = (bf16[128,768]{1,0:T(8,128)(2,1)S(1)}, bf16[128,768]{1,0:T(8,128)(2,1)S(1)}, u32[]{:S(2)}, u32[]{:S(2)}) collective-permute-start(bf16[128,768]{1,0:T(8,128)(2,1)S(1)} %get-tuple-element.34), channel_id=1, source_target_pairs={{0,8},{4,12},{8,0},{12,4},{1,9},{5,13},{9,1},{13,5},{2,10},{6,14},... | collective-permute-start | bytes 589832 | tf_op jit(solution)/shard_map/ppermute | solution.py:366
  78.3 18.6 %copy-start.1 = (f32[2,640]{1,0:T(2,128)S(1)}, f32[2,640]{1,0:T(2,128)}, u32[]{:S(2)}) copy-start(f32[2,640]{1,0:T(2,128)} %shift_ref.1) | copy-start | bytes 15364
  78.3 18.6 %copy-start.4 = (f32[640]{0:T(1024)S(1)}, f32[640]{0:T(1024)}, u32[]{:S(2)}) copy-start(f32[640]{0:T(1024)} %bias_ref.6) | copy-start | bytes 7684
  79.3 22.8 %copy-start = (bf16[128,640]{1,0:T(8,128)(2,1)S(1)}, bf16[128,640]{1,0:T(8,128)(2,1)}, u32[]{:S(2)}) copy-start(bf16[128,640]{1,0:T(8,128)(2,1)} %constant.8.clone.scatter_ref) | copy-start | bytes 491524
  79.3 22.8 %copy-start.2 = (f32[640]{0:T(1024)S(1)}, f32[640]{0:T(1024)}, u32[]{:S(2)}) copy-start(f32[640]{0:T(1024)} %gain_ref.5) | copy-start | bytes 7684
  79.3 22.8 %copy-start.3 = (f32[640]{0:T(1024)S(1)}, f32[640]{0:T(1024)}, u32[]{:S(2)}) copy-start(f32[640]{0:T(1024)} %bias_ref.7) | copy-start | bytes 7684
  79.3 4.9 %collective-permute-start.15 = (f32[8,128]{1,0:T(8,128)S(1)}, f32[8,128]{1,0:T(8,128)S(1)}, u32[]{:S(2)}, u32[]{:S(2)}) collective-permute-start(f32[8,128]{1,0:T(8,128)S(1)} %get-tuple-element.37.refs_0_), channel_id=1, source_target_pairs={{0,4},{4,8},{8,12},{12,0},{1,5},{5,9},{9,13},{13,1},{2,6},{6,10},{... | collective-permute-start | bytes 12296 | tf_op jit(solution)/shard_map/ppermute | solution.py:395
  79.4 4.8 %collective-permute-start.16 = (f32[8,128]{1,0:T(8,128)S(1)}, f32[8,128]{1,0:T(8,128)S(1)}, u32[]{:S(2)}, u32[]{:S(2)}) collective-permute-start(f32[8,128]{1,0:T(8,128)S(1)} %get-tuple-element.37.refs_0_), channel_id=1, source_target_pairs={{0,12},{4,0},{8,4},{12,8},{1,13},{5,1},{9,5},{13,9},{2,14},{6,2},{... | collective-permute-start | bytes 12296 | tf_op jit(solution)/shard_map/ppermute | solution.py:395
  82.6 5.1 %collective-permute-start.17 = (f32[8,128]{1,0:T(8,128)S(1)}, f32[8,128]{1,0:T(8,128)S(1)}, u32[]{:S(2)}, u32[]{:S(2)}) collective-permute-start(f32[8,128]{1,0:T(8,128)S(1)} %get-tuple-element.37.refs_0_), channel_id=1, source_target_pairs={{0,8},{4,12},{8,0},{12,4},{1,9},{5,13},{9,1},{13,5},{2,10},{6,14},... | collective-permute-start | bytes 12296 | tf_op jit(solution)/shard_map/ppermute | solution.py:395
  87.8 11.0 %collective-permute-start.18 = (f32[8,128]{1,0:T(8,128)S(1)}, f32[8,128]{1,0:T(8,128)S(1)}, u32[]{:S(2)}, u32[]{:S(2)}) collective-permute-start(f32[8,128]{1,0:T(8,128)S(1)} %shard_map.160.s0_ref), channel_id=1, source_target_pairs={{0,1},{1,2},{2,3},{3,0},{4,5},{5,6},{6,7},{7,4},{8,9},{9,10},{10,1... | collective-permute-start | bytes 12296 | tf_op jit(solution)/shard_map/ppermute | solution.py:397
  91.6 7.2 %collective-permute-start.19 = (f32[8,128]{1,0:T(8,128)S(1)}, f32[8,128]{1,0:T(8,128)S(1)}, u32[]{:S(2)}, u32[]{:S(2)}) collective-permute-start(f32[8,128]{1,0:T(8,128)S(1)} %shard_map.160.s0_ref), channel_id=1, source_target_pairs={{0,3},{1,0},{2,1},{3,2},{4,7},{5,4},{6,5},{7,6},{8,11},{9,8},{10,9... | collective-permute-start | bytes 12296 | tf_op jit(solution)/shard_map/ppermute | solution.py:397
  94.6 7.5 %collective-permute-start.20 = (f32[8,128]{1,0:T(8,128)S(1)}, f32[8,128]{1,0:T(8,128)S(1)}, u32[]{:S(2)}, u32[]{:S(2)}) collective-permute-start(f32[8,128]{1,0:T(8,128)S(1)} %shard_map.160.s0_ref), channel_id=1, source_target_pairs={{0,2},{1,3},{2,0},{3,1},{4,6},{5,7},{6,4},{7,5},{8,10},{9,11},{10,... | collective-permute-start | bytes 12296 | tf_op jit(solution)/shard_map/ppermute | solution.py:397

commit v6 on v5

--- a/solution.py
+++ b/solution.py
@@ -53,14 +53,29 @@
     )
 
 
-def project(x, wk_ref, wv_ref, kv_scr, slot):
+def project(x, wk_ref, wv_ref):
     weights = jnp.concatenate([wk_ref[...], wv_ref[...]], axis=1)
-    kv_scr[slot] = jnp.dot(x, weights, preferred_element_type=F32).astype(BF16)
+    return jnp.dot(x, weights, preferred_element_type=F32).astype(BF16)
+
+
+def early_kernel(*refs):
+    fresh_ref, *stale_refs, wk_ref, wv_ref, out_ref, x_scr = refs
+    rows = stale_refs[0].shape[0]
+
+    @pl.when(pl.program_id(0) == 0)
+    def _():
+        for sample, ref in enumerate(stale_refs):
+            base = 2 * sample * rows
+            x_scr[base : base + rows, :] = fresh_ref[sample * rows : (sample + 1) * rows, :]
+            x_scr[base + rows : base + 2 * rows, :] = ref[...]
+
+    lanes = pl.ds(pl.multiple_of(pl.program_id(0) * 2 * LANES, LANES), 2 * LANES)
+    out_ref[:, lanes] = project(x_scr[...], wk_ref, wv_ref)
 
 
 def attend_kernel(
     q0_ref, q1_ref, q2_ref, q3_ref,
-    z1_ref, z2_ref, z3_ref, fresh_ref, own_ref,
+    z1_ref, z2_ref, z3_ref, early_ref,
     wk0_ref, wv0_ref, wk_ref, wv_ref, conv_ref,
     o0_ref, o1_ref, o2_ref, o3_ref,
     *refs, sample,
@@ -68,8 +83,7 @@
     x_scr, kv_scr, tile_scr = refs[-4:-1]
     pair = pl.program_id(0)
     fetch = pltpu.make_async_copy(conv_ref, refs[0], refs[-1]) if len(refs) > 4 else None
-    rows = z2_ref.shape[0]
-    channels = fresh_ref.shape[1]
+    rows, channels = z2_ref.shape
     part = slice(sample * rows, (sample + 1) * rows)
     out_refs = (o0_ref, o1_ref, o2_ref, o3_ref)
 
@@ -77,13 +91,16 @@
     def _():
         if fetch:
             fetch.start()
-        for index, ref in enumerate((z1_ref, z2_ref, z3_ref, fresh_ref, own_ref)):
-            x_scr[index * rows : (index + 1) * rows, :] = ref[part, :] if index == 3 else ref[...]
+        for index, ref in enumerate((z1_ref, z2_ref, z3_ref)):
+            x_scr[index * rows : (index + 1) * rows, :] = ref[...]
         tile_scr[...] = jnp.zeros_like(tile_scr)
-        project(x_scr[...], wk0_ref, wv0_ref, kv_scr, 0)
+        kv_scr[0] = project(x_scr[...], wk0_ref, wv0_ref)
 
     current = pair & 1
-    keys, values = kv_scr[current, :, :LANES], kv_scr[current, :, LANES:]
+    both_lanes = pl.ds(pl.multiple_of(pair * 2 * LANES, LANES), 2 * LANES)
+    early = early_ref[2 * sample * rows : 2 * (sample + 1) * rows, both_lanes]
+    pairs = jnp.concatenate([kv_scr[current], early], 0)
+    keys, values = pairs[:, :LANES], pairs[:, LANES:]
     low_all = lax.broadcasted_iota(jnp.int32, keys.shape, 1) < HEAD_DIM
     zero = jnp.zeros((), BF16)
     one = jnp.ones((), BF16)
@@ -103,14 +120,16 @@
         return jnp.concatenate([jnp.where(low_part, x, zero), jnp.where(low_part, zero, x)], 0)
 
     mine, others = halves(mine), halves(others)
-    shared = scores_of(jnp.concatenate([mine, others], 0), keys[common])
-    single = jnp.concatenate([scores_of(mine, keys[fresh]), scores_of(others, keys[own])], 0)
-    top = single
-    for index in range(3):
-        top = jnp.maximum(top, shared[:, index * LANES : (index + 1) * LANES])
-    top = jnp.max(top, -1, keepdims=True)
-    shared = jnp.exp(shared - top).astype(BF16)
-    single = jnp.exp(single - top).astype(BF16)
+    scores = jnp.concatenate(
+        [
+            scores_of(mine, keys[: 4 * rows]),
+            scores_of(others, jnp.concatenate([keys[common], keys[own]], 0)),
+        ],
+        0,
+    )
+    top = jnp.max(scores, -1, keepdims=True)
+    scores = jnp.exp(scores - top).astype(BF16)
+    shared, single = scores[:, : 3 * rows], scores[:, 3 * rows :]
 
     def paired(x):
         return (
@@ -153,7 +172,7 @@
         tile = jnp.where(slot == pair + piece * PIECES, rounded, tile)
         rest = rest - rounded
     tile_scr[...] = tile
-    project(x_scr[...], wk_ref, wv_ref, kv_scr, 1 - current)
+    kv_scr[1 - current] = project(x_scr[...], wk_ref, wv_ref)
 
     @pl.when(pair == pl.num_programs(0) - 1)
     def _():
@@ -325,6 +344,20 @@
         flops=6 * 10 ** 9,
     )
     all_queries = [queries] + [lax.ppermute(queries, "y", ring(by, y_count)) for by in shifts]
+    early = call(
+        early_kernel, pltpu.VMEM((2 * every, 2 * channels), BF16),
+        fresh, *stale, w_qkv, w_qkv,
+        grid=(pair_count,),
+        in_specs=[VMEM] * (1 + samples)
+        + [
+            pl.BlockSpec((channels, LANES), lambda p: (0, pair_count + p)),
+            pl.BlockSpec((channels, LANES), lambda p: (0, 2 * pair_count + p)),
+        ],
+        out_specs=VMEM,
+        scratch_shapes=[pltpu.VMEM((2 * every, channels), BF16)],
+        chip=range(1 + samples),
+        flops=6 * 10 ** 9,
+    )
     conv_rows = stale_conv_in.reshape(every, channels)
     above = lax.ppermute(conv_rows, ("y", "z"), [(i, i + 1) for i in range(count - 1)])
     below = lax.ppermute(conv_rows, ("y", "z"), [(i + 1, i) for i in range(count - 1)])
@@ -339,10 +372,10 @@
         extra = [pltpu.VMEM(conv_weight.shape, BF16)] * (s == samples - 1)
         outs = call(
             functools.partial(attend_kernel, sample=s), [ext] * 4 + extra,
-            *all_queries, *along[s], fresh, stale[s],
+            *all_queries, *along[s], early,
             w_qkv, w_qkv, w_qkv, w_qkv, conv_weight,
             grid=(pair_count,),
-            in_specs=[VMEM] * 9
+            in_specs=[VMEM] * 8
             + [
                 pl.BlockSpec((channels, LANES), lambda p: (0, pair_count)),
                 pl.BlockSpec((channels, LANES), lambda p: (0, 2 * pair_count)),
@@ -352,14 +385,14 @@
             ],
             out_specs=[VMEM] * (4 + len(extra)),
             scratch_shapes=[
-                pltpu.VMEM((5 * tokens, channels), BF16),
-                pltpu.VMEM((2, 5 * tokens, 2 * LANES), BF16),
+                pltpu.VMEM((3 * tokens, channels), BF16),
+                pltpu.VMEM((2, 3 * tokens, 2 * LANES), BF16),
                 pltpu.VMEM((4 * tokens, LANES), F32),
                 pltpu.SemaphoreType.DMA,
             ],
             flops=6 * 10 ** 9,
-            chip=range(9),
-            slow=(13,),
+            chip=range(8),
+            slow=(12,),
         )
         back.append(
             [outs[0]]

time: 104 us -> 102 us (0.981)
  the two profiles are of different devices: /device:TPU:6 before, /device:TPU:2 now
where the time goes in v6:
time: 102 us; the launch traced here: 101 us
  starting transfers between devices  49.7 us (49%)
  waiting for transfers between devices  26.6 us (26%)
  Pallas kernels  24.9 us (24%)
    pallas_call x10, Pallas kernels, call(): pl.pallas_call(kernel, out_shape=out_shape, compiler_params=pltpu.Compile...  24.9 us
    ppermute x4, starting transfers between devices, shards(): up, down = (lax.ppermute(one, 'z', ring(by, z_count)) for by in (1, 3))  14.3 us
    ppermute x6, waiting for transfers between devices, shards(): lax.ppermute(one, 'y', ring(-by, y_count))  8.9 us
    ppermute x6, starting transfers between devices, shards(): lax.ppermute(one, 'y', ring(-by, y_count))  8.75 us
    ppermute x1, waiting for transfers between devices, shards(): lax.ppermute(down, 'z', ring(3, z_count))  8.09 us
    ppermute x3, starting transfers between devices, shards(): lax.ppermute(stat, 'z', ring(by, z_count))  6.6 us
    ppermute x3, starting transfers between devices, shards(): lax.ppermute(queries, 'y', ring(by, y_count))  5.3 us
    ppermute x3, waiting for transfers between devices, shards(): lax.ppermute(stat, 'y', ring(by, y_count))  5.06 us
  transfers between devices with their start and end apart: 23, of which 7 were waited for; matrix products, arithmetic and copies ran while one was open for 0% of the time, Pallas kernels for 21%

profile of v6, /device:TPU:2, one launch (start us, length us, event | category | flops | bytes accessed | tf_op | source)
XLA Modules:
  0.0 101.4 jit_solution(6807040834329936839)
XLA Ops:
  0.0 0.0 copy-start.9
  0.0 1.4 %shard_map.155 = (bf16[128,640]{1,0:T(8,128)(2,1)S(1)}, bf16[128,640]{1,0:T(8,128)(2,1)S(1)}) custom-call(bf16[256,640]{1,0:T(8,128)(2,1)} %bitcast.9, f32[640]{0:T(1024)} %gain_ref.4, f32[640]{0:T(1024)} %bias_ref.5), custom_call_target="tpu_custom_call" | custom-call | flops 6000000000 | bytes 1000000 | tf_op jit(solution)/shard_map/pallas_call | solution.py:297
  1.4 3.3 %collective-permute-start.3 = (bf16[128,640]{1,0:T(8,128)(2,1)S(1)}, bf16[128,640]{1,0:T(8,128)(2,1)S(1)}, u32[]{:S(2)}, u32[]{:S(2)}) collective-permute-start(bf16[128,640]{1,0:T(8,128)(2,1)S(1)} %get-tuple-element.23.refs_1_), channel_id=1, source_target_pairs={{0,1},{1,2},{2,3},{3,0},{4,5},{5,6},{6,7},{7,4},{8,9},{9,10},{10,1... | collective-permute-start | bytes 491528 | tf_op jit(solution)/shard_map/ppermute | solution.py:334
  4.8 3.1 %collective-permute-start.5 = (bf16[128,640]{1,0:T(8,128)(2,1)S(1)}, bf16[128,640]{1,0:T(8,128)(2,1)S(1)}, u32[]{:S(2)}, u32[]{:S(2)}) collective-permute-start(bf16[128,640]{1,0:T(8,128)(2,1)S(1)} %get-tuple-element.23.refs_1_), channel_id=1, source_target_pairs={{0,3},{1,0},{2,1},{3,2},{4,7},{5,4},{6,5},{7,6},{8,11},{9,8},{10,9... | collective-permute-start | bytes 491528 | tf_op jit(solution)/shard_map/ppermute | solution.py:334
  7.9 0.0 copy-done.5
  7.9 0.0 copy-done.7
  7.9 0.0 copy-done.8
  7.9 0.0 copy-done.9
  7.9 0.7 shard_map.154
  8.6 1.7 %collective-permute-start = (bf16[256,640]{1,0:T(8,128)(2,1)S(1)}, bf16[256,640]{1,0:T(8,128)(2,1)S(1)}, u32[]{:S(2)}, u32[]{:S(2)}) collective-permute-start(bf16[256,640]{1,0:T(8,128)(2,1)S(1)} %get-tuple-element.22.q0_ref), channel_id=1, source_target_pairs={{0,4},{4,8},{8,12},{12,0},{1,5},{5,9},{9,13},{13,1},{2,6},{6,10},{... | collective-permute-start | bytes 983048 | tf_op jit(solution)/shard_map/ppermute | solution.py:346
  10.3 1.7 %collective-permute-start.1 = (bf16[256,640]{1,0:T(8,128)(2,1)S(1)}, bf16[256,640]{1,0:T(8,128)(2,1)S(1)}, u32[]{:S(2)}, u32[]{:S(2)}) collective-permute-start(bf16[256,640]{1,0:T(8,128)(2,1)S(1)} %get-tuple-element.22.q0_ref), channel_id=1, source_target_pairs={{0,12},{4,0},{8,4},{12,8},{1,13},{5,1},{9,5},{13,9},{2,14},{6,2},{... | collective-permute-start | bytes 983048 | tf_op jit(solution)/shard_map/ppermute | solution.py:346
  12.0 2.0 %collective-permute-start.2 = (bf16[256,640]{1,0:T(8,128)(2,1)S(1)}, bf16[256,640]{1,0:T(8,128)(2,1)S(1)}, u32[]{:S(2)}, u32[]{:S(2)}) collective-permute-start(bf16[256,640]{1,0:T(8,128)(2,1)S(1)} %get-tuple-element.22.q0_ref), channel_id=1, source_target_pairs={{0,8},{4,12},{8,0},{12,4},{1,9},{5,13},{9,1},{13,5},{2,10},{6,14},... | collective-permute-start | bytes 983048 | tf_op jit(solution)/shard_map/ppermute | solution.py:346
  13.9 0.0 collective-permute-done.3.z1_ref
  13.9 4.3 %collective-permute-start.10 = (bf16[128,640]{1,0:T(8,128)(2,1)S(1)}, bf16[128,640]{1,0:T(8,128)(2,1)S(1)}, u32[]{:S(2)}, u32[]{:S(2)}) collective-permute-start(bf16[128,640]{1,0:T(8,128)(2,1)S(1)} %get-tuple-element.25.refs_2_), channel_id=1, source_target_pairs={{0,3},{1,0},{2,1},{3,2},{4,7},{5,4},{6,5},{7,6},{8,11},{9,8},{10,9... | collective-permute-start | bytes 491528 | tf_op jit(solution)/shard_map/ppermute | solution.py:334
  18.2 0.0 collective-permute-done.5.z3_ref
  18.2 2.3 %collective-permute-start.4 = (bf16[128,640]{1,0:T(8,128)(2,1)S(1)}, bf16[128,640]{1,0:T(8,128)(2,1)S(1)}, u32[]{:S(2)}, u32[]{:S(2)}) collective-permute-start(bf16[128,640]{1,0:T(8,128)(2,1)S(1)} %collective-permute-done.3.z1_ref), channel_id=1, source_target_pairs={{0,1},{1,2},{2,3},{3,0},{4,5},{5,6},{6,7},{7,4},{8,9},{9,10},{10,1... | collective-permute-start | bytes 491528 | tf_op jit(solution)/shard_map/ppermute | solution.py:335
  20.5 2.3 %shard_map.156.early_ref = bf16[512,1280]{1,0:T(8,128)(2,1)S(1)} custom-call(bf16[256,640]{1,0:T(8,128)(2,1)S(1)} %get-tuple-element.24.refs_0_, bf16[128,640]{1,0:T(8,128)(2,1)S(1)} %get-tuple-element.23.refs_1_, bf16[128,640]{1,0:T(8,128)(2,1)S(1)} %get-tuple-element.25.refs_2_, bf16[640,1920]{1,0:T(8,128)(2,1)S(1)} %copy-done.5, ...), custom_call_target="tpu_custom_call" | custom-call | flops 6000000000 | bytes 1000000 | tf_op jit(solution)/shard_map/pallas_call | solution.py:297
  22.9 1.4 %collective-permute-done.10.z3_ref = bf16[128,640]{1,0:T(8,128)(2,1)S(1)} collective-permute-done((bf16[128,640]{1,0:T(8,128)(2,1)S(1)}, bf16[128,640]{1,0:T(8,128)(2,1)S(1)}, u32[]{:S(2)}, u32[]{:S(2)}) %collective-permute-start.10) | collective-permute-done | bytes 163872 | tf_op jit(solution)/shard_map/ppermute | solution.py:334
  24.2 3.6 %collective-permute-start.9 = (bf16[128,640]{1,0:T(8,128)(2,1)S(1)}, bf16[128,640]{1,0:T(8,128)(2,1)S(1)}, u32[]{:S(2)}, u32[]{:S(2)}) collective-permute-start(bf16[128,640]{1,0:T(8,128)(2,1)S(1)} %get-tuple-element.25.refs_2_), channel_id=1, source_target_pairs={{0,1},{1,2},{2,3},{3,0},{4,5},{5,6},{6,7},{7,4},{8,9},{9,10},{10,1... | collective-permute-start | bytes 491528 | tf_op jit(solution)/shard_map/ppermute | solution.py:334
  27.8 0.0 collective-permute-done.q1_ref
  27.8 0.0 copy-done.12
  27.8 4.8 %collective-permute-start.21 = (bf16[256,640]{1,0:T(8,128)(2,1)S(1)}, bf16[256,640]{1,0:T(8,128)(2,1)S(1)}, u32[]{:S(2)}, u32[]{:S(2)}) collective-permute-start(bf16[256,640]{1,0:T(8,128)(2,1)S(1)} %bitcast.10), channel_id=1, source_target_pairs={{0,1},{1,2},{2,3},{3,4},{4,5},{5,6},{6,7},{7,8},{8,9},{9,10},{10,1... | collective-permute-start | bytes 983048 | tf_op jit(solution)/shard_map/ppermute | solution.py:362
  32.6 0.0 collective-permute-done.1.q2_ref
  32.7 1.3 %collective-permute-start.22 = (bf16[256,640]{1,0:T(8,128)(2,1)S(1)}, bf16[256,640]{1,0:T(8,128)(2,1)S(1)}, u32[]{:S(2)}, u32[]{:S(2)}) collective-permute-start(bf16[256,640]{1,0:T(8,128)(2,1)S(1)} %bitcast.11), channel_id=1, source_target_pairs={{1,0},{2,1},{3,2},{4,3},{5,4},{6,5},{7,6},{8,7},{9,8},{10,9},{11,1... | collective-permute-start | bytes 983048 | tf_op jit(solution)/shard_map/ppermute | solution.py:363
  34.0 0.0 collective-permute-done.2.q3_ref
  34.0 2.9 %collective-permute-start.11 = (bf16[128,640]{1,0:T(8,128)(2,1)S(1)}, bf16[128,640]{1,0:T(8,128)(2,1)S(1)}, u32[]{:S(2)}, u32[]{:S(2)}) collective-permute-start(bf16[128,640]{1,0:T(8,128)(2,1)S(1)} %collective-permute-done.10.z3_ref), channel_id=1, source_target_pairs={{0,3},{1,0},{2,1},{3,2},{4,7},{5,4},{6,5},{7,6},{8,11},{9,8},{10,9... | collective-permute-start | bytes 491528 | tf_op jit(solution)/shard_map/ppermute | solution.py:335
  36.9 0.0 collective-permute-done.4.z2_ref
  36.9 7.3 %shard_map.157 = (bf16[128,768]{1,0:T(8,128)(2,1)S(1)}, bf16[128,768]{1,0:T(8,128)(2,1)S(1)}, bf16[128,768]{1,0:T(8,128)(2,1)S(1)}, bf16[128,768]{1,0:T(8,128)(2,1)S(1)}) custom-call(bf16[256,640]{1,0:T(8,128)(2,1)S(1)} %get-tuple-element.22.q0_ref, bf16[256,640]{1,0:T(8,128)(2,1)S(1)} %collective-permute-done.q1_ref, ...), custom_call_target="tpu_custom_call" | custom-call | flops 6000000000 | bytes 1000000 | tf_op jit(solution)/shard_map/pallas_call | solution.py:297
  44.2 3.0 %collective-permute-start.6 = (bf16[128,768]{1,0:T(8,128)(2,1)S(1)}, bf16[128,768]{1,0:T(8,128)(2,1)S(1)}, u32[]{:S(2)}, u32[]{:S(2)}) collective-permute-start(bf16[128,768]{1,0:T(8,128)(2,1)S(1)} %get-tuple-element.27), channel_id=1, source_target_pairs={{0,12},{4,0},{8,4},{12,8},{1,13},{5,1},{9,5},{13,9},{2,14},{6,2},{... | collective-permute-start | bytes 589832 | tf_op jit(solution)/shard_map/ppermute | solution.py:399
  47.2 0.0 collective-permute-done.9.z1_ref
  47.2 0.0 collective-permute-start.7
  47.2 8.1 %collective-permute-done.11.z2_ref = bf16[128,640]{1,0:T(8,128)(2,1)S(1)} collective-permute-done((bf16[128,640]{1,0:T(8,128)(2,1)S(1)}, bf16[128,640]{1,0:T(8,128)(2,1)S(1)}, u32[]{:S(2)}, u32[]{:S(2)}) %collective-permute-start.11) | collective-permute-done | bytes 163872 | tf_op jit(solution)/shard_map/ppermute | solution.py:335
  55.3 2.8 %collective-permute-start.8 = (bf16[128,768]{1,0:T(8,128)(2,1)S(1)}, bf16[128,768]{1,0:T(8,128)(2,1)S(1)}, u32[]{:S(2)}, u32[]{:S(2)}) collective-permute-start(bf16[128,768]{1,0:T(8,128)(2,1)S(1)} %get-tuple-element.29), channel_id=1, source_target_pairs={{0,8},{4,12},{8,0},{12,4},{1,9},{5,13},{9,1},{13,5},{2,10},{6,14},... | collective-permute-start | bytes 589832 | tf_op jit(solution)/shard_map/ppermute | solution.py:399
  58.1 7.3 %shard_map.159 = (bf16[128,768]{1,0:T(8,128)(2,1)S(1)}, bf16[128,768]{1,0:T(8,128)(2,1)S(1)}, bf16[128,768]{1,0:T(8,128)(2,1)S(1)}, bf16[128,768]{1,0:T(8,128)(2,1)S(1)}, bf16[3,3,640,640]{3,2,1,0:T(8,128)(2,1)S(1)}) custom-call(bf16[256,640]{1,0:T(8,128)(2,1)S(1)} %get-tuple-element.22.q0_ref, bf16[256,640]{1,0:T(8,128)(2,1)S(1)} %collective-permute-done.q1_ref, ...), custom_call_target="tpu_custom_call" | custom-call | flops 6000000000 | bytes 1000000 | tf_op jit(solution)/shard_map/pallas_call | solution.py:297
  65.4 0.0 collective-permute-done.6.o1_ref
  65.4 1.1 %collective-permute-start.12 = (bf16[128,768]{1,0:T(8,128)(2,1)S(1)}, bf16[128,768]{1,0:T(8,128)(2,1)S(1)}, u32[]{:S(2)}, u32[]{:S(2)}) collective-permute-start(bf16[128,768]{1,0:T(8,128)(2,1)S(1)} %get-tuple-element.32), channel_id=1, source_target_pairs={{0,12},{4,0},{8,4},{12,8},{1,13},{5,1},{9,5},{13,9},{2,14},{6,2},{... | collective-permute-start | bytes 589832 | tf_op jit(solution)/shard_map/ppermute | solution.py:399
  66.5 0.0 collective-permute-done.7.o2_ref
  66.5 1.0 collective-permute-start.13
  67.5 0.0 collective-permute-done.8.o3_ref
  67.5 0.8 collective-permute-start.14
  68.3 0.0 copy-done.6
  68.3 0.0 copy-done.10
  68.3 1.0 shard_map.158
  69.3 3.9 %collective-permute-done.12.o1_ref = bf16[128,768]{1,0:T(8,128)(2,1)S(1)} collective-permute-done((bf16[128,768]{1,0:T(8,128)(2,1)S(1)}, bf16[128,768]{1,0:T(8,128)(2,1)S(1)}, u32[]{:S(2)}, u32[]{:S(2)}) %collective-permute-start.12) | collective-permute-done | bytes 196640 | tf_op jit(solution)/shard_map/ppermute | solution.py:399
  73.3 5.0 %collective-permute-done.13.o2_ref = bf16[128,768]{1,0:T(8,128)(2,1)S(1)} collective-permute-done((bf16[128,768]{1,0:T(8,128)(2,1)S(1)}, bf16[128,768]{1,0:T(8,128)(2,1)S(1)}, u32[]{:S(2)}, u32[]{:S(2)}) %collective-permute-start.13) | collective-permute-done | bytes 196640 | tf_op jit(solution)/shard_map/ppermute | solution.py:399
  78.2 0.0 collective-permute-done.14.o3_ref
  78.2 1.0 shard_map.160
  79.3 0.1 collective-permute-start.15
  79.4 3.2 %collective-permute-start.16 = (f32[8,128]{1,0:T(8,128)S(1)}, f32[8,128]{1,0:T(8,128)S(1)}, u32[]{:S(2)}, u32[]{:S(2)}) collective-permute-start(f32[8,128]{1,0:T(8,128)S(1)} %get-tuple-element.37.refs_0_), channel_id=1, source_target_pairs={{0,12},{4,0},{8,4},{12,8},{1,13},{5,1},{9,5},{13,9},{2,14},{6,2},{... | collective-permute-start | bytes 12296 | tf_op jit(solution)/shard_map/ppermute | solution.py:428
  82.6 0.1 collective-permute-start.17
  82.6 1.5 %collective-permute-done.15.refs_1_ = f32[8,128]{1,0:T(8,128)S(1)} collective-permute-done((f32[8,128]{1,0:T(8,128)S(1)}, f32[8,128]{1,0:T(8,128)S(1)}, u32[]{:S(2)}, u32[]{:S(2)}) %collective-permute-start.15) | collective-permute-done | bytes 4128 | tf_op jit(solution)/shard_map/ppermute | solution.py:428
  84.2 0.0 collective-permute-done.16.refs_2_
  84.2 3.5 %collective-permute-done.17.refs_3_ = f32[8,128]{1,0:T(8,128)S(1)} collective-permute-done((f32[8,128]{1,0:T(8,128)S(1)}, f32[8,128]{1,0:T(8,128)S(1)}, u32[]{:S(2)}, u32[]{:S(2)}) %collective-permute-start.17) | collective-permute-done | bytes 4128 | tf_op jit(solution)/shard_map/ppermute | solution.py:428
  87.7 2.5 %collective-permute-start.18 = (f32[8,128]{1,0:T(8,128)S(1)}, f32[8,128]{1,0:T(8,128)S(1)}, u32[]{:S(2)}, u32[]{:S(2)}) collective-permute-start(f32[8,128]{1,0:T(8,128)S(1)} %shard_map.161.s0_ref), channel_id=1, source_target_pairs={{0,1},{1,2},{2,3},{3,0},{4,5},{5,6},{6,7},{7,4},{8,9},{9,10},{10,1... | collective-permute-start | bytes 12296 | tf_op jit(solution)/shard_map/ppermute | solution.py:430
  90.2 1.6 %collective-permute-start.19 = (f32[8,128]{1,0:T(8,128)S(1)}, f32[8,128]{1,0:T(8,128)S(1)}, u32[]{:S(2)}, u32[]{:S(2)}) collective-permute-start(f32[8,128]{1,0:T(8,128)S(1)} %shard_map.161.s0_ref), channel_id=1, source_target_pairs={{0,3},{1,0},{2,1},{3,2},{4,7},{5,4},{6,5},{7,6},{8,11},{9,8},{10,9... | collective-permute-start | bytes 12296 | tf_op jit(solution)/shard_map/ppermute | solution.py:430
  91.8 2.5 %collective-permute-start.20 = (f32[8,128]{1,0:T(8,128)S(1)}, f32[8,128]{1,0:T(8,128)S(1)}, u32[]{:S(2)}, u32[]{:S(2)}) collective-permute-start(f32[8,128]{1,0:T(8,128)S(1)} %shard_map.161.s0_ref), channel_id=1, source_target_pairs={{0,2},{1,3},{2,0},{3,1},{4,6},{5,7},{6,4},{7,5},{8,10},{9,11},{10,... | collective-permute-start | bytes 12296 | tf_op jit(solution)/shard_map/ppermute | solution.py:430
  94.3 0.0 collective-permute-done.21.above_ref
  94.3 0.0 collective-permute-done.22.below_ref
  94.3 0.0 copy-done.1
  94.3 1.8 %shard_map.162.rim_ref = f32[256,640]{1,0:T(8,128)S(1)} custom-call(bf16[256,640]{1,0:T(8,128)(2,1)S(1)} %collective-permute-done.21.above_ref, bf16[256,640]{1,0:T(8,128)(2,1)S(1)} %collective-permute-done.22.below_ref, bf16[3,3,640,640]{3,2,1,0:T(8,128)(2,1)S(1)} %get-tuple-element.38.w_ref, f32[640]{0:T(1024)S(1)} %copy-done.4, f32[2,640]{1,0:T(2,128)S(1)} %copy-done.1), custom_call_target="tpu_custom_call" | custom-call | flops 1258291200 | bytes 1000000 | tf_op jit(solution)/shard_map/pallas_call | solution.py:297
  96.2 0.0 collective-permute-done.18.s1_ref
  96.2 0.0 collective-permute-done.19.s2_ref
  96.2 3.2 %collective-permute-done.20.s3_ref = f32[8,128]{1,0:T(8,128)S(1)} collective-permute-done((f32[8,128]{1,0:T(8,128)S(1)}, f32[8,128]{1,0:T(8,128)S(1)}, u32[]{:S(2)}, u32[]{:S(2)}) %collective-permute-start.20) | collective-permute-done | bytes 4128 | tf_op jit(solution)/shard_map/ppermute | solution.py:430
  99.4 2.1 %shard_map.163 = bf16[256,640]{1,0:T(8,128)(2,1)} custom-call(bf16[128,640]{1,0:T(8,128)(2,1)S(1)} %get-tuple-element.30.res0_ref, bf16[128,640]{1,0:T(8,128)(2,1)S(1)} %get-tuple-element.36.res1_ref, f32[8,128]{1,0:T(8,128)S(1)} %shard_map.161.s0_ref, f32[8,128]{1,0:T(8,128)S(1)} %collective-permute-done.18.s1_ref, ...), custom_call_target="tpu_custom_call" | custom-call | flops 629145600 | bytes 1000000 | tf_op jit(solution)/shard_map/pallas_call | solution.py:297
  (18 shorter events, 0.0 us)
Async XLA Ops:
  0.0 7.9 %copy-start.5 = (bf16[640,1920]{1,0:T(8,128)(2,1)S(1)}, bf16[640,1920]{1,0:T(8,128)(2,1)}, u32[]{:S(2)}) copy-start(bf16[640,1920]{1,0:T(8,128)(2,1)} %wv_ref.3) | copy-start | bytes 7372804
  0.0 7.9 %copy-start.7 = (bf16[2,1,128,640]{3,2,1,0:T(8,128)(2,1)S(1)}, bf16[2,1,128,640]{3,2,1,0:T(8,128)(2,1)}, u32[]{:S(2)}) copy-start(bf16[2,1,128,640]{3,2,1,0:T(8,128)(2,1)} %param.16) | copy-start | bytes 983044
  0.0 7.9 %copy-start.8 = (f32[640]{0:T(1024)S(1)}, f32[640]{0:T(1024)}, u32[]{:S(2)}) copy-start(f32[640]{0:T(1024)} %gain_ref.4) | copy-start | bytes 7684
  0.0 7.9 %copy-start.9 = (f32[640]{0:T(1024)S(1)}, f32[640]{0:T(1024)}, u32[]{:S(2)}) copy-start(f32[640]{0:T(1024)} %bias_ref.5) | copy-start | bytes 7684
  1.4 12.5 %collective-permute-start.3 = (bf16[128,640]{1,0:T(8,128)(2,1)S(1)}, bf16[128,640]{1,0:T(8,128)(2,1)S(1)}, u32[]{:S(2)}, u32[]{:S(2)}) collective-permute-start(bf16[128,640]{1,0:T(8,128)(2,1)S(1)} %get-tuple-element.23.refs_1_), channel_id=1, source_target_pairs={{0,1},{1,2},{2,3},{3,0},{4,5},{5,6},{6,7},{7,4},{8,9},{9,10},{10,1... | collective-permute-start | bytes 491528 | tf_op jit(solution)/shard_map/ppermute | solution.py:334
  4.8 13.4 %collective-permute-start.5 = (bf16[128,640]{1,0:T(8,128)(2,1)S(1)}, bf16[128,640]{1,0:T(8,128)(2,1)S(1)}, u32[]{:S(2)}, u32[]{:S(2)}) collective-permute-start(bf16[128,640]{1,0:T(8,128)(2,1)S(1)} %get-tuple-element.23.refs_1_), channel_id=1, source_target_pairs={{0,3},{1,0},{2,1},{3,2},{4,7},{5,4},{6,5},{7,6},{8,11},{9,8},{10,9... | collective-permute-start | bytes 491528 | tf_op jit(solution)/shard_map/ppermute | solution.py:334
  8.6 19.2 %collective-permute-start = (bf16[256,640]{1,0:T(8,128)(2,1)S(1)}, bf16[256,640]{1,0:T(8,128)(2,1)S(1)}, u32[]{:S(2)}, u32[]{:S(2)}) collective-permute-start(bf16[256,640]{1,0:T(8,128)(2,1)S(1)} %get-tuple-element.22.q0_ref), channel_id=1, source_target_pairs={{0,4},{4,8},{8,12},{12,0},{1,5},{5,9},{9,13},{13,1},{2,6},{6,10},{... | collective-permute-start | bytes 983048 | tf_op jit(solution)/shard_map/ppermute | solution.py:346
  10.3 22.4 %collective-permute-start.1 = (bf16[256,640]{1,0:T(8,128)(2,1)S(1)}, bf16[256,640]{1,0:T(8,128)(2,1)S(1)}, u32[]{:S(2)}, u32[]{:S(2)}) collective-permute-start(bf16[256,640]{1,0:T(8,128)(2,1)S(1)} %get-tuple-element.22.q0_ref), channel_id=1, source_target_pairs={{0,12},{4,0},{8,4},{12,8},{1,13},{5,1},{9,5},{13,9},{2,14},{6,2},{... | collective-permute-start | bytes 983048 | tf_op jit(solution)/shard_map/ppermute | solution.py:346
  12.0 22.0 %collective-permute-start.2 = (bf16[256,640]{1,0:T(8,128)(2,1)S(1)}, bf16[256,640]{1,0:T(8,128)(2,1)S(1)}, u32[]{:S(2)}, u32[]{:S(2)}) collective-permute-start(bf16[256,640]{1,0:T(8,128)(2,1)S(1)} %get-tuple-element.22.q0_ref), channel_id=1, source_target_pairs={{0,8},{4,12},{8,0},{12,4},{1,9},{5,13},{9,1},{13,5},{2,10},{6,14},... | collective-permute-start | bytes 983048 | tf_op jit(solution)/shard_map/ppermute | solution.py:346
  13.9 10.3 %collective-permute-start.10 = (bf16[128,640]{1,0:T(8,128)(2,1)S(1)}, bf16[128,640]{1,0:T(8,128)(2,1)S(1)}, u32[]{:S(2)}, u32[]{:S(2)}) collective-permute-start(bf16[128,640]{1,0:T(8,128)(2,1)S(1)} %get-tuple-element.25.refs_2_), channel_id=1, source_target_pairs={{0,3},{1,0},{2,1},{3,2},{4,7},{5,4},{6,5},{7,6},{8,11},{9,8},{10,9... | collective-permute-start | bytes 491528 | tf_op jit(solution)/shard_map/ppermute | solution.py:334
  18.2 18.7 %collective-permute-start.4 = (bf16[128,640]{1,0:T(8,128)(2,1)S(1)}, bf16[128,640]{1,0:T(8,128)(2,1)S(1)}, u32[]{:S(2)}, u32[]{:S(2)}) collective-permute-start(bf16[128,640]{1,0:T(8,128)(2,1)S(1)} %collective-permute-done.3.z1_ref), channel_id=1, source_target_pairs={{0,1},{1,2},{2,3},{3,0},{4,5},{5,6},{6,7},{7,4},{8,9},{9,10},{10,1... | collective-permute-start | bytes 491528 | tf_op jit(solution)/shard_map/ppermute | solution.py:335
  20.5 7.3 %copy-start.12 = (bf16[2,1,128,640]{3,2,1,0:T(8,128)(2,1)S(1)}, bf16[2,1,128,640]{3,2,1,0:T(8,128)(2,1)}, u32[]{:S(2)}) copy-start(bf16[2,1,128,640]{3,2,1,0:T(8,128)(2,1)} %param.18) | copy-start | bytes 983044
  24.2 23.0 %collective-permute-start.9 = (bf16[128,640]{1,0:T(8,128)(2,1)S(1)}, bf16[128,640]{1,0:T(8,128)(2,1)S(1)}, u32[]{:S(2)}, u32[]{:S(2)}) collective-permute-start(bf16[128,640]{1,0:T(8,128)(2,1)S(1)} %get-tuple-element.25.refs_2_), channel_id=1, source_target_pairs={{0,1},{1,2},{2,3},{3,0},{4,5},{5,6},{6,7},{7,4},{8,9},{9,10},{10,1... | collective-permute-start | bytes 491528 | tf_op jit(solution)/shard_map/ppermute | solution.py:334
  27.8 66.5 %collective-permute-start.21 = (bf16[256,640]{1,0:T(8,128)(2,1)S(1)}, bf16[256,640]{1,0:T(8,128)(2,1)S(1)}, u32[]{:S(2)}, u32[]{:S(2)}) collective-permute-start(bf16[256,640]{1,0:T(8,128)(2,1)S(1)} %bitcast.10), channel_id=1, source_target_pairs={{0,1},{1,2},{2,3},{3,4},{4,5},{5,6},{6,7},{7,8},{8,9},{9,10},{10,1... | collective-permute-start | bytes 983048 | tf_op jit(solution)/shard_map/ppermute | solution.py:362
  32.7 61.6 %collective-permute-start.22 = (bf16[256,640]{1,0:T(8,128)(2,1)S(1)}, bf16[256,640]{1,0:T(8,128)(2,1)S(1)}, u32[]{:S(2)}, u32[]{:S(2)}) collective-permute-start(bf16[256,640]{1,0:T(8,128)(2,1)S(1)} %bitcast.11), channel_id=1, source_target_pairs={{1,0},{2,1},{3,2},{4,3},{5,4},{6,5},{7,6},{8,7},{9,8},{10,9},{11,1... | collective-permute-start | bytes 983048 | tf_op jit(solution)/shard_map/ppermute | solution.py:363
  34.0 21.3 %collective-permute-start.11 = (bf16[128,640]{1,0:T(8,128)(2,1)S(1)}, bf16[128,640]{1,0:T(8,128)(2,1)S(1)}, u32[]{:S(2)}, u32[]{:S(2)}) collective-permute-start(bf16[128,640]{1,0:T(8,128)(2,1)S(1)} %collective-permute-done.10.z3_ref), channel_id=1, source_target_pairs={{0,3},{1,0},{2,1},{3,2},{4,7},{5,4},{6,5},{7,6},{8,11},{9,8},{10,9... | collective-permute-start | bytes 491528 | tf_op jit(solution)/shard_map/ppermute | solution.py:335
  44.2 21.2 %collective-permute-start.6 = (bf16[128,768]{1,0:T(8,128)(2,1)S(1)}, bf16[128,768]{1,0:T(8,128)(2,1)S(1)}, u32[]{:S(2)}, u32[]{:S(2)}) collective-permute-start(bf16[128,768]{1,0:T(8,128)(2,1)S(1)} %get-tuple-element.27), channel_id=1, source_target_pairs={{0,12},{4,0},{8,4},{12,8},{1,13},{5,1},{9,5},{13,9},{2,14},{6,2},{... | collective-permute-start | bytes 589832 | tf_op jit(solution)/shard_map/ppermute | solution.py:399
  47.2 19.3 %collective-permute-start.7 = (bf16[128,768]{1,0:T(8,128)(2,1)S(1)}, bf16[128,768]{1,0:T(8,128)(2,1)S(1)}, u32[]{:S(2)}, u32[]{:S(2)}) collective-permute-start(bf16[128,768]{1,0:T(8,128)(2,1)S(1)} %get-tuple-element.28), channel_id=1, source_target_pairs={{0,4},{4,8},{8,12},{12,0},{1,5},{5,9},{9,13},{13,1},{2,6},{6,10},{... | collective-permute-start | bytes 589832 | tf_op jit(solution)/shard_map/ppermute | solution.py:399
  55.3 13.0 %copy-start.6 = (bf16[640,640]{1,0:T(8,128)(2,1)S(1)}, bf16[640,640]{1,0:T(8,128)(2,1)}, u32[]{:S(2)}) copy-start(bf16[640,640]{1,0:T(8,128)(2,1)} %w_ref.5) | copy-start | bytes 2457604
  55.3 13.0 %copy-start.10 = (bf16[128,640]{1,0:T(8,128)(2,1)S(1)}, bf16[128,640]{1,0:T(8,128)(2,1)}, u32[]{:S(2)}) copy-start(bf16[128,640]{1,0:T(8,128)(2,1)} %constant.6.clone.spread_ref) | copy-start | bytes 491524
  55.3 13.0 %copy-start.11 = (bf16[640,128]{1,0:T(8,128)(2,1)S(1)}, bf16[640,128]{1,0:T(8,128)(2,1)}, u32[]{:S(2)}) copy-start(bf16[640,128]{1,0:T(8,128)(2,1)} %constant.7.clone.gather_ref) | copy-start | bytes 491524
  55.3 12.2 %collective-permute-start.8 = (bf16[128,768]{1,0:T(8,128)(2,1)S(1)}, bf16[128,768]{1,0:T(8,128)(2,1)S(1)}, u32[]{:S(2)}, u32[]{:S(2)}) collective-permute-start(bf16[128,768]{1,0:T(8,128)(2,1)S(1)} %get-tuple-element.29), channel_id=1, source_target_pairs={{0,8},{4,12},{8,0},{12,4},{1,9},{5,13},{9,1},{13,5},{2,10},{6,14},... | collective-permute-start | bytes 589832 | tf_op jit(solution)/shard_map/ppermute | solution.py:399
  65.4 7.9 %collective-permute-start.12 = (bf16[128,768]{1,0:T(8,128)(2,1)S(1)}, bf16[128,768]{1,0:T(8,128)(2,1)S(1)}, u32[]{:S(2)}, u32[]{:S(2)}) collective-permute-start(bf16[128,768]{1,0:T(8,128)(2,1)S(1)} %get-tuple-element.32), channel_id=1, source_target_pairs={{0,12},{4,0},{8,4},{12,8},{1,13},{5,1},{9,5},{13,9},{2,14},{6,2},{... | collective-permute-start | bytes 589832 | tf_op jit(solution)/shard_map/ppermute | solution.py:399
  66.5 11.7 %collective-permute-start.13 = (bf16[128,768]{1,0:T(8,128)(2,1)S(1)}, bf16[128,768]{1,0:T(8,128)(2,1)S(1)}, u32[]{:S(2)}, u32[]{:S(2)}) collective-permute-start(bf16[128,768]{1,0:T(8,128)(2,1)S(1)} %get-tuple-element.33), channel_id=1, source_target_pairs={{0,4},{4,8},{8,12},{12,0},{1,5},{5,9},{9,13},{13,1},{2,6},{6,10},{... | collective-permute-start | bytes 589832 | tf_op jit(solution)/shard_map/ppermute | solution.py:399
  67.5 10.7 %collective-permute-start.14 = (bf16[128,768]{1,0:T(8,128)(2,1)S(1)}, bf16[128,768]{1,0:T(8,128)(2,1)S(1)}, u32[]{:S(2)}, u32[]{:S(2)}) collective-permute-start(bf16[128,768]{1,0:T(8,128)(2,1)S(1)} %get-tuple-element.34), channel_id=1, source_target_pairs={{0,8},{4,12},{8,0},{12,4},{1,9},{5,13},{9,1},{13,5},{2,10},{6,14},... | collective-permute-start | bytes 589832 | tf_op jit(solution)/shard_map/ppermute | solution.py:399
  78.2 16.1 %copy-start.1 = (f32[2,640]{1,0:T(2,128)S(1)}, f32[2,640]{1,0:T(2,128)}, u32[]{:S(2)}) copy-start(f32[2,640]{1,0:T(2,128)} %shift_ref.1) | copy-start | bytes 15364
  78.2 16.1 %copy-start.4 = (f32[640]{0:T(1024)S(1)}, f32[640]{0:T(1024)}, u32[]{:S(2)}) copy-start(f32[640]{0:T(1024)} %bias_ref.6) | copy-start | bytes 7684
  79.2 20.1 %copy-start = (bf16[128,640]{1,0:T(8,128)(2,1)S(1)}, bf16[128,640]{1,0:T(8,128)(2,1)}, u32[]{:S(2)}) copy-start(bf16[128,640]{1,0:T(8,128)(2,1)} %constant.8.clone.scatter_ref) | copy-start | bytes 491524
  79.2 20.1 %copy-start.2 = (f32[640]{0:T(1024)S(1)}, f32[640]{0:T(1024)}, u32[]{:S(2)}) copy-start(f32[640]{0:T(1024)} %gain_ref.5) | copy-start | bytes 7684
  79.2 20.1 %copy-start.3 = (f32[640]{0:T(1024)S(1)}, f32[640]{0:T(1024)}, u32[]{:S(2)}) copy-start(f32[640]{0:T(1024)} %bias_ref.7) | copy-start | bytes 7684
  79.3 4.9 %collective-permute-start.15 = (f32[8,128]{1,0:T(8,128)S(1)}, f32[8,128]{1,0:T(8,128)S(1)}, u32[]{:S(2)}, u32[]{:S(2)}) collective-permute-start(f32[8,128]{1,0:T(8,128)S(1)} %get-tuple-element.37.refs_0_), channel_id=1, source_target_pairs={{0,4},{4,8},{8,12},{12,0},{1,5},{5,9},{9,13},{13,1},{2,6},{6,10},{... | collective-permute-start | bytes 12296 | tf_op jit(solution)/shard_map/ppermute | solution.py:428
  79.4 4.8 %collective-permute-start.16 = (f32[8,128]{1,0:T(8,128)S(1)}, f32[8,128]{1,0:T(8,128)S(1)}, u32[]{:S(2)}, u32[]{:S(2)}) collective-permute-start(f32[8,128]{1,0:T(8,128)S(1)} %get-tuple-element.37.refs_0_), channel_id=1, source_target_pairs={{0,12},{4,0},{8,4},{12,8},{1,13},{5,1},{9,5},{13,9},{2,14},{6,2},{... | collective-permute-start | bytes 12296 | tf_op jit(solution)/shard_map/ppermute | solution.py:428
  82.6 5.1 %collective-permute-start.17 = (f32[8,128]{1,0:T(8,128)S(1)}, f32[8,128]{1,0:T(8,128)S(1)}, u32[]{:S(2)}, u32[]{:S(2)}) collective-permute-start(f32[8,128]{1,0:T(8,128)S(1)} %get-tuple-element.37.refs_0_), channel_id=1, source_target_pairs={{0,8},{4,12},{8,0},{12,4},{1,9},{5,13},{9,1},{13,5},{2,10},{6,14},... | collective-permute-start | bytes 12296 | tf_op jit(solution)/shard_map/ppermute | solution.py:428
  87.7 8.5 %collective-permute-start.18 = (f32[8,128]{1,0:T(8,128)S(1)}, f32[8,128]{1,0:T(8,128)S(1)}, u32[]{:S(2)}, u32[]{:S(2)}) collective-permute-start(f32[8,128]{1,0:T(8,128)S(1)} %shard_map.161.s0_ref), channel_id=1, source_target_pairs={{0,1},{1,2},{2,3},{3,0},{4,5},{5,6},{6,7},{7,4},{8,9},{9,10},{10,1... | collective-permute-start | bytes 12296 | tf_op jit(solution)/shard_map/ppermute | solution.py:430
  90.2 6.0 %collective-permute-start.19 = (f32[8,128]{1,0:T(8,128)S(1)}, f32[8,128]{1,0:T(8,128)S(1)}, u32[]{:S(2)}, u32[]{:S(2)}) collective-permute-start(f32[8,128]{1,0:T(8,128)S(1)} %shard_map.161.s0_ref), channel_id=1, source_target_pairs={{0,3},{1,0},{2,1},{3,2},{4,7},{5,4},{6,5},{7,6},{8,11},{9,8},{10,9... | collective-permute-start | bytes 12296 | tf_op jit(solution)/shard_map/ppermute | solution.py:430
  91.8 7.5 %collective-permute-start.20 = (f32[8,128]{1,0:T(8,128)S(1)}, f32[8,128]{1,0:T(8,128)S(1)}, u32[]{:S(2)}, u32[]{:S(2)}) collective-permute-start(f32[8,128]{1,0:T(8,128)S(1)} %shard_map.161.s0_ref), channel_id=1, source_target_pairs={{0,2},{1,3},{2,0},{3,1},{4,6},{5,7},{6,4},{7,5},{8,10},{9,11},{10,... | collective-permute-start | bytes 12296 | tf_op jit(solution)/shard_map/ppermute | solution.py:430

commit v7 on v6

--- a/solution.py
+++ b/solution.py
@@ -110,76 +110,60 @@
     high_values = jnp.concatenate(
         [jnp.where(low_all, zero, values), jnp.where(low_all, zero, one)], axis=1
     )
-    common, fresh, own = slice(0, 3 * rows), slice(3 * rows, 4 * rows), slice(4 * rows, 5 * rows)
+    common, own = slice(0, 3 * rows), slice(4 * rows, 5 * rows)
     lanes = pl.ds(pl.multiple_of(pair * LANES, LANES), LANES)
     mine = q0_ref[part, lanes]
-    others = jnp.concatenate([ref[part, lanes] for ref in (q1_ref, q2_ref, q3_ref)], 0)
-
-    def halves(x):
-        low_part = lax.broadcasted_iota(jnp.int32, x.shape, 1) < HEAD_DIM
-        return jnp.concatenate([jnp.where(low_part, x, zero), jnp.where(low_part, zero, x)], 0)
-
-    mine, others = halves(mine), halves(others)
-    scores = jnp.concatenate(
-        [
-            scores_of(mine, keys[: 4 * rows]),
-            scores_of(others, jnp.concatenate([keys[common], keys[own]], 0)),
-        ],
-        0,
-    )
-    top = jnp.max(scores, -1, keepdims=True)
-    scores = jnp.exp(scores - top).astype(BF16)
-    shared, single = scores[:, : 3 * rows], scores[:, 3 * rows :]
-
-    def paired(x):
-        return (
-            jnp.concatenate([x[:rows], x[2 * rows : 5 * rows]], 0),
-            jnp.concatenate([x[rows : 2 * rows], x[5 * rows :]], 0),
+    others = [ref[part, lanes] for ref in (q1_ref, q2_ref, q3_ref)]
+
+    own_keys, other_keys = keys[: 4 * rows], jnp.concatenate([keys[common], keys[own]], 0)
+    low_part = lax.broadcasted_iota(jnp.int32, (rows, LANES), 1) < HEAD_DIM
+    lows = [jnp.where(low_part, q, zero) for q in (mine, *others)]
+    highs = [jnp.where(low_part, zero, q) for q in (mine, *others)]
+    scores = [
+        (scores_of(part[0], own_keys), scores_of(jnp.concatenate(part[1:], 0), other_keys))
+        for part in (lows, highs)
+    ]
+    tops, sums = [], []
+    for (first, rest), head_values in zip(scores, (low_values, high_values)):
+        both = jnp.concatenate([first, rest], 0)
+        top = jnp.max(both, -1, keepdims=True)
+        both = jnp.exp(both - top).astype(BF16)
+        tops.append(top)
+        sums.append(
+            jnp.concatenate(
+                [
+                    jnp.dot(both[:rows], head_values[: 4 * rows], preferred_element_type=F32),
+                    jnp.dot(
+                        both[rows:],
+                        jnp.concatenate([head_values[common], head_values[own]], 0),
+                        preferred_element_type=F32,
+                    ),
+                ],
+                0,
+            )
         )
-
-    summed = jnp.dot(
-        jnp.concatenate(paired(shared), 1),
-        jnp.concatenate([low_values[common], high_values[common]], 0),
-        preferred_element_type=F32,
-    )
-    single = jnp.concatenate(paired(single), 1)
-    summed = summed + jnp.concatenate(
-        [
-            jnp.dot(
-                single[:rows],
-                jnp.concatenate([low_values[fresh], high_values[fresh]], 0),
-                preferred_element_type=F32,
-            ),
-            jnp.dot(
-                single[rows:],
-                jnp.concatenate([low_values[own], high_values[own]], 0),
-                preferred_element_type=F32,
-            ),
-        ],
-        0,
-    )
+    summed = sums[0] + sums[1]
     total = summed[:, LANES:]
     mixed = (summed[:, :LANES] / total).astype(BF16)
     for index, o_ref in enumerate(out_refs):
         o_ref[:, lanes] = mixed[index * rows : (index + 1) * rows]
     lane = lax.broadcasted_iota(jnp.int32, total.shape, 1)
-    low_top, high_top = paired(top)
-    rest = jnp.where(lane < HEAD_DIM, low_top, high_top) + jnp.log(total)
-    slot = lane & (HEAD_DIM - 1)
-    tile = tile_scr[...]
-    for piece in range(3):
-        rounded = rest.astype(BF16).astype(F32)
-        tile = jnp.where(slot == pair + piece * PIECES, rounded, tile)
-        rest = rest - rounded
-    tile_scr[...] = tile
+    logs = jnp.where(lane < HEAD_DIM, tops[0], tops[1]) + jnp.log(total)
+    tile_scr[...] = jnp.where((lane & (HEAD_DIM - 1)) == pair, logs, tile_scr[...])
     kv_scr[1 - current] = project(x_scr[...], wk_ref, wv_ref)
 
     @pl.when(pair == pl.num_programs(0) - 1)
     def _():
         if fetch:
             fetch.wait()
+        rest = tile_scr[...]
+        tile = jnp.zeros_like(rest)
+        for piece in range(3):
+            rounded = rest.astype(BF16).astype(F32)
+            rest = rest - rounded
+            tile = tile + (pltpu.roll(rounded, piece * PIECES, 1) if piece else rounded)
         for index, o_ref in enumerate(out_refs):
-            o_ref[:, channels:] = tile_scr[index * rows : (index + 1) * rows, :].astype(BF16)
+            o_ref[:, channels:] = tile[index * rows : (index + 1) * rows].astype(BF16)
 
 
 def spread_matrix(channels):

time: 102 us -> 100 us (0.980)
  Pallas kernels: 24.9 us -> 22 us
  waiting for transfers between devices: 26.6 us -> 28 us
    pallas_call x10, Pallas kernels: 24.9 us -> 22 us  [call(): pl.pallas_call(kernel, out_shape=out_shape, compiler_params=pltpu.Compile...]
    ppermute x1, waiting for transfers between devices: 8.09 us -> 9.52 us  [shards(): lax.ppermute(down, 'z', ring(3, z_count))]
  transfers between devices with their start and end apart: 23 -> 23, of which waited for: 7 -> 7; matrix products, arithmetic and copies ran while one was open for 0% -> 0% of each run, Pallas kernels for 21% -> 19%
where the time goes in v7:
time: 100 us
  starting transfers between devices  49.7 us (50%)
  waiting for transfers between devices  28 us (28%)
  Pallas kernels  22 us (22%)
    pallas_call x10, Pallas kernels, call(): pl.pallas_call(kernel, out_shape=out_shape, compiler_params=pltpu.Compile...  22 us
    ppermute x4, starting transfers between devices, shards(): up, down = (lax.ppermute(one, 'z', ring(by, z_count)) for by in (1, 3))  14.3 us
    ppermute x1, waiting for transfers between devices, shards(): lax.ppermute(down, 'z', ring(3, z_count))  9.52 us
    ppermute x6, waiting for transfers between devices, shards(): lax.ppermute(one, 'y', ring(-by, y_count))  8.91 us
    ppermute x6, starting transfers between devices, shards(): lax.ppermute(one, 'y', ring(-by, y_count))  8.75 us
    ppermute x3, starting transfers between devices, shards(): lax.ppermute(stat, 'z', ring(by, z_count))  6.61 us
    ppermute x3, starting transfers between devices, shards(): lax.ppermute(queries, 'y', ring(by, y_count))  5.3 us
    ppermute x3, waiting for transfers between devices, shards(): lax.ppermute(stat, 'y', ring(by, y_count))  5.06 us
  transfers between devices with their start and end apart: 23, of which 7 were waited for; matrix products, arithmetic and copies ran while one was open for 0% of the time, Pallas kernels for 19%

profile of v7, /device:TPU:2, one launch (start us, length us, event | category | flops | bytes accessed | tf_op | source)
XLA Modules:
  0.0 100.0 jit_solution(2676786781056911654)
XLA Ops:
  0.0 0.0 copy-start.9
  0.0 1.4 %shard_map.155 = (bf16[128,640]{1,0:T(8,128)(2,1)S(1)}, bf16[128,640]{1,0:T(8,128)(2,1)S(1)}) custom-call(bf16[256,640]{1,0:T(8,128)(2,1)} %bitcast.9, f32[640]{0:T(1024)} %gain_ref.4, f32[640]{0:T(1024)} %bias_ref.5), custom_call_target="tpu_custom_call" | custom-call | flops 6000000000 | bytes 1000000 | tf_op jit(solution)/shard_map/pallas_call | solution.py:281
  1.4 3.3 %collective-permute-start.3 = (bf16[128,640]{1,0:T(8,128)(2,1)S(1)}, bf16[128,640]{1,0:T(8,128)(2,1)S(1)}, u32[]{:S(2)}, u32[]{:S(2)}) collective-permute-start(bf16[128,640]{1,0:T(8,128)(2,1)S(1)} %get-tuple-element.23.refs_1_), channel_id=1, source_target_pairs={{0,1},{1,2},{2,3},{3,0},{4,5},{5,6},{6,7},{7,4},{8,9},{9,10},{10,1... | collective-permute-start | bytes 491528 | tf_op jit(solution)/shard_map/ppermute | solution.py:318
  4.8 3.1 %collective-permute-start.5 = (bf16[128,640]{1,0:T(8,128)(2,1)S(1)}, bf16[128,640]{1,0:T(8,128)(2,1)S(1)}, u32[]{:S(2)}, u32[]{:S(2)}) collective-permute-start(bf16[128,640]{1,0:T(8,128)(2,1)S(1)} %get-tuple-element.23.refs_1_), channel_id=1, source_target_pairs={{0,3},{1,0},{2,1},{3,2},{4,7},{5,4},{6,5},{7,6},{8,11},{9,8},{10,9... | collective-permute-start | bytes 491528 | tf_op jit(solution)/shard_map/ppermute | solution.py:318
  7.9 0.0 copy-done.5
  7.9 0.0 copy-done.7
  7.9 0.0 copy-done.8
  7.9 0.0 copy-done.9
  7.9 0.7 shard_map.154
  8.6 1.7 %collective-permute-start = (bf16[256,640]{1,0:T(8,128)(2,1)S(1)}, bf16[256,640]{1,0:T(8,128)(2,1)S(1)}, u32[]{:S(2)}, u32[]{:S(2)}) collective-permute-start(bf16[256,640]{1,0:T(8,128)(2,1)S(1)} %get-tuple-element.22.q0_ref), channel_id=1, source_target_pairs={{0,4},{4,8},{8,12},{12,0},{1,5},{5,9},{9,13},{13,1},{2,6},{6,10},{... | collective-permute-start | bytes 983048 | tf_op jit(solution)/shard_map/ppermute | solution.py:330
  10.3 1.7 %collective-permute-start.1 = (bf16[256,640]{1,0:T(8,128)(2,1)S(1)}, bf16[256,640]{1,0:T(8,128)(2,1)S(1)}, u32[]{:S(2)}, u32[]{:S(2)}) collective-permute-start(bf16[256,640]{1,0:T(8,128)(2,1)S(1)} %get-tuple-element.22.q0_ref), channel_id=1, source_target_pairs={{0,12},{4,0},{8,4},{12,8},{1,13},{5,1},{9,5},{13,9},{2,14},{6,2},{... | collective-permute-start | bytes 983048 | tf_op jit(solution)/shard_map/ppermute | solution.py:330
  12.0 2.0 %collective-permute-start.2 = (bf16[256,640]{1,0:T(8,128)(2,1)S(1)}, bf16[256,640]{1,0:T(8,128)(2,1)S(1)}, u32[]{:S(2)}, u32[]{:S(2)}) collective-permute-start(bf16[256,640]{1,0:T(8,128)(2,1)S(1)} %get-tuple-element.22.q0_ref), channel_id=1, source_target_pairs={{0,8},{4,12},{8,0},{12,4},{1,9},{5,13},{9,1},{13,5},{2,10},{6,14},... | collective-permute-start | bytes 983048 | tf_op jit(solution)/shard_map/ppermute | solution.py:330
  13.9 0.0 collective-permute-done.3.z1_ref
  13.9 4.3 %collective-permute-start.10 = (bf16[128,640]{1,0:T(8,128)(2,1)S(1)}, bf16[128,640]{1,0:T(8,128)(2,1)S(1)}, u32[]{:S(2)}, u32[]{:S(2)}) collective-permute-start(bf16[128,640]{1,0:T(8,128)(2,1)S(1)} %get-tuple-element.25.refs_2_), channel_id=1, source_target_pairs={{0,3},{1,0},{2,1},{3,2},{4,7},{5,4},{6,5},{7,6},{8,11},{9,8},{10,9... | collective-permute-start | bytes 491528 | tf_op jit(solution)/shard_map/ppermute | solution.py:318
  18.2 0.0 collective-permute-done.5.z3_ref
  18.2 2.3 %collective-permute-start.4 = (bf16[128,640]{1,0:T(8,128)(2,1)S(1)}, bf16[128,640]{1,0:T(8,128)(2,1)S(1)}, u32[]{:S(2)}, u32[]{:S(2)}) collective-permute-start(bf16[128,640]{1,0:T(8,128)(2,1)S(1)} %collective-permute-done.3.z1_ref), channel_id=1, source_target_pairs={{0,1},{1,2},{2,3},{3,0},{4,5},{5,6},{6,7},{7,4},{8,9},{9,10},{10,1... | collective-permute-start | bytes 491528 | tf_op jit(solution)/shard_map/ppermute | solution.py:319
  20.5 2.3 %shard_map.156.early_ref = bf16[512,1280]{1,0:T(8,128)(2,1)S(1)} custom-call(bf16[256,640]{1,0:T(8,128)(2,1)S(1)} %get-tuple-element.24.refs_0_, bf16[128,640]{1,0:T(8,128)(2,1)S(1)} %get-tuple-element.23.refs_1_, bf16[128,640]{1,0:T(8,128)(2,1)S(1)} %get-tuple-element.25.refs_2_, bf16[640,1920]{1,0:T(8,128)(2,1)S(1)} %copy-done.5, ...), custom_call_target="tpu_custom_call" | custom-call | flops 6000000000 | bytes 1000000 | tf_op jit(solution)/shard_map/pallas_call | solution.py:281
  22.9 1.4 %collective-permute-done.10.z3_ref = bf16[128,640]{1,0:T(8,128)(2,1)S(1)} collective-permute-done((bf16[128,640]{1,0:T(8,128)(2,1)S(1)}, bf16[128,640]{1,0:T(8,128)(2,1)S(1)}, u32[]{:S(2)}, u32[]{:S(2)}) %collective-permute-start.10) | collective-permute-done | bytes 163872 | tf_op jit(solution)/shard_map/ppermute | solution.py:318
  24.2 3.6 %collective-permute-start.9 = (bf16[128,640]{1,0:T(8,128)(2,1)S(1)}, bf16[128,640]{1,0:T(8,128)(2,1)S(1)}, u32[]{:S(2)}, u32[]{:S(2)}) collective-permute-start(bf16[128,640]{1,0:T(8,128)(2,1)S(1)} %get-tuple-element.25.refs_2_), channel_id=1, source_target_pairs={{0,1},{1,2},{2,3},{3,0},{4,5},{5,6},{6,7},{7,4},{8,9},{9,10},{10,1... | collective-permute-start | bytes 491528 | tf_op jit(solution)/shard_map/ppermute | solution.py:318
  27.8 0.0 collective-permute-done.q1_ref
  27.8 0.0 copy-done.12
  27.8 4.8 %collective-permute-start.21 = (bf16[256,640]{1,0:T(8,128)(2,1)S(1)}, bf16[256,640]{1,0:T(8,128)(2,1)S(1)}, u32[]{:S(2)}, u32[]{:S(2)}) collective-permute-start(bf16[256,640]{1,0:T(8,128)(2,1)S(1)} %bitcast.10), channel_id=1, source_target_pairs={{0,1},{1,2},{2,3},{3,4},{4,5},{5,6},{6,7},{7,8},{8,9},{9,10},{10,1... | collective-permute-start | bytes 983048 | tf_op jit(solution)/shard_map/ppermute | solution.py:346
  32.6 0.0 collective-permute-done.1.q2_ref
  32.7 1.3 %collective-permute-start.22 = (bf16[256,640]{1,0:T(8,128)(2,1)S(1)}, bf16[256,640]{1,0:T(8,128)(2,1)S(1)}, u32[]{:S(2)}, u32[]{:S(2)}) collective-permute-start(bf16[256,640]{1,0:T(8,128)(2,1)S(1)} %bitcast.11), channel_id=1, source_target_pairs={{1,0},{2,1},{3,2},{4,3},{5,4},{6,5},{7,6},{8,7},{9,8},{10,9},{11,1... | collective-permute-start | bytes 983048 | tf_op jit(solution)/shard_map/ppermute | solution.py:347
  34.0 0.0 collective-permute-done.2.q3_ref
  34.0 2.9 %collective-permute-start.11 = (bf16[128,640]{1,0:T(8,128)(2,1)S(1)}, bf16[128,640]{1,0:T(8,128)(2,1)S(1)}, u32[]{:S(2)}, u32[]{:S(2)}) collective-permute-start(bf16[128,640]{1,0:T(8,128)(2,1)S(1)} %collective-permute-done.10.z3_ref), channel_id=1, source_target_pairs={{0,3},{1,0},{2,1},{3,2},{4,7},{5,4},{6,5},{7,6},{8,11},{9,8},{10,9... | collective-permute-start | bytes 491528 | tf_op jit(solution)/shard_map/ppermute | solution.py:319
  36.9 0.0 collective-permute-done.4.z2_ref
  36.9 5.8 %shard_map.157 = (bf16[128,768]{1,0:T(8,128)(2,1)S(1)}, bf16[128,768]{1,0:T(8,128)(2,1)S(1)}, bf16[128,768]{1,0:T(8,128)(2,1)S(1)}, bf16[128,768]{1,0:T(8,128)(2,1)S(1)}) custom-call(bf16[256,640]{1,0:T(8,128)(2,1)S(1)} %get-tuple-element.22.q0_ref, bf16[256,640]{1,0:T(8,128)(2,1)S(1)} %collective-permute-done.q1_ref, ...), custom_call_target="tpu_custom_call" | custom-call | flops 6000000000 | bytes 1000000 | tf_op jit(solution)/shard_map/pallas_call | solution.py:281
  42.8 3.0 %collective-permute-start.6 = (bf16[128,768]{1,0:T(8,128)(2,1)S(1)}, bf16[128,768]{1,0:T(8,128)(2,1)S(1)}, u32[]{:S(2)}, u32[]{:S(2)}) collective-permute-start(bf16[128,768]{1,0:T(8,128)(2,1)S(1)} %get-tuple-element.27), channel_id=1, source_target_pairs={{0,12},{4,0},{8,4},{12,8},{1,13},{5,1},{9,5},{13,9},{2,14},{6,2},{... | collective-permute-start | bytes 589832 | tf_op jit(solution)/shard_map/ppermute | solution.py:383
  45.8 0.0 collective-permute-done.9.z1_ref
  45.8 0.0 collective-permute-start.7
  45.8 9.5 %collective-permute-done.11.z2_ref = bf16[128,640]{1,0:T(8,128)(2,1)S(1)} collective-permute-done((bf16[128,640]{1,0:T(8,128)(2,1)S(1)}, bf16[128,640]{1,0:T(8,128)(2,1)S(1)}, u32[]{:S(2)}, u32[]{:S(2)}) %collective-permute-start.11) | collective-permute-done | bytes 163872 | tf_op jit(solution)/shard_map/ppermute | solution.py:319
  55.3 2.8 %collective-permute-start.8 = (bf16[128,768]{1,0:T(8,128)(2,1)S(1)}, bf16[128,768]{1,0:T(8,128)(2,1)S(1)}, u32[]{:S(2)}, u32[]{:S(2)}) collective-permute-start(bf16[128,768]{1,0:T(8,128)(2,1)S(1)} %get-tuple-element.29), channel_id=1, source_target_pairs={{0,8},{4,12},{8,0},{12,4},{1,9},{5,13},{9,1},{13,5},{2,10},{6,14},... | collective-permute-start | bytes 589832 | tf_op jit(solution)/shard_map/ppermute | solution.py:383
  58.1 5.8 %shard_map.159 = (bf16[128,768]{1,0:T(8,128)(2,1)S(1)}, bf16[128,768]{1,0:T(8,128)(2,1)S(1)}, bf16[128,768]{1,0:T(8,128)(2,1)S(1)}, bf16[128,768]{1,0:T(8,128)(2,1)S(1)}, bf16[3,3,640,640]{3,2,1,0:T(8,128)(2,1)S(1)}) custom-call(bf16[256,640]{1,0:T(8,128)(2,1)S(1)} %get-tuple-element.22.q0_ref, bf16[256,640]{1,0:T(8,128)(2,1)S(1)} %collective-permute-done.q1_ref, ...), custom_call_target="tpu_custom_call" | custom-call | flops 6000000000 | bytes 1000000 | tf_op jit(solution)/shard_map/pallas_call | solution.py:281
  64.0 0.0 collective-permute-done.6.o1_ref
  64.0 1.1 %collective-permute-start.12 = (bf16[128,768]{1,0:T(8,128)(2,1)S(1)}, bf16[128,768]{1,0:T(8,128)(2,1)S(1)}, u32[]{:S(2)}, u32[]{:S(2)}) collective-permute-start(bf16[128,768]{1,0:T(8,128)(2,1)S(1)} %get-tuple-element.32), channel_id=1, source_target_pairs={{0,12},{4,0},{8,4},{12,8},{1,13},{5,1},{9,5},{13,9},{2,14},{6,2},{... | collective-permute-start | bytes 589832 | tf_op jit(solution)/shard_map/ppermute | solution.py:383
  65.1 0.0 collective-permute-done.7.o2_ref
  65.1 1.0 collective-permute-start.13
  66.1 0.0 collective-permute-done.8.o3_ref
  66.1 0.8 collective-permute-start.14
  66.9 0.0 copy-done.10
  66.9 1.0 shard_map.158
  67.9 3.9 %collective-permute-done.12.o1_ref = bf16[128,768]{1,0:T(8,128)(2,1)S(1)} collective-permute-done((bf16[128,768]{1,0:T(8,128)(2,1)S(1)}, bf16[128,768]{1,0:T(8,128)(2,1)S(1)}, u32[]{:S(2)}, u32[]{:S(2)}) %collective-permute-start.12) | collective-permute-done | bytes 196640 | tf_op jit(solution)/shard_map/ppermute | solution.py:383
  71.8 5.0 %collective-permute-done.13.o2_ref = bf16[128,768]{1,0:T(8,128)(2,1)S(1)} collective-permute-done((bf16[128,768]{1,0:T(8,128)(2,1)S(1)}, bf16[128,768]{1,0:T(8,128)(2,1)S(1)}, u32[]{:S(2)}, u32[]{:S(2)}) %collective-permute-start.13) | collective-permute-done | bytes 196640 | tf_op jit(solution)/shard_map/ppermute | solution.py:383
  76.8 0.0 collective-permute-done.14.o3_ref
  76.8 1.0 shard_map.160
  77.8 0.1 collective-permute-start.15
  77.9 3.2 %collective-permute-start.16 = (f32[8,128]{1,0:T(8,128)S(1)}, f32[8,128]{1,0:T(8,128)S(1)}, u32[]{:S(2)}, u32[]{:S(2)}) collective-permute-start(f32[8,128]{1,0:T(8,128)S(1)} %get-tuple-element.37.refs_0_), channel_id=1, source_target_pairs={{0,12},{4,0},{8,4},{12,8},{1,13},{5,1},{9,5},{13,9},{2,14},{6,2},{... | collective-permute-start | bytes 12296 | tf_op jit(solution)/shard_map/ppermute | solution.py:412
  81.1 0.0 collective-permute-start.17
  81.2 1.5 %collective-permute-done.15.refs_1_ = f32[8,128]{1,0:T(8,128)S(1)} collective-permute-done((f32[8,128]{1,0:T(8,128)S(1)}, f32[8,128]{1,0:T(8,128)S(1)}, u32[]{:S(2)}, u32[]{:S(2)}) %collective-permute-start.15) | collective-permute-done | bytes 4128 | tf_op jit(solution)/shard_map/ppermute | solution.py:412
  82.7 0.0 collective-permute-done.16.refs_2_
  82.7 3.5 %collective-permute-done.17.refs_3_ = f32[8,128]{1,0:T(8,128)S(1)} collective-permute-done((f32[8,128]{1,0:T(8,128)S(1)}, f32[8,128]{1,0:T(8,128)S(1)}, u32[]{:S(2)}, u32[]{:S(2)}) %collective-permute-start.17) | collective-permute-done | bytes 4128 | tf_op jit(solution)/shard_map/ppermute | solution.py:412
  86.3 2.5 %collective-permute-start.18 = (f32[8,128]{1,0:T(8,128)S(1)}, f32[8,128]{1,0:T(8,128)S(1)}, u32[]{:S(2)}, u32[]{:S(2)}) collective-permute-start(f32[8,128]{1,0:T(8,128)S(1)} %shard_map.161.s0_ref), channel_id=1, source_target_pairs={{0,1},{1,2},{2,3},{3,0},{4,5},{5,6},{6,7},{7,4},{8,9},{9,10},{10,1... | collective-permute-start | bytes 12296 | tf_op jit(solution)/shard_map/ppermute | solution.py:414
  88.8 1.6 %collective-permute-start.19 = (f32[8,128]{1,0:T(8,128)S(1)}, f32[8,128]{1,0:T(8,128)S(1)}, u32[]{:S(2)}, u32[]{:S(2)}) collective-permute-start(f32[8,128]{1,0:T(8,128)S(1)} %shard_map.161.s0_ref), channel_id=1, source_target_pairs={{0,3},{1,0},{2,1},{3,2},{4,7},{5,4},{6,5},{7,6},{8,11},{9,8},{10,9... | collective-permute-start | bytes 12296 | tf_op jit(solution)/shard_map/ppermute | solution.py:414
  90.4 2.5 %collective-permute-start.20 = (f32[8,128]{1,0:T(8,128)S(1)}, f32[8,128]{1,0:T(8,128)S(1)}, u32[]{:S(2)}, u32[]{:S(2)}) collective-permute-start(f32[8,128]{1,0:T(8,128)S(1)} %shard_map.161.s0_ref), channel_id=1, source_target_pairs={{0,2},{1,3},{2,0},{3,1},{4,6},{5,7},{6,4},{7,5},{8,10},{9,11},{10,... | collective-permute-start | bytes 12296 | tf_op jit(solution)/shard_map/ppermute | solution.py:414
  92.9 0.0 collective-permute-done.21.above_ref
  92.9 0.0 collective-permute-done.22.below_ref
  92.9 0.0 copy-done.1
  92.9 1.8 %shard_map.162.rim_ref = f32[256,640]{1,0:T(8,128)S(1)} custom-call(bf16[256,640]{1,0:T(8,128)(2,1)S(1)} %collective-permute-done.21.above_ref, bf16[256,640]{1,0:T(8,128)(2,1)S(1)} %collective-permute-done.22.below_ref, bf16[3,3,640,640]{3,2,1,0:T(8,128)(2,1)S(1)} %get-tuple-element.38.w_ref, f32[640]{0:T(1024)S(1)} %copy-done.4, f32[2,640]{1,0:T(2,128)S(1)} %copy-done.1), custom_call_target="tpu_custom_call" | custom-call | flops 1258291200 | bytes 1000000 | tf_op jit(solution)/shard_map/pallas_call | solution.py:281
  94.7 0.0 collective-permute-done.18.s1_ref
  94.7 0.0 collective-permute-done.19.s2_ref
  94.7 3.2 %collective-permute-done.20.s3_ref = f32[8,128]{1,0:T(8,128)S(1)} collective-permute-done((f32[8,128]{1,0:T(8,128)S(1)}, f32[8,128]{1,0:T(8,128)S(1)}, u32[]{:S(2)}, u32[]{:S(2)}) %collective-permute-start.20) | collective-permute-done | bytes 4128 | tf_op jit(solution)/shard_map/ppermute | solution.py:414
  97.9 0.0 copy-done.3
  97.9 2.1 %shard_map.163 = bf16[256,640]{1,0:T(8,128)(2,1)} custom-call(bf16[128,640]{1,0:T(8,128)(2,1)S(1)} %get-tuple-element.30.res0_ref, bf16[128,640]{1,0:T(8,128)(2,1)S(1)} %get-tuple-element.36.res1_ref, f32[8,128]{1,0:T(8,128)S(1)} %shard_map.161.s0_ref, f32[8,128]{1,0:T(8,128)S(1)} %collective-permute-done.18.s1_ref, ...), custom_call_target="tpu_custom_call" | custom-call | flops 629145600 | bytes 1000000 | tf_op jit(solution)/shard_map/pallas_call | solution.py:281
  (18 shorter events, 0.0 us)
Async XLA Ops:
  0.0 7.9 %copy-start.5 = (bf16[640,1920]{1,0:T(8,128)(2,1)S(1)}, bf16[640,1920]{1,0:T(8,128)(2,1)}, u32[]{:S(2)}) copy-start(bf16[640,1920]{1,0:T(8,128)(2,1)} %wv_ref.3) | copy-start | bytes 7372804
  0.0 7.9 %copy-start.7 = (bf16[2,1,128,640]{3,2,1,0:T(8,128)(2,1)S(1)}, bf16[2,1,128,640]{3,2,1,0:T(8,128)(2,1)}, u32[]{:S(2)}) copy-start(bf16[2,1,128,640]{3,2,1,0:T(8,128)(2,1)} %param.16) | copy-start | bytes 983044
  0.0 7.9 %copy-start.8 = (f32[640]{0:T(1024)S(1)}, f32[640]{0:T(1024)}, u32[]{:S(2)}) copy-start(f32[640]{0:T(1024)} %gain_ref.4) | copy-start | bytes 7684
  0.0 7.9 %copy-start.9 = (f32[640]{0:T(1024)S(1)}, f32[640]{0:T(1024)}, u32[]{:S(2)}) copy-start(f32[640]{0:T(1024)} %bias_ref.5) | copy-start | bytes 7684
  1.4 12.5 %collective-permute-start.3 = (bf16[128,640]{1,0:T(8,128)(2,1)S(1)}, bf16[128,640]{1,0:T(8,128)(2,1)S(1)}, u32[]{:S(2)}, u32[]{:S(2)}) collective-permute-start(bf16[128,640]{1,0:T(8,128)(2,1)S(1)} %get-tuple-element.23.refs_1_), channel_id=1, source_target_pairs={{0,1},{1,2},{2,3},{3,0},{4,5},{5,6},{6,7},{7,4},{8,9},{9,10},{10,1... | collective-permute-start | bytes 491528 | tf_op jit(solution)/shard_map/ppermute | solution.py:318
  4.8 13.4 %collective-permute-start.5 = (bf16[128,640]{1,0:T(8,128)(2,1)S(1)}, bf16[128,640]{1,0:T(8,128)(2,1)S(1)}, u32[]{:S(2)}, u32[]{:S(2)}) collective-permute-start(bf16[128,640]{1,0:T(8,128)(2,1)S(1)} %get-tuple-element.23.refs_1_), channel_id=1, source_target_pairs={{0,3},{1,0},{2,1},{3,2},{4,7},{5,4},{6,5},{7,6},{8,11},{9,8},{10,9... | collective-permute-start | bytes 491528 | tf_op jit(solution)/shard_map/ppermute | solution.py:318
  8.6 19.2 %collective-permute-start = (bf16[256,640]{1,0:T(8,128)(2,1)S(1)}, bf16[256,640]{1,0:T(8,128)(2,1)S(1)}, u32[]{:S(2)}, u32[]{:S(2)}) collective-permute-start(bf16[256,640]{1,0:T(8,128)(2,1)S(1)} %get-tuple-element.22.q0_ref), channel_id=1, source_target_pairs={{0,4},{4,8},{8,12},{12,0},{1,5},{5,9},{9,13},{13,1},{2,6},{6,10},{... | collective-permute-start | bytes 983048 | tf_op jit(solution)/shard_map/ppermute | solution.py:330
  10.3 22.4 %collective-permute-start.1 = (bf16[256,640]{1,0:T(8,128)(2,1)S(1)}, bf16[256,640]{1,0:T(8,128)(2,1)S(1)}, u32[]{:S(2)}, u32[]{:S(2)}) collective-permute-start(bf16[256,640]{1,0:T(8,128)(2,1)S(1)} %get-tuple-element.22.q0_ref), channel_id=1, source_target_pairs={{0,12},{4,0},{8,4},{12,8},{1,13},{5,1},{9,5},{13,9},{2,14},{6,2},{... | collective-permute-start | bytes 983048 | tf_op jit(solution)/shard_map/ppermute | solution.py:330
  12.0 22.0 %collective-permute-start.2 = (bf16[256,640]{1,0:T(8,128)(2,1)S(1)}, bf16[256,640]{1,0:T(8,128)(2,1)S(1)}, u32[]{:S(2)}, u32[]{:S(2)}) collective-permute-start(bf16[256,640]{1,0:T(8,128)(2,1)S(1)} %get-tuple-element.22.q0_ref), channel_id=1, source_target_pairs={{0,8},{4,12},{8,0},{12,4},{1,9},{5,13},{9,1},{13,5},{2,10},{6,14},... | collective-permute-start | bytes 983048 | tf_op jit(solution)/shard_map/ppermute | solution.py:330
  13.9 10.3 %collective-permute-start.10 = (bf16[128,640]{1,0:T(8,128)(2,1)S(1)}, bf16[128,640]{1,0:T(8,128)(2,1)S(1)}, u32[]{:S(2)}, u32[]{:S(2)}) collective-permute-start(bf16[128,640]{1,0:T(8,128)(2,1)S(1)} %get-tuple-element.25.refs_2_), channel_id=1, source_target_pairs={{0,3},{1,0},{2,1},{3,2},{4,7},{5,4},{6,5},{7,6},{8,11},{9,8},{10,9... | collective-permute-start | bytes 491528 | tf_op jit(solution)/shard_map/ppermute | solution.py:318
  18.2 18.7 %collective-permute-start.4 = (bf16[128,640]{1,0:T(8,128)(2,1)S(1)}, bf16[128,640]{1,0:T(8,128)(2,1)S(1)}, u32[]{:S(2)}, u32[]{:S(2)}) collective-permute-start(bf16[128,640]{1,0:T(8,128)(2,1)S(1)} %collective-permute-done.3.z1_ref), channel_id=1, source_target_pairs={{0,1},{1,2},{2,3},{3,0},{4,5},{5,6},{6,7},{7,4},{8,9},{9,10},{10,1... | collective-permute-start | bytes 491528 | tf_op jit(solution)/shard_map/ppermute | solution.py:319
  20.5 7.3 %copy-start.12 = (bf16[2,1,128,640]{3,2,1,0:T(8,128)(2,1)S(1)}, bf16[2,1,128,640]{3,2,1,0:T(8,128)(2,1)}, u32[]{:S(2)}) copy-start(bf16[2,1,128,640]{3,2,1,0:T(8,128)(2,1)} %param.18) | copy-start | bytes 983044
  24.2 21.5 %collective-permute-start.9 = (bf16[128,640]{1,0:T(8,128)(2,1)S(1)}, bf16[128,640]{1,0:T(8,128)(2,1)S(1)}, u32[]{:S(2)}, u32[]{:S(2)}) collective-permute-start(bf16[128,640]{1,0:T(8,128)(2,1)S(1)} %get-tuple-element.25.refs_2_), channel_id=1, source_target_pairs={{0,1},{1,2},{2,3},{3,0},{4,5},{5,6},{6,7},{7,4},{8,9},{9,10},{10,1... | collective-permute-start | bytes 491528 | tf_op jit(solution)/shard_map/ppermute | solution.py:318
  27.8 65.0 %collective-permute-start.21 = (bf16[256,640]{1,0:T(8,128)(2,1)S(1)}, bf16[256,640]{1,0:T(8,128)(2,1)S(1)}, u32[]{:S(2)}, u32[]{:S(2)}) collective-permute-start(bf16[256,640]{1,0:T(8,128)(2,1)S(1)} %bitcast.10), channel_id=1, source_target_pairs={{0,1},{1,2},{2,3},{3,4},{4,5},{5,6},{6,7},{7,8},{8,9},{9,10},{10,1... | collective-permute-start | bytes 983048 | tf_op jit(solution)/shard_map/ppermute | solution.py:346
  32.7 60.2 %collective-permute-start.22 = (bf16[256,640]{1,0:T(8,128)(2,1)S(1)}, bf16[256,640]{1,0:T(8,128)(2,1)S(1)}, u32[]{:S(2)}, u32[]{:S(2)}) collective-permute-start(bf16[256,640]{1,0:T(8,128)(2,1)S(1)} %bitcast.11), channel_id=1, source_target_pairs={{1,0},{2,1},{3,2},{4,3},{5,4},{6,5},{7,6},{8,7},{9,8},{10,9},{11,1... | collective-permute-start | bytes 983048 | tf_op jit(solution)/shard_map/ppermute | solution.py:347
  34.0 21.3 %collective-permute-start.11 = (bf16[128,640]{1,0:T(8,128)(2,1)S(1)}, bf16[128,640]{1,0:T(8,128)(2,1)S(1)}, u32[]{:S(2)}, u32[]{:S(2)}) collective-permute-start(bf16[128,640]{1,0:T(8,128)(2,1)S(1)} %collective-permute-done.10.z3_ref), channel_id=1, source_target_pairs={{0,3},{1,0},{2,1},{3,2},{4,7},{5,4},{6,5},{7,6},{8,11},{9,8},{10,9... | collective-permute-start | bytes 491528 | tf_op jit(solution)/shard_map/ppermute | solution.py:319
  42.8 21.2 %collective-permute-start.6 = (bf16[128,768]{1,0:T(8,128)(2,1)S(1)}, bf16[128,768]{1,0:T(8,128)(2,1)S(1)}, u32[]{:S(2)}, u32[]{:S(2)}) collective-permute-start(bf16[128,768]{1,0:T(8,128)(2,1)S(1)} %get-tuple-element.27), channel_id=1, source_target_pairs={{0,12},{4,0},{8,4},{12,8},{1,13},{5,1},{9,5},{13,9},{2,14},{6,2},{... | collective-permute-start | bytes 589832 | tf_op jit(solution)/shard_map/ppermute | solution.py:383
  45.8 19.3 %collective-permute-start.7 = (bf16[128,768]{1,0:T(8,128)(2,1)S(1)}, bf16[128,768]{1,0:T(8,128)(2,1)S(1)}, u32[]{:S(2)}, u32[]{:S(2)}) collective-permute-start(bf16[128,768]{1,0:T(8,128)(2,1)S(1)} %get-tuple-element.28), channel_id=1, source_target_pairs={{0,4},{4,8},{8,12},{12,0},{1,5},{5,9},{9,13},{13,1},{2,6},{6,10},{... | collective-permute-start | bytes 589832 | tf_op jit(solution)/shard_map/ppermute | solution.py:383
  55.3 11.6 %copy-start.6 = (bf16[640,640]{1,0:T(8,128)(2,1)S(1)}, bf16[640,640]{1,0:T(8,128)(2,1)}, u32[]{:S(2)}) copy-start(bf16[640,640]{1,0:T(8,128)(2,1)} %w_ref.5) | copy-start | bytes 2457604
  55.3 11.6 %copy-start.10 = (bf16[128,640]{1,0:T(8,128)(2,1)S(1)}, bf16[128,640]{1,0:T(8,128)(2,1)}, u32[]{:S(2)}) copy-start(bf16[128,640]{1,0:T(8,128)(2,1)} %constant.6.clone.spread_ref) | copy-start | bytes 491524
  55.3 11.6 %copy-start.11 = (bf16[640,128]{1,0:T(8,128)(2,1)S(1)}, bf16[640,128]{1,0:T(8,128)(2,1)}, u32[]{:S(2)}) copy-start(bf16[640,128]{1,0:T(8,128)(2,1)} %constant.7.clone.gather_ref) | copy-start | bytes 491524
  55.3 10.8 %collective-permute-start.8 = (bf16[128,768]{1,0:T(8,128)(2,1)S(1)}, bf16[128,768]{1,0:T(8,128)(2,1)S(1)}, u32[]{:S(2)}, u32[]{:S(2)}) collective-permute-start(bf16[128,768]{1,0:T(8,128)(2,1)S(1)} %get-tuple-element.29), channel_id=1, source_target_pairs={{0,8},{4,12},{8,0},{12,4},{1,9},{5,13},{9,1},{13,5},{2,10},{6,14},... | collective-permute-start | bytes 589832 | tf_op jit(solution)/shard_map/ppermute | solution.py:383
  64.0 7.9 %collective-permute-start.12 = (bf16[128,768]{1,0:T(8,128)(2,1)S(1)}, bf16[128,768]{1,0:T(8,128)(2,1)S(1)}, u32[]{:S(2)}, u32[]{:S(2)}) collective-permute-start(bf16[128,768]{1,0:T(8,128)(2,1)S(1)} %get-tuple-element.32), channel_id=1, source_target_pairs={{0,12},{4,0},{8,4},{12,8},{1,13},{5,1},{9,5},{13,9},{2,14},{6,2},{... | collective-permute-start | bytes 589832 | tf_op jit(solution)/shard_map/ppermute | solution.py:383
  65.1 11.7 %collective-permute-start.13 = (bf16[128,768]{1,0:T(8,128)(2,1)S(1)}, bf16[128,768]{1,0:T(8,128)(2,1)S(1)}, u32[]{:S(2)}, u32[]{:S(2)}) collective-permute-start(bf16[128,768]{1,0:T(8,128)(2,1)S(1)} %get-tuple-element.33), channel_id=1, source_target_pairs={{0,4},{4,8},{8,12},{12,0},{1,5},{5,9},{9,13},{13,1},{2,6},{6,10},{... | collective-permute-start | bytes 589832 | tf_op jit(solution)/shard_map/ppermute | solution.py:383
  66.1 10.7 %collective-permute-start.14 = (bf16[128,768]{1,0:T(8,128)(2,1)S(1)}, bf16[128,768]{1,0:T(8,128)(2,1)S(1)}, u32[]{:S(2)}, u32[]{:S(2)}) collective-permute-start(bf16[128,768]{1,0:T(8,128)(2,1)S(1)} %get-tuple-element.34), channel_id=1, source_target_pairs={{0,8},{4,12},{8,0},{12,4},{1,9},{5,13},{9,1},{13,5},{2,10},{6,14},... | collective-permute-start | bytes 589832 | tf_op jit(solution)/shard_map/ppermute | solution.py:383
  76.8 16.1 %copy-start.1 = (f32[2,640]{1,0:T(2,128)S(1)}, f32[2,640]{1,0:T(2,128)}, u32[]{:S(2)}) copy-start(f32[2,640]{1,0:T(2,128)} %shift_ref.1) | copy-start | bytes 15364
  76.8 16.1 %copy-start.4 = (f32[640]{0:T(1024)S(1)}, f32[640]{0:T(1024)}, u32[]{:S(2)}) copy-start(f32[640]{0:T(1024)} %bias_ref.6) | copy-start | bytes 7684
  77.8 20.1 %copy-start = (bf16[128,640]{1,0:T(8,128)(2,1)S(1)}, bf16[128,640]{1,0:T(8,128)(2,1)}, u32[]{:S(2)}) copy-start(bf16[128,640]{1,0:T(8,128)(2,1)} %constant.8.clone.scatter_ref) | copy-start | bytes 491524
  77.8 20.1 %copy-start.2 = (f32[640]{0:T(1024)S(1)}, f32[640]{0:T(1024)}, u32[]{:S(2)}) copy-start(f32[640]{0:T(1024)} %gain_ref.5) | copy-start | bytes 7684
  77.8 20.1 %copy-start.3 = (f32[640]{0:T(1024)S(1)}, f32[640]{0:T(1024)}, u32[]{:S(2)}) copy-start(f32[640]{0:T(1024)} %bias_ref.7) | copy-start | bytes 7684
  77.8 4.9 %collective-permute-start.15 = (f32[8,128]{1,0:T(8,128)S(1)}, f32[8,128]{1,0:T(8,128)S(1)}, u32[]{:S(2)}, u32[]{:S(2)}) collective-permute-start(f32[8,128]{1,0:T(8,128)S(1)} %get-tuple-element.37.refs_0_), channel_id=1, source_target_pairs={{0,4},{4,8},{8,12},{12,0},{1,5},{5,9},{9,13},{13,1},{2,6},{6,10},{... | collective-permute-start | bytes 12296 | tf_op jit(solution)/shard_map/ppermute | solution.py:412
  77.9 4.8 %collective-permute-start.16 = (f32[8,128]{1,0:T(8,128)S(1)}, f32[8,128]{1,0:T(8,128)S(1)}, u32[]{:S(2)}, u32[]{:S(2)}) collective-permute-start(f32[8,128]{1,0:T(8,128)S(1)} %get-tuple-element.37.refs_0_), channel_id=1, source_target_pairs={{0,12},{4,0},{8,4},{12,8},{1,13},{5,1},{9,5},{13,9},{2,14},{6,2},{... | collective-permute-start | bytes 12296 | tf_op jit(solution)/shard_map/ppermute | solution.py:412
  81.1 5.1 %collective-permute-start.17 = (f32[8,128]{1,0:T(8,128)S(1)}, f32[8,128]{1,0:T(8,128)S(1)}, u32[]{:S(2)}, u32[]{:S(2)}) collective-permute-start(f32[8,128]{1,0:T(8,128)S(1)} %get-tuple-element.37.refs_0_), channel_id=1, source_target_pairs={{0,8},{4,12},{8,0},{12,4},{1,9},{5,13},{9,1},{13,5},{2,10},{6,14},... | collective-permute-start | bytes 12296 | tf_op jit(solution)/shard_map/ppermute | solution.py:412
  86.3 8.5 %collective-permute-start.18 = (f32[8,128]{1,0:T(8,128)S(1)}, f32[8,128]{1,0:T(8,128)S(1)}, u32[]{:S(2)}, u32[]{:S(2)}) collective-permute-start(f32[8,128]{1,0:T(8,128)S(1)} %shard_map.161.s0_ref), channel_id=1, source_target_pairs={{0,1},{1,2},{2,3},{3,0},{4,5},{5,6},{6,7},{7,4},{8,9},{9,10},{10,1... | collective-permute-start | bytes 12296 | tf_op jit(solution)/shard_map/ppermute | solution.py:414
  88.8 6.0 %collective-permute-start.19 = (f32[8,128]{1,0:T(8,128)S(1)}, f32[8,128]{1,0:T(8,128)S(1)}, u32[]{:S(2)}, u32[]{:S(2)}) collective-permute-start(f32[8,128]{1,0:T(8,128)S(1)} %shard_map.161.s0_ref), channel_id=1, source_target_pairs={{0,3},{1,0},{2,1},{3,2},{4,7},{5,4},{6,5},{7,6},{8,11},{9,8},{10,9... | collective-permute-start | bytes 12296 | tf_op jit(solution)/shard_map/ppermute | solution.py:414
  90.4 7.5 %collective-permute-start.20 = (f32[8,128]{1,0:T(8,128)S(1)}, f32[8,128]{1,0:T(8,128)S(1)}, u32[]{:S(2)}, u32[]{:S(2)}) collective-permute-start(f32[8,128]{1,0:T(8,128)S(1)} %shard_map.161.s0_ref), channel_id=1, source_target_pairs={{0,2},{1,3},{2,0},{3,1},{4,6},{5,7},{6,4},{7,5},{8,10},{9,11},{10,... | collective-permute-start | bytes 12296 | tf_op jit(solution)/shard_map/ppermute | solution.py:414

commit v8 on v7

--- a/solution.py
+++ b/solution.py
@@ -186,37 +186,36 @@
     return total
 
 
-def merge_kernel(
-    o0_ref, o1_ref, o2_ref, o3_ref, hidden_ref, w_ref, spread_ref, gather_ref, *rest_refs, sample
-):
+def merge_kernel(*refs):
+    *o_refs, hidden_ref, w_ref, spread_ref, gather_ref, res_ref, stat_ref = refs
     channels = hidden_ref.shape[1]
-    rows = hidden_ref.shape[0]
-    refs = (o0_ref, o1_ref, o2_ref, o3_ref)
-    tiles = jnp.concatenate([ref[:, channels:] for ref in refs], 0)
-    logs = jnp.dot(tiles, spread_ref[...], preferred_element_type=F32)
-    logs = [logs[index * rows : (index + 1) * rows] for index in range(4)]
-    top = jnp.maximum(jnp.maximum(logs[0], logs[1]), jnp.maximum(logs[2], logs[3]))
-    numer = denom = None
-    for ref, one in zip(refs, logs):
-        factor = jnp.exp(one - top)
-        upper = factor * ref[:, :channels].astype(F32)
-        numer, denom = (upper, factor) if numer is None else (numer + upper, denom + factor)
-    attended = (numer / denom).astype(BF16)
+    rows = o_refs[0].shape[0]
+    samples = len(o_refs) // 4
+    attended = []
+    for sample in range(samples):
+        parts = o_refs[4 * sample : 4 * sample + 4]
+        tiles = jnp.concatenate([ref[:, channels:] for ref in parts], 0)
+        logs = jnp.dot(tiles, spread_ref[...], preferred_element_type=F32)
+        logs = [logs[index * rows : (index + 1) * rows] for index in range(4)]
+        top = jnp.maximum(jnp.maximum(logs[0], logs[1]), jnp.maximum(logs[2], logs[3]))
+        numer = denom = None
+        for ref, one in zip(parts, logs):
+            factor = jnp.exp(one - top)
+            upper = factor * ref[:, :channels].astype(F32)
+            numer, denom = (upper, factor) if numer is None else (numer + upper, denom + factor)
+        attended.append((numer / denom).astype(BF16))
     residual = (
-        hidden_ref[...].astype(F32) + jnp.dot(attended, w_ref[...], preferred_element_type=F32)
+        hidden_ref[...].astype(F32)
+        + jnp.dot(jnp.concatenate(attended, 0), w_ref[...], preferred_element_type=F32)
     ).astype(BF16)
-    res_ref, stat_ref = rest_refs[-2:]
     res_ref[...] = residual
     wide = residual.astype(F32)
-    sums = jnp.concatenate(
-        [jnp.sum(wide, 0, keepdims=True), jnp.sum(wide * wide, 0, keepdims=True)]
-        + [jnp.zeros((6, channels), F32)],
-        0,
-    )
-    sums = exact_dot(sums, gather_ref[...])
-    if sample:
-        sums = pltpu.roll(sums, 2 * sample, 0) + rest_refs[0][...]
-    stat_ref[...] = sums
+    sums = []
+    for sample in range(samples):
+        part = wide[sample * rows : (sample + 1) * rows]
+        sums += [jnp.sum(part, 0, keepdims=True), jnp.sum(part * part, 0, keepdims=True)]
+    sums = jnp.concatenate(sums + [jnp.zeros((8 - len(sums), channels), F32)], 0)
+    stat_ref[...] = exact_dot(sums, gather_ref[...])
 
 
 def shifted(x, by, cols):
@@ -246,25 +245,24 @@
 
 
 def final_kernel(
-    res0_ref, res1_ref, s0_ref, s1_ref, s2_ref, s3_ref, gain_ref, bias_ref, scatter_ref, w_ref, rim_ref, out_ref,
+    res_ref, s0_ref, s1_ref, s2_ref, s3_ref, gain_ref, bias_ref, scatter_ref, w_ref, rim_ref, out_ref,
     *, cols, cells
 ):
     activated = []
-    wide = []
     sums = (s0_ref[...] + s1_ref[...]) + (s2_ref[...] + s3_ref[...])
     sums = exact_dot(sums, scatter_ref[...])
     gain, bias = as_row(gain_ref), as_row(bias_ref)
-    for sample, res_ref in enumerate((res0_ref, res1_ref)):
+    wide = res_ref[...].astype(F32)
+    for sample in range(wide.shape[0] // cols):
         mean = sums[2 * sample : 2 * sample + 1] / cells
         var = sums[2 * sample + 1 : 2 * sample + 2] / cells - mean * mean
-        residual = res_ref[...].astype(F32)
-        wide.append(residual)
+        residual = wide[sample * cols : (sample + 1) * cols]
         normalized = (residual - mean) * lax.rsqrt(var + EPSILON)
         value = normalized * gain + bias
         activated.append((value / (1.0 + jnp.exp(-value))).astype(BF16))
     x = jnp.concatenate(activated, 0)
     out_ref[...] = (
-        taps(x, w_ref[1], cols) + rim_ref[...] + jnp.concatenate(wide, 0)
+        taps(x, w_ref[1], cols) + rim_ref[...] + wide
     ).astype(BF16)
 
 
@@ -392,23 +390,16 @@
         flops=12 * every * channels * channels,
         chip=(0, 1, 2),
     )
-    residuals, stats = [], []
-    for s in range(samples):
-        small = pltpu.VMEM((8, LANES), F32)
-        res, stat = call(
-            functools.partial(merge_kernel, sample=s), [block, small],
-            *back[s], hid, w_out, spread, jnp.asarray(gather, BF16), *stats,
-            grid=(1,),
-            in_specs=[VMEM] * 4
-            + [pl.BlockSpec((tokens, channels), lambda i, s=s: (s, 0))]
-            + [VMEM] * (3 + len(stats)),
-            out_specs=[VMEM, VMEM],
-            flops=6 * 10 ** 9,
-            chip=(0, 1, 2, 3, 5) + (8,) * s,
-        )
-        residuals.append(res)
-        stats = [stat]
-    stat = stats[0]
+    small = pltpu.VMEM((8, LANES), F32)
+    residual, stat = call(
+        merge_kernel, [both, small],
+        *sum(back, []), hid, w_out, spread, jnp.asarray(gather, BF16),
+        grid=(1,),
+        in_specs=[VMEM] * (4 * samples + 4),
+        out_specs=[VMEM, VMEM],
+        flops=6 * 10 ** 9,
+        chip=tuple(range(4 * samples)) + (4 * samples + 1,),
+    )
     along_y = [stat] + [lax.ppermute(stat, "y", ring(by, y_count)) for by in shifts]
     stat = call(add_kernel, small, *along_y, in_specs=[VMEM] * 4, out_specs=VMEM, chip=range(4))
     along_z = [stat] + [lax.ppermute(stat, "z", ring(by, z_count)) for by in shifts]
@@ -417,10 +408,10 @@
             final_kernel, cols=cols, cells=float(count * tokens * (channels // GROUPS))
         ),
         jax.ShapeDtypeStruct((every, channels), BF16),
-        *residuals, *along_z, gn_gain, gn_bias, jnp.asarray(gather.T, BF16), conv_on_chip, rim,
-        in_specs=[VMEM] * 11,
+        residual, *along_z, gn_gain, gn_bias, jnp.asarray(gather.T, BF16), conv_on_chip, rim,
+        in_specs=[VMEM] * 10,
         out_specs=VMEM,
-        chip=(0, 1, 2, 3, 4, 5, 9, 10),
+        chip=(0, 1, 2, 3, 4, 8, 9),
         flops=6 * every * channels * channels,
     )
     return out.reshape(hidden.shape)

time: 100 us -> 84.8 us (0.85)
  the two profiles are of different devices: /device:TPU:2 before, /device:TPU:38 now
where the time goes in v8:
time: 84.8 us; the launch traced here: 84.7 us
  starting transfers between devices  39 us (46%)
  waiting for transfers between devices  23.9 us (28%)
  Pallas kernels  21.5 us (25%)
    pallas_call x9, Pallas kernels, call(): pl.pallas_call(kernel, out_shape=out_shape, compiler_params=pltpu.Compile...  21.5 us
    ppermute x4, starting transfers between devices, shards(): up, down = (lax.ppermute(one, 'z', ring(by, z_count)) for by in (1, 3))  8.77 us
    ppermute x6, starting transfers between devices, shards(): lax.ppermute(one, 'y', ring(-by, y_count))  8.74 us
    ppermute x6, waiting for transfers between devices, shards(): lax.ppermute(one, 'y', ring(-by, y_count))  6.68 us
    ppermute x3, waiting for transfers between devices, shards(): lax.ppermute(stat, 'z', ring(by, z_count))  5.63 us
    ppermute x3, starting transfers between devices, shards(): lax.ppermute(queries, 'y', ring(by, y_count))  5.3 us
    ppermute x3, waiting for transfers between devices, shards(): lax.ppermute(stat, 'y', ring(by, y_count))  4.51 us
    ppermute x1, waiting for transfers between devices, shards(): lax.ppermute(up, 'z', ring(1, z_count))  4.48 us
  transfers between devices with their start and end apart: 23, of which 8 were waited for; matrix products, arithmetic and copies ran while one was open for 0% of the time, Pallas kernels for 21%

profile of v8, /device:TPU:38, one launch (start us, length us, event | category | flops | bytes accessed | tf_op | source)
XLA Modules:
  0.0 84.7 jit_solution(7898555932578733128)
XLA Ops:
  0.0 0.0 copy-start.9
  0.0 1.4 %shard_map.146 = (bf16[128,640]{1,0:T(8,128)(2,1)S(1)}, bf16[128,640]{1,0:T(8,128)(2,1)S(1)}) custom-call(bf16[256,640]{1,0:T(8,128)(2,1)} %bitcast.8, f32[640]{0:T(1024)} %gain_ref.4, f32[640]{0:T(1024)} %bias_ref.5), custom_call_target="tpu_custom_call" | custom-call | flops 6000000000 | bytes 1000000 | tf_op jit(solution)/shard_map/pallas_call | solution.py:279
  1.4 3.3 %collective-permute-start.3 = (bf16[128,640]{1,0:T(8,128)(2,1)S(1)}, bf16[128,640]{1,0:T(8,128)(2,1)S(1)}, u32[]{:S(2)}, u32[]{:S(2)}) collective-permute-start(bf16[128,640]{1,0:T(8,128)(2,1)S(1)} %get-tuple-element.21.refs_1_), channel_id=1, source_target_pairs={{0,1},{1,2},{2,3},{3,0},{4,5},{5,6},{6,7},{7,4},{8,9},{9,10},{10,1... | collective-permute-start | bytes 491528 | tf_op jit(solution)/shard_map/ppermute | solution.py:316
  4.8 2.2 %collective-permute-start.5 = (bf16[128,640]{1,0:T(8,128)(2,1)S(1)}, bf16[128,640]{1,0:T(8,128)(2,1)S(1)}, u32[]{:S(2)}, u32[]{:S(2)}) collective-permute-start(bf16[128,640]{1,0:T(8,128)(2,1)S(1)} %get-tuple-element.21.refs_1_), channel_id=1, source_target_pairs={{0,3},{1,0},{2,1},{3,2},{4,7},{5,4},{6,5},{7,6},{8,11},{9,8},{10,9... | collective-permute-start | bytes 491528 | tf_op jit(solution)/shard_map/ppermute | solution.py:316
  7.0 0.0 copy-done.5
  7.0 0.0 copy-done.7
  7.0 0.0 copy-done.8
  7.0 0.0 copy-done.9
  7.0 0.7 shard_map.145
  7.7 1.7 %collective-permute-start = (bf16[256,640]{1,0:T(8,128)(2,1)S(1)}, bf16[256,640]{1,0:T(8,128)(2,1)S(1)}, u32[]{:S(2)}, u32[]{:S(2)}) collective-permute-start(bf16[256,640]{1,0:T(8,128)(2,1)S(1)} %get-tuple-element.20.q0_ref), channel_id=1, source_target_pairs={{0,4},{4,8},{8,12},{12,0},{1,5},{5,9},{9,13},{13,1},{2,6},{6,10},{... | collective-permute-start | bytes 983048 | tf_op jit(solution)/shard_map/ppermute | solution.py:328
  9.4 1.7 %collective-permute-start.1 = (bf16[256,640]{1,0:T(8,128)(2,1)S(1)}, bf16[256,640]{1,0:T(8,128)(2,1)S(1)}, u32[]{:S(2)}, u32[]{:S(2)}) collective-permute-start(bf16[256,640]{1,0:T(8,128)(2,1)S(1)} %get-tuple-element.20.q0_ref), channel_id=1, source_target_pairs={{0,12},{4,0},{8,4},{12,8},{1,13},{5,1},{9,5},{13,9},{2,14},{6,2},{... | collective-permute-start | bytes 983048 | tf_op jit(solution)/shard_map/ppermute | solution.py:328
  11.1 2.0 %collective-permute-start.2 = (bf16[256,640]{1,0:T(8,128)(2,1)S(1)}, bf16[256,640]{1,0:T(8,128)(2,1)S(1)}, u32[]{:S(2)}, u32[]{:S(2)}) collective-permute-start(bf16[256,640]{1,0:T(8,128)(2,1)S(1)} %get-tuple-element.20.q0_ref), channel_id=1, source_target_pairs={{0,8},{4,12},{8,0},{12,4},{1,9},{5,13},{9,1},{13,5},{2,10},{6,14},... | collective-permute-start | bytes 983048 | tf_op jit(solution)/shard_map/ppermute | solution.py:328
  13.0 1.6 %collective-permute-done.3.z1_ref = bf16[128,640]{1,0:T(8,128)(2,1)S(1)} collective-permute-done((bf16[128,640]{1,0:T(8,128)(2,1)S(1)}, bf16[128,640]{1,0:T(8,128)(2,1)S(1)}, u32[]{:S(2)}, u32[]{:S(2)}) %collective-permute-start.3) | collective-permute-done | bytes 163872 | tf_op jit(solution)/shard_map/ppermute | solution.py:316
  14.6 2.3 %collective-permute-start.10 = (bf16[128,640]{1,0:T(8,128)(2,1)S(1)}, bf16[128,640]{1,0:T(8,128)(2,1)S(1)}, u32[]{:S(2)}, u32[]{:S(2)}) collective-permute-start(bf16[128,640]{1,0:T(8,128)(2,1)S(1)} %get-tuple-element.23.refs_2_), channel_id=1, source_target_pairs={{0,3},{1,0},{2,1},{3,2},{4,7},{5,4},{6,5},{7,6},{8,11},{9,8},{10,9... | collective-permute-start | bytes 491528 | tf_op jit(solution)/shard_map/ppermute | solution.py:316
  17.0 0.0 collective-permute-done.5.z3_ref
  17.0 2.2 %collective-permute-start.4 = (bf16[128,640]{1,0:T(8,128)(2,1)S(1)}, bf16[128,640]{1,0:T(8,128)(2,1)S(1)}, u32[]{:S(2)}, u32[]{:S(2)}) collective-permute-start(bf16[128,640]{1,0:T(8,128)(2,1)S(1)} %collective-permute-done.3.z1_ref), channel_id=1, source_target_pairs={{0,1},{1,2},{2,3},{3,0},{4,5},{5,6},{6,7},{7,4},{8,9},{9,10},{10,1... | collective-permute-start | bytes 491528 | tf_op jit(solution)/shard_map/ppermute | solution.py:317
  19.2 2.3 %shard_map.147.early_ref = bf16[512,1280]{1,0:T(8,128)(2,1)S(1)} custom-call(bf16[256,640]{1,0:T(8,128)(2,1)S(1)} %get-tuple-element.22.refs_0_, bf16[128,640]{1,0:T(8,128)(2,1)S(1)} %get-tuple-element.21.refs_1_, bf16[128,640]{1,0:T(8,128)(2,1)S(1)} %get-tuple-element.23.refs_2_, bf16[640,1920]{1,0:T(8,128)(2,1)S(1)} %copy-done.5, ...), custom_call_target="tpu_custom_call" | custom-call | flops 6000000000 | bytes 1000000 | tf_op jit(solution)/shard_map/pallas_call | solution.py:279
  21.5 1.0 %collective-permute-done.10.z3_ref = bf16[128,640]{1,0:T(8,128)(2,1)S(1)} collective-permute-done((bf16[128,640]{1,0:T(8,128)(2,1)S(1)}, bf16[128,640]{1,0:T(8,128)(2,1)S(1)}, u32[]{:S(2)}, u32[]{:S(2)}) %collective-permute-start.10) | collective-permute-done | bytes 163872 | tf_op jit(solution)/shard_map/ppermute | solution.py:316
  22.5 0.9 %collective-permute-start.9 = (bf16[128,640]{1,0:T(8,128)(2,1)S(1)}, bf16[128,640]{1,0:T(8,128)(2,1)S(1)}, u32[]{:S(2)}, u32[]{:S(2)}) collective-permute-start(bf16[128,640]{1,0:T(8,128)(2,1)S(1)} %get-tuple-element.23.refs_2_), channel_id=1, source_target_pairs={{0,1},{1,2},{2,3},{3,0},{4,5},{5,6},{6,7},{7,4},{8,9},{9,10},{10,1... | collective-permute-start | bytes 491528 | tf_op jit(solution)/shard_map/ppermute | solution.py:316
  23.4 0.0 collective-permute-done.q1_ref
  23.4 3.3 %collective-permute-start.11 = (bf16[128,640]{1,0:T(8,128)(2,1)S(1)}, bf16[128,640]{1,0:T(8,128)(2,1)S(1)}, u32[]{:S(2)}, u32[]{:S(2)}) collective-permute-start(bf16[128,640]{1,0:T(8,128)(2,1)S(1)} %collective-permute-done.10.z3_ref), channel_id=1, source_target_pairs={{0,3},{1,0},{2,1},{3,2},{4,7},{5,4},{6,5},{7,6},{8,11},{9,8},{10,9... | collective-permute-start | bytes 491528 | tf_op jit(solution)/shard_map/ppermute | solution.py:317
  26.7 0.0 collective-permute-done.1.q2_ref
  26.7 0.0 collective-permute-done.2.q3_ref
  26.7 4.5 %collective-permute-done.4.z2_ref = bf16[128,640]{1,0:T(8,128)(2,1)S(1)} collective-permute-done((bf16[128,640]{1,0:T(8,128)(2,1)S(1)}, bf16[128,640]{1,0:T(8,128)(2,1)S(1)}, u32[]{:S(2)}, u32[]{:S(2)}) %collective-permute-start.4) | collective-permute-done | bytes 163872 | tf_op jit(solution)/shard_map/ppermute | solution.py:317
  31.2 5.8 %shard_map.148 = (bf16[128,768]{1,0:T(8,128)(2,1)S(1)}, bf16[128,768]{1,0:T(8,128)(2,1)S(1)}, bf16[128,768]{1,0:T(8,128)(2,1)S(1)}, bf16[128,768]{1,0:T(8,128)(2,1)S(1)}) custom-call(bf16[256,640]{1,0:T(8,128)(2,1)S(1)} %get-tuple-element.20.q0_ref, bf16[256,640]{1,0:T(8,128)(2,1)S(1)} %collective-permute-done.q1_ref, ...), custom_call_target="tpu_custom_call" | custom-call | flops 6000000000 | bytes 1000000 | tf_op jit(solution)/shard_map/pallas_call | solution.py:279
  37.0 2.2 %collective-permute-start.6 = (bf16[128,768]{1,0:T(8,128)(2,1)S(1)}, bf16[128,768]{1,0:T(8,128)(2,1)S(1)}, u32[]{:S(2)}, u32[]{:S(2)}) collective-permute-start(bf16[128,768]{1,0:T(8,128)(2,1)S(1)} %get-tuple-element.25), channel_id=1, source_target_pairs={{0,12},{4,0},{8,4},{12,8},{1,13},{5,1},{9,5},{13,9},{2,14},{6,2},{... | collective-permute-start | bytes 589832 | tf_op jit(solution)/shard_map/ppermute | solution.py:381
  39.2 0.0 collective-permute-start.7
  39.3 0.0 copy-start.11
  39.3 2.5 %collective-permute-start.8 = (bf16[128,768]{1,0:T(8,128)(2,1)S(1)}, bf16[128,768]{1,0:T(8,128)(2,1)S(1)}, u32[]{:S(2)}, u32[]{:S(2)}) collective-permute-start(bf16[128,768]{1,0:T(8,128)(2,1)S(1)} %get-tuple-element.27), channel_id=1, source_target_pairs={{0,8},{4,12},{8,0},{12,4},{1,9},{5,13},{9,1},{13,5},{2,10},{6,14},... | collective-permute-start | bytes 589832 | tf_op jit(solution)/shard_map/ppermute | solution.py:381
  41.7 0.0 collective-permute-done.9.z1_ref
  41.7 0.0 collective-permute-done.11.z2_ref
  41.7 5.8 %shard_map.149 = (bf16[128,768]{1,0:T(8,128)(2,1)S(1)}, bf16[128,768]{1,0:T(8,128)(2,1)S(1)}, bf16[128,768]{1,0:T(8,128)(2,1)S(1)}, bf16[128,768]{1,0:T(8,128)(2,1)S(1)}, bf16[3,3,640,640]{3,2,1,0:T(8,128)(2,1)S(1)}) custom-call(bf16[256,640]{1,0:T(8,128)(2,1)S(1)} %get-tuple-element.20.q0_ref, bf16[256,640]{1,0:T(8,128)(2,1)S(1)} %collective-permute-done.q1_ref, ...), custom_call_target="tpu_custom_call" | custom-call | flops 6000000000 | bytes 1000000 | tf_op jit(solution)/shard_map/pallas_call | solution.py:279
  47.6 1.2 %collective-permute-start.12 = (bf16[128,768]{1,0:T(8,128)(2,1)S(1)}, bf16[128,768]{1,0:T(8,128)(2,1)S(1)}, u32[]{:S(2)}, u32[]{:S(2)}) collective-permute-start(bf16[128,768]{1,0:T(8,128)(2,1)S(1)} %get-tuple-element.29), channel_id=1, source_target_pairs={{0,12},{4,0},{8,4},{12,8},{1,13},{5,1},{9,5},{13,9},{2,14},{6,2},{... | collective-permute-start | bytes 589832 | tf_op jit(solution)/shard_map/ppermute | solution.py:381
  48.7 0.9 %collective-permute-start.13 = (bf16[128,768]{1,0:T(8,128)(2,1)S(1)}, bf16[128,768]{1,0:T(8,128)(2,1)S(1)}, u32[]{:S(2)}, u32[]{:S(2)}) collective-permute-start(bf16[128,768]{1,0:T(8,128)(2,1)S(1)} %get-tuple-element.30), channel_id=1, source_target_pairs={{0,4},{4,8},{8,12},{12,0},{1,5},{5,9},{9,13},{13,1},{2,6},{6,10},{... | collective-permute-start | bytes 589832 | tf_op jit(solution)/shard_map/ppermute | solution.py:381
  49.7 0.0 collective-permute-done.6.refs_1_
  49.7 1.9 %collective-permute-start.14 = (bf16[128,768]{1,0:T(8,128)(2,1)S(1)}, bf16[128,768]{1,0:T(8,128)(2,1)S(1)}, u32[]{:S(2)}, u32[]{:S(2)}) collective-permute-start(bf16[128,768]{1,0:T(8,128)(2,1)S(1)} %get-tuple-element.31), channel_id=1, source_target_pairs={{0,8},{4,12},{8,0},{12,4},{1,9},{5,13},{9,1},{13,5},{2,10},{6,14},... | collective-permute-start | bytes 589832 | tf_op jit(solution)/shard_map/ppermute | solution.py:381
  51.6 0.0 collective-permute-done.7.refs_2_
  51.6 0.0 copy-done.12
  51.6 1.3 %collective-permute-start.21 = (bf16[256,640]{1,0:T(8,128)(2,1)S(1)}, bf16[256,640]{1,0:T(8,128)(2,1)S(1)}, u32[]{:S(2)}, u32[]{:S(2)}) collective-permute-start(bf16[256,640]{1,0:T(8,128)(2,1)S(1)} %bitcast.9), channel_id=1, source_target_pairs={{0,1},{1,2},{2,3},{3,4},{4,5},{5,6},{6,7},{7,8},{8,9},{9,10},{10,1... | collective-permute-start | bytes 983048 | tf_op jit(solution)/shard_map/ppermute | solution.py:344
  52.9 0.0 collective-permute-done.8.refs_3_
  52.9 1.3 %collective-permute-start.22 = (bf16[256,640]{1,0:T(8,128)(2,1)S(1)}, bf16[256,640]{1,0:T(8,128)(2,1)S(1)}, u32[]{:S(2)}, u32[]{:S(2)}) collective-permute-start(bf16[256,640]{1,0:T(8,128)(2,1)S(1)} %bitcast.10), channel_id=1, source_target_pairs={{1,0},{2,1},{3,2},{4,3},{5,4},{6,5},{7,6},{8,7},{9,8},{10,9},{11,1... | collective-permute-start | bytes 983048 | tf_op jit(solution)/shard_map/ppermute | solution.py:345
  54.2 0.0 collective-permute-done.12.refs_5_
  54.3 2.1 %collective-permute-done.13.refs_6_ = bf16[128,768]{1,0:T(8,128)(2,1)S(1)} collective-permute-done((bf16[128,768]{1,0:T(8,128)(2,1)S(1)}, bf16[128,768]{1,0:T(8,128)(2,1)S(1)}, u32[]{:S(2)}, u32[]{:S(2)}) %collective-permute-start.13) | collective-permute-done | bytes 196640 | tf_op jit(solution)/shard_map/ppermute | solution.py:381
  56.4 4.5 %collective-permute-done.14.refs_7_ = bf16[128,768]{1,0:T(8,128)(2,1)S(1)} collective-permute-done((bf16[128,768]{1,0:T(8,128)(2,1)S(1)}, bf16[128,768]{1,0:T(8,128)(2,1)S(1)}, u32[]{:S(2)}, u32[]{:S(2)}) %collective-permute-start.14) | collective-permute-done | bytes 196640 | tf_op jit(solution)/shard_map/ppermute | solution.py:381
  60.9 0.0 copy-start.1
  60.9 0.0 copy-start.4
  61.0 1.5 %shard_map.150 = (bf16[256,640]{1,0:T(8,128)(2,1)S(1)}, f32[8,128]{1,0:T(8,128)S(1)}) custom-call(bf16[128,768]{1,0:T(8,128)(2,1)S(1)} %get-tuple-element.24.refs_0_, bf16[128,768]{1,0:T(8,128)(2,1)S(1)} %collective-permute-done.6.refs_1_, bf16[128,768]{1,0:T(8,128)(2,1)S(1)} %collective-permute-done.7.refs_2_, ...), custom_call_target="tpu_custom_call" | custom-call | flops 6000000000 | bytes 1000000 | tf_op jit(solution)/shard_map/pallas_call | solution.py:279
  62.5 0.9 %collective-permute-start.15 = (f32[8,128]{1,0:T(8,128)S(1)}, f32[8,128]{1,0:T(8,128)S(1)}, u32[]{:S(2)}, u32[]{:S(2)}) collective-permute-start(f32[8,128]{1,0:T(8,128)S(1)} %get-tuple-element.33.refs_0_), channel_id=1, source_target_pairs={{0,4},{4,8},{8,12},{12,0},{1,5},{5,9},{9,13},{13,1},{2,6},{6,10},{... | collective-permute-start | bytes 12296 | tf_op jit(solution)/shard_map/ppermute | solution.py:403
  63.4 2.4 %collective-permute-start.16 = (f32[8,128]{1,0:T(8,128)S(1)}, f32[8,128]{1,0:T(8,128)S(1)}, u32[]{:S(2)}, u32[]{:S(2)}) collective-permute-start(f32[8,128]{1,0:T(8,128)S(1)} %get-tuple-element.33.refs_0_), channel_id=1, source_target_pairs={{0,12},{4,0},{8,4},{12,8},{1,13},{5,1},{9,5},{13,9},{2,14},{6,2},{... | collective-permute-start | bytes 12296 | tf_op jit(solution)/shard_map/ppermute | solution.py:403
  65.8 0.6 collective-permute-start.17
  66.4 1.0 %collective-permute-done.15.refs_1_ = f32[8,128]{1,0:T(8,128)S(1)} collective-permute-done((f32[8,128]{1,0:T(8,128)S(1)}, f32[8,128]{1,0:T(8,128)S(1)}, u32[]{:S(2)}, u32[]{:S(2)}) %collective-permute-start.15) | collective-permute-done | bytes 4128 | tf_op jit(solution)/shard_map/ppermute | solution.py:403
  67.4 0.0 collective-permute-done.16.refs_2_
  67.4 3.5 %collective-permute-done.17.refs_3_ = f32[8,128]{1,0:T(8,128)S(1)} collective-permute-done((f32[8,128]{1,0:T(8,128)S(1)}, f32[8,128]{1,0:T(8,128)S(1)}, u32[]{:S(2)}, u32[]{:S(2)}) %collective-permute-start.17) | collective-permute-done | bytes 4128 | tf_op jit(solution)/shard_map/ppermute | solution.py:403
  70.9 0.0 collective-permute-start.18
  70.9 4.1 %collective-permute-start.19 = (f32[8,128]{1,0:T(8,128)S(1)}, f32[8,128]{1,0:T(8,128)S(1)}, u32[]{:S(2)}, u32[]{:S(2)}) collective-permute-start(f32[8,128]{1,0:T(8,128)S(1)} %shard_map.151.s0_ref), channel_id=1, source_target_pairs={{0,3},{1,0},{2,1},{3,2},{4,7},{5,4},{6,5},{7,6},{8,11},{9,8},{10,9... | collective-permute-start | bytes 12296 | tf_op jit(solution)/shard_map/ppermute | solution.py:405
  75.0 0.0 collective-permute-start.20
  75.1 0.0 collective-permute-done.21.above_ref
  75.1 0.0 collective-permute-done.22.below_ref
  75.1 1.8 %shard_map.152.rim_ref = f32[256,640]{1,0:T(8,128)S(1)} custom-call(bf16[256,640]{1,0:T(8,128)(2,1)S(1)} %collective-permute-done.21.above_ref, bf16[256,640]{1,0:T(8,128)(2,1)S(1)} %collective-permute-done.22.below_ref, bf16[3,3,640,640]{3,2,1,0:T(8,128)(2,1)S(1)} %get-tuple-element.34.w_ref, f32[640]{0:T(1024)S(1)} %copy-done.4, f32[2,640]{1,0:T(2,128)S(1)} %copy-done.1), custom_call_target="tpu_custom_call" | custom-call | flops 1258291200 | bytes 1000000 | tf_op jit(solution)/shard_map/pallas_call | solution.py:279
  76.9 0.0 collective-permute-done.18.s1_ref
  76.9 0.0 collective-permute-done.19.s2_ref
  76.9 5.6 %collective-permute-done.20.s3_ref = f32[8,128]{1,0:T(8,128)S(1)} collective-permute-done((f32[8,128]{1,0:T(8,128)S(1)}, f32[8,128]{1,0:T(8,128)S(1)}, u32[]{:S(2)}, u32[]{:S(2)}) %collective-permute-start.20) | collective-permute-done | bytes 4128 | tf_op jit(solution)/shard_map/ppermute | solution.py:405
  82.6 0.0 copy-done.2
  82.6 2.1 %shard_map.153 = bf16[256,640]{1,0:T(8,128)(2,1)} custom-call(bf16[256,640]{1,0:T(8,128)(2,1)S(1)} %get-tuple-element.32.res_ref, f32[8,128]{1,0:T(8,128)S(1)} %shard_map.151.s0_ref, f32[8,128]{1,0:T(8,128)S(1)} %collective-permute-done.18.s1_ref, f32[8,128]{1,0:T(8,128)S(1)} %collective-permute-done.19.s2_ref, f32[8,128]{1,0:T(8,128)S(1)} %collective-permute-done.20.s3_ref, ...), custom_call_target="tpu_custom_call" | custom-call | flops 629145600 | bytes 1000000 | tf_op jit(solution)/shard_map/pallas_call | solution.py:279
  (17 shorter events, 0.0 us)
Async XLA Ops:
  0.0 7.0 %copy-start.5 = (bf16[640,1920]{1,0:T(8,128)(2,1)S(1)}, bf16[640,1920]{1,0:T(8,128)(2,1)}, u32[]{:S(2)}) copy-start(bf16[640,1920]{1,0:T(8,128)(2,1)} %wv_ref.3) | copy-start | bytes 7372804
  0.0 7.0 %copy-start.7 = (bf16[2,1,128,640]{3,2,1,0:T(8,128)(2,1)S(1)}, bf16[2,1,128,640]{3,2,1,0:T(8,128)(2,1)}, u32[]{:S(2)}) copy-start(bf16[2,1,128,640]{3,2,1,0:T(8,128)(2,1)} %param.15) | copy-start | bytes 983044
  0.0 7.0 %copy-start.8 = (f32[640]{0:T(1024)S(1)}, f32[640]{0:T(1024)}, u32[]{:S(2)}) copy-start(f32[640]{0:T(1024)} %gain_ref.4) | copy-start | bytes 7684
  0.0 7.0 %copy-start.9 = (f32[640]{0:T(1024)S(1)}, f32[640]{0:T(1024)}, u32[]{:S(2)}) copy-start(f32[640]{0:T(1024)} %bias_ref.5) | copy-start | bytes 7684
  1.4 13.2 %collective-permute-start.3 = (bf16[128,640]{1,0:T(8,128)(2,1)S(1)}, bf16[128,640]{1,0:T(8,128)(2,1)S(1)}, u32[]{:S(2)}, u32[]{:S(2)}) collective-permute-start(bf16[128,640]{1,0:T(8,128)(2,1)S(1)} %get-tuple-element.21.refs_1_), channel_id=1, source_target_pairs={{0,1},{1,2},{2,3},{3,0},{4,5},{5,6},{6,7},{7,4},{8,9},{9,10},{10,1... | collective-permute-start | bytes 491528 | tf_op jit(solution)/shard_map/ppermute | solution.py:316
  4.8 12.2 %collective-permute-start.5 = (bf16[128,640]{1,0:T(8,128)(2,1)S(1)}, bf16[128,640]{1,0:T(8,128)(2,1)S(1)}, u32[]{:S(2)}, u32[]{:S(2)}) collective-permute-start(bf16[128,640]{1,0:T(8,128)(2,1)S(1)} %get-tuple-element.21.refs_1_), channel_id=1, source_target_pairs={{0,3},{1,0},{2,1},{3,2},{4,7},{5,4},{6,5},{7,6},{8,11},{9,8},{10,9... | collective-permute-start | bytes 491528 | tf_op jit(solution)/shard_map/ppermute | solution.py:316
  7.7 15.7 %collective-permute-start = (bf16[256,640]{1,0:T(8,128)(2,1)S(1)}, bf16[256,640]{1,0:T(8,128)(2,1)S(1)}, u32[]{:S(2)}, u32[]{:S(2)}) collective-permute-start(bf16[256,640]{1,0:T(8,128)(2,1)S(1)} %get-tuple-element.20.q0_ref), channel_id=1, source_target_pairs={{0,4},{4,8},{8,12},{12,0},{1,5},{5,9},{9,13},{13,1},{2,6},{6,10},{... | collective-permute-start | bytes 983048 | tf_op jit(solution)/shard_map/ppermute | solution.py:328
  9.4 17.3 %collective-permute-start.1 = (bf16[256,640]{1,0:T(8,128)(2,1)S(1)}, bf16[256,640]{1,0:T(8,128)(2,1)S(1)}, u32[]{:S(2)}, u32[]{:S(2)}) collective-permute-start(bf16[256,640]{1,0:T(8,128)(2,1)S(1)} %get-tuple-element.20.q0_ref), channel_id=1, source_target_pairs={{0,12},{4,0},{8,4},{12,8},{1,13},{5,1},{9,5},{13,9},{2,14},{6,2},{... | collective-permute-start | bytes 983048 | tf_op jit(solution)/shard_map/ppermute | solution.py:328
  11.1 15.6 %collective-permute-start.2 = (bf16[256,640]{1,0:T(8,128)(2,1)S(1)}, bf16[256,640]{1,0:T(8,128)(2,1)S(1)}, u32[]{:S(2)}, u32[]{:S(2)}) collective-permute-start(bf16[256,640]{1,0:T(8,128)(2,1)S(1)} %get-tuple-element.20.q0_ref), channel_id=1, source_target_pairs={{0,8},{4,12},{8,0},{12,4},{1,9},{5,13},{9,1},{13,5},{2,10},{6,14},... | collective-permute-start | bytes 983048 | tf_op jit(solution)/shard_map/ppermute | solution.py:328
  14.6 7.9 %collective-permute-start.10 = (bf16[128,640]{1,0:T(8,128)(2,1)S(1)}, bf16[128,640]{1,0:T(8,128)(2,1)S(1)}, u32[]{:S(2)}, u32[]{:S(2)}) collective-permute-start(bf16[128,640]{1,0:T(8,128)(2,1)S(1)} %get-tuple-element.23.refs_2_), channel_id=1, source_target_pairs={{0,3},{1,0},{2,1},{3,2},{4,7},{5,4},{6,5},{7,6},{8,11},{9,8},{10,9... | collective-permute-start | bytes 491528 | tf_op jit(solution)/shard_map/ppermute | solution.py:316
  17.0 14.2 %collective-permute-start.4 = (bf16[128,640]{1,0:T(8,128)(2,1)S(1)}, bf16[128,640]{1,0:T(8,128)(2,1)S(1)}, u32[]{:S(2)}, u32[]{:S(2)}) collective-permute-start(bf16[128,640]{1,0:T(8,128)(2,1)S(1)} %collective-permute-done.3.z1_ref), channel_id=1, source_target_pairs={{0,1},{1,2},{2,3},{3,0},{4,5},{5,6},{6,7},{7,4},{8,9},{9,10},{10,1... | collective-permute-start | bytes 491528 | tf_op jit(solution)/shard_map/ppermute | solution.py:317
  22.5 19.2 %collective-permute-start.9 = (bf16[128,640]{1,0:T(8,128)(2,1)S(1)}, bf16[128,640]{1,0:T(8,128)(2,1)S(1)}, u32[]{:S(2)}, u32[]{:S(2)}) collective-permute-start(bf16[128,640]{1,0:T(8,128)(2,1)S(1)} %get-tuple-element.23.refs_2_), channel_id=1, source_target_pairs={{0,1},{1,2},{2,3},{3,0},{4,5},{5,6},{6,7},{7,4},{8,9},{9,10},{10,1... | collective-permute-start | bytes 491528 | tf_op jit(solution)/shard_map/ppermute | solution.py:316
  23.4 18.3 %collective-permute-start.11 = (bf16[128,640]{1,0:T(8,128)(2,1)S(1)}, bf16[128,640]{1,0:T(8,128)(2,1)S(1)}, u32[]{:S(2)}, u32[]{:S(2)}) collective-permute-start(bf16[128,640]{1,0:T(8,128)(2,1)S(1)} %collective-permute-done.10.z3_ref), channel_id=1, source_target_pairs={{0,3},{1,0},{2,1},{3,2},{4,7},{5,4},{6,5},{7,6},{8,11},{9,8},{10,9... | collective-permute-start | bytes 491528 | tf_op jit(solution)/shard_map/ppermute | solution.py:317
  37.0 12.7 %collective-permute-start.6 = (bf16[128,768]{1,0:T(8,128)(2,1)S(1)}, bf16[128,768]{1,0:T(8,128)(2,1)S(1)}, u32[]{:S(2)}, u32[]{:S(2)}) collective-permute-start(bf16[128,768]{1,0:T(8,128)(2,1)S(1)} %get-tuple-element.25), channel_id=1, source_target_pairs={{0,12},{4,0},{8,4},{12,8},{1,13},{5,1},{9,5},{13,9},{2,14},{6,2},{... | collective-permute-start | bytes 589832 | tf_op jit(solution)/shard_map/ppermute | solution.py:381
  39.2 12.4 %collective-permute-start.7 = (bf16[128,768]{1,0:T(8,128)(2,1)S(1)}, bf16[128,768]{1,0:T(8,128)(2,1)S(1)}, u32[]{:S(2)}, u32[]{:S(2)}) collective-permute-start(bf16[128,768]{1,0:T(8,128)(2,1)S(1)} %get-tuple-element.26), channel_id=1, source_target_pairs={{0,4},{4,8},{8,12},{12,0},{1,5},{5,9},{9,13},{13,1},{2,6},{6,10},{... | collective-permute-start | bytes 589832 | tf_op jit(solution)/shard_map/ppermute | solution.py:381
  39.3 12.4 %copy-start.12 = (bf16[2,1,128,640]{3,2,1,0:T(8,128)(2,1)S(1)}, bf16[2,1,128,640]{3,2,1,0:T(8,128)(2,1)}, u32[]{:S(2)}) copy-start(bf16[2,1,128,640]{3,2,1,0:T(8,128)(2,1)} %param.17) | copy-start | bytes 983044
  39.3 21.7 %copy-start.6 = (bf16[640,640]{1,0:T(8,128)(2,1)S(1)}, bf16[640,640]{1,0:T(8,128)(2,1)}, u32[]{:S(2)}) copy-start(bf16[640,640]{1,0:T(8,128)(2,1)} %refs_9_.1) | copy-start | bytes 2457604
  39.3 21.7 %copy-start.10 = (bf16[128,640]{1,0:T(8,128)(2,1)S(1)}, bf16[128,640]{1,0:T(8,128)(2,1)}, u32[]{:S(2)}) copy-start(bf16[128,640]{1,0:T(8,128)(2,1)} %constant.6.clone.refs_10_) | copy-start | bytes 491524
  39.3 21.7 %copy-start.11 = (bf16[640,128]{1,0:T(8,128)(2,1)S(1)}, bf16[640,128]{1,0:T(8,128)(2,1)}, u32[]{:S(2)}) copy-start(bf16[640,128]{1,0:T(8,128)(2,1)} %constant.7.clone.refs_11_) | copy-start | bytes 491524
  39.3 13.7 %collective-permute-start.8 = (bf16[128,768]{1,0:T(8,128)(2,1)S(1)}, bf16[128,768]{1,0:T(8,128)(2,1)S(1)}, u32[]{:S(2)}, u32[]{:S(2)}) collective-permute-start(bf16[128,768]{1,0:T(8,128)(2,1)S(1)} %get-tuple-element.27), channel_id=1, source_target_pairs={{0,8},{4,12},{8,0},{12,4},{1,9},{5,13},{9,1},{13,5},{2,10},{6,14},... | collective-permute-start | bytes 589832 | tf_op jit(solution)/shard_map/ppermute | solution.py:381
  47.6 6.7 %collective-permute-start.12 = (bf16[128,768]{1,0:T(8,128)(2,1)S(1)}, bf16[128,768]{1,0:T(8,128)(2,1)S(1)}, u32[]{:S(2)}, u32[]{:S(2)}) collective-permute-start(bf16[128,768]{1,0:T(8,128)(2,1)S(1)} %get-tuple-element.29), channel_id=1, source_target_pairs={{0,12},{4,0},{8,4},{12,8},{1,13},{5,1},{9,5},{13,9},{2,14},{6,2},{... | collective-permute-start | bytes 589832 | tf_op jit(solution)/shard_map/ppermute | solution.py:381
  48.7 7.6 %collective-permute-start.13 = (bf16[128,768]{1,0:T(8,128)(2,1)S(1)}, bf16[128,768]{1,0:T(8,128)(2,1)S(1)}, u32[]{:S(2)}, u32[]{:S(2)}) collective-permute-start(bf16[128,768]{1,0:T(8,128)(2,1)S(1)} %get-tuple-element.30), channel_id=1, source_target_pairs={{0,4},{4,8},{8,12},{12,0},{1,5},{5,9},{9,13},{13,1},{2,6},{6,10},{... | collective-permute-start | bytes 589832 | tf_op jit(solution)/shard_map/ppermute | solution.py:381
  49.7 11.2 %collective-permute-start.14 = (bf16[128,768]{1,0:T(8,128)(2,1)S(1)}, bf16[128,768]{1,0:T(8,128)(2,1)S(1)}, u32[]{:S(2)}, u32[]{:S(2)}) collective-permute-start(bf16[128,768]{1,0:T(8,128)(2,1)S(1)} %get-tuple-element.31), channel_id=1, source_target_pairs={{0,8},{4,12},{8,0},{12,4},{1,9},{5,13},{9,1},{13,5},{2,10},{6,14},... | collective-permute-start | bytes 589832 | tf_op jit(solution)/shard_map/ppermute | solution.py:381
  51.6 23.4 %collective-permute-start.21 = (bf16[256,640]{1,0:T(8,128)(2,1)S(1)}, bf16[256,640]{1,0:T(8,128)(2,1)S(1)}, u32[]{:S(2)}, u32[]{:S(2)}) collective-permute-start(bf16[256,640]{1,0:T(8,128)(2,1)S(1)} %bitcast.9), channel_id=1, source_target_pairs={{0,1},{1,2},{2,3},{3,4},{4,5},{5,6},{6,7},{7,8},{8,9},{9,10},{10,1... | collective-permute-start | bytes 983048 | tf_op jit(solution)/shard_map/ppermute | solution.py:344
  52.9 22.1 %collective-permute-start.22 = (bf16[256,640]{1,0:T(8,128)(2,1)S(1)}, bf16[256,640]{1,0:T(8,128)(2,1)S(1)}, u32[]{:S(2)}, u32[]{:S(2)}) collective-permute-start(bf16[256,640]{1,0:T(8,128)(2,1)S(1)} %bitcast.10), channel_id=1, source_target_pairs={{1,0},{2,1},{3,2},{4,3},{5,4},{6,5},{7,6},{8,7},{9,8},{10,9},{11,1... | collective-permute-start | bytes 983048 | tf_op jit(solution)/shard_map/ppermute | solution.py:345
  60.9 14.1 %copy-start.1 = (f32[2,640]{1,0:T(2,128)S(1)}, f32[2,640]{1,0:T(2,128)}, u32[]{:S(2)}) copy-start(f32[2,640]{1,0:T(2,128)} %shift_ref.1) | copy-start | bytes 15364
  60.9 14.1 %copy-start.4 = (f32[640]{0:T(1024)S(1)}, f32[640]{0:T(1024)}, u32[]{:S(2)}) copy-start(f32[640]{0:T(1024)} %bias_ref.6) | copy-start | bytes 7684
  62.5 20.1 %copy-start = (bf16[128,640]{1,0:T(8,128)(2,1)S(1)}, bf16[128,640]{1,0:T(8,128)(2,1)}, u32[]{:S(2)}) copy-start(bf16[128,640]{1,0:T(8,128)(2,1)} %constant.8.clone.scatter_ref) | copy-start | bytes 491524
  62.5 20.1 %copy-start.2 = (f32[640]{0:T(1024)S(1)}, f32[640]{0:T(1024)}, u32[]{:S(2)}) copy-start(f32[640]{0:T(1024)} %gain_ref.5) | copy-start | bytes 7684
  62.5 20.1 %copy-start.3 = (f32[640]{0:T(1024)S(1)}, f32[640]{0:T(1024)}, u32[]{:S(2)}) copy-start(f32[640]{0:T(1024)} %bias_ref.7) | copy-start | bytes 7684
  62.5 4.9 %collective-permute-start.15 = (f32[8,128]{1,0:T(8,128)S(1)}, f32[8,128]{1,0:T(8,128)S(1)}, u32[]{:S(2)}, u32[]{:S(2)}) collective-permute-start(f32[8,128]{1,0:T(8,128)S(1)} %get-tuple-element.33.refs_0_), channel_id=1, source_target_pairs={{0,4},{4,8},{8,12},{12,0},{1,5},{5,9},{9,13},{13,1},{2,6},{6,10},{... | collective-permute-start | bytes 12296 | tf_op jit(solution)/shard_map/ppermute | solution.py:403
  63.4 4.0 %collective-permute-start.16 = (f32[8,128]{1,0:T(8,128)S(1)}, f32[8,128]{1,0:T(8,128)S(1)}, u32[]{:S(2)}, u32[]{:S(2)}) collective-permute-start(f32[8,128]{1,0:T(8,128)S(1)} %get-tuple-element.33.refs_0_), channel_id=1, source_target_pairs={{0,12},{4,0},{8,4},{12,8},{1,13},{5,1},{9,5},{13,9},{2,14},{6,2},{... | collective-permute-start | bytes 12296 | tf_op jit(solution)/shard_map/ppermute | solution.py:403
  65.8 5.1 %collective-permute-start.17 = (f32[8,128]{1,0:T(8,128)S(1)}, f32[8,128]{1,0:T(8,128)S(1)}, u32[]{:S(2)}, u32[]{:S(2)}) collective-permute-start(f32[8,128]{1,0:T(8,128)S(1)} %get-tuple-element.33.refs_0_), channel_id=1, source_target_pairs={{0,8},{4,12},{8,0},{12,4},{1,9},{5,13},{9,1},{13,5},{2,10},{6,14},... | collective-permute-start | bytes 12296 | tf_op jit(solution)/shard_map/ppermute | solution.py:403
  70.9 6.0 %collective-permute-start.18 = (f32[8,128]{1,0:T(8,128)S(1)}, f32[8,128]{1,0:T(8,128)S(1)}, u32[]{:S(2)}, u32[]{:S(2)}) collective-permute-start(f32[8,128]{1,0:T(8,128)S(1)} %shard_map.151.s0_ref), channel_id=1, source_target_pairs={{0,1},{1,2},{2,3},{3,0},{4,5},{5,6},{6,7},{7,4},{8,9},{9,10},{10,1... | collective-permute-start | bytes 12296 | tf_op jit(solution)/shard_map/ppermute | solution.py:405
  70.9 6.0 %collective-permute-start.19 = (f32[8,128]{1,0:T(8,128)S(1)}, f32[8,128]{1,0:T(8,128)S(1)}, u32[]{:S(2)}, u32[]{:S(2)}) collective-permute-start(f32[8,128]{1,0:T(8,128)S(1)} %shard_map.151.s0_ref), channel_id=1, source_target_pairs={{0,3},{1,0},{2,1},{3,2},{4,7},{5,4},{6,5},{7,6},{8,11},{9,8},{10,9... | collective-permute-start | bytes 12296 | tf_op jit(solution)/shard_map/ppermute | solution.py:405
  75.0 7.5 %collective-permute-start.20 = (f32[8,128]{1,0:T(8,128)S(1)}, f32[8,128]{1,0:T(8,128)S(1)}, u32[]{:S(2)}, u32[]{:S(2)}) collective-permute-start(f32[8,128]{1,0:T(8,128)S(1)} %shard_map.151.s0_ref), channel_id=1, source_target_pairs={{0,2},{1,3},{2,0},{3,1},{4,6},{5,7},{6,4},{7,5},{8,10},{9,11},{10,... | collective-permute-start | bytes 12296 | tf_op jit(solution)/shard_map/ppermute | solution.py:405

commit v9 on v8

--- a/solution.py
+++ b/solution.py
@@ -232,12 +232,15 @@
     return jnp.dot(unfolded, weights, preferred_element_type=F32)
 
 
-def rim_kernel(above_ref, below_ref, w_ref, bias_ref, shift_ref, out_ref, *, cols):
-    total = taps(above_ref[...], w_ref[0], cols) + taps(below_ref[...], w_ref[2], cols)
-    total += as_row(bias_ref)
+def above_kernel(x_ref, w_ref, bias_ref, shift_ref, out_ref, *, cols):
+    total = taps(x_ref[...], w_ref[0], cols) + as_row(bias_ref)
     for sample in range(total.shape[0] // cols):
         part = slice(sample * cols, (sample + 1) * cols)
         out_ref[part, :] = total[part] + shift_ref[sample : sample + 1, :]
+
+
+def below_kernel(x_ref, w_ref, above_ref, out_ref, *, cols):
+    out_ref[...] = taps(x_ref[...], w_ref[2], cols) + above_ref[...]
 
 
 def add_kernel(*refs):
@@ -381,14 +384,17 @@
             + [lax.ppermute(one, "y", ring(-by, y_count)) for one, by in zip(outs[1:4], shifts)]
         )
     conv_on_chip = outs[4]
+    rim = pltpu.VMEM((every, channels), F32)
+    upper = call(
+        functools.partial(above_kernel, cols=cols), rim,
+        above, conv_on_chip, conv_bias, time_shift,
+        in_specs=[VMEM] * 4, out_specs=VMEM, chip=(0, 1),
+        flops=6 * every * channels * channels,
+    )
     rim = call(
-        functools.partial(rim_kernel, cols=cols),
-        pltpu.VMEM((every, channels), F32),
-        above, below, conv_on_chip, conv_bias, time_shift,
-        in_specs=[VMEM] * 5,
-        out_specs=VMEM,
-        flops=12 * every * channels * channels,
-        chip=(0, 1, 2),
+        functools.partial(below_kernel, cols=cols), rim, below, conv_on_chip, upper,
+        in_specs=[VMEM] * 3, out_specs=VMEM, chip=(0, 1, 2),
+        flops=6 * every * channels * channels,
     )
     small = pltpu.VMEM((8, LANES), F32)
     residual, stat = call(

time: 84.8 us -> 86 us (1.014)
  the two profiles are of different devices: /device:TPU:38 before, /device:TPU:40 now
where the time goes in v9:
time: 86 us; the launch traced here: 85.8 us
  starting transfers between devices  44.9 us (52%)
  Pallas kernels  21.6 us (25%)
  waiting for transfers between devices  19 us (22%)
    pallas_call x10, Pallas kernels, call(): pl.pallas_call(kernel, out_shape=out_shape, compiler_params=pltpu.Compile...  21.6 us
    ppermute x6, starting transfers between devices, shards(): lax.ppermute(one, 'y', ring(-by, y_count))  9.24 us
    ppermute x4, starting transfers between devices, shards(): up, down = (lax.ppermute(one, 'z', ring(by, z_count)) for by in (1, 3))  8.78 us
    ppermute x1, waiting for transfers between devices, shards(): lax.ppermute(conv_rows, ('y', 'z'), [(i, i + 1) for i in range(count - 1)])  7.01 us
    ppermute x3, starting transfers between devices, shards(): lax.ppermute(stat, 'z', ring(by, z_count))  5.92 us
    ppermute x1, starting transfers between devices, shards(): lax.ppermute(conv_rows, ('y', 'z'), [(i, i + 1) for i in range(count - 1)])  4.82 us
    ppermute x3, waiting for transfers between devices, shards(): lax.ppermute(stat, 'z', ring(by, z_count))  4.78 us
    ppermute x3, starting transfers between devices, shards(): lax.ppermute(queries, 'y', ring(by, y_count))  4.4 us
  transfers between devices with their start and end apart: 23, of which 5 were waited for; matrix products, arithmetic and copies ran while one was open for 0% of the time, Pallas kernels for 21%

profile of v9, /device:TPU:40, one launch (start us, length us, event | category | flops | bytes accessed | tf_op | source)
XLA Modules:
  0.0 85.8 jit_solution(13709757462518931939)
XLA Ops:
  0.0 0.0 copy-start.9
  0.0 1.4 %shard_map.146 = (bf16[128,640]{1,0:T(8,128)(2,1)S(1)}, bf16[128,640]{1,0:T(8,128)(2,1)S(1)}) custom-call(bf16[256,640]{1,0:T(8,128)(2,1)} %bitcast.8, f32[640]{0:T(1024)} %gain_ref.4, f32[640]{0:T(1024)} %bias_ref.5), custom_call_target="tpu_custom_call" | custom-call | flops 6000000000 | bytes 1000000 | tf_op jit(solution)/shard_map/pallas_call | solution.py:282
  1.4 3.3 %collective-permute-start.3 = (bf16[128,640]{1,0:T(8,128)(2,1)S(1)}, bf16[128,640]{1,0:T(8,128)(2,1)S(1)}, u32[]{:S(2)}, u32[]{:S(2)}) collective-permute-start(bf16[128,640]{1,0:T(8,128)(2,1)S(1)} %get-tuple-element.21.refs_1_), channel_id=1, source_target_pairs={{0,1},{1,2},{2,3},{3,0},{4,5},{5,6},{6,7},{7,4},{8,9},{9,10},{10,1... | collective-permute-start | bytes 491528 | tf_op jit(solution)/shard_map/ppermute | solution.py:319
  4.8 2.2 %collective-permute-start.5 = (bf16[128,640]{1,0:T(8,128)(2,1)S(1)}, bf16[128,640]{1,0:T(8,128)(2,1)S(1)}, u32[]{:S(2)}, u32[]{:S(2)}) collective-permute-start(bf16[128,640]{1,0:T(8,128)(2,1)S(1)} %get-tuple-element.21.refs_1_), channel_id=1, source_target_pairs={{0,3},{1,0},{2,1},{3,2},{4,7},{5,4},{6,5},{7,6},{8,11},{9,8},{10,9... | collective-permute-start | bytes 491528 | tf_op jit(solution)/shard_map/ppermute | solution.py:319
  7.0 0.0 copy-done.5
  7.0 0.0 copy-done.8
  7.0 0.7 shard_map.145
  7.7 1.7 %collective-permute-start = (bf16[256,640]{1,0:T(8,128)(2,1)S(1)}, bf16[256,640]{1,0:T(8,128)(2,1)S(1)}, u32[]{:S(2)}, u32[]{:S(2)}) collective-permute-start(bf16[256,640]{1,0:T(8,128)(2,1)S(1)} %get-tuple-element.20.q0_ref), channel_id=1, source_target_pairs={{0,4},{4,8},{8,12},{12,0},{1,5},{5,9},{9,13},{13,1},{2,6},{6,10},{... | collective-permute-start | bytes 983048 | tf_op jit(solution)/shard_map/ppermute | solution.py:331
  9.4 0.4 collective-permute-start.1
  9.8 2.3 %collective-permute-start.2 = (bf16[256,640]{1,0:T(8,128)(2,1)S(1)}, bf16[256,640]{1,0:T(8,128)(2,1)S(1)}, u32[]{:S(2)}, u32[]{:S(2)}) collective-permute-start(bf16[256,640]{1,0:T(8,128)(2,1)S(1)} %get-tuple-element.20.q0_ref), channel_id=1, source_target_pairs={{0,8},{4,12},{8,0},{12,4},{1,9},{5,13},{9,1},{13,5},{2,10},{6,14},... | collective-permute-start | bytes 983048 | tf_op jit(solution)/shard_map/ppermute | solution.py:331
  12.1 2.5 %collective-permute-done.3.z1_ref = bf16[128,640]{1,0:T(8,128)(2,1)S(1)} collective-permute-done((bf16[128,640]{1,0:T(8,128)(2,1)S(1)}, bf16[128,640]{1,0:T(8,128)(2,1)S(1)}, u32[]{:S(2)}, u32[]{:S(2)}) %collective-permute-start.3) | collective-permute-done | bytes 163872 | tf_op jit(solution)/shard_map/ppermute | solution.py:319
  14.6 2.3 %collective-permute-start.10 = (bf16[128,640]{1,0:T(8,128)(2,1)S(1)}, bf16[128,640]{1,0:T(8,128)(2,1)S(1)}, u32[]{:S(2)}, u32[]{:S(2)}) collective-permute-start(bf16[128,640]{1,0:T(8,128)(2,1)S(1)} %get-tuple-element.23.refs_2_), channel_id=1, source_target_pairs={{0,3},{1,0},{2,1},{3,2},{4,7},{5,4},{6,5},{7,6},{8,11},{9,8},{10,9... | collective-permute-start | bytes 491528 | tf_op jit(solution)/shard_map/ppermute | solution.py:319
  17.0 0.0 collective-permute-done.5.z3_ref
  17.0 2.2 %collective-permute-start.4 = (bf16[128,640]{1,0:T(8,128)(2,1)S(1)}, bf16[128,640]{1,0:T(8,128)(2,1)S(1)}, u32[]{:S(2)}, u32[]{:S(2)}) collective-permute-start(bf16[128,640]{1,0:T(8,128)(2,1)S(1)} %collective-permute-done.3.z1_ref), channel_id=1, source_target_pairs={{0,1},{1,2},{2,3},{3,0},{4,5},{5,6},{6,7},{7,4},{8,9},{9,10},{10,1... | collective-permute-start | bytes 491528 | tf_op jit(solution)/shard_map/ppermute | solution.py:320
  19.2 2.3 %shard_map.147.early_ref = bf16[512,1280]{1,0:T(8,128)(2,1)S(1)} custom-call(bf16[256,640]{1,0:T(8,128)(2,1)S(1)} %get-tuple-element.22.refs_0_, bf16[128,640]{1,0:T(8,128)(2,1)S(1)} %get-tuple-element.21.refs_1_, bf16[128,640]{1,0:T(8,128)(2,1)S(1)} %get-tuple-element.23.refs_2_, bf16[640,1920]{1,0:T(8,128)(2,1)S(1)} %copy-done.5, ...), custom_call_target="tpu_custom_call" | custom-call | flops 6000000000 | bytes 1000000 | tf_op jit(solution)/shard_map/pallas_call | solution.py:282
  21.5 0.7 collective-permute-done.10.z3_ref
  22.2 0.9 %collective-permute-start.9 = (bf16[128,640]{1,0:T(8,128)(2,1)S(1)}, bf16[128,640]{1,0:T(8,128)(2,1)S(1)}, u32[]{:S(2)}, u32[]{:S(2)}) collective-permute-start(bf16[128,640]{1,0:T(8,128)(2,1)S(1)} %get-tuple-element.23.refs_2_), channel_id=1, source_target_pairs={{0,1},{1,2},{2,3},{3,0},{4,5},{5,6},{6,7},{7,4},{8,9},{9,10},{10,1... | collective-permute-start | bytes 491528 | tf_op jit(solution)/shard_map/ppermute | solution.py:319
  23.1 0.0 collective-permute-done.q1_ref
  23.1 3.3 %collective-permute-start.11 = (bf16[128,640]{1,0:T(8,128)(2,1)S(1)}, bf16[128,640]{1,0:T(8,128)(2,1)S(1)}, u32[]{:S(2)}, u32[]{:S(2)}) collective-permute-start(bf16[128,640]{1,0:T(8,128)(2,1)S(1)} %collective-permute-done.10.z3_ref), channel_id=1, source_target_pairs={{0,3},{1,0},{2,1},{3,2},{4,7},{5,4},{6,5},{7,6},{8,11},{9,8},{10,9... | collective-permute-start | bytes 491528 | tf_op jit(solution)/shard_map/ppermute | solution.py:320
  26.3 0.0 collective-permute-done.1.q2_ref
  26.3 0.0 collective-permute-done.2.q3_ref
  26.3 4.0 %collective-permute-done.4.z2_ref = bf16[128,640]{1,0:T(8,128)(2,1)S(1)} collective-permute-done((bf16[128,640]{1,0:T(8,128)(2,1)S(1)}, bf16[128,640]{1,0:T(8,128)(2,1)S(1)}, u32[]{:S(2)}, u32[]{:S(2)}) %collective-permute-start.4) | collective-permute-done | bytes 163872 | tf_op jit(solution)/shard_map/ppermute | solution.py:320
  30.3 5.8 %shard_map.148 = (bf16[128,768]{1,0:T(8,128)(2,1)S(1)}, bf16[128,768]{1,0:T(8,128)(2,1)S(1)}, bf16[128,768]{1,0:T(8,128)(2,1)S(1)}, bf16[128,768]{1,0:T(8,128)(2,1)S(1)}) custom-call(bf16[256,640]{1,0:T(8,128)(2,1)S(1)} %get-tuple-element.20.q0_ref, bf16[256,640]{1,0:T(8,128)(2,1)S(1)} %collective-permute-done.q1_ref, ...), custom_call_target="tpu_custom_call" | custom-call | flops 6000000000 | bytes 1000000 | tf_op jit(solution)/shard_map/pallas_call | solution.py:282
  36.2 1.3 %collective-permute-start.6 = (bf16[128,768]{1,0:T(8,128)(2,1)S(1)}, bf16[128,768]{1,0:T(8,128)(2,1)S(1)}, u32[]{:S(2)}, u32[]{:S(2)}) collective-permute-start(bf16[128,768]{1,0:T(8,128)(2,1)S(1)} %get-tuple-element.25), channel_id=1, source_target_pairs={{0,12},{4,0},{8,4},{12,8},{1,13},{5,1},{9,5},{13,9},{2,14},{6,2},{... | collective-permute-start | bytes 589832 | tf_op jit(solution)/shard_map/ppermute | solution.py:384
  37.5 0.8 collective-permute-start.7
  38.3 3.8 %collective-permute-start.8 = (bf16[128,768]{1,0:T(8,128)(2,1)S(1)}, bf16[128,768]{1,0:T(8,128)(2,1)S(1)}, u32[]{:S(2)}, u32[]{:S(2)}) collective-permute-start(bf16[128,768]{1,0:T(8,128)(2,1)S(1)} %get-tuple-element.27), channel_id=1, source_target_pairs={{0,8},{4,12},{8,0},{12,4},{1,9},{5,13},{9,1},{13,5},{2,10},{6,14},... | collective-permute-start | bytes 589832 | tf_op jit(solution)/shard_map/ppermute | solution.py:384
  42.0 0.0 collective-permute-done.9.z1_ref
  42.0 0.0 collective-permute-done.11.z2_ref
  42.0 5.8 %shard_map.149 = (bf16[128,768]{1,0:T(8,128)(2,1)S(1)}, bf16[128,768]{1,0:T(8,128)(2,1)S(1)}, bf16[128,768]{1,0:T(8,128)(2,1)S(1)}, bf16[128,768]{1,0:T(8,128)(2,1)S(1)}, bf16[3,3,640,640]{3,2,1,0:T(8,128)(2,1)S(1)}) custom-call(bf16[256,640]{1,0:T(8,128)(2,1)S(1)} %get-tuple-element.20.q0_ref, bf16[256,640]{1,0:T(8,128)(2,1)S(1)} %collective-permute-done.q1_ref, ...), custom_call_target="tpu_custom_call" | custom-call | flops 6000000000 | bytes 1000000 | tf_op jit(solution)/shard_map/pallas_call | solution.py:282
  47.9 0.2 collective-permute-start.12
  48.1 1.9 %collective-permute-start.13 = (bf16[128,768]{1,0:T(8,128)(2,1)S(1)}, bf16[128,768]{1,0:T(8,128)(2,1)S(1)}, u32[]{:S(2)}, u32[]{:S(2)}) collective-permute-start(bf16[128,768]{1,0:T(8,128)(2,1)S(1)} %get-tuple-element.30), channel_id=1, source_target_pairs={{0,4},{4,8},{8,12},{12,0},{1,5},{5,9},{9,13},{13,1},{2,6},{6,10},{... | collective-permute-start | bytes 589832 | tf_op jit(solution)/shard_map/ppermute | solution.py:384
  50.0 0.0 collective-permute-done.6.refs_1_
  50.0 1.3 %collective-permute-start.14 = (bf16[128,768]{1,0:T(8,128)(2,1)S(1)}, bf16[128,768]{1,0:T(8,128)(2,1)S(1)}, u32[]{:S(2)}, u32[]{:S(2)}) collective-permute-start(bf16[128,768]{1,0:T(8,128)(2,1)S(1)} %get-tuple-element.31), channel_id=1, source_target_pairs={{0,8},{4,12},{8,0},{12,4},{1,9},{5,13},{9,1},{13,5},{2,10},{6,14},... | collective-permute-start | bytes 589832 | tf_op jit(solution)/shard_map/ppermute | solution.py:384
  51.3 0.0 collective-permute-done.7.refs_2_
  51.3 1.9 %collective-permute-start.21 = (bf16[256,640]{1,0:T(8,128)(2,1)S(1)}, bf16[256,640]{1,0:T(8,128)(2,1)S(1)}, u32[]{:S(2)}, u32[]{:S(2)}) collective-permute-start(bf16[256,640]{1,0:T(8,128)(2,1)S(1)} %bitcast.9), channel_id=1, source_target_pairs={{1,0},{2,1},{3,2},{4,3},{5,4},{6,5},{7,6},{8,7},{9,8},{10,9},{11,1... | collective-permute-start | bytes 983048 | tf_op jit(solution)/shard_map/ppermute | solution.py:348
  53.2 0.0 collective-permute-done.8.refs_3_
  53.2 4.8 %collective-permute-start.22 = (bf16[256,640]{1,0:T(8,128)(2,1)S(1)}, bf16[256,640]{1,0:T(8,128)(2,1)S(1)}, u32[]{:S(2)}, u32[]{:S(2)}) collective-permute-start(bf16[256,640]{1,0:T(8,128)(2,1)S(1)} %bitcast.10), channel_id=1, source_target_pairs={{0,1},{1,2},{2,3},{3,4},{4,5},{5,6},{6,7},{7,8},{8,9},{9,10},{10,1... | collective-permute-start | bytes 983048 | tf_op jit(solution)/shard_map/ppermute | solution.py:347
  58.0 0.0 collective-permute-done.12.refs_5_
  58.0 0.0 collective-permute-done.13.refs_6_
  58.0 0.0 collective-permute-done.14.refs_7_
  58.1 0.0 copy-done.6
  58.1 0.0 copy-done.10
  58.1 0.0 copy-done.11
  58.1 0.0 copy-start.1
  58.1 0.0 copy-start.2
  58.1 1.5 %shard_map.150 = (bf16[256,640]{1,0:T(8,128)(2,1)S(1)}, f32[8,128]{1,0:T(8,128)S(1)}) custom-call(bf16[128,768]{1,0:T(8,128)(2,1)S(1)} %get-tuple-element.24.refs_0_, bf16[128,768]{1,0:T(8,128)(2,1)S(1)} %collective-permute-done.6.refs_1_, bf16[128,768]{1,0:T(8,128)(2,1)S(1)} %collective-permute-done.7.refs_2_, ...), custom_call_target="tpu_custom_call" | custom-call | flops 6000000000 | bytes 1000000 | tf_op jit(solution)/shard_map/pallas_call | solution.py:282
  59.6 0.4 collective-permute-start.15
  60.0 1.7 %collective-permute-start.16 = (f32[8,128]{1,0:T(8,128)S(1)}, f32[8,128]{1,0:T(8,128)S(1)}, u32[]{:S(2)}, u32[]{:S(2)}) collective-permute-start(f32[8,128]{1,0:T(8,128)S(1)} %get-tuple-element.33.refs_0_), channel_id=1, source_target_pairs={{0,12},{4,0},{8,4},{12,8},{1,13},{5,1},{9,5},{13,9},{2,14},{6,2},{... | collective-permute-start | bytes 12296 | tf_op jit(solution)/shard_map/ppermute | solution.py:409
  61.7 2.2 %collective-permute-start.17 = (f32[8,128]{1,0:T(8,128)S(1)}, f32[8,128]{1,0:T(8,128)S(1)}, u32[]{:S(2)}, u32[]{:S(2)}) collective-permute-start(f32[8,128]{1,0:T(8,128)S(1)} %get-tuple-element.33.refs_0_), channel_id=1, source_target_pairs={{0,8},{4,12},{8,0},{12,4},{1,9},{5,13},{9,1},{13,5},{2,10},{6,14},... | collective-permute-start | bytes 12296 | tf_op jit(solution)/shard_map/ppermute | solution.py:409
  63.9 7.0 %collective-permute-done.22.x_ref = bf16[256,640]{1,0:T(8,128)(2,1)S(1)} collective-permute-done((bf16[256,640]{1,0:T(8,128)(2,1)S(1)}, bf16[256,640]{1,0:T(8,128)(2,1)S(1)}, u32[]{:S(2)}, u32[]{:S(2)}) %collective-permute-start.22) | collective-permute-done | bytes 327712 | tf_op jit(solution)/shard_map/ppermute | solution.py:347
  71.0 0.0 copy-start.4
  71.0 1.0 %shard_map.152.above_ref = f32[256,640]{1,0:T(8,128)S(1)} custom-call(bf16[256,640]{1,0:T(8,128)(2,1)S(1)} %collective-permute-done.22.x_ref, bf16[3,3,640,640]{3,2,1,0:T(8,128)(2,1)S(1)} %get-tuple-element.34.w_ref, f32[640]{0:T(1024)S(1)} %copy-done.2, f32[2,640]{1,0:T(2,128)S(1)} %copy-done.1), custom_call_target="tpu_custom_call" | custom-call | flops 629145600 | bytes 1000000 | tf_op jit(solution)/shard_map/pallas_call | solution.py:282
  72.0 0.0 collective-permute-done.15.refs_1_
  72.0 0.0 collective-permute-done.16.refs_2_
  72.0 0.0 collective-permute-done.17.refs_3_
  72.0 0.1 collective-permute-start.18
  72.1 4.1 %collective-permute-start.19 = (f32[8,128]{1,0:T(8,128)S(1)}, f32[8,128]{1,0:T(8,128)S(1)}, u32[]{:S(2)}, u32[]{:S(2)}) collective-permute-start(f32[8,128]{1,0:T(8,128)S(1)} %shard_map.151.s0_ref), channel_id=1, source_target_pairs={{0,3},{1,0},{2,1},{3,2},{4,7},{5,4},{6,5},{7,6},{8,11},{9,8},{10,9... | collective-permute-start | bytes 12296 | tf_op jit(solution)/shard_map/ppermute | solution.py:411
  76.2 1.7 %collective-permute-start.20 = (f32[8,128]{1,0:T(8,128)S(1)}, f32[8,128]{1,0:T(8,128)S(1)}, u32[]{:S(2)}, u32[]{:S(2)}) collective-permute-start(f32[8,128]{1,0:T(8,128)S(1)} %shard_map.151.s0_ref), channel_id=1, source_target_pairs={{0,2},{1,3},{2,0},{3,1},{4,6},{5,7},{6,4},{7,5},{8,10},{9,11},{10,... | collective-permute-start | bytes 12296 | tf_op jit(solution)/shard_map/ppermute | solution.py:411
  77.9 0.0 collective-permute-done.21.x_ref
  77.9 1.0 %shard_map.153.rim_ref = f32[256,640]{1,0:T(8,128)S(1)} custom-call(bf16[256,640]{1,0:T(8,128)(2,1)S(1)} %collective-permute-done.21.x_ref, bf16[3,3,640,640]{3,2,1,0:T(8,128)(2,1)S(1)} %get-tuple-element.34.w_ref, f32[256,640]{1,0:T(8,128)S(1)} %shard_map.152.above_ref), custom_call_target="tpu_custom_call" | custom-call | flops 629145600 | bytes 1000000 | tf_op jit(solution)/shard_map/pallas_call | solution.py:282
  78.9 0.0 collective-permute-done.18.s1_ref
  79.0 0.0 collective-permute-done.19.s2_ref
  79.0 4.8 %collective-permute-done.20.s3_ref = f32[8,128]{1,0:T(8,128)S(1)} collective-permute-done((f32[8,128]{1,0:T(8,128)S(1)}, f32[8,128]{1,0:T(8,128)S(1)}, u32[]{:S(2)}, u32[]{:S(2)}) %collective-permute-start.20) | collective-permute-done | bytes 4128 | tf_op jit(solution)/shard_map/ppermute | solution.py:411
  83.7 2.1 %shard_map.154 = bf16[256,640]{1,0:T(8,128)(2,1)} custom-call(bf16[256,640]{1,0:T(8,128)(2,1)S(1)} %get-tuple-element.32.res_ref, f32[8,128]{1,0:T(8,128)S(1)} %shard_map.151.s0_ref, f32[8,128]{1,0:T(8,128)S(1)} %collective-permute-done.18.s1_ref, f32[8,128]{1,0:T(8,128)S(1)} %collective-permute-done.19.s2_ref, f32[8,128]{1,0:T(8,128)S(1)} %collective-permute-done.20.s3_ref, ...), custom_call_target="tpu_custom_call" | custom-call | flops 629145600 | bytes 1000000 | tf_op jit(solution)/shard_map/pallas_call | solution.py:282
  (18 shorter events, 0.0 us)
Async XLA Ops:
  0.0 7.0 %copy-start.5 = (bf16[640,1920]{1,0:T(8,128)(2,1)S(1)}, bf16[640,1920]{1,0:T(8,128)(2,1)}, u32[]{:S(2)}) copy-start(bf16[640,1920]{1,0:T(8,128)(2,1)} %wv_ref.3) | copy-start | bytes 7372804
  0.0 7.0 %copy-start.7 = (bf16[2,1,128,640]{3,2,1,0:T(8,128)(2,1)S(1)}, bf16[2,1,128,640]{3,2,1,0:T(8,128)(2,1)}, u32[]{:S(2)}) copy-start(bf16[2,1,128,640]{3,2,1,0:T(8,128)(2,1)} %param.15) | copy-start | bytes 983044
  0.0 7.0 %copy-start.8 = (f32[640]{0:T(1024)S(1)}, f32[640]{0:T(1024)}, u32[]{:S(2)}) copy-start(f32[640]{0:T(1024)} %gain_ref.4) | copy-start | bytes 7684
  0.0 7.0 %copy-start.9 = (f32[640]{0:T(1024)S(1)}, f32[640]{0:T(1024)}, u32[]{:S(2)}) copy-start(f32[640]{0:T(1024)} %bias_ref.5) | copy-start | bytes 7684
  1.4 13.2 %collective-permute-start.3 = (bf16[128,640]{1,0:T(8,128)(2,1)S(1)}, bf16[128,640]{1,0:T(8,128)(2,1)S(1)}, u32[]{:S(2)}, u32[]{:S(2)}) collective-permute-start(bf16[128,640]{1,0:T(8,128)(2,1)S(1)} %get-tuple-element.21.refs_1_), channel_id=1, source_target_pairs={{0,1},{1,2},{2,3},{3,0},{4,5},{5,6},{6,7},{7,4},{8,9},{9,10},{10,1... | collective-permute-start | bytes 491528 | tf_op jit(solution)/shard_map/ppermute | solution.py:319
  4.8 12.2 %collective-permute-start.5 = (bf16[128,640]{1,0:T(8,128)(2,1)S(1)}, bf16[128,640]{1,0:T(8,128)(2,1)S(1)}, u32[]{:S(2)}, u32[]{:S(2)}) collective-permute-start(bf16[128,640]{1,0:T(8,128)(2,1)S(1)} %get-tuple-element.21.refs_1_), channel_id=1, source_target_pairs={{0,3},{1,0},{2,1},{3,2},{4,7},{5,4},{6,5},{7,6},{8,11},{9,8},{10,9... | collective-permute-start | bytes 491528 | tf_op jit(solution)/shard_map/ppermute | solution.py:319
  7.7 15.3 %collective-permute-start = (bf16[256,640]{1,0:T(8,128)(2,1)S(1)}, bf16[256,640]{1,0:T(8,128)(2,1)S(1)}, u32[]{:S(2)}, u32[]{:S(2)}) collective-permute-start(bf16[256,640]{1,0:T(8,128)(2,1)S(1)} %get-tuple-element.20.q0_ref), channel_id=1, source_target_pairs={{0,4},{4,8},{8,12},{12,0},{1,5},{5,9},{9,13},{13,1},{2,6},{6,10},{... | collective-permute-start | bytes 983048 | tf_op jit(solution)/shard_map/ppermute | solution.py:331
  9.4 16.9 %collective-permute-start.1 = (bf16[256,640]{1,0:T(8,128)(2,1)S(1)}, bf16[256,640]{1,0:T(8,128)(2,1)S(1)}, u32[]{:S(2)}, u32[]{:S(2)}) collective-permute-start(bf16[256,640]{1,0:T(8,128)(2,1)S(1)} %get-tuple-element.20.q0_ref), channel_id=1, source_target_pairs={{0,12},{4,0},{8,4},{12,8},{1,13},{5,1},{9,5},{13,9},{2,14},{6,2},{... | collective-permute-start | bytes 983048 | tf_op jit(solution)/shard_map/ppermute | solution.py:331
  9.8 16.5 %collective-permute-start.2 = (bf16[256,640]{1,0:T(8,128)(2,1)S(1)}, bf16[256,640]{1,0:T(8,128)(2,1)S(1)}, u32[]{:S(2)}, u32[]{:S(2)}) collective-permute-start(bf16[256,640]{1,0:T(8,128)(2,1)S(1)} %get-tuple-element.20.q0_ref), channel_id=1, source_target_pairs={{0,8},{4,12},{8,0},{12,4},{1,9},{5,13},{9,1},{13,5},{2,10},{6,14},... | collective-permute-start | bytes 983048 | tf_op jit(solution)/shard_map/ppermute | solution.py:331
  14.6 7.5 %collective-permute-start.10 = (bf16[128,640]{1,0:T(8,128)(2,1)S(1)}, bf16[128,640]{1,0:T(8,128)(2,1)S(1)}, u32[]{:S(2)}, u32[]{:S(2)}) collective-permute-start(bf16[128,640]{1,0:T(8,128)(2,1)S(1)} %get-tuple-element.23.refs_2_), channel_id=1, source_target_pairs={{0,3},{1,0},{2,1},{3,2},{4,7},{5,4},{6,5},{7,6},{8,11},{9,8},{10,9... | collective-permute-start | bytes 491528 | tf_op jit(solution)/shard_map/ppermute | solution.py:319
  17.0 13.4 %collective-permute-start.4 = (bf16[128,640]{1,0:T(8,128)(2,1)S(1)}, bf16[128,640]{1,0:T(8,128)(2,1)S(1)}, u32[]{:S(2)}, u32[]{:S(2)}) collective-permute-start(bf16[128,640]{1,0:T(8,128)(2,1)S(1)} %collective-permute-done.3.z1_ref), channel_id=1, source_target_pairs={{0,1},{1,2},{2,3},{3,0},{4,5},{5,6},{6,7},{7,4},{8,9},{9,10},{10,1... | collective-permute-start | bytes 491528 | tf_op jit(solution)/shard_map/ppermute | solution.py:320
  22.2 19.9 %collective-permute-start.9 = (bf16[128,640]{1,0:T(8,128)(2,1)S(1)}, bf16[128,640]{1,0:T(8,128)(2,1)S(1)}, u32[]{:S(2)}, u32[]{:S(2)}) collective-permute-start(bf16[128,640]{1,0:T(8,128)(2,1)S(1)} %get-tuple-element.23.refs_2_), channel_id=1, source_target_pairs={{0,1},{1,2},{2,3},{3,0},{4,5},{5,6},{6,7},{7,4},{8,9},{9,10},{10,1... | collective-permute-start | bytes 491528 | tf_op jit(solution)/shard_map/ppermute | solution.py:319
  23.1 19.0 %collective-permute-start.11 = (bf16[128,640]{1,0:T(8,128)(2,1)S(1)}, bf16[128,640]{1,0:T(8,128)(2,1)S(1)}, u32[]{:S(2)}, u32[]{:S(2)}) collective-permute-start(bf16[128,640]{1,0:T(8,128)(2,1)S(1)} %collective-permute-done.10.z3_ref), channel_id=1, source_target_pairs={{0,3},{1,0},{2,1},{3,2},{4,7},{5,4},{6,5},{7,6},{8,11},{9,8},{10,9... | collective-permute-start | bytes 491528 | tf_op jit(solution)/shard_map/ppermute | solution.py:320
  36.2 13.8 %collective-permute-start.6 = (bf16[128,768]{1,0:T(8,128)(2,1)S(1)}, bf16[128,768]{1,0:T(8,128)(2,1)S(1)}, u32[]{:S(2)}, u32[]{:S(2)}) collective-permute-start(bf16[128,768]{1,0:T(8,128)(2,1)S(1)} %get-tuple-element.25), channel_id=1, source_target_pairs={{0,12},{4,0},{8,4},{12,8},{1,13},{5,1},{9,5},{13,9},{2,14},{6,2},{... | collective-permute-start | bytes 589832 | tf_op jit(solution)/shard_map/ppermute | solution.py:384
  37.5 13.8 %collective-permute-start.7 = (bf16[128,768]{1,0:T(8,128)(2,1)S(1)}, bf16[128,768]{1,0:T(8,128)(2,1)S(1)}, u32[]{:S(2)}, u32[]{:S(2)}) collective-permute-start(bf16[128,768]{1,0:T(8,128)(2,1)S(1)} %get-tuple-element.26), channel_id=1, source_target_pairs={{0,4},{4,8},{8,12},{12,0},{1,5},{5,9},{9,13},{13,1},{2,6},{6,10},{... | collective-permute-start | bytes 589832 | tf_op jit(solution)/shard_map/ppermute | solution.py:384
  38.3 13.0 %copy-start.12 = (bf16[2,1,128,640]{3,2,1,0:T(8,128)(2,1)S(1)}, bf16[2,1,128,640]{3,2,1,0:T(8,128)(2,1)}, u32[]{:S(2)}) copy-start(bf16[2,1,128,640]{3,2,1,0:T(8,128)(2,1)} %param.17) | copy-start | bytes 983044
  38.3 19.8 %copy-start.6 = (bf16[640,640]{1,0:T(8,128)(2,1)S(1)}, bf16[640,640]{1,0:T(8,128)(2,1)}, u32[]{:S(2)}) copy-start(bf16[640,640]{1,0:T(8,128)(2,1)} %refs_9_.1) | copy-start | bytes 2457604
  38.3 19.8 %copy-start.10 = (bf16[128,640]{1,0:T(8,128)(2,1)S(1)}, bf16[128,640]{1,0:T(8,128)(2,1)}, u32[]{:S(2)}) copy-start(bf16[128,640]{1,0:T(8,128)(2,1)} %constant.6.clone.refs_10_) | copy-start | bytes 491524
  38.3 19.8 %copy-start.11 = (bf16[640,128]{1,0:T(8,128)(2,1)S(1)}, bf16[640,128]{1,0:T(8,128)(2,1)}, u32[]{:S(2)}) copy-start(bf16[640,128]{1,0:T(8,128)(2,1)} %constant.7.clone.refs_11_) | copy-start | bytes 491524
  38.3 14.9 %collective-permute-start.8 = (bf16[128,768]{1,0:T(8,128)(2,1)S(1)}, bf16[128,768]{1,0:T(8,128)(2,1)S(1)}, u32[]{:S(2)}, u32[]{:S(2)}) collective-permute-start(bf16[128,768]{1,0:T(8,128)(2,1)S(1)} %get-tuple-element.27), channel_id=1, source_target_pairs={{0,8},{4,12},{8,0},{12,4},{1,9},{5,13},{9,1},{13,5},{2,10},{6,14},... | collective-permute-start | bytes 589832 | tf_op jit(solution)/shard_map/ppermute | solution.py:384
  47.9 10.1 %collective-permute-start.12 = (bf16[128,768]{1,0:T(8,128)(2,1)S(1)}, bf16[128,768]{1,0:T(8,128)(2,1)S(1)}, u32[]{:S(2)}, u32[]{:S(2)}) collective-permute-start(bf16[128,768]{1,0:T(8,128)(2,1)S(1)} %get-tuple-element.29), channel_id=1, source_target_pairs={{0,12},{4,0},{8,4},{12,8},{1,13},{5,1},{9,5},{13,9},{2,14},{6,2},{... | collective-permute-start | bytes 589832 | tf_op jit(solution)/shard_map/ppermute | solution.py:384
  48.1 9.9 %collective-permute-start.13 = (bf16[128,768]{1,0:T(8,128)(2,1)S(1)}, bf16[128,768]{1,0:T(8,128)(2,1)S(1)}, u32[]{:S(2)}, u32[]{:S(2)}) collective-permute-start(bf16[128,768]{1,0:T(8,128)(2,1)S(1)} %get-tuple-element.30), channel_id=1, source_target_pairs={{0,4},{4,8},{8,12},{12,0},{1,5},{5,9},{9,13},{13,1},{2,6},{6,10},{... | collective-permute-start | bytes 589832 | tf_op jit(solution)/shard_map/ppermute | solution.py:384
  50.0 8.1 %collective-permute-start.14 = (bf16[128,768]{1,0:T(8,128)(2,1)S(1)}, bf16[128,768]{1,0:T(8,128)(2,1)S(1)}, u32[]{:S(2)}, u32[]{:S(2)}) collective-permute-start(bf16[128,768]{1,0:T(8,128)(2,1)S(1)} %get-tuple-element.31), channel_id=1, source_target_pairs={{0,8},{4,12},{8,0},{12,4},{1,9},{5,13},{9,1},{13,5},{2,10},{6,14},... | collective-permute-start | bytes 589832 | tf_op jit(solution)/shard_map/ppermute | solution.py:384
  51.3 26.7 %collective-permute-start.21 = (bf16[256,640]{1,0:T(8,128)(2,1)S(1)}, bf16[256,640]{1,0:T(8,128)(2,1)S(1)}, u32[]{:S(2)}, u32[]{:S(2)}) collective-permute-start(bf16[256,640]{1,0:T(8,128)(2,1)S(1)} %bitcast.9), channel_id=1, source_target_pairs={{1,0},{2,1},{3,2},{4,3},{5,4},{6,5},{7,6},{8,7},{9,8},{10,9},{11,1... | collective-permute-start | bytes 983048 | tf_op jit(solution)/shard_map/ppermute | solution.py:348
  53.2 17.8 %collective-permute-start.22 = (bf16[256,640]{1,0:T(8,128)(2,1)S(1)}, bf16[256,640]{1,0:T(8,128)(2,1)S(1)}, u32[]{:S(2)}, u32[]{:S(2)}) collective-permute-start(bf16[256,640]{1,0:T(8,128)(2,1)S(1)} %bitcast.10), channel_id=1, source_target_pairs={{0,1},{1,2},{2,3},{3,4},{4,5},{5,6},{6,7},{7,8},{8,9},{9,10},{10,1... | collective-permute-start | bytes 983048 | tf_op jit(solution)/shard_map/ppermute | solution.py:347
  58.1 12.9 %copy-start.1 = (f32[2,640]{1,0:T(2,128)S(1)}, f32[2,640]{1,0:T(2,128)}, u32[]{:S(2)}) copy-start(f32[2,640]{1,0:T(2,128)} %shift_ref.1) | copy-start | bytes 15364
  58.1 12.9 %copy-start.2 = (f32[640]{0:T(1024)S(1)}, f32[640]{0:T(1024)}, u32[]{:S(2)}) copy-start(f32[640]{0:T(1024)} %bias_ref.6) | copy-start | bytes 7684
  59.6 12.3 %collective-permute-start.15 = (f32[8,128]{1,0:T(8,128)S(1)}, f32[8,128]{1,0:T(8,128)S(1)}, u32[]{:S(2)}, u32[]{:S(2)}) collective-permute-start(f32[8,128]{1,0:T(8,128)S(1)} %get-tuple-element.33.refs_0_), channel_id=1, source_target_pairs={{0,4},{4,8},{8,12},{12,0},{1,5},{5,9},{9,13},{13,1},{2,6},{6,10},{... | collective-permute-start | bytes 12296 | tf_op jit(solution)/shard_map/ppermute | solution.py:409
  60.0 12.0 %collective-permute-start.16 = (f32[8,128]{1,0:T(8,128)S(1)}, f32[8,128]{1,0:T(8,128)S(1)}, u32[]{:S(2)}, u32[]{:S(2)}) collective-permute-start(f32[8,128]{1,0:T(8,128)S(1)} %get-tuple-element.33.refs_0_), channel_id=1, source_target_pairs={{0,12},{4,0},{8,4},{12,8},{1,13},{5,1},{9,5},{13,9},{2,14},{6,2},{... | collective-permute-start | bytes 12296 | tf_op jit(solution)/shard_map/ppermute | solution.py:409
  61.7 10.3 %collective-permute-start.17 = (f32[8,128]{1,0:T(8,128)S(1)}, f32[8,128]{1,0:T(8,128)S(1)}, u32[]{:S(2)}, u32[]{:S(2)}) collective-permute-start(f32[8,128]{1,0:T(8,128)S(1)} %get-tuple-element.33.refs_0_), channel_id=1, source_target_pairs={{0,8},{4,12},{8,0},{12,4},{1,9},{5,13},{9,1},{13,5},{2,10},{6,14},... | collective-permute-start | bytes 12296 | tf_op jit(solution)/shard_map/ppermute | solution.py:409
  71.0 12.8 %copy-start = (bf16[128,640]{1,0:T(8,128)(2,1)S(1)}, bf16[128,640]{1,0:T(8,128)(2,1)}, u32[]{:S(2)}) copy-start(bf16[128,640]{1,0:T(8,128)(2,1)} %constant.8.clone.scatter_ref) | copy-start | bytes 491524
  71.0 12.8 %copy-start.3 = (f32[640]{0:T(1024)S(1)}, f32[640]{0:T(1024)}, u32[]{:S(2)}) copy-start(f32[640]{0:T(1024)} %gain_ref.5) | copy-start | bytes 7684
  71.0 12.8 %copy-start.4 = (f32[640]{0:T(1024)S(1)}, f32[640]{0:T(1024)}, u32[]{:S(2)}) copy-start(f32[640]{0:T(1024)} %bias_ref.7) | copy-start | bytes 7684
  72.0 6.9 %collective-permute-start.18 = (f32[8,128]{1,0:T(8,128)S(1)}, f32[8,128]{1,0:T(8,128)S(1)}, u32[]{:S(2)}, u32[]{:S(2)}) collective-permute-start(f32[8,128]{1,0:T(8,128)S(1)} %shard_map.151.s0_ref), channel_id=1, source_target_pairs={{0,1},{1,2},{2,3},{3,0},{4,5},{5,6},{6,7},{7,4},{8,9},{9,10},{10,1... | collective-permute-start | bytes 12296 | tf_op jit(solution)/shard_map/ppermute | solution.py:411
  72.1 6.9 %collective-permute-start.19 = (f32[8,128]{1,0:T(8,128)S(1)}, f32[8,128]{1,0:T(8,128)S(1)}, u32[]{:S(2)}, u32[]{:S(2)}) collective-permute-start(f32[8,128]{1,0:T(8,128)S(1)} %shard_map.151.s0_ref), channel_id=1, source_target_pairs={{0,3},{1,0},{2,1},{3,2},{4,7},{5,4},{6,5},{7,6},{8,11},{9,8},{10,9... | collective-permute-start | bytes 12296 | tf_op jit(solution)/shard_map/ppermute | solution.py:411
  76.2 7.5 %collective-permute-start.20 = (f32[8,128]{1,0:T(8,128)S(1)}, f32[8,128]{1,0:T(8,128)S(1)}, u32[]{:S(2)}, u32[]{:S(2)}) collective-permute-start(f32[8,128]{1,0:T(8,128)S(1)} %shard_map.151.s0_ref), channel_id=1, source_target_pairs={{0,2},{1,3},{2,0},{3,1},{4,6},{5,7},{6,4},{7,5},{8,10},{9,11},{10,... | collective-permute-start | bytes 12296 | tf_op jit(solution)/shard_map/ppermute | solution.py:411
